TPU v7x, 32 devices: a whole 2x2x4 slice. The times are simulated.
32 devices in a mesh: img: 4 (over y, core), depth: 8 (over z, x).
Axes of the slice: x: 2, y: 2, z: 4, core: 2. Of those that a mesh axis runs over, the one named last changes fastest.
Arguments:
- counts: int32 [256, 256, 512], P('depth', 'img'), may hold values from 0 to 5, as said below
Outputs:
- image: float32 [4, 256, 512], P(None, ('img', 'depth'))
Inputs may be any that keep to these rules, and one draw needn't show every extreme that they name: `counts`: whole numbers of atoms.
All inputs are finite; a program needn't handle non-finite values.
Results may differ from a plain program's by a relative error of at most 0.0003.
Values sent between devices are 32-bit elements; how exact they have to be, the bound alone decides.
No kernel may reach another device: no remote copies, remote signals or barrier semaphores. Data moves between devices by JAX's collectives and lax.ppermute only.
A program may use at most 64 MiB of HBM per device.

v0:
```python
import math

import jax
import jax.numpy as jnp
from jax import lax
from jax.sharding import PartitionSpec as P

gauss_taps = [
    math.exp(-offset * offset / 8.0)
    / sum((math.exp(-other * other / 8.0) for other in range(-4, 5)))
    for offset in range(-4, 5)
]
light_z = 0.48
light_x = 0.6
light_y = 0.64


def extended(block, sides, width):
    for axis, dim in sides:
        count = lax.axis_size(axis)
        forward = [(i, i + 1) for i in range(count - 1)]
        backward = [(target, source) for source, target in forward]
        low = lax.ppermute(
            lax.slice_in_dim(block, block.shape[dim] - width, None, axis=dim), axis, forward
        )
        high = lax.ppermute(lax.slice_in_dim(block, 0, width, axis=dim), axis, backward)
        block = jnp.concatenate([low, block, high], axis=dim)
    return block


def smooth_valid(values, axis):
    length = values.shape[axis] - 8
    total = gauss_taps[0] * lax.slice_in_dim(values, 0, length, axis=axis)
    for offset in range(1, 9):
        total = total + gauss_taps[offset] * lax.slice_in_dim(
            values, offset, offset + length, axis=axis
        )
    return total


def smooth_last(values):
    widths = [(0, 0)] * (values.ndim - 1) + [(4, 4)]
    return smooth_valid(jnp.pad(values, widths), values.ndim - 1)


def render_terms(smooth_ext, depth_total):
    smoothed = smooth_ext[1:-1, 1:-1, :]
    grad_z = 0.5 * (smooth_ext[2:, 1:-1, :] - smooth_ext[:-2, 1:-1, :])
    grad_x = 0.5 * (smooth_ext[1:-1, 2:, :] - smooth_ext[1:-1, :-2, :])
    padded = jnp.pad(smoothed, ((0, 0), (0, 0), (1, 1)))
    grad_y = 0.5 * (padded[:, :, 2:] - padded[:, :, :-2])
    shading = 0.55 + 0.45 * jnp.tanh(3.0 * (light_z * grad_z + light_x * grad_x + light_y * grad_y))
    gradient_sq = grad_z * grad_z + grad_x * grad_x + grad_y * grad_y
    optical = (
        1.5
        / depth_total
        * smoothed
        * smoothed
        / (1.0 + smoothed * smoothed)
        * (1.0 + 4.0 * gradient_sq)
    )
    sigma_red = jax.nn.sigmoid(2.0 * (smoothed - 2.5))
    red_light = shading * sigma_red
    green_light = shading * jnp.exp(-((smoothed - 2.5) ** 2))
    blue_light = shading * (1.0 - sigma_red)
    return (optical, red_light, green_light, blue_light)


def integrate(optical, red_light, green_light, blue_light):
    before = jnp.cumsum(optical, axis=0) - optical
    weight = jnp.exp(-before) * (1.0 - jnp.exp(-optical))
    colors = jnp.stack(
        [
            jnp.sum(weight * red_light, 0),
            jnp.sum(weight * green_light, 0),
            jnp.sum(weight * blue_light, 0),
        ],
        0,
    )
    transmit = jnp.exp(-jnp.sum(optical, 0))
    return (colors, transmit)


def local(counts):
    density = smooth_last(counts.astype(jnp.float32))
    slab_depth, tile_rows, columns = density.shape
    depth_count = lax.axis_size("depth")
    depth_total = slab_depth * depth_count
    smooth_x = smooth_valid(extended(density, (("img", 1),), 4), 1)
    smoothed = smooth_valid(extended(smooth_x, (("depth", 0),), 4), 0)
    smooth_ext = extended(smoothed, (("depth", 0), ("img", 1)), 1)
    colors, transmit = integrate(*render_terms(smooth_ext, depth_total))
    layers = jnp.concatenate([colors, transmit[None]], 0)
    rows_owned = tile_rows // depth_count
    pieces = layers.reshape(4, depth_count, rows_owned, columns)
    arrived = lax.all_to_all(pieces, "depth", split_axis=1, concat_axis=1, tiled=True)
    running = jnp.cumprod(arrived[3], axis=0)
    exclusive = jnp.concatenate([jnp.ones_like(running[:1]), running[:-1]], 0)
    shaded = jnp.sum(exclusive[None] * arrived[:3], axis=1)
    result = jnp.concatenate([shaded, running[-1:]], 0)
    return jnp.concatenate([result[:3], 1.0 - result[3:]], 0)


def solution(mesh):
    in_specs = (P("depth", "img", None),)
    out_specs = P(None, ("img", "depth"), None)
    return jax.shard_map(local, mesh=mesh, in_specs=in_specs, out_specs=out_specs, check_vma=False)
```

profile of v0, /device:TPU:0, one launch (start us, length us, event | category | flops | bytes accessed | tf_op | source)
XLA Modules:
  0.0 130.0 jit_solution(4387701367737960592)
XLA Ops:
  0.0 4.9 %convert_element_type.7 = f32[32,64,512]{2,1,0:T(8,128)} convert(s32[32,64,512]{2,1,0:T(8,128)} %param.1) | non-fusion elementwise | flops 1048576 | bytes 8388608 | tf_op jit(solution)/shard_map/convert_element_type | solution.py:85
  4.9 22.1 %fusion.51 = f32[32,64,512]{2,1,0:T(8,128)S(1)} fusion(f32[32,64,512]{2,1,0:T(8,128)} %convert_element_type.7), kind=kLoop, calls=%fused_computation.86 | loop fusion | flops 17825792 | bytes 8388608 | tf_op jit(solution)/shard_map/add | solution.py:35
  27.0 0.1 fusion.69
  27.1 2.4 %collective-permute-start = (f32[32,4,512]{2,1,0:T(4,128)S(1)}, f32[32,4,512]{2,1,0:T(4,128)S(1)}, u32[]{:S(2)}, u32[]{:S(2)}) collective-permute-start(f32[32,4,512]{2,1,0:T(4,128)S(1)} %get-tuple-element.15), channel_id=1, source_target_pairs={{0,8},{8,16},{16,24},{1,9},{9,17},{17,25},{2,10},{10,18},{18,26},{... | collective-permute-start | bytes 786440 | tf_op jit(solution)/shard_map/ppermute | solution.py:23
  29.6 1.3 collective-permute-start.1
  30.9 4.2 %collective-permute-done.1 = f32[32,4,512]{2,1,0:T(4,128)S(1)} collective-permute-done((f32[32,4,512]{2,1,0:T(4,128)S(1)}, f32[32,4,512]{2,1,0:T(4,128)S(1)}, u32[]{:S(2)}, u32[]{:S(2)}) %collective-permute-start.1) | collective-permute-done | bytes 262176 | tf_op jit(solution)/shard_map/ppermute | solution.py:26
  35.1 5.4 %fusion.23 = f32[32,64,512]{2,1,0:T(8,128)S(1)} fusion(f32[32,64,512]{2,1,0:T(8,128)S(1)} %fusion.51, f32[32,4,512]{2,1,0:T(4,128)S(1)} %collective-permute-done.1, f32[32,4,512]{2,1,0:T(4,128)S(1)} %collective-permute-done), kind=kLoop, calls=%fused_computation.58 | loop fusion | flops 26214400 | bytes 8912896 | tf_op jit(solution)/shard_map/add | solution.py:35
  40.5 0.1 fusion.68
  40.6 3.4 %collective-permute-start.2 = (f32[4,64,512]{2,1,0:T(8,128)S(1)}, f32[4,64,512]{2,1,0:T(8,128)S(1)}, u32[]{:S(2)}, u32[]{:S(2)}) collective-permute-start(f32[4,64,512]{2,1,0:T(8,128)S(1)} %get-tuple-element.13), channel_id=1, source_target_pairs={{0,1},{1,2},{2,3},{3,4},{4,5},{5,6},{6,7},{8,9},{9,10},{10,11},{11... | collective-permute-start | bytes 1572872 | tf_op jit(solution)/shard_map/ppermute | solution.py:23
  44.0 1.3 collective-permute-start.3
  45.3 18.4 %collective-permute-done.2 = f32[4,64,512]{2,1,0:T(8,128)S(1)} collective-permute-done((f32[4,64,512]{2,1,0:T(8,128)S(1)}, f32[4,64,512]{2,1,0:T(8,128)S(1)}, u32[]{:S(2)}, u32[]{:S(2)}) %collective-permute-start.2) | collective-permute-done | bytes 524320 | tf_op jit(solution)/shard_map/ppermute | solution.py:23
  63.7 4.8 %fusion.3 = f32[32,64,512]{2,1,0:T(8,128)S(1)} fusion(f32[32,64,512]{2,1,0:T(8,128)S(1)} %fusion.23, f32[4,64,512]{2,1,0:T(8,128)S(1)} %collective-permute-done.3, f32[4,64,512]{2,1,0:T(8,128)S(1)} %collective-permute-done.2), kind=kLoop, calls=%fused_computation.38 | loop fusion | flops 26214400 | bytes 9437184 | tf_op jit(solution)/shard_map/add | solution.py:35
  68.5 1.3 collective-permute-start.4
  69.8 5.0 %collective-permute-start.5 = (f32[1,64,512]{2,1,0:T(8,128)S(1)}, f32[1,64,512]{2,1,0:T(8,128)S(1)}, u32[]{:S(2)}, u32[]{:S(2)}) collective-permute-start(f32[1,64,512]{2,1,0:T(8,128)S(1)} %get-tuple-element.12), channel_id=1, source_target_pairs={{0,1},{1,2},{2,3},{3,4},{4,5},{5,6},{6,7},{8,9},{9,10},{10,11},{11... | collective-permute-start | bytes 393224 | tf_op jit(solution)/shard_map/ppermute | solution.py:23
  74.9 1.0 collective-permute-done.4
  75.9 1.5 %collective-permute-done.5 = f32[1,64,512]{2,1,0:T(8,128)S(1)} collective-permute-done((f32[1,64,512]{2,1,0:T(8,128)S(1)}, f32[1,64,512]{2,1,0:T(8,128)S(1)}, u32[]{:S(2)}, u32[]{:S(2)}) %collective-permute-start.5) | collective-permute-done | bytes 131104 | tf_op jit(solution)/shard_map/ppermute | solution.py:23
  77.4 0.1 pad_maximum_fusion.15
  77.5 1.3 collective-permute-start.6
  78.8 7.2 %collective-permute-start.7 = (f32[34,1,512]{2,1,0:T(1,128)S(1)}, f32[34,1,512]{2,1,0:T(1,128)S(1)}, u32[]{:S(2)}, u32[]{:S(2)}) collective-permute-start(f32[34,1,512]{2,1,0:T(1,128)S(1)} %get-tuple-element.10), channel_id=1, source_target_pairs={{0,8},{8,16},{16,24},{1,9},{9,17},{17,25},{2,10},{10,18},{18,26},{... | collective-permute-start | bytes 208904 | tf_op jit(solution)/shard_map/ppermute | solution.py:23
  86.0 0.7 collective-permute-done.7
  86.7 4.3 %fusion.70 = f32[32,64,512]{2,1,0:T(8,128)S(1)} fusion(f32[32,64,512]{2,1,0:T(8,128)S(1)} %fusion.3, f32[1,64,512]{2,1,0:T(8,128)S(1)} %collective-permute-done.5, f32[1,64,512]{2,1,0:T(8,128)S(1)} %collective-permute-done.4, f32[34,1,512]{2,1,0:T(1,128)S(1)} %collective-permute-done.7, f32[34,1,512]{2,1,0:T(1,128)S(1)} %collective-permute-done.6), kind=kOutput, calls=%fused_computation.132 | output fusion | flops 60817408 | bytes 8790016 | tf_op jit(solution)/shard_map/jit(cumsum)/reduce_window_sum | solution.py:70
  91.0 14.8 %multiply_reduce_fusion.2 = (f32[64,512]{1,0:T(8,128)S(1)}, f32[64,512]{1,0:T(8,128)S(1)}, f32[64,512]{1,0:T(8,128)S(1)}, f32[64,512]{1,0:T(8,128)S(1)}) fusion(f32[32,64,512]{2,1,0:T(8,128)S(1)} %fusion.3, f32[32,64,512]{2,1,0:T(8,128)S(1)} %fusion.70, f32[1,64,512]{2,1,0:T(8,128)S(1)} %collective-permute-done.4, ...), kind=kLoop, calls=%fused_computation.114 | loop fusion | flops 61734912 | bytes 9314304 | tf_op jit(solution)/shard_map/reduce_sum | solution.py:74
  105.9 23.3 %all_to_all.5 = f32[4,8,8,512]{3,2,0,1:T(8,128)S(1)} all-to-all(f32[4,8,8,512]{3,2,0,1:T(8,128)S(1)} %pad_maximum_fusion.12), channel_id=1, replica_groups=mesh['img'=4,'depth'=8] {'depth'}, dimensions={1} | all-to-all | bytes 1048576 | tf_op jit(solution)/shard_map/all_to_all | solution.py:96
  129.3 0.6 pad_maximum_fusion.16
  (11 shorter events, 0.2 us)
Async XLA Ops:
  27.1 3.7 %collective-permute-start = (f32[32,4,512]{2,1,0:T(4,128)S(1)}, f32[32,4,512]{2,1,0:T(4,128)S(1)}, u32[]{:S(2)}, u32[]{:S(2)}) collective-permute-start(f32[32,4,512]{2,1,0:T(4,128)S(1)} %get-tuple-element.15), channel_id=1, source_target_pairs={{0,8},{8,16},{16,24},{1,9},{9,17},{17,25},{2,10},{10,18},{18,26},{... | collective-permute-start | bytes 786440 | tf_op jit(solution)/shard_map/ppermute | solution.py:23
  29.6 5.5 %collective-permute-start.1 = (f32[32,4,512]{2,1,0:T(4,128)S(1)}, f32[32,4,512]{2,1,0:T(4,128)S(1)}, u32[]{:S(2)}, u32[]{:S(2)}) collective-permute-start(f32[32,4,512]{2,1,0:T(4,128)S(1)} %get-tuple-element.16), channel_id=1, source_target_pairs={{8,0},{16,8},{24,16},{9,1},{17,9},{25,17},{10,2},{18,10},{26,18},{... | collective-permute-start | bytes 786440 | tf_op jit(solution)/shard_map/ppermute | solution.py:26
  40.6 23.1 %collective-permute-start.2 = (f32[4,64,512]{2,1,0:T(8,128)S(1)}, f32[4,64,512]{2,1,0:T(8,128)S(1)}, u32[]{:S(2)}, u32[]{:S(2)}) collective-permute-start(f32[4,64,512]{2,1,0:T(8,128)S(1)} %get-tuple-element.13), channel_id=1, source_target_pairs={{0,1},{1,2},{2,3},{3,4},{4,5},{5,6},{6,7},{8,9},{9,10},{10,11},{11... | collective-permute-start | bytes 1572872 | tf_op jit(solution)/shard_map/ppermute | solution.py:23
  44.0 19.7 %collective-permute-start.3 = (f32[4,64,512]{2,1,0:T(8,128)S(1)}, f32[4,64,512]{2,1,0:T(8,128)S(1)}, u32[]{:S(2)}, u32[]{:S(2)}) collective-permute-start(f32[4,64,512]{2,1,0:T(8,128)S(1)} %get-tuple-element.14), channel_id=1, source_target_pairs={{1,0},{2,1},{3,2},{4,3},{5,4},{6,5},{7,6},{9,8},{10,9},{11,10},{12... | collective-permute-start | bytes 1572872 | tf_op jit(solution)/shard_map/ppermute | solution.py:26
  68.5 7.3 %collective-permute-start.4 = (f32[1,64,512]{2,1,0:T(8,128)S(1)}, f32[1,64,512]{2,1,0:T(8,128)S(1)}, u32[]{:S(2)}, u32[]{:S(2)}) collective-permute-start(f32[1,64,512]{2,1,0:T(8,128)S(1)} %get-tuple-element.11), channel_id=1, source_target_pairs={{1,0},{2,1},{3,2},{4,3},{5,4},{6,5},{7,6},{9,8},{10,9},{11,10},{12... | collective-permute-start | bytes 393224 | tf_op jit(solution)/shard_map/ppermute | solution.py:26
  69.8 7.5 %collective-permute-start.5 = (f32[1,64,512]{2,1,0:T(8,128)S(1)}, f32[1,64,512]{2,1,0:T(8,128)S(1)}, u32[]{:S(2)}, u32[]{:S(2)}) collective-permute-start(f32[1,64,512]{2,1,0:T(8,128)S(1)} %get-tuple-element.12), channel_id=1, source_target_pairs={{0,1},{1,2},{2,3},{3,4},{4,5},{5,6},{6,7},{8,9},{9,10},{10,11},{11... | collective-permute-start | bytes 393224 | tf_op jit(solution)/shard_map/ppermute | solution.py:23
  77.5 8.5 %collective-permute-start.6 = (f32[34,1,512]{2,1,0:T(1,128)S(1)}, f32[34,1,512]{2,1,0:T(1,128)S(1)}, u32[]{:S(2)}, u32[]{:S(2)}) collective-permute-start(f32[34,1,512]{2,1,0:T(1,128)S(1)} %get-tuple-element.9), channel_id=1, source_target_pairs={{8,0},{16,8},{24,16},{9,1},{17,9},{25,17},{10,2},{18,10},{26,18},{... | collective-permute-start | bytes 208904 | tf_op jit(solution)/shard_map/ppermute | solution.py:26
  78.8 7.9 %collective-permute-start.7 = (f32[34,1,512]{2,1,0:T(1,128)S(1)}, f32[34,1,512]{2,1,0:T(1,128)S(1)}, u32[]{:S(2)}, u32[]{:S(2)}) collective-permute-start(f32[34,1,512]{2,1,0:T(1,128)S(1)} %get-tuple-element.10), channel_id=1, source_target_pairs={{0,8},{8,16},{16,24},{1,9},{9,17},{17,25},{2,10},{10,18},{18,26},{... | collective-permute-start | bytes 208904 | tf_op jit(solution)/shard_map/ppermute | solution.py:23
where the time goes:
time: 130 us
  other arithmetic  57.2 us (44%)
  waiting for transfers between devices  25.8 us (20%)
  starting transfers between devices  23.3 us (18%)
  blocking collectives  23.3 us (18%)
    add x3, other arithmetic, smooth_valid(): total + gauss_taps[offset] * lax.slice_in_dim(values, offset, offset + le...  32.3 us
    all_to_all x1, blocking collectives, local(): lax.all_to_all(pieces, 'depth', split_axis=1, concat_axis=1, tiled=True)  23.3 us
    ppermute x4, waiting for transfers between devices, extended(): lax.ppermute(lax.slice_in_dim(block, block.shape[dim] - width, None, axis...  20.6 us
    ppermute x4, starting transfers between devices, extended(): lax.ppermute(lax.slice_in_dim(block, block.shape[dim] - width, None, axis...  18.1 us
    reduce_sum x1, other arithmetic, integrate(): jnp.sum(weight * red_light, 0)  14.8 us
    ppermute x4, waiting for transfers between devices, extended(): lax.ppermute(lax.slice_in_dim(block, 0, width, axis=dim), axis, backward)  5.23 us
    ppermute x4, starting transfers between devices, extended(): lax.ppermute(lax.slice_in_dim(block, 0, width, axis=dim), axis, backward)  5.17 us
    convert_element_type x1, other arithmetic, local(): density = smooth_last(counts.astype(jnp.float32))  4.88 us
  transfers between devices with their start and end apart: 8, of which 5 were waited for; matrix products, arithmetic and copies ran while one was open for 0% of the time, Pallas kernels for 0%

commit v1 on v0

v1 whole, which is shorter than its diff:
```python
import functools
import math

import jax
import jax.numpy as jnp
import numpy as np
from jax import lax
from jax.experimental import pallas as pl
from jax.experimental.pallas import tpu as pltpu
from jax.sharding import PartitionSpec as P

gauss_taps = [
    math.exp(-offset * offset / 8.0)
    / sum((math.exp(-other * other / 8.0) for other in range(-4, 5)))
    for offset in range(-4, 5)
]
light_z = 0.48
light_x = 0.6
light_y = 0.64

REACH = 5
PAD = 8


def band(size):
    index = np.arange(size)
    apart = np.abs(index[:, None] - index[None, :])
    taps = np.array(gauss_taps[4:] + [0.0], np.float64)
    return taps[np.minimum(apart, 5)]


def split_terms(matrix):
    high = matrix.astype(jnp.bfloat16)
    low = (matrix - high.astype(np.float64)).astype(jnp.bfloat16)
    return high, low


def column_matrix(columns):
    return np.concatenate(split_terms(band(columns)), 0)


def row_matrix(rows):
    high, low = split_terms(band(rows))
    return np.concatenate([high, high, low], 1)


def smooth_plane(counts, by, lx):
    rows = counts[0].shape[0]
    exact = jnp.concatenate([c.astype(jnp.float32).astype(jnp.bfloat16) for c in counts], 0)
    half = by.shape[0] // 2
    wide = jnp.dot(exact, by[:half], preferred_element_type=jnp.float32) + jnp.dot(
        exact, by[half:], preferred_element_type=jnp.float32
    )
    high = wide.astype(jnp.bfloat16)
    low = (wide - high.astype(jnp.float32)).astype(jnp.bfloat16)
    planes = []
    for n in range(len(counts)):
        part = slice(n * rows, (n + 1) * rows)
        stacked = jnp.concatenate([high[part], low[part], high[part]], 0)
        planes.append(jnp.dot(lx, stacked, preferred_element_type=jnp.float32))
    return planes


def smooth_depth(read, k):
    total = gauss_taps[4] * read(k)
    for offset in range(1, 5):
        total = total + gauss_taps[4 + offset] * (read(k - offset) + read(k + offset))
    return total


def depth_pass(flags, source, target, layers, first):
    tiles = source.shape[1] // 8

    def one_layer(j, _):
        for tile in range(tiles):
            rows = pl.ds(tile * 8, 8)
            value = smooth_depth(lambda k: source[k, rows, :], j + first)
            if tile == 0:
                value = value * flags[0]
            if tile == tiles - 1:
                value = value * flags[1]
            target[j, rows, :] = value
        return 0

    lax.fori_loop(0, layers, one_layer, 0)


def shade_voxels(prev, mid, above, below, following, scale):
    columns = mid.shape[1]
    lane = lax.broadcasted_iota(jnp.int32, mid.shape, 1)
    right = jnp.where(lane == columns - 1, 0.0, pltpu.roll(mid, columns - 1, 1))
    left = jnp.where(lane == 0, 0.0, pltpu.roll(mid, 1, 1))
    dz = following - prev
    dx = below - above
    dy = right - left
    slope = (1.5 * light_z) * dz + (1.5 * light_x) * dx + (1.5 * light_y) * dy
    shading = 0.55 + 0.45 * jnp.tanh(slope)
    gradient_sq4 = dz * dz + dx * dx + dy * dy
    square = mid * mid
    optical = scale * (square / (1.0 + square)) * (1.0 + gradient_sq4)
    centred = mid - 2.5
    red_share = 0.5 + 0.5 * jnp.tanh(centred)
    green_share = jnp.exp(-(centred * centred))
    return optical, shading, red_share, green_share


def render_pass(smoothed, layers, start, carry_in, store, scale):
    tiles = smoothed.shape[1] // 8 - 2

    def one_tile(tile, _):
        base = pl.multiple_of(tile * 8 + 8, 8)
        rows = pl.ds(base, 8)

        def one_layer(j, carry):
            red, green, blue, transmit = carry
            k = j + start
            mid = smoothed[k, rows, :]
            before = smoothed[k, pl.ds(base - 8, 8), :]
            after = smoothed[k, pl.ds(base + 8, 8), :]
            sub = lax.broadcasted_iota(jnp.int32, mid.shape, 0)
            above = pltpu.roll(jnp.where(sub == 7, before, mid), 1, 0)
            below = pltpu.roll(jnp.where(sub == 0, after, mid), 7, 0)
            optical, shading, red_share, green_share = shade_voxels(
                smoothed[k - 1, rows, :], mid, above, below, smoothed[k + 1, rows, :], scale
            )
            remaining = transmit * jnp.exp(-optical)
            lit = (transmit - remaining) * shading
            red_part = lit * red_share
            return (
                red + red_part,
                green + lit * green_share,
                blue + (lit - red_part),
                remaining,
            )

        out = lax.fori_loop(0, layers, one_layer, carry_in(tile))
        store(tile, out)
        return 0

    lax.fori_loop(0, tiles, one_tile, 0)


def interior_kernel(scale, flags, c, xl, xh, by, lx, front, back, image, plane, smoothed):
    layers = c.shape[0]
    group = 4

    def smooth_group(g, _):
        first = g * group
        counts = [
            jnp.concatenate([xl[first + n], c[first + n], xh[first + n]], 0) for n in range(group)
        ]
        for n, value in enumerate(smooth_plane(counts, by, lx[...])):
            plane[first + n] = value
        return 0

    lax.fori_loop(0, layers // group, smooth_group, 0)
    front[...] = plane[: 2 * REACH]
    back[...] = plane[layers - 2 * REACH :]
    depth_pass(flags, plane, smoothed, layers - 8, 4)

    def carry_in(tile):
        zero = jnp.zeros((8, c.shape[2]), jnp.float32)
        return zero, zero, zero, jnp.ones_like(zero)

    def store(tile, out):
        rows = pl.ds(pl.multiple_of(tile * 8, 8), 8)
        for n, value in enumerate(out):
            image[n, rows, :] = value

    render_pass(smoothed, layers - 10, 1, carry_in, store, scale)


def edge_kernel(scale, is_back, flags, own, edge, middle, cl, ch, by, lx, ahead, image, plane, smoothed):
    depth = edge.shape[0]
    if is_back:
        plane[: 2 * REACH] = own[...]
        at = 2 * REACH
    else:
        plane[REACH:] = own[...]
        at = 0
    counts = [
        jnp.concatenate([cl[n], edge[n, :PAD], middle[n], edge[n, PAD:], ch[n]], 0)
        for n in range(depth)
    ]
    for n, value in enumerate(smooth_plane(counts, by, lx[...])):
        plane[at + n] = value
    depth_pass(flags, plane, smoothed, REACH + 2, 4)
    outside = REACH + 1 if is_back else 0
    smoothed[outside] = smoothed[outside] * flags[2]

    def carry_in(tile):
        if not is_back:
            zero = jnp.zeros((8, own.shape[2]), jnp.float32)
            return zero, zero, zero, jnp.ones_like(zero)
        rows = pl.ds(pl.multiple_of(tile * 8, 8), 8)
        through = ahead[3, rows, :]
        colors = tuple(
            ahead[n, rows, :] + through * ahead[4 + n, rows, :] for n in range(3)
        )
        return colors + (through * ahead[7, rows, :],)

    def store(tile, out):
        rows = pl.ds(pl.multiple_of(tile * 8, 8), 8)
        for n, value in enumerate(out):
            image[n, rows, :] = value

    render_pass(smoothed, REACH, 1, carry_in, store, scale)


def whole(count):
    return [pl.BlockSpec(memory_space=pltpu.VMEM)] * count


def smem():
    return pl.BlockSpec(memory_space=pltpu.SMEM)


def call_interior(scale, flags, c, xl, xh, by, lx):
    layers, rows, columns = c.shape
    ext = rows + 2 * PAD
    f32 = jnp.float32
    return pl.pallas_call(
        functools.partial(interior_kernel, scale),
        out_shape=(
            jax.ShapeDtypeStruct((2 * REACH, ext, columns), f32),
            jax.ShapeDtypeStruct((2 * REACH, ext, columns), f32),
            jax.ShapeDtypeStruct((4, rows, columns), f32),
        ),
        in_specs=[smem()] + whole(5),
        out_specs=tuple(whole(3)),
        scratch_shapes=[
            pltpu.VMEM((layers, ext, columns), f32),
            pltpu.VMEM((layers - 8, ext, columns), f32),
        ],
        compiler_params=pltpu.CompilerParams(vmem_limit_bytes=48 * 1024 * 1024),
        cost_estimate=pl.CostEstimate(
            flops=2_000_000_000, transcendentals=0, bytes_accessed=8_000_000
        ),
        name="interior",
    )(flags, c, xl, xh, by, lx)


def call_edge(scale, is_back, flags, own, edge, middle, cl, ch, by, lx, ahead):
    _, ext, columns = own.shape
    f32 = jnp.float32
    return pl.pallas_call(
        functools.partial(edge_kernel, scale, is_back),
        out_shape=jax.ShapeDtypeStruct((4, ext - 2 * PAD, columns), f32),
        in_specs=[smem()] + whole(8),
        out_specs=whole(1)[0],
        scratch_shapes=[
            pltpu.VMEM((3 * REACH, ext, columns), f32),
            pltpu.VMEM((REACH + 2, ext, columns), f32),
        ],
        compiler_params=pltpu.CompilerParams(vmem_limit_bytes=32 * 1024 * 1024),
        cost_estimate=pl.CostEstimate(
            flops=200_000_000, transcendentals=0, bytes_accessed=3_000_000
        ),
        name="back" if is_back else "front",
    )(flags, own, edge, middle, cl, ch, by, lx, ahead)


def shift(value, axis, step):
    count = lax.axis_size(axis)
    pairs = [(i, i + step) for i in range(count) if 0 <= i + step < count]
    return lax.ppermute(value, axis, pairs)


def over(front, back):
    through = front[3:]
    return jnp.concatenate([front[:3] + through * back[:3], through * back[3:]], 0)


def exchange(layers):
    count = lax.axis_size("depth")
    me = lax.axis_index("depth")
    _, rows, columns = layers.shape
    owned = rows // count
    parity, pair = me % 2, me // 2
    pairs = count // 2
    pieces = layers.reshape(4, pairs, 2, owned, columns)
    send = lax.dynamic_index_in_dim(pieces, 1 - parity, 2, keepdims=False)
    keep = lax.dynamic_index_in_dim(pieces, parity, 2, keepdims=False)
    got = lax.ppermute(send, "depth", [(i, i ^ 1) for i in range(count)])
    joined = jnp.where(parity == 0, over(keep, got), over(got, keep))
    parts = []
    for step in range(pairs):
        piece = lax.dynamic_index_in_dim(joined, pair ^ step, 1, keepdims=False)
        if step:
            piece = lax.ppermute(piece, "depth", [(i, i ^ (2 * step)) for i in range(count)])
        parts.append(piece)
    result = jnp.zeros((3, owned, columns), jnp.float32)
    through = jnp.ones((1, owned, columns), jnp.float32)
    for step in range(pairs):
        ahead = jnp.ones((1, owned, columns), jnp.float32)
        for other in range(pairs):
            if other != step:
                nearer = (pair ^ other) < (pair ^ step)
                ahead = ahead * jnp.where(nearer, parts[other][3:], 1.0)
        result = result + ahead * parts[step][:3]
        through = through * parts[step][3:]
    return jnp.concatenate([result, 1.0 - through], 0)


def local(counts):
    slab, rows, columns = counts.shape
    img, depth = lax.axis_index("img"), lax.axis_index("depth")
    imgs, depths = lax.axis_size("img"), lax.axis_size("depth")
    scale = 1.5 / (slab * depths)
    top, bottom = counts[:REACH], counts[slab - REACH :]

    def edges(block):
        return jnp.concatenate([block[:, :PAD], block[:, rows - PAD :]], 1)

    front_edge = shift(edges(bottom), "depth", 1)
    back_edge = shift(edges(top), "depth", -1)
    xl = shift(counts[:, rows - PAD :], "img", 1)
    xh = shift(counts[:, :PAD], "img", -1)
    front_mid = shift(bottom[:, PAD : rows - PAD], "depth", 1)
    back_mid = shift(top[:, PAD : rows - PAD], "depth", -1)
    ends = jnp.concatenate([front_edge, back_edge], 0)
    cl = shift(ends[:, PAD:], "img", 1)
    ch = shift(ends[:, :PAD], "img", -1)
    one = jnp.float32(1.0)
    row_flags = [(img > 0) * one, (img < imgs - 1) * one]
    front_flags = jnp.stack(row_flags + [(depth > 0) * one])
    back_flags = jnp.stack(row_flags + [(depth < depths - 1) * one])
    by = jnp.asarray(column_matrix(columns))
    lx = jnp.asarray(row_matrix(rows + 2 * PAD))
    own_front, own_back, inner = call_interior(scale, front_flags, counts, xl, xh, by, lx)
    ahead = call_edge(
        scale, False, front_flags, own_front, front_edge, front_mid, cl[:REACH], ch[:REACH], by, lx,
        jnp.zeros((8, 8, columns), jnp.float32),
    )
    ahead = jnp.concatenate([ahead, inner], 0)
    layers = call_edge(
        scale, True, back_flags, own_back, back_edge, back_mid, cl[REACH:], ch[REACH:], by, lx, ahead
    )
    return exchange(layers)


def solution(mesh):
    in_specs = (P("depth", "img", None),)
    out_specs = P(None, ("img", "depth"), None)
    return jax.shard_map(local, mesh=mesh, in_specs=in_specs, out_specs=out_specs, check_vma=False)
```

time: 130 us -> 94.8 us (0.73); the launches traced: 130 us -> 92.9 us
  other arithmetic: 57.2 us -> 1.74 us
  Pallas kernels: 0 us -> 40.2 us
  blocking collectives: 23.3 us -> 0 us
  waiting for transfers between devices: 25.8 us -> 18.2 us
  local copies, waits for them, and re-layouts: 0.22 us -> 7.2 us
  starting transfers between devices: 23.3 us -> 25.4 us
    pallas_call x0 -> x3, Pallas kernels: none -> 40.2 us  [the longest x1 27.9 us: call_interior(): pl.pallas_call(functools.partial(interior_kernel, scale), out_shape=(jax....]
    add x3 -> x2, other arithmetic: 32.3 us -> 0.08 us  [the longest x1 0.05 us: over(): front[:3] + through * back[:3]]
    all_to_all x1 -> x0, blocking collectives: 23.3 us -> none  [local(): lax.all_to_all(pieces, 'depth', split_axis=1, concat_axis=1, tiled=True)]
    reduce_sum x2 -> x0, other arithmetic: 14.9 us -> none  [the longest x1 14.8 us: integrate(): jnp.sum(weight * red_light, 0)]
    ppermute x8 -> x12, waiting for transfers between devices: 25.8 us -> 18.2 us  [the longest x8 9.14 us: shift(): return lax.ppermute(value, axis, pairs)]
    slice x4 -> x6, local copies, waits for them, and re-layouts: 0.21 us -> 7.1 us  [the longest x1 2.21 us: local(): front_mid = shift(bottom[:, PAD:rows - PAD], 'depth', 1)]
    convert_element_type x1 -> x0, other arithmetic: 4.88 us -> none  [local(): density = smooth_last(counts.astype(jnp.float32))]
    another operation x2, other arithmetic: 4.36 us -> 0.15 us  [the longest x1 0.08 us: local(): back_flags = jnp.stack(row_flags + [(depth < depths - 1) * one])]
  transfers between devices with their start and end apart: 8 -> 12, of which waited for: 5 -> 6; matrix products, arithmetic and copies ran while one was open for 0% -> 6% of each run, Pallas kernels for 0% -> 37%
where the time goes in v1:
time: 94.8 us; the launch traced here: 92.9 us
  Pallas kernels  40.2 us (42%)
  starting transfers between devices  25.4 us (27%)
  waiting for transfers between devices  18.2 us (19%)
  local copies, waits for them, and re-layouts  7.2 us (8%)
  other arithmetic  1.74 us (2%)
    pallas_call x1, Pallas kernels, call_interior(): pl.pallas_call(functools.partial(interior_kernel, scale), out_shape=(jax....  27.9 us
    ppermute x8, starting transfers between devices, shift(): return lax.ppermute(value, axis, pairs)  19.2 us
    pallas_call x2, Pallas kernels, call_edge(): pl.pallas_call(functools.partial(edge_kernel, scale, is_back), out_shape=...  12.2 us
    ppermute x8, waiting for transfers between devices, shift(): return lax.ppermute(value, axis, pairs)  9.14 us
    ppermute x1, waiting for transfers between devices, exchange(): got = lax.ppermute(send, 'depth', [(i, i ^ 1) for i in range(count)])  4.73 us
    ppermute x3, starting transfers between devices, exchange(): lax.ppermute(piece, 'depth', [(i, i ^ 2 * step) for i in range(count)])  4.45 us
    ppermute x3, waiting for transfers between devices, exchange(): lax.ppermute(piece, 'depth', [(i, i ^ 2 * step) for i in range(count)])  4.35 us
    slice x1, local copies, waits for them, and re-layouts, local(): front_mid = shift(bottom[:, PAD:rows - PAD], 'depth', 1)  2.21 us
  transfers between devices with their start and end apart: 12, of which 6 were waited for; matrix products, arithmetic and copies ran while one was open for 6% of the time, Pallas kernels for 37%

profile of v1, /device:TPU:0, one launch (start us, length us, event | category | flops | bytes accessed | tf_op | source)
XLA Modules:
  0.0 92.9 jit_solution(9186348857493182071)
XLA Ops:
  0.0 2.2 %fusion.7 = (s32[32,8,512]{2,1,0:T(8,128)S(1)}, s32[32,8,512]{2,1,0:T(8,128)}) fusion(s32[32,64,512]{2,1,0:T(8,128)} %c.1), kind=kLoop, calls=%fused_computation.38 | loop fusion | bytes 2097152 | tf_op jit(solution)/shard_map/slice | solution.py:318
  2.2 2.4 %collective-permute-start = (s32[32,8,512]{2,1,0:T(8,128)}, s32[32,8,512]{2,1,0:T(8,128)S(1)}, u32[]{:S(2)}, u32[]{:S(2)}) collective-permute-start(s32[32,8,512]{2,1,0:T(8,128)} %get-tuple-element.18), channel_id=1, source_target_pairs={{0,8},{8,16},{16,24},{1,9},{9,17},{17,25},{2,10},{10,18},{18,26},{... | collective-permute-start | bytes 1572872 | tf_op jit(solution)/shard_map/ppermute | solution.py:266
  4.6 1.3 %collective-permute-start.1 = (s32[32,8,512]{2,1,0:T(8,128)S(1)}, s32[32,8,512]{2,1,0:T(8,128)}, u32[]{:S(2)}, u32[]{:S(2)}) collective-permute-start(s32[32,8,512]{2,1,0:T(8,128)S(1)} %get-tuple-element.17), channel_id=1, source_target_pairs={{8,0},{16,8},{24,16},{9,1},{17,9},{25,17},{10,2},{18,10},{26,18},{... | collective-permute-start | bytes 1572872 | tf_op jit(solution)/shard_map/ppermute | solution.py:266
  5.9 1.0 %fusion.6 = (s32[5,8,512]{2,1,0:T(8,128)S(1)}, s32[5,8,512]{2,1,0:T(8,128)S(1)}, s32[5,8,512]{2,1,0:T(8,128)S(1)}, s32[5,8,512]{2,1,0:T(8,128)S(1)}) fusion(s32[32,64,512]{2,1,0:T(8,128)} %c.1), kind=kLoop, calls=%fused_computation.37 | loop fusion | bytes 655360 | tf_op jit(solution)/shard_map/slice | solution.py:313
  7.6 1.3 %collective-permute-start.2 = (s32[5,16,512]{2,1,0:T(8,128)}, s32[5,16,512]{2,1,0:T(8,128)S(1)}, u32[]{:S(2)}, u32[]{:S(2)}) collective-permute-start(s32[5,16,512]{2,1,0:T(8,128)} %pad_add_fusion), channel_id=1, source_target_pairs={{1,0},{2,1},{3,2},{4,3},{5,4},{6,5},{7,6},{9,8},{10,9},{11,10},{12... | collective-permute-start | bytes 491528 | tf_op jit(solution)/shard_map/ppermute | solution.py:266
  8.9 4.9 %collective-permute-start.4 = (s32[5,16,512]{2,1,0:T(8,128)S(1)}, s32[5,16,512]{2,1,0:T(8,128)S(1)}, u32[]{:S(2)}, u32[]{:S(2)}) collective-permute-start(s32[5,16,512]{2,1,0:T(8,128)S(1)} %pad_add_fusion.1), channel_id=1, source_target_pairs={{0,1},{1,2},{2,3},{3,4},{4,5},{5,6},{6,7},{8,9},{9,10},{10,11},{11... | collective-permute-start | bytes 491528 | tf_op jit(solution)/shard_map/ppermute | solution.py:266
  13.8 2.2 %fusion.5 = (s32[5,48,512]{2,1,0:T(8,128)}, s32[5,48,512]{2,1,0:T(8,128)}) fusion(s32[32,64,512]{2,1,0:T(8,128)} %c.1), kind=kLoop, calls=%fused_computation.36 | loop fusion | bytes 1966080 | tf_op jit(solution)/shard_map/slice | solution.py:319
  16.0 1.3 %collective-permute-start.3 = (s32[5,48,512]{2,1,0:T(8,128)}, s32[5,48,512]{2,1,0:T(8,128)S(1)}, u32[]{:S(2)}, u32[]{:S(2)}) collective-permute-start(s32[5,48,512]{2,1,0:T(8,128)} %get-tuple-element.12), channel_id=1, source_target_pairs={{1,0},{2,1},{3,2},{4,3},{5,4},{6,5},{7,6},{9,8},{10,9},{11,10},{12... | collective-permute-start | bytes 1474568 | tf_op jit(solution)/shard_map/ppermute | solution.py:266
  17.3 3.6 %collective-permute-done.4.edge = s32[5,16,512]{2,1,0:T(8,128)S(1)} collective-permute-done((s32[5,16,512]{2,1,0:T(8,128)S(1)}, s32[5,16,512]{2,1,0:T(8,128)S(1)}, u32[]{:S(2)}, u32[]{:S(2)}) %collective-permute-start.4) | collective-permute-done | bytes 163872 | tf_op jit(solution)/shard_map/ppermute | solution.py:266
  20.9 4.4 %collective-permute-start.7 = (s32[5,48,512]{2,1,0:T(8,128)}, s32[5,48,512]{2,1,0:T(8,128)S(1)}, u32[]{:S(2)}, u32[]{:S(2)}) collective-permute-start(s32[5,48,512]{2,1,0:T(8,128)} %get-tuple-element.11), channel_id=1, source_target_pairs={{0,1},{1,2},{2,3},{3,4},{4,5},{5,6},{6,7},{8,9},{9,10},{10,11},{11... | collective-permute-start | bytes 1474568 | tf_op jit(solution)/shard_map/ppermute | solution.py:266
  26.1 2.4 %collective-permute-start.5 = (s32[10,8,512]{2,1,0:T(8,128)}, s32[10,8,512]{2,1,0:T(8,128)}, u32[]{:S(2)}, u32[]{:S(2)}) collective-permute-start(s32[10,8,512]{2,1,0:T(8,128)} %get-tuple-element.25), channel_id=1, source_target_pairs={{0,8},{8,16},{16,24},{1,9},{9,17},{17,25},{2,10},{10,18},{18,26},{... | collective-permute-start | bytes 491528 | tf_op jit(solution)/shard_map/ppermute | solution.py:266
  29.2 1.3 %collective-permute-start.6 = (s32[10,8,512]{2,1,0:T(8,128)}, s32[10,8,512]{2,1,0:T(8,128)S(1)}, u32[]{:S(2)}, u32[]{:S(2)}) collective-permute-start(s32[10,8,512]{2,1,0:T(8,128)} %get-tuple-element.24), channel_id=1, source_target_pairs={{8,0},{16,8},{24,16},{9,1},{17,9},{25,17},{10,2},{18,10},{26,18},{... | collective-permute-start | bytes 491528 | tf_op jit(solution)/shard_map/ppermute | solution.py:266
  30.5 0.9 %fusion.10 = (s32[5,8,512]{2,1,0:T(8,128)S(1)}, s32[5,8,512]{2,1,0:T(8,128)S(1)}) fusion(s32[10,8,512]{2,1,0:T(8,128)} %collective-permute-done.5), kind=kLoop, calls=%fused_computation.41 | loop fusion | bytes 327680 | tf_op jit(solution)/shard_map/slice | solution.py:332
  31.4 5.0 %collective-permute-done.6 = s32[10,8,512]{2,1,0:T(8,128)S(1)} collective-permute-done((s32[10,8,512]{2,1,0:T(8,128)}, s32[10,8,512]{2,1,0:T(8,128)S(1)}, u32[]{:S(2)}, u32[]{:S(2)}) %collective-permute-start.6) | collective-permute-done | bytes 163872 | tf_op jit(solution)/shard_map/ppermute | solution.py:266
  36.5 27.9 %interior.1 = (f32[10,80,512]{2,1,0:T(8,128)S(1)}, f32[10,80,512]{2,1,0:T(8,128)S(1)}, f32[4,64,512]{2,1,0:T(8,128)S(1)}) custom-call(f32[3]{0:T(128)S(1)} %pad_maximum_fusion.6.flags, s32[32,64,512]{2,1,0:T(8,128)} %c.1, s32[32,8,512]{2,1,0:T(8,128)S(1)} %collective-permute-done.xl, s32[32,8,512]{2,1,0:T(8,128)} %collective-permute-done.1.xh, ...), custom_call_target="tpu_custom_call" | custom-call | flops 2000000000 | bytes 8000000 | tf_op jit(solution)/shard_map/interior/pallas_call | solution.py:222
  64.4 6.1 %front.1 = f32[4,64,512]{2,1,0:T(8,128)S(1)} custom-call(f32[3]{0:T(128)S(1)} %pad_maximum_fusion.6.flags, f32[10,80,512]{2,1,0:T(8,128)S(1)} %get-tuple-element.9.own, s32[5,16,512]{2,1,0:T(8,128)S(1)} %collective-permute-done.4.edge, s32[5,48,512]{2,1,0:T(8,128)S(1)} %collective-permute-done.7.middle, s32[5,8,512]{2,1,0:T(8,128)S(1)} %get-tuple-element.33.cl, ...), custom_call_target="tpu_custom_call" | custom-call | flops 200000000 | bytes 3000000 | tf_op jit(solution)/shard_map/front/pallas_call | solution.py:246
  70.6 6.1 %back.1 = f32[4,64,512]{2,1,0:T(8,128)S(1)} custom-call(f32[3]{0:T(128)S(1)} %pad_maximum_fusion.4.flags, f32[10,80,512]{2,1,0:T(8,128)S(1)} %get-tuple-element.8.own, s32[5,16,512]{2,1,0:T(8,128)S(1)} %collective-permute-done.2.edge, s32[5,48,512]{2,1,0:T(8,128)S(1)} %collective-permute-done.3.middle, s32[5,8,512]{2,1,0:T(8,128)S(1)} %get-tuple-element.34.cl, ...), custom_call_target="tpu_custom_call" | custom-call | flops 200000000 | bytes 3000000 | tf_op jit(solution)/shard_map/back/pallas_call | solution.py:246
  76.8 1.7 %collective-permute-start.8 = (f32[4,4,8,512]{3,2,1,0:T(8,128)S(1)}, f32[4,4,8,512]{3,2,1,0:T(8,128)S(1)}, u32[]{:S(2)}, u32[]{:S(2)}) collective-permute-start(f32[4,4,8,512]{3,2,1,0:T(8,128)S(1)} %dynamic-slice_bitcast_fusion), channel_id=1, source_target_pairs={{0,1},{1,0},{2,3},{3,2},{4,5},{5,4},{6,7},{7,6},{8,9},{9,8},{10,11... | collective-permute-start | bytes 786440 | tf_op jit(solution)/shard_map/ppermute | solution.py:284
  78.5 4.7 %collective-permute-done.8 = f32[4,4,8,512]{3,2,1,0:T(8,128)S(1)} collective-permute-done((f32[4,4,8,512]{3,2,1,0:T(8,128)S(1)}, f32[4,4,8,512]{3,2,1,0:T(8,128)S(1)}, u32[]{:S(2)}, u32[]{:S(2)}) %collective-permute-start.8) | collective-permute-done | bytes 262176 | tf_op jit(solution)/shard_map/ppermute | solution.py:284
  83.4 2.3 %collective-permute-start.11 = (f32[4,8,512]{2,1,0:T(8,128)S(1)}, f32[4,8,512]{2,1,0:T(8,128)S(1)}, u32[]{:S(2)}, u32[]{:S(2)}) collective-permute-start(f32[4,8,512]{2,1,0:T(8,128)S(1)} %get-tuple-element.27), channel_id=1, source_target_pairs={{0,6},{1,7},{2,4},{3,5},{4,2},{5,3},{6,0},{7,1},{8,14},{9,15},{10,... | collective-permute-start | bytes 196616 | tf_op jit(solution)/shard_map/ppermute | solution.py:290
  85.7 0.8 collective-permute-start.10
  86.5 1.4 %collective-permute-start.9 = (f32[4,8,512]{2,1,0:T(8,128)S(1)}, f32[4,8,512]{2,1,0:T(8,128)S(1)}, u32[]{:S(2)}, u32[]{:S(2)}) collective-permute-start(f32[4,8,512]{2,1,0:T(8,128)S(1)} %get-tuple-element.26), channel_id=1, source_target_pairs={{0,2},{1,3},{2,0},{3,1},{4,6},{5,7},{6,4},{7,5},{8,10},{9,11},{10,... | collective-permute-start | bytes 196616 | tf_op jit(solution)/shard_map/ppermute | solution.py:290
  87.9 1.7 %collective-permute-done.11 = f32[4,8,512]{2,1,0:T(8,128)S(1)} collective-permute-done((f32[4,8,512]{2,1,0:T(8,128)S(1)}, f32[4,8,512]{2,1,0:T(8,128)S(1)}, u32[]{:S(2)}, u32[]{:S(2)}) %collective-permute-start.11) | collective-permute-done | bytes 65568 | tf_op jit(solution)/shard_map/ppermute | solution.py:290
  89.5 2.7 %collective-permute-done.10 = f32[4,8,512]{2,1,0:T(8,128)S(1)} collective-permute-done((f32[4,8,512]{2,1,0:T(8,128)S(1)}, f32[4,8,512]{2,1,0:T(8,128)S(1)}, u32[]{:S(2)}, u32[]{:S(2)}) %collective-permute-start.10) | collective-permute-done | bytes 65568 | tf_op jit(solution)/shard_map/ppermute | solution.py:290
  (31 shorter events, 3.1 us)
Async XLA Ops:
  0.0 36.4 %copy-start = (bf16[1024,512]{1,0:T(8,128)(2,1)S(1)}, bf16[1024,512]{1,0:T(8,128)(2,1)}, u32[]{:S(2)}) copy-start(bf16[1024,512]{1,0:T(8,128)(2,1)} %constant.65.clone.by) | copy-start | bytes 3145732
  0.0 36.4 %copy-start.1 = (bf16[80,240]{1,0:T(8,128)(2,1)S(1)}, bf16[80,240]{1,0:T(8,128)(2,1)}, u32[]{:S(2)}) copy-start(bf16[80,240]{1,0:T(8,128)(2,1)} %constant.66.clone.lx) | copy-start | bytes 115204
  2.2 34.3 %collective-permute-start = (s32[32,8,512]{2,1,0:T(8,128)}, s32[32,8,512]{2,1,0:T(8,128)S(1)}, u32[]{:S(2)}, u32[]{:S(2)}) collective-permute-start(s32[32,8,512]{2,1,0:T(8,128)} %get-tuple-element.18), channel_id=1, source_target_pairs={{0,8},{8,16},{16,24},{1,9},{9,17},{17,25},{2,10},{10,18},{18,26},{... | collective-permute-start | bytes 1572872 | tf_op jit(solution)/shard_map/ppermute | solution.py:266
  4.6 31.8 %collective-permute-start.1 = (s32[32,8,512]{2,1,0:T(8,128)S(1)}, s32[32,8,512]{2,1,0:T(8,128)}, u32[]{:S(2)}, u32[]{:S(2)}) collective-permute-start(s32[32,8,512]{2,1,0:T(8,128)S(1)} %get-tuple-element.17), channel_id=1, source_target_pairs={{8,0},{16,8},{24,16},{9,1},{17,9},{25,17},{10,2},{18,10},{26,18},{... | collective-permute-start | bytes 1572872 | tf_op jit(solution)/shard_map/ppermute | solution.py:266
  7.6 17.7 %collective-permute-start.2 = (s32[5,16,512]{2,1,0:T(8,128)}, s32[5,16,512]{2,1,0:T(8,128)S(1)}, u32[]{:S(2)}, u32[]{:S(2)}) collective-permute-start(s32[5,16,512]{2,1,0:T(8,128)} %pad_add_fusion), channel_id=1, source_target_pairs={{1,0},{2,1},{3,2},{4,3},{5,4},{6,5},{7,6},{9,8},{10,9},{11,10},{12... | collective-permute-start | bytes 491528 | tf_op jit(solution)/shard_map/ppermute | solution.py:266
  8.9 12.0 %collective-permute-start.4 = (s32[5,16,512]{2,1,0:T(8,128)S(1)}, s32[5,16,512]{2,1,0:T(8,128)S(1)}, u32[]{:S(2)}, u32[]{:S(2)}) collective-permute-start(s32[5,16,512]{2,1,0:T(8,128)S(1)} %pad_add_fusion.1), channel_id=1, source_target_pairs={{0,1},{1,2},{2,3},{3,4},{4,5},{5,6},{6,7},{8,9},{9,10},{10,11},{11... | collective-permute-start | bytes 491528 | tf_op jit(solution)/shard_map/ppermute | solution.py:266
  16.0 54.7 %collective-permute-start.3 = (s32[5,48,512]{2,1,0:T(8,128)}, s32[5,48,512]{2,1,0:T(8,128)S(1)}, u32[]{:S(2)}, u32[]{:S(2)}) collective-permute-start(s32[5,48,512]{2,1,0:T(8,128)} %get-tuple-element.12), channel_id=1, source_target_pairs={{1,0},{2,1},{3,2},{4,3},{5,4},{6,5},{7,6},{9,8},{10,9},{11,10},{12... | collective-permute-start | bytes 1474568 | tf_op jit(solution)/shard_map/ppermute | solution.py:266
  20.9 43.5 %collective-permute-start.7 = (s32[5,48,512]{2,1,0:T(8,128)}, s32[5,48,512]{2,1,0:T(8,128)S(1)}, u32[]{:S(2)}, u32[]{:S(2)}) collective-permute-start(s32[5,48,512]{2,1,0:T(8,128)} %get-tuple-element.11), channel_id=1, source_target_pairs={{0,1},{1,2},{2,3},{3,4},{4,5},{5,6},{6,7},{8,9},{9,10},{10,11},{11... | collective-permute-start | bytes 1474568 | tf_op jit(solution)/shard_map/ppermute | solution.py:266
  26.1 3.1 %collective-permute-start.5 = (s32[10,8,512]{2,1,0:T(8,128)}, s32[10,8,512]{2,1,0:T(8,128)}, u32[]{:S(2)}, u32[]{:S(2)}) collective-permute-start(s32[10,8,512]{2,1,0:T(8,128)} %get-tuple-element.25), channel_id=1, source_target_pairs={{0,8},{8,16},{16,24},{1,9},{9,17},{17,25},{2,10},{10,18},{18,26},{... | collective-permute-start | bytes 491528 | tf_op jit(solution)/shard_map/ppermute | solution.py:266
  29.2 7.2 %collective-permute-start.6 = (s32[10,8,512]{2,1,0:T(8,128)}, s32[10,8,512]{2,1,0:T(8,128)S(1)}, u32[]{:S(2)}, u32[]{:S(2)}) collective-permute-start(s32[10,8,512]{2,1,0:T(8,128)} %get-tuple-element.24), channel_id=1, source_target_pairs={{8,0},{16,8},{24,16},{9,1},{17,9},{25,17},{10,2},{18,10},{26,18},{... | collective-permute-start | bytes 491528 | tf_op jit(solution)/shard_map/ppermute | solution.py:266
  76.8 6.4 %collective-permute-start.8 = (f32[4,4,8,512]{3,2,1,0:T(8,128)S(1)}, f32[4,4,8,512]{3,2,1,0:T(8,128)S(1)}, u32[]{:S(2)}, u32[]{:S(2)}) collective-permute-start(f32[4,4,8,512]{3,2,1,0:T(8,128)S(1)} %dynamic-slice_bitcast_fusion), channel_id=1, source_target_pairs={{0,1},{1,0},{2,3},{3,2},{4,5},{5,4},{6,7},{7,6},{8,9},{9,8},{10,11... | collective-permute-start | bytes 786440 | tf_op jit(solution)/shard_map/ppermute | solution.py:284
  83.4 6.1 %collective-permute-start.11 = (f32[4,8,512]{2,1,0:T(8,128)S(1)}, f32[4,8,512]{2,1,0:T(8,128)S(1)}, u32[]{:S(2)}, u32[]{:S(2)}) collective-permute-start(f32[4,8,512]{2,1,0:T(8,128)S(1)} %get-tuple-element.27), channel_id=1, source_target_pairs={{0,6},{1,7},{2,4},{3,5},{4,2},{5,3},{6,0},{7,1},{8,14},{9,15},{10,... | collective-permute-start | bytes 196616 | tf_op jit(solution)/shard_map/ppermute | solution.py:290
  85.7 6.5 %collective-permute-start.10 = (f32[4,8,512]{2,1,0:T(8,128)S(1)}, f32[4,8,512]{2,1,0:T(8,128)S(1)}, u32[]{:S(2)}, u32[]{:S(2)}) collective-permute-start(f32[4,8,512]{2,1,0:T(8,128)S(1)} %get-tuple-element.28), channel_id=1, source_target_pairs={{0,4},{1,5},{2,6},{3,7},{4,0},{5,1},{6,2},{7,3},{8,12},{9,13},{10,... | collective-permute-start | bytes 196616 | tf_op jit(solution)/shard_map/ppermute | solution.py:290
  86.5 5.7 %collective-permute-start.9 = (f32[4,8,512]{2,1,0:T(8,128)S(1)}, f32[4,8,512]{2,1,0:T(8,128)S(1)}, u32[]{:S(2)}, u32[]{:S(2)}) collective-permute-start(f32[4,8,512]{2,1,0:T(8,128)S(1)} %get-tuple-element.26), channel_id=1, source_target_pairs={{0,2},{1,3},{2,0},{3,1},{4,6},{5,7},{6,4},{7,5},{8,10},{9,11},{10,... | collective-permute-start | bytes 196616 | tf_op jit(solution)/shard_map/ppermute | solution.py:290

commit v2 on v1

--- a/solution.py
+++ b/solution.py
@@ -8,6 +8,7 @@
 from jax.experimental import pallas as pl
 from jax.experimental.pallas import tpu as pltpu
 from jax.sharding import PartitionSpec as P
+
 
 gauss_taps = [
     math.exp(-offset * offset / 8.0)
@@ -68,21 +69,15 @@
     return total
 
 
-def depth_pass(flags, source, target, layers, first):
-    tiles = source.shape[1] // 8
-
-    def one_layer(j, _):
-        for tile in range(tiles):
-            rows = pl.ds(tile * 8, 8)
-            value = smooth_depth(lambda k: source[k, rows, :], j + first)
-            if tile == 0:
-                value = value * flags[0]
-            if tile == tiles - 1:
-                value = value * flags[1]
-            target[j, rows, :] = value
-        return 0
-
-    lax.fori_loop(0, layers, one_layer, 0)
+def smooth_depth_layer(flags, read, k, tiles, write):
+    for tile in range(tiles):
+        rows = pl.ds(tile * 8, 8)
+        value = smooth_depth(lambda j: read(j, rows), k)
+        if tile == 0:
+            value = value * flags[0]
+        if tile == tiles - 1:
+            value = value * flags[1]
+        write(rows, value)
 
 
 def shade_voxels(prev, mid, above, below, following, scale):
@@ -104,16 +99,14 @@
     return optical, shading, red_share, green_share
 
 
-def render_pass(smoothed, layers, start, carry_in, store, scale):
+def render_pass(smoothed, layers, carry_in, store, scale):
     tiles = smoothed.shape[1] // 8 - 2
 
     def one_tile(tile, _):
         base = pl.multiple_of(tile * 8 + 8, 8)
         rows = pl.ds(base, 8)
-
-        def one_layer(j, carry):
-            red, green, blue, transmit = carry
-            k = j + start
+        red, green, blue, transmit = carry_in(tile)
+        for k in range(1, layers + 1):
             mid = smoothed[k, rows, :]
             before = smoothed[k, pl.ds(base - 8, 8), :]
             after = smoothed[k, pl.ds(base + 8, 8), :]
@@ -126,26 +119,29 @@
             remaining = transmit * jnp.exp(-optical)
             lit = (transmit - remaining) * shading
             red_part = lit * red_share
-            return (
-                red + red_part,
-                green + lit * green_share,
-                blue + (lit - red_part),
-                remaining,
-            )
-
-        out = lax.fori_loop(0, layers, one_layer, carry_in(tile))
-        store(tile, out)
+            red = red + red_part
+            green = green + lit * green_share
+            blue = blue + (lit - red_part)
+            transmit = remaining
+        store(tile, (red, green, blue, transmit))
         return 0
 
     lax.fori_loop(0, tiles, one_tile, 0)
 
 
-def interior_kernel(scale, flags, c, xl, xh, by, lx, front, back, image, plane, smoothed):
-    layers = c.shape[0]
-    group = 4
+def smooth_kernel(group, c_hbm, xl, xh, by, lx, plane, c, sems):
+    groups = c.shape[0] // group
+
+    def fetch(g):
+        part = pl.ds(g * group, group)
+        return pltpu.make_async_copy(c_hbm.at[part], c.at[part], sems.at[g])
+
+    for g in range(groups):
+        fetch(g).start()
 
     def smooth_group(g, _):
         first = g * group
+        fetch(g).wait()
         counts = [
             jnp.concatenate([xl[first + n], c[first + n], xh[first + n]], 0) for n in range(group)
         ]
@@ -153,13 +149,23 @@
             plane[first + n] = value
         return 0
 
-    lax.fori_loop(0, layers // group, smooth_group, 0)
-    front[...] = plane[: 2 * REACH]
-    back[...] = plane[layers - 2 * REACH :]
-    depth_pass(flags, plane, smoothed, layers - 8, 4)
+    lax.fori_loop(0, groups, smooth_group, 0)
+
+
+def interior_kernel(scale, flags, plane, image, smoothed):
+    layers, ext, columns = plane.shape
+
+    def one_layer(j, _):
+        def write(rows, value):
+            smoothed[j, rows, :] = value
+
+        smooth_depth_layer(flags, lambda k, rows: plane[k, rows, :], j + 4, ext // 8, write)
+        return 0
+
+    lax.fori_loop(0, layers - 8, one_layer, 0)
 
     def carry_in(tile):
-        zero = jnp.zeros((8, c.shape[2]), jnp.float32)
+        zero = jnp.zeros((8, columns), jnp.float32)
         return zero, zero, zero, jnp.ones_like(zero)
 
     def store(tile, out):
@@ -167,44 +173,53 @@
         for n, value in enumerate(out):
             image[n, rows, :] = value
 
-    render_pass(smoothed, layers - 10, 1, carry_in, store, scale)
-
-
-def edge_kernel(scale, is_back, flags, own, edge, middle, cl, ch, by, lx, ahead, image, plane, smoothed):
+    render_pass(smoothed, layers - 10, carry_in, store, scale)
+
+
+def edge_kernel(scale, is_back, flags, own, edge, middle, cl, ch, by, lx, *refs):
+    ahead = refs[0]
+    image, plane, smoothed = refs[-3:]
     depth = edge.shape[0]
-    if is_back:
-        plane[: 2 * REACH] = own[...]
-        at = 2 * REACH
-    else:
-        plane[REACH:] = own[...]
-        at = 0
     counts = [
         jnp.concatenate([cl[n], edge[n, :PAD], middle[n], edge[n, PAD:], ch[n]], 0)
         for n in range(depth)
     ]
     for n, value in enumerate(smooth_plane(counts, by, lx[...])):
-        plane[at + n] = value
-    depth_pass(flags, plane, smoothed, REACH + 2, 4)
-    outside = REACH + 1 if is_back else 0
-    smoothed[outside] = smoothed[outside] * flags[2]
+        plane[n] = value
+    held = own.shape[0]
+
+    def read(k, rows):
+        if is_back:
+            return own[held - 2 * REACH + k, rows, :] if k < 2 * REACH else plane[k - 2 * REACH, rows, :]
+        return plane[k, rows, :] if k < REACH else own[k - REACH, rows, :]
+
+    for j in range(REACH + 2):
+        outside = j == (REACH + 1 if is_back else 0)
+
+        def write(rows, value, j=j, outside=outside):
+            smoothed[j, rows, :] = value * flags[2] if outside else value
+
+        smooth_depth_layer(flags, read, j + 4, own.shape[1] // 8, write)
+
+    def tile_of(ref, tile):
+        rows = pl.ds(pl.multiple_of(tile * 8, 8), 8)
+        return tuple(ref[n, rows, :] for n in range(4))
 
     def carry_in(tile):
-        if not is_back:
-            zero = jnp.zeros((8, own.shape[2]), jnp.float32)
-            return zero, zero, zero, jnp.ones_like(zero)
-        rows = pl.ds(pl.multiple_of(tile * 8, 8), 8)
-        through = ahead[3, rows, :]
-        colors = tuple(
-            ahead[n, rows, :] + through * ahead[4 + n, rows, :] for n in range(3)
-        )
-        return colors + (through * ahead[7, rows, :],)
+        if is_back:
+            return tile_of(ahead, tile)
+        zero = jnp.zeros((8, own.shape[2]), jnp.float32)
+        return zero, zero, zero, jnp.ones_like(zero)
 
     def store(tile, out):
         rows = pl.ds(pl.multiple_of(tile * 8, 8), 8)
+        if not is_back:
+            inner = tile_of(ahead, tile)
+            out = tuple(out[n] + out[3] * inner[n] for n in range(3)) + (out[3] * inner[3],)
         for n, value in enumerate(out):
             image[n, rows, :] = value
 
-    render_pass(smoothed, REACH, 1, carry_in, store, scale)
+    render_pass(smoothed, REACH, carry_in, store, scale)
 
 
 def whole(count):
@@ -215,49 +230,61 @@
     return pl.BlockSpec(memory_space=pltpu.SMEM)
 
 
-def call_interior(scale, flags, c, xl, xh, by, lx):
+def call_smooth(c, xl, xh, by, lx):
     layers, rows, columns = c.shape
     ext = rows + 2 * PAD
-    f32 = jnp.float32
+    group = 4
+    return pl.pallas_call(
+        functools.partial(smooth_kernel, group),
+        out_shape=jax.ShapeDtypeStruct((layers, ext, columns), jnp.float32),
+        in_specs=[pl.BlockSpec(memory_space=pltpu.HBM)] + whole(4),
+        out_specs=whole(1)[0],
+        scratch_shapes=[
+            pltpu.VMEM((layers, rows, columns), jnp.int32),
+            pltpu.SemaphoreType.DMA((layers // group,)),
+        ],
+        compiler_params=pltpu.CompilerParams(vmem_limit_bytes=24 * 1024 * 1024),
+        cost_estimate=pl.CostEstimate(
+            flops=1_000_000_000, transcendentals=0, bytes_accessed=8_000_000
+        ),
+        name="smooth",
+    )(c, xl, xh, by, lx)
+
+
+def call_interior(scale, flags, plane):
+    layers, ext, columns = plane.shape
     return pl.pallas_call(
         functools.partial(interior_kernel, scale),
-        out_shape=(
-            jax.ShapeDtypeStruct((2 * REACH, ext, columns), f32),
-            jax.ShapeDtypeStruct((2 * REACH, ext, columns), f32),
-            jax.ShapeDtypeStruct((4, rows, columns), f32),
-        ),
-        in_specs=[smem()] + whole(5),
-        out_specs=tuple(whole(3)),
-        scratch_shapes=[
-            pltpu.VMEM((layers, ext, columns), f32),
-            pltpu.VMEM((layers - 8, ext, columns), f32),
-        ],
-        compiler_params=pltpu.CompilerParams(vmem_limit_bytes=48 * 1024 * 1024),
+        out_shape=jax.ShapeDtypeStruct((4, ext - 2 * PAD, columns), jnp.float32),
+        in_specs=[smem()] + whole(1),
+        out_specs=whole(1)[0],
+        scratch_shapes=[pltpu.VMEM((layers - 8, ext, columns), jnp.float32)],
+        compiler_params=pltpu.CompilerParams(vmem_limit_bytes=24 * 1024 * 1024),
         cost_estimate=pl.CostEstimate(
-            flops=2_000_000_000, transcendentals=0, bytes_accessed=8_000_000
+            flops=1_000_000_000, transcendentals=0, bytes_accessed=8_000_000
         ),
         name="interior",
-    )(flags, c, xl, xh, by, lx)
-
-
-def call_edge(scale, is_back, flags, own, edge, middle, cl, ch, by, lx, ahead):
-    _, ext, columns = own.shape
+    )(flags, plane)
+
+
+def call_edge(scale, is_back, flags, plane, edge, middle, cl, ch, by, lx, *ahead):
+    _, ext, columns = plane.shape
     f32 = jnp.float32
     return pl.pallas_call(
         functools.partial(edge_kernel, scale, is_back),
         out_shape=jax.ShapeDtypeStruct((4, ext - 2 * PAD, columns), f32),
-        in_specs=[smem()] + whole(8),
+        in_specs=[smem()] + whole(7 + len(ahead)),
         out_specs=whole(1)[0],
         scratch_shapes=[
-            pltpu.VMEM((3 * REACH, ext, columns), f32),
+            pltpu.VMEM((REACH, ext, columns), f32),
             pltpu.VMEM((REACH + 2, ext, columns), f32),
         ],
-        compiler_params=pltpu.CompilerParams(vmem_limit_bytes=32 * 1024 * 1024),
+        compiler_params=pltpu.CompilerParams(vmem_limit_bytes=24 * 1024 * 1024),
         cost_estimate=pl.CostEstimate(
             flops=200_000_000, transcendentals=0, bytes_accessed=3_000_000
         ),
         name="back" if is_back else "front",
-    )(flags, own, edge, middle, cl, ch, by, lx, ahead)
+    )(flags, plane, edge, middle, cl, ch, by, lx, *ahead)
 
 
 def shift(value, axis, step):
@@ -327,14 +354,16 @@
     back_flags = jnp.stack(row_flags + [(depth < depths - 1) * one])
     by = jnp.asarray(column_matrix(columns))
     lx = jnp.asarray(row_matrix(rows + 2 * PAD))
-    own_front, own_back, inner = call_interior(scale, front_flags, counts, xl, xh, by, lx)
-    ahead = call_edge(
-        scale, False, front_flags, own_front, front_edge, front_mid, cl[:REACH], ch[:REACH], by, lx,
-        jnp.zeros((8, 8, columns), jnp.float32),
+    held = pltpu.with_memory_space_constraint(counts, pltpu.HBM)
+    plane = call_smooth(held, xl, xh, by, lx)
+    inner = call_interior(scale, front_flags, plane)
+    front = call_edge(
+        scale, False, front_flags, plane, front_edge, front_mid, cl[:REACH], ch[:REACH], by, lx,
+        inner,
     )
-    ahead = jnp.concatenate([ahead, inner], 0)
     layers = call_edge(
-        scale, True, back_flags, own_back, back_edge, back_mid, cl[REACH:], ch[REACH:], by, lx, ahead
+        scale, True, back_flags, plane, back_edge, back_mid, cl[REACH:], ch[REACH:], by, lx,
+        front,
     )
     return exchange(layers)
 

time: 94.8 us -> 76.1 us (0.80); the launches traced: 92.9 us -> 75.7 us
  Pallas kernels: 40.2 us -> 21 us
  starting transfers between devices: 25.4 us -> 29.6 us
  waiting for transfers between devices: 18.2 us -> 16.7 us
    pallas_call x1 -> x2, Pallas kernels: 27.9 us -> 14.3 us  [the longest x1 7.29 us: call_interior(): pl.pallas_call(functools.partial(interior_kernel, scale), out_shape=jax.S...]
    pallas_call x2, Pallas kernels: 12.2 us -> 6.69 us  [call_edge(): pl.pallas_call(functools.partial(edge_kernel, scale, is_back), out_shape=...]
    ppermute x8, waiting for transfers between devices: 9.14 us -> 4.91 us  [shift(): return lax.ppermute(value, axis, pairs)]
    ppermute x8, starting transfers between devices: 19.2 us -> 22.6 us  [shift(): return lax.ppermute(value, axis, pairs)]
    ppermute x1, waiting for transfers between devices: 4.73 us -> 6.53 us  [exchange(): got = lax.ppermute(send, 'depth', [(i, i ^ 1) for i in range(count)])]
  transfers between devices with their start and end apart: 12 -> 12, of which waited for: 6 -> 6; matrix products, arithmetic and copies ran while one was open for 6% -> 8% of each run, Pallas kernels for 37% -> 24%
where the time goes in v2:
time: 76.1 us; the launch traced here: 75.7 us
  starting transfers between devices  29.6 us (39%)
  Pallas kernels  21 us (28%)
  waiting for transfers between devices  16.7 us (22%)
  local copies, waits for them, and re-layouts  7.17 us (9%)
  other arithmetic  0.89 us (1%)
    ppermute x8, starting transfers between devices, shift(): return lax.ppermute(value, axis, pairs)  22.6 us
    pallas_call x1, Pallas kernels, call_interior(): pl.pallas_call(functools.partial(interior_kernel, scale), out_shape=jax.S...  7.29 us
    pallas_call x1, Pallas kernels, call_smooth(): pl.pallas_call(functools.partial(smooth_kernel, group), out_shape=jax.Sha...  7.04 us
    pallas_call x2, Pallas kernels, call_edge(): pl.pallas_call(functools.partial(edge_kernel, scale, is_back), out_shape=...  6.69 us
    ppermute x1, waiting for transfers between devices, exchange(): got = lax.ppermute(send, 'depth', [(i, i ^ 1) for i in range(count)])  6.53 us
    ppermute x3, waiting for transfers between devices, exchange(): lax.ppermute(piece, 'depth', [(i, i ^ 2 * step) for i in range(count)])  5.28 us
    ppermute x8, waiting for transfers between devices, shift(): return lax.ppermute(value, axis, pairs)  4.91 us
    ppermute x3, starting transfers between devices, exchange(): lax.ppermute(piece, 'depth', [(i, i ^ 2 * step) for i in range(count)])  4.45 us
  transfers between devices with their start and end apart: 12, of which 6 were waited for; matrix products, arithmetic and copies ran while one was open for 8% of the time, Pallas kernels for 24%

profile of v2, /device:TPU:0, one launch (start us, length us, event | category | flops | bytes accessed | tf_op | source)
XLA Modules:
  0.0 75.7 jit_solution(16986589314294489422)
XLA Ops:
  0.0 1.1 %fusion.6 = (s32[5,8,512]{2,1,0:T(8,128)S(1)}, s32[5,8,512]{2,1,0:T(8,128)S(1)}, s32[5,8,512]{2,1,0:T(8,128)S(1)}, s32[5,8,512]{2,1,0:T(8,128)S(1)}) fusion(s32[32,64,512]{2,1,0:T(8,128)} %c_hbm.1), kind=kLoop, calls=%fused_computation.36 | loop fusion | bytes 655360 | tf_op jit(solution)/shard_map/slice | solution.py:340
  1.1 1.3 %collective-permute-start.2 = (s32[5,16,512]{2,1,0:T(8,128)S(1)}, s32[5,16,512]{2,1,0:T(8,128)S(1)}, u32[]{:S(2)}, u32[]{:S(2)}) collective-permute-start(s32[5,16,512]{2,1,0:T(8,128)S(1)} %pad_add_fusion), channel_id=1, source_target_pairs={{1,0},{2,1},{3,2},{4,3},{5,4},{6,5},{7,6},{9,8},{10,9},{11,10},{12... | collective-permute-start | bytes 491528 | tf_op jit(solution)/shard_map/ppermute | solution.py:293
  2.5 5.5 %collective-permute-start.4 = (s32[5,16,512]{2,1,0:T(8,128)S(1)}, s32[5,16,512]{2,1,0:T(8,128)S(1)}, u32[]{:S(2)}, u32[]{:S(2)}) collective-permute-start(s32[5,16,512]{2,1,0:T(8,128)S(1)} %pad_add_fusion.1), channel_id=1, source_target_pairs={{0,1},{1,2},{2,3},{3,4},{4,5},{5,6},{6,7},{8,9},{9,10},{10,11},{11... | collective-permute-start | bytes 491528 | tf_op jit(solution)/shard_map/ppermute | solution.py:293
  8.0 2.1 %fusion.7 = (s32[32,8,512]{2,1,0:T(8,128)S(1)}, s32[32,8,512]{2,1,0:T(8,128)}) fusion(s32[32,64,512]{2,1,0:T(8,128)} %c_hbm.1), kind=kLoop, calls=%fused_computation.37 | loop fusion | bytes 2097152 | tf_op jit(solution)/shard_map/slice | solution.py:345
  10.1 1.5 %collective-permute-start = (s32[32,8,512]{2,1,0:T(8,128)}, s32[32,8,512]{2,1,0:T(8,128)S(1)}, u32[]{:S(2)}, u32[]{:S(2)}) collective-permute-start(s32[32,8,512]{2,1,0:T(8,128)} %get-tuple-element.12), channel_id=1, source_target_pairs={{0,8},{8,16},{16,24},{1,9},{9,17},{17,25},{2,10},{10,18},{18,26},{... | collective-permute-start | bytes 1572872 | tf_op jit(solution)/shard_map/ppermute | solution.py:293
  11.5 1.3 %collective-permute-start.1 = (s32[32,8,512]{2,1,0:T(8,128)S(1)}, s32[32,8,512]{2,1,0:T(8,128)S(1)}, u32[]{:S(2)}, u32[]{:S(2)}) collective-permute-start(s32[32,8,512]{2,1,0:T(8,128)S(1)} %get-tuple-element.11), channel_id=1, source_target_pairs={{8,0},{16,8},{24,16},{9,1},{17,9},{25,17},{10,2},{18,10},{26,18},{... | collective-permute-start | bytes 1572872 | tf_op jit(solution)/shard_map/ppermute | solution.py:293
  12.8 1.0 %collective-permute-done.4.edge = s32[5,16,512]{2,1,0:T(8,128)S(1)} collective-permute-done((s32[5,16,512]{2,1,0:T(8,128)S(1)}, s32[5,16,512]{2,1,0:T(8,128)S(1)}, u32[]{:S(2)}, u32[]{:S(2)}) %collective-permute-start.4) | collective-permute-done | bytes 163872 | tf_op jit(solution)/shard_map/ppermute | solution.py:293
  14.7 4.8 %collective-permute-start.5 = (s32[10,8,512]{2,1,0:T(8,128)}, s32[10,8,512]{2,1,0:T(8,128)}, u32[]{:S(2)}, u32[]{:S(2)}) collective-permute-start(s32[10,8,512]{2,1,0:T(8,128)} %get-tuple-element.19), channel_id=1, source_target_pairs={{0,8},{8,16},{16,24},{1,9},{9,17},{17,25},{2,10},{10,18},{18,26},{... | collective-permute-start | bytes 491528 | tf_op jit(solution)/shard_map/ppermute | solution.py:293
  19.4 2.2 %fusion.5 = (s32[5,48,512]{2,1,0:T(8,128)}, s32[5,48,512]{2,1,0:T(8,128)}) fusion(s32[32,64,512]{2,1,0:T(8,128)} %c_hbm.1), kind=kLoop, calls=%fused_computation.35 | loop fusion | bytes 1966080 | tf_op jit(solution)/shard_map/slice | solution.py:346
  21.6 1.3 %collective-permute-start.3 = (s32[5,48,512]{2,1,0:T(8,128)}, s32[5,48,512]{2,1,0:T(8,128)S(1)}, u32[]{:S(2)}, u32[]{:S(2)}) collective-permute-start(s32[5,48,512]{2,1,0:T(8,128)} %get-tuple-element.6), channel_id=1, source_target_pairs={{1,0},{2,1},{3,2},{4,3},{5,4},{6,5},{7,6},{9,8},{10,9},{11,10},{12... | collective-permute-start | bytes 1474568 | tf_op jit(solution)/shard_map/ppermute | solution.py:293
  22.9 5.7 %collective-permute-start.7 = (s32[5,48,512]{2,1,0:T(8,128)}, s32[5,48,512]{2,1,0:T(8,128)}, u32[]{:S(2)}, u32[]{:S(2)}) collective-permute-start(s32[5,48,512]{2,1,0:T(8,128)} %get-tuple-element.5), channel_id=1, source_target_pairs={{0,1},{1,2},{2,3},{3,4},{4,5},{5,6},{6,7},{8,9},{9,10},{10,11},{11... | collective-permute-start | bytes 1474568 | tf_op jit(solution)/shard_map/ppermute | solution.py:293
  28.7 1.3 %collective-permute-start.6 = (s32[10,8,512]{2,1,0:T(8,128)}, s32[10,8,512]{2,1,0:T(8,128)S(1)}, u32[]{:S(2)}, u32[]{:S(2)}) collective-permute-start(s32[10,8,512]{2,1,0:T(8,128)} %get-tuple-element.18), channel_id=1, source_target_pairs={{8,0},{16,8},{24,16},{9,1},{17,9},{25,17},{10,2},{18,10},{26,18},{... | collective-permute-start | bytes 491528 | tf_op jit(solution)/shard_map/ppermute | solution.py:293
  31.0 1.6 %collective-permute-done.6 = s32[10,8,512]{2,1,0:T(8,128)S(1)} collective-permute-done((s32[10,8,512]{2,1,0:T(8,128)}, s32[10,8,512]{2,1,0:T(8,128)S(1)}, u32[]{:S(2)}, u32[]{:S(2)}) %collective-permute-start.6) | collective-permute-done | bytes 163872 | tf_op jit(solution)/shard_map/ppermute | solution.py:293
  32.6 7.0 %smooth.1.plane.own = f32[32,80,512]{2,1,0:T(8,128)S(1)} custom-call(s32[32,64,512]{2,1,0:T(8,128)} %c_hbm.1, s32[32,8,512]{2,1,0:T(8,128)S(1)} %collective-permute-done.xl, s32[32,8,512]{2,1,0:T(8,128)S(1)} %collective-permute-done.1.xh, bf16[1024,512]{1,0:T(8,128)(2,1)S(1)} %copy-done, bf16[80,240]{1,0:T(8,128)(2,1)S(1)} %copy-done.1), custom_call_target="tpu_custom_call" | custom-call | flops 1000000000 | bytes 8000000 | tf_op jit(solution)/shard_map/smooth/pallas_call | solution.py:237
  39.6 7.3 %interior.1.refs_0_ = f32[4,64,512]{2,1,0:T(8,128)S(1)} custom-call(f32[3]{0:T(128)S(1)} %get-tuple-element.32.flags, f32[32,80,512]{2,1,0:T(8,128)S(1)} %smooth.1.plane.own), custom_call_target="tpu_custom_call" | custom-call | flops 1000000000 | bytes 8000000 | tf_op jit(solution)/shard_map/interior/pallas_call | solution.py:256
  46.9 2.3 %collective-permute-done.7.middle = s32[5,48,512]{2,1,0:T(8,128)} collective-permute-done((s32[5,48,512]{2,1,0:T(8,128)}, s32[5,48,512]{2,1,0:T(8,128)}, u32[]{:S(2)}, u32[]{:S(2)}) %collective-permute-start.7) | collective-permute-done | bytes 491552 | tf_op jit(solution)/shard_map/ppermute | solution.py:293
  49.3 3.6 %front.1.refs_0_ = f32[4,64,512]{2,1,0:T(8,128)S(1)} custom-call(f32[3]{0:T(128)S(1)} %get-tuple-element.32.flags, f32[32,80,512]{2,1,0:T(8,128)S(1)} %smooth.1.plane.own, s32[5,16,512]{2,1,0:T(8,128)S(1)} %collective-permute-done.4.edge, s32[5,48,512]{2,1,0:T(8,128)} %collective-permute-done.7.middle, s32[5,8,512]{2,1,0:T(8,128)S(1)} %get-tuple-element.27.cl, ...), custom_call_target="tpu_custom_call" | custom-call | flops 200000000 | bytes 3000000 | tf_op jit(solution)/shard_map/front/pallas_call | solution.py:273
  52.9 3.1 %back.1 = f32[4,64,512]{2,1,0:T(8,128)S(1)} custom-call(f32[3]{0:T(128)S(1)} %get-tuple-element.31.flags, f32[32,80,512]{2,1,0:T(8,128)S(1)} %smooth.1.plane.own, s32[5,16,512]{2,1,0:T(8,128)S(1)} %collective-permute-done.2.edge, s32[5,48,512]{2,1,0:T(8,128)S(1)} %collective-permute-done.3.middle, s32[5,8,512]{2,1,0:T(8,128)S(1)} %get-tuple-element.28.cl, ...), custom_call_target="tpu_custom_call" | custom-call | flops 200000000 | bytes 3000000 | tf_op jit(solution)/shard_map/back/pallas_call | solution.py:273
  56.0 2.5 %collective-permute-start.8 = (f32[4,4,8,512]{3,2,1,0:T(8,128)S(1)}, f32[4,4,8,512]{3,2,1,0:T(8,128)S(1)}, u32[]{:S(2)}, u32[]{:S(2)}) collective-permute-start(f32[4,4,8,512]{3,2,1,0:T(8,128)S(1)} %dynamic-slice_bitcast_fusion), channel_id=1, source_target_pairs={{0,1},{1,0},{2,3},{3,2},{4,5},{5,4},{6,7},{7,6},{8,9},{9,8},{10,11... | collective-permute-start | bytes 786440 | tf_op jit(solution)/shard_map/ppermute | solution.py:311
  58.6 6.5 %collective-permute-done.8 = f32[4,4,8,512]{3,2,1,0:T(8,128)S(1)} collective-permute-done((f32[4,4,8,512]{3,2,1,0:T(8,128)S(1)}, f32[4,4,8,512]{3,2,1,0:T(8,128)S(1)}, u32[]{:S(2)}, u32[]{:S(2)}) %collective-permute-start.8) | collective-permute-done | bytes 262176 | tf_op jit(solution)/shard_map/ppermute | solution.py:311
  65.3 3.0 %collective-permute-start.10 = (f32[4,8,512]{2,1,0:T(8,128)S(1)}, f32[4,8,512]{2,1,0:T(8,128)S(1)}, u32[]{:S(2)}, u32[]{:S(2)}) collective-permute-start(f32[4,8,512]{2,1,0:T(8,128)S(1)} %get-tuple-element.22), channel_id=1, source_target_pairs={{0,4},{1,5},{2,6},{3,7},{4,0},{5,1},{6,2},{7,3},{8,12},{9,13},{10,... | collective-permute-start | bytes 196616 | tf_op jit(solution)/shard_map/ppermute | solution.py:317
  68.4 1.3 %collective-permute-start.9 = (f32[4,8,512]{2,1,0:T(8,128)S(1)}, f32[4,8,512]{2,1,0:T(8,128)S(1)}, u32[]{:S(2)}, u32[]{:S(2)}) collective-permute-start(f32[4,8,512]{2,1,0:T(8,128)S(1)} %get-tuple-element.20), channel_id=1, source_target_pairs={{0,2},{1,3},{2,0},{3,1},{4,6},{5,7},{6,4},{7,5},{8,10},{9,11},{10,... | collective-permute-start | bytes 196616 | tf_op jit(solution)/shard_map/ppermute | solution.py:317
  69.7 2.0 %collective-permute-done.11 = f32[4,8,512]{2,1,0:T(8,128)S(1)} collective-permute-done((f32[4,8,512]{2,1,0:T(8,128)S(1)}, f32[4,8,512]{2,1,0:T(8,128)S(1)}, u32[]{:S(2)}, u32[]{:S(2)}) %collective-permute-start.11) | collective-permute-done | bytes 65568 | tf_op jit(solution)/shard_map/ppermute | solution.py:317
  71.7 3.2 %collective-permute-done.10 = f32[4,8,512]{2,1,0:T(8,128)S(1)} collective-permute-done((f32[4,8,512]{2,1,0:T(8,128)S(1)}, f32[4,8,512]{2,1,0:T(8,128)S(1)}, u32[]{:S(2)}, u32[]{:S(2)}) %collective-permute-start.10) | collective-permute-done | bytes 65568 | tf_op jit(solution)/shard_map/ppermute | solution.py:317
  (29 shorter events, 2.8 us)
Async XLA Ops:
  0.0 32.6 %copy-start = (bf16[1024,512]{1,0:T(8,128)(2,1)S(1)}, bf16[1024,512]{1,0:T(8,128)(2,1)}, u32[]{:S(2)}) copy-start(bf16[1024,512]{1,0:T(8,128)(2,1)} %constant.63.clone.by) | copy-start | bytes 3145732
  0.0 32.6 %copy-start.1 = (bf16[80,240]{1,0:T(8,128)(2,1)S(1)}, bf16[80,240]{1,0:T(8,128)(2,1)}, u32[]{:S(2)}) copy-start(bf16[80,240]{1,0:T(8,128)(2,1)} %constant.64.clone.lx) | copy-start | bytes 115204
  1.1 12.7 %collective-permute-start.2 = (s32[5,16,512]{2,1,0:T(8,128)S(1)}, s32[5,16,512]{2,1,0:T(8,128)S(1)}, u32[]{:S(2)}, u32[]{:S(2)}) collective-permute-start(s32[5,16,512]{2,1,0:T(8,128)S(1)} %pad_add_fusion), channel_id=1, source_target_pairs={{1,0},{2,1},{3,2},{4,3},{5,4},{6,5},{7,6},{9,8},{10,9},{11,10},{12... | collective-permute-start | bytes 491528 | tf_op jit(solution)/shard_map/ppermute | solution.py:293
  2.5 11.4 %collective-permute-start.4 = (s32[5,16,512]{2,1,0:T(8,128)S(1)}, s32[5,16,512]{2,1,0:T(8,128)S(1)}, u32[]{:S(2)}, u32[]{:S(2)}) collective-permute-start(s32[5,16,512]{2,1,0:T(8,128)S(1)} %pad_add_fusion.1), channel_id=1, source_target_pairs={{0,1},{1,2},{2,3},{3,4},{4,5},{5,6},{6,7},{8,9},{9,10},{10,11},{11... | collective-permute-start | bytes 491528 | tf_op jit(solution)/shard_map/ppermute | solution.py:293
  10.1 22.5 %collective-permute-start = (s32[32,8,512]{2,1,0:T(8,128)}, s32[32,8,512]{2,1,0:T(8,128)S(1)}, u32[]{:S(2)}, u32[]{:S(2)}) collective-permute-start(s32[32,8,512]{2,1,0:T(8,128)} %get-tuple-element.12), channel_id=1, source_target_pairs={{0,8},{8,16},{16,24},{1,9},{9,17},{17,25},{2,10},{10,18},{18,26},{... | collective-permute-start | bytes 1572872 | tf_op jit(solution)/shard_map/ppermute | solution.py:293
  11.5 21.0 %collective-permute-start.1 = (s32[32,8,512]{2,1,0:T(8,128)S(1)}, s32[32,8,512]{2,1,0:T(8,128)S(1)}, u32[]{:S(2)}, u32[]{:S(2)}) collective-permute-start(s32[32,8,512]{2,1,0:T(8,128)S(1)} %get-tuple-element.11), channel_id=1, source_target_pairs={{8,0},{16,8},{24,16},{9,1},{17,9},{25,17},{10,2},{18,10},{26,18},{... | collective-permute-start | bytes 1572872 | tf_op jit(solution)/shard_map/ppermute | solution.py:293
  14.7 14.1 %collective-permute-start.5 = (s32[10,8,512]{2,1,0:T(8,128)}, s32[10,8,512]{2,1,0:T(8,128)}, u32[]{:S(2)}, u32[]{:S(2)}) collective-permute-start(s32[10,8,512]{2,1,0:T(8,128)} %get-tuple-element.19), channel_id=1, source_target_pairs={{0,8},{8,16},{16,24},{1,9},{9,17},{17,25},{2,10},{10,18},{18,26},{... | collective-permute-start | bytes 491528 | tf_op jit(solution)/shard_map/ppermute | solution.py:293
  21.6 31.2 %collective-permute-start.3 = (s32[5,48,512]{2,1,0:T(8,128)}, s32[5,48,512]{2,1,0:T(8,128)S(1)}, u32[]{:S(2)}, u32[]{:S(2)}) collective-permute-start(s32[5,48,512]{2,1,0:T(8,128)} %get-tuple-element.6), channel_id=1, source_target_pairs={{1,0},{2,1},{3,2},{4,3},{5,4},{6,5},{7,6},{9,8},{10,9},{11,10},{12... | collective-permute-start | bytes 1474568 | tf_op jit(solution)/shard_map/ppermute | solution.py:293
  22.9 26.3 %collective-permute-start.7 = (s32[5,48,512]{2,1,0:T(8,128)}, s32[5,48,512]{2,1,0:T(8,128)}, u32[]{:S(2)}, u32[]{:S(2)}) collective-permute-start(s32[5,48,512]{2,1,0:T(8,128)} %get-tuple-element.5), channel_id=1, source_target_pairs={{0,1},{1,2},{2,3},{3,4},{4,5},{5,6},{6,7},{8,9},{9,10},{10,11},{11... | collective-permute-start | bytes 1474568 | tf_op jit(solution)/shard_map/ppermute | solution.py:293
  28.7 3.8 %collective-permute-start.6 = (s32[10,8,512]{2,1,0:T(8,128)}, s32[10,8,512]{2,1,0:T(8,128)S(1)}, u32[]{:S(2)}, u32[]{:S(2)}) collective-permute-start(s32[10,8,512]{2,1,0:T(8,128)} %get-tuple-element.18), channel_id=1, source_target_pairs={{8,0},{16,8},{24,16},{9,1},{17,9},{25,17},{10,2},{18,10},{26,18},{... | collective-permute-start | bytes 491528 | tf_op jit(solution)/shard_map/ppermute | solution.py:293
  56.0 9.1 %collective-permute-start.8 = (f32[4,4,8,512]{3,2,1,0:T(8,128)S(1)}, f32[4,4,8,512]{3,2,1,0:T(8,128)S(1)}, u32[]{:S(2)}, u32[]{:S(2)}) collective-permute-start(f32[4,4,8,512]{3,2,1,0:T(8,128)S(1)} %dynamic-slice_bitcast_fusion), channel_id=1, source_target_pairs={{0,1},{1,0},{2,3},{3,2},{4,5},{5,4},{6,7},{7,6},{8,9},{9,8},{10,11... | collective-permute-start | bytes 786440 | tf_op jit(solution)/shard_map/ppermute | solution.py:311
  65.2 6.5 %collective-permute-start.11 = (f32[4,8,512]{2,1,0:T(8,128)S(1)}, f32[4,8,512]{2,1,0:T(8,128)S(1)}, u32[]{:S(2)}, u32[]{:S(2)}) collective-permute-start(f32[4,8,512]{2,1,0:T(8,128)S(1)} %get-tuple-element.21), channel_id=1, source_target_pairs={{0,6},{1,7},{2,4},{3,5},{4,2},{5,3},{6,0},{7,1},{8,14},{9,15},{10,... | collective-permute-start | bytes 196616 | tf_op jit(solution)/shard_map/ppermute | solution.py:317
  65.3 9.7 %collective-permute-start.10 = (f32[4,8,512]{2,1,0:T(8,128)S(1)}, f32[4,8,512]{2,1,0:T(8,128)S(1)}, u32[]{:S(2)}, u32[]{:S(2)}) collective-permute-start(f32[4,8,512]{2,1,0:T(8,128)S(1)} %get-tuple-element.22), channel_id=1, source_target_pairs={{0,4},{1,5},{2,6},{3,7},{4,0},{5,1},{6,2},{7,3},{8,12},{9,13},{10,... | collective-permute-start | bytes 196616 | tf_op jit(solution)/shard_map/ppermute | solution.py:317
  68.4 6.6 %collective-permute-start.9 = (f32[4,8,512]{2,1,0:T(8,128)S(1)}, f32[4,8,512]{2,1,0:T(8,128)S(1)}, u32[]{:S(2)}, u32[]{:S(2)}) collective-permute-start(f32[4,8,512]{2,1,0:T(8,128)S(1)} %get-tuple-element.20), channel_id=1, source_target_pairs={{0,2},{1,3},{2,0},{3,1},{4,6},{5,7},{6,4},{7,5},{8,10},{9,11},{10,... | collective-permute-start | bytes 196616 | tf_op jit(solution)/shard_map/ppermute | solution.py:317

commit v3 on v2

v3 whole, which is shorter than its diff:
```python
import functools
import math

import jax
import jax.numpy as jnp
import numpy as np
from jax import lax
from jax.experimental import pallas as pl
from jax.experimental.pallas import tpu as pltpu
from jax.sharding import PartitionSpec as P


gauss_taps = [
    math.exp(-offset * offset / 8.0)
    / sum((math.exp(-other * other / 8.0) for other in range(-4, 5)))
    for offset in range(-4, 5)
]
light_z = 0.48
light_x = 0.6
light_y = 0.64

REACH = 5
PAD = 8


def band(size):
    index = np.arange(size)
    apart = np.abs(index[:, None] - index[None, :])
    taps = np.array(gauss_taps[4:] + [0.0], np.float64)
    return taps[np.minimum(apart, 5)]


def split_terms(matrix):
    high = matrix.astype(jnp.bfloat16)
    low = (matrix - high.astype(np.float64)).astype(jnp.bfloat16)
    return high, low


def column_matrix(columns):
    return np.concatenate(split_terms(band(columns)), 0)


def row_matrices(rows):
    high, low = split_terms(band(rows + 2 * PAD))
    order = np.arange(rows + 2 * PAD)
    swapped = np.concatenate([order[rows + PAD :], order[PAD : rows + PAD], order[:PAD]])
    both = []
    for columns in (order, swapped):
        both.append(np.concatenate([high[:, columns], high[:, columns], low[:, columns]], 1))
    return np.stack(both)


def smooth_plane(counts, by, lx):
    rows = counts[0].shape[0]
    exact = jnp.concatenate([c.astype(jnp.float32).astype(jnp.bfloat16) for c in counts], 0)
    half = by.shape[0] // 2
    wide = jnp.dot(exact, by[:half], preferred_element_type=jnp.float32) + jnp.dot(
        exact, by[half:], preferred_element_type=jnp.float32
    )
    high = wide.astype(jnp.bfloat16)
    low = (wide - high.astype(jnp.float32)).astype(jnp.bfloat16)
    planes = []
    for n in range(len(counts)):
        part = slice(n * rows, (n + 1) * rows)
        stacked = jnp.concatenate([high[part], low[part], high[part]], 0)
        planes.append(jnp.dot(lx, stacked, preferred_element_type=jnp.float32))
    return planes


def smooth_depth(read, k):
    total = gauss_taps[4] * read(k)
    for offset in range(1, 5):
        total = total + gauss_taps[4 + offset] * (read(k - offset) + read(k + offset))
    return total


def smooth_depth_layer(flags, read, k, tiles, write):
    for tile in range(tiles):
        rows = pl.ds(tile * 8, 8)
        value = smooth_depth(lambda j: read(j, rows), k)
        if tile == 0:
            value = value * flags[0]
        if tile == tiles - 1:
            value = value * flags[1]
        write(rows, value)


def shade_voxels(prev, mid, above, below, following, scale):
    columns = mid.shape[1]
    lane = lax.broadcasted_iota(jnp.int32, mid.shape, 1)
    right = jnp.where(lane == columns - 1, 0.0, pltpu.roll(mid, columns - 1, 1))
    left = jnp.where(lane == 0, 0.0, pltpu.roll(mid, 1, 1))
    dz = following - prev
    dx = below - above
    dy = right - left
    slope = (1.5 * light_z) * dz + (1.5 * light_x) * dx + (1.5 * light_y) * dy
    shading = 0.55 + 0.45 * jnp.tanh(slope)
    gradient_sq4 = dz * dz + dx * dx + dy * dy
    square = mid * mid
    optical = scale * (square / (1.0 + square)) * (1.0 + gradient_sq4)
    centred = mid - 2.5
    red_share = 0.5 + 0.5 * jnp.tanh(centred)
    green_share = jnp.exp(-(centred * centred))
    return optical, shading, red_share, green_share


def render_layer(layer, k, base, carry, scale):
    red, green, blue, transmit = carry
    rows = pl.ds(base, 8)
    mid = layer(k, rows)
    before = layer(k, pl.ds(base - 8, 8))
    after = layer(k, pl.ds(base + 8, 8))
    sub = lax.broadcasted_iota(jnp.int32, mid.shape, 0)
    above = pltpu.roll(jnp.where(sub == 7, before, mid), 1, 0)
    below = pltpu.roll(jnp.where(sub == 0, after, mid), 7, 0)
    optical, shading, red_share, green_share = shade_voxels(
        layer(k - 1, rows), mid, above, below, layer(k + 1, rows), scale
    )
    remaining = transmit * jnp.exp(-optical)
    lit = (transmit - remaining) * shading
    red_part = lit * red_share
    return red + red_part, green + lit * green_share, blue + (lit - red_part), remaining


def empty_carry(columns):
    zero = jnp.zeros((8, columns), jnp.float32)
    return zero, zero, zero, jnp.ones_like(zero)


def read_tile(ref, tile):
    rows = pl.ds(pl.multiple_of(tile * 8, 8), 8)
    return tuple(ref[n, rows, :] for n in range(4))


def store_tile(ref, tile, values):
    rows = pl.ds(pl.multiple_of(tile * 8, 8), 8)
    for n, value in enumerate(values):
        ref[n, rows, :] = value


def run_copies(copies):
    for copy in copies:
        copy.start()
    for copy in copies:
        copy.wait()


def pack_edges_kernel(where, c, edge_a, edge_b, sems):
    rows = c.shape[1]
    copies = []
    for n, target in enumerate((edge_a, edge_b)):
        layers = pl.ds(where[n], REACH)
        for half, start in enumerate((0, rows - PAD)):
            source = c.at[layers, pl.ds(start, PAD)]
            part = target.at[:, pl.ds(half * PAD, PAD)]
            copies.append(pltpu.make_async_copy(source, part, sems.at[2 * n + half]))
    run_copies(copies)


def pack_rest_kernel(where, c, side_a, side_b, middle_a, middle_b, sems):
    rows = c.shape[1]
    copies = []
    for n, target in enumerate((side_a, side_b)):
        source = c.at[:, pl.ds(pl.multiple_of(where[2 + n], PAD), PAD)]
        copies.append(pltpu.make_async_copy(source, target, sems.at[n]))
    for n, target in enumerate((middle_a, middle_b)):
        source = c.at[pl.ds(where[n], REACH), pl.ds(PAD, rows - 2 * PAD)]
        copies.append(pltpu.make_async_copy(source, target, sems.at[2 + n]))
    run_copies(copies)


def smooth_kernel(group, order, c_hbm, xa, xb, by, lx, plane, c, sems):
    groups = c.shape[0] // group
    rows_of = order[0]

    def fetch(g):
        part = pl.ds(g * group, group)
        return pltpu.make_async_copy(c_hbm.at[part], c.at[part], sems.at[g])

    for g in range(groups):
        fetch(g).start()

    def smooth_group(g, _):
        first = g * group
        fetch(g).wait()
        counts = [
            jnp.concatenate([xa[first + n], c[first + n], xb[first + n]], 0) for n in range(group)
        ]
        for n, value in enumerate(smooth_plane(counts, by, lx[rows_of])):
            plane[first + n] = value
        return 0

    lax.fori_loop(0, groups, smooth_group, 0)


def interior_kernel(scale, flags, plane, image, smoothed):
    layers, ext, columns = plane.shape

    def one_layer(j, _):
        def write(rows, value):
            smoothed[j, rows, :] = value

        smooth_depth_layer(flags, lambda k, rows: plane[k, rows, :], j + 4, ext // 8, write)
        return 0

    lax.fori_loop(0, layers - 8, one_layer, 0)

    def one_tile(tile, _):
        base = pl.multiple_of(tile * 8 + 8, 8)
        carry = empty_carry(columns)
        for k in range(1, layers - 9):
            carry = render_layer(lambda k, rows: smoothed[k, rows, :], k, base, carry, scale)
        store_tile(image, tile, carry)
        return 0

    lax.fori_loop(0, ext // 8 - 2, one_tile, 0)


def edge_kernel(
    scale, flags, order, plane, smoothed, edge_a, edge_b, mid_a, mid_b, ca, cb, by, lx, inner,
    image, halo, ends,
):
    layers, ext, columns = plane.shape
    rows_of, depth_of = order[0], order[1]
    counts = []
    for n, (edge, middle) in enumerate(((edge_a, mid_a), (edge_b, mid_b))):
        for j in range(REACH):
            at = n * REACH + j
            counts.append(
                jnp.concatenate([ca[at], edge[j, :PAD], middle[j], edge[j, PAD:], cb[at]], 0)
            )
    for at, value in enumerate(smooth_plane(counts, by, lx[rows_of])):
        slot = jnp.where(depth_of == 1, at, (at + REACH) % (2 * REACH))
        halo[slot] = value

    def counted(k, rows):
        if k < 0:
            return halo[k + REACH, rows, :]
        if k >= layers:
            return halo[k - layers + REACH, rows, :]
        return plane[k, rows, :]

    front_layers = range(-1, 4)
    back_layers = range(layers - 4, layers + 1)
    for j, k in enumerate([*front_layers, *back_layers]):

        def write(rows, value, j=j, k=k):
            if k < 0:
                value = value * flags[2]
            if k >= layers:
                value = value * flags[3]
            ends[j, rows, :] = value

        smooth_depth_layer(flags, counted, k, ext // 8, write)

    def layer(k, rows):
        if k < 4:
            return ends[k + 1, rows, :]
        if k >= layers - 4:
            return ends[k - (layers - 4) + REACH, rows, :]
        return smoothed[k - 4, rows, :]

    def one_tile(tile, _):
        base = pl.multiple_of(tile * 8 + 8, 8)
        carry = empty_carry(columns)
        for k in range(REACH):
            carry = render_layer(layer, k, base, carry, scale)
        behind = read_tile(inner, tile)
        carry = tuple(carry[n] + carry[3] * behind[n] for n in range(3)) + (carry[3] * behind[3],)
        for k in range(layers - REACH, layers):
            carry = render_layer(layer, k, base, carry, scale)
        store_tile(image, tile, carry)
        return 0

    lax.fori_loop(0, ext // 8 - 2, one_tile, 0)


def whole(count):
    return [pl.BlockSpec(memory_space=pltpu.VMEM)] * count


def smem():
    return pl.BlockSpec(memory_space=pltpu.SMEM)


def in_hbm():
    return pl.BlockSpec(memory_space=pltpu.HBM)


def params(mib):
    return pltpu.CompilerParams(vmem_limit_bytes=mib * 1024 * 1024)


def cost(flops):
    return pl.CostEstimate(flops=flops, transcendentals=0, bytes_accessed=4_000_000)


def call_pack_edges(where, c):
    _, _, columns = c.shape
    shape = jax.ShapeDtypeStruct((REACH, 2 * PAD, columns), c.dtype)
    return pl.pallas_call(
        pack_edges_kernel,
        out_shape=(shape, shape),
        in_specs=[smem(), in_hbm()],
        out_specs=tuple(whole(2)),
        scratch_shapes=[pltpu.SemaphoreType.DMA((4,))],
        compiler_params=params(8),
        name="pack_edges",
    )(where, c)


def call_pack_rest(where, c):
    layers, rows, columns = c.shape
    side = jax.ShapeDtypeStruct((layers, PAD, columns), c.dtype)
    middle = jax.ShapeDtypeStruct((REACH, rows - 2 * PAD, columns), c.dtype)
    return pl.pallas_call(
        pack_rest_kernel,
        out_shape=(side, side, middle, middle),
        in_specs=[smem(), in_hbm()],
        out_specs=tuple(whole(4)),
        scratch_shapes=[pltpu.SemaphoreType.DMA((4,))],
        compiler_params=params(8),
        name="pack_rest",
    )(where, c)


def call_smooth(order, c, xa, xb, by, lx):
    layers, rows, columns = c.shape
    ext = rows + 2 * PAD
    group = 4
    return pl.pallas_call(
        functools.partial(smooth_kernel, group),
        out_shape=jax.ShapeDtypeStruct((layers, ext, columns), jnp.float32),
        in_specs=[smem(), in_hbm()] + whole(4),
        out_specs=whole(1)[0],
        scratch_shapes=[
            pltpu.VMEM((layers, rows, columns), jnp.int32),
            pltpu.SemaphoreType.DMA((layers // group,)),
        ],
        compiler_params=params(24),
        cost_estimate=cost(1_000_000_000),
        name="smooth",
    )(order, c, xa, xb, by, lx)


def call_interior(scale, flags, plane):
    layers, ext, columns = plane.shape
    return pl.pallas_call(
        functools.partial(interior_kernel, scale),
        out_shape=(
            jax.ShapeDtypeStruct((4, ext - 2 * PAD, columns), jnp.float32),
            jax.ShapeDtypeStruct((layers - 8, ext, columns), jnp.float32),
        ),
        in_specs=[smem()] + whole(1),
        out_specs=tuple(whole(2)),
        compiler_params=params(24),
        cost_estimate=cost(1_000_000_000),
        name="interior",
    )(flags, plane)


def call_edge(scale, flags, order, plane, *operands):
    _, ext, columns = plane.shape
    f32 = jnp.float32
    return pl.pallas_call(
        functools.partial(edge_kernel, scale),
        out_shape=jax.ShapeDtypeStruct((4, ext - 2 * PAD, columns), f32),
        in_specs=[smem(), smem()] + whole(1 + len(operands)),
        out_specs=whole(1)[0],
        scratch_shapes=[
            pltpu.VMEM((2 * REACH, ext, columns), f32),
            pltpu.VMEM((2 * REACH, ext, columns), f32),
        ],
        compiler_params=params(32),
        cost_estimate=cost(300_000_000),
        name="edges",
    )(flags, order, plane, *operands)


def swap(value, axis, first):
    count = lax.axis_size(axis)
    pairs = []
    for low in range(first, count - 1, 2):
        pairs += [(low, low + 1), (low + 1, low)]
    return lax.ppermute(value, axis, pairs)


def over(front, back):
    through = front[3:]
    return jnp.concatenate([front[:3] + through * back[:3], through * back[3:]], 0)


def exchange(layers):
    count = lax.axis_size("depth")
    me = lax.axis_index("depth")
    _, rows, columns = layers.shape
    owned = rows // count
    parity, pair = me % 2, me // 2
    pairs = count // 2
    pieces = layers.reshape(4, pairs, 2, owned, columns)
    send = lax.dynamic_index_in_dim(pieces, 1 - parity, 2, keepdims=False)
    keep = lax.dynamic_index_in_dim(pieces, parity, 2, keepdims=False)
    got = lax.ppermute(send, "depth", [(i, i ^ 1) for i in range(count)])
    joined = jnp.where(parity == 0, over(keep, got), over(got, keep))
    parts = []
    for step in range(pairs):
        piece = lax.dynamic_index_in_dim(joined, pair ^ step, 1, keepdims=False)
        if step:
            piece = lax.ppermute(piece, "depth", [(i, i ^ (2 * step)) for i in range(count)])
        parts.append(piece)
    result = jnp.zeros((3, owned, columns), jnp.float32)
    through = jnp.ones((1, owned, columns), jnp.float32)
    for step in range(pairs):
        ahead = jnp.ones((1, owned, columns), jnp.float32)
        for other in range(pairs):
            if other != step:
                nearer = (pair ^ other) < (pair ^ step)
                ahead = ahead * jnp.where(nearer, parts[other][3:], 1.0)
        result = result + ahead * parts[step][:3]
        through = through * parts[step][3:]
    return jnp.concatenate([result, 1.0 - through], 0)


def local(counts):
    slab, rows, columns = counts.shape
    img, depth = lax.axis_index("img"), lax.axis_index("depth")
    imgs, depths = lax.axis_size("img"), lax.axis_size("depth")
    scale = 1.5 / (slab * depths)
    row_odd, depth_odd = img % 2, depth % 2
    first_a, first_b = (1 - depth_odd) * (slab - REACH), depth_odd * (slab - REACH)
    row_a, row_b = (1 - row_odd) * (rows - PAD), row_odd * (rows - PAD)
    where = jnp.stack([first_a, first_b, row_a, row_b])
    order = jnp.stack([1 - row_odd, depth_odd])
    one = jnp.float32(1.0)
    flags = jnp.stack(
        [(img > 0) * one, (img < imgs - 1) * one, (depth > 0) * one, (depth < depths - 1) * one]
    )
    by = jnp.asarray(column_matrix(columns))
    lx = jnp.asarray(row_matrices(rows))
    held = pltpu.with_memory_space_constraint(counts, pltpu.HBM)
    edge_a, edge_b = call_pack_edges(where, held)
    side_a, side_b, mid_a, mid_b = call_pack_rest(where, held)
    edge_a = swap(edge_a, "depth", 0)
    edge_b = swap(edge_b, "depth", 1)
    xa = swap(side_a, "img", 0)
    xb = swap(side_b, "img", 1)
    mid_a = swap(mid_a, "depth", 0)
    mid_b = swap(mid_b, "depth", 1)
    halves = jnp.concatenate([edge_a, edge_b], 0).reshape(2 * REACH, 2, PAD, columns)
    corner_a = lax.dynamic_index_in_dim(halves, 1 - row_odd, 1, keepdims=False)
    corner_b = lax.dynamic_index_in_dim(halves, row_odd, 1, keepdims=False)
    ca = swap(corner_a, "img", 0)
    cb = swap(corner_b, "img", 1)
    plane = call_smooth(order, held, xa, xb, by, lx)
    inner, smoothed = call_interior(scale, flags, plane)
    layers = call_edge(
        scale, flags, order, plane, smoothed, edge_a, edge_b, mid_a, mid_b, ca, cb, by, lx, inner
    )
    return exchange(layers)


def solution(mesh):
    in_specs = (P("depth", "img", None),)
    out_specs = P(None, ("img", "depth"), None)
    return jax.shard_map(local, mesh=mesh, in_specs=in_specs, out_specs=out_specs, check_vma=False)
```

time: 76.1 us -> 68.4 us (0.90)
  local copies, waits for them, and re-layouts: 7.17 us -> 0.1 us
  Pallas kernels: 21 us -> 25.4 us
  waiting for transfers between devices: 16.7 us -> 13.5 us
  starting transfers between devices: 29.6 us -> 27.9 us
    slice x6 -> x0, local copies, waits for them, and re-layouts: 7.09 us -> none  [the longest x1 2.19 us: local(): front_mid = shift(bottom[:, PAD:rows - PAD], 'depth', 1)]
    ppermute x8, starting transfers between devices: 22.6 us -> 18 us  [swap(): return lax.ppermute(value, axis, pairs)]
    pallas_call x3 -> x4, Pallas kernels: 14 us -> 17.9 us  [the longest x1 7.31 us: call_interior(): pl.pallas_call(functools.partial(interior_kernel, scale), out_shape=(jax....]
    ppermute x1, starting transfers between devices: 2.55 us -> 5.07 us  [exchange(): got = lax.ppermute(send, 'depth', [(i, i ^ 1) for i in range(count)])]
    ppermute x8, waiting for transfers between devices: 4.91 us -> 2.69 us  [swap(): return lax.ppermute(value, axis, pairs)]
    ppermute x1, waiting for transfers between devices: 6.53 us -> 4.86 us  [exchange(): got = lax.ppermute(send, 'depth', [(i, i ^ 1) for i in range(count)])]
  transfers between devices with their start and end apart: 12 -> 12, of which waited for: 6 -> 5; matrix products, arithmetic and copies ran while one was open for 8% -> 0% of each run, Pallas kernels for 24% -> 25%
where the time goes in v3:
time: 68.4 us; the launch traced here: 68.1 us
  starting transfers between devices  27.9 us (41%)
  Pallas kernels  25.4 us (37%)
  waiting for transfers between devices  13.5 us (20%)
  other arithmetic  1.05 us (2%)
    ppermute x8, starting transfers between devices, swap(): return lax.ppermute(value, axis, pairs)  18 us
    pallas_call x1, Pallas kernels, call_smooth(): pl.pallas_call(functools.partial(smooth_kernel, group), out_shape=jax.Sha...  7.54 us
    pallas_call x1, Pallas kernels, call_interior(): pl.pallas_call(functools.partial(interior_kernel, scale), out_shape=(jax....  7.31 us
    ppermute x3, waiting for transfers between devices, exchange(): lax.ppermute(piece, 'depth', [(i, i ^ 2 * step) for i in range(count)])  5.9 us
    pallas_call x1, Pallas kernels, call_edge(): pl.pallas_call(functools.partial(edge_kernel, scale), out_shape=jax.Shape...  5.18 us
    ppermute x1, starting transfers between devices, exchange(): got = lax.ppermute(send, 'depth', [(i, i ^ 1) for i in range(count)])  5.07 us
    ppermute x3, starting transfers between devices, exchange(): lax.ppermute(piece, 'depth', [(i, i ^ 2 * step) for i in range(count)])  4.87 us
    ppermute x1, waiting for transfers between devices, exchange(): got = lax.ppermute(send, 'depth', [(i, i ^ 1) for i in range(count)])  4.86 us
  transfers between devices with their start and end apart: 12, of which 5 were waited for; matrix products, arithmetic and copies ran while one was open for 0% of the time, Pallas kernels for 25%

profile of v3, /device:TPU:0, one launch (start us, length us, event | category | flops | bytes accessed | tf_op | source)
XLA Modules:
  0.0 68.1 jit_solution(16295296883844649724)
XLA Ops:
  0.1 3.1 %pack_rest.1 = (s32[32,8,512]{2,1,0:T(8,128)}, s32[32,8,512]{2,1,0:T(8,128)S(1)}, s32[5,48,512]{2,1,0:T(8,128)}, s32[5,48,512]{2,1,0:T(8,128)S(1)}) custom-call(s32[4]{0:T(128)S(1)} %pad_add_fusion.1.where, s32[32,64,512]{2,1,0:T(8,128)} %c.3), custom_call_target="tpu_custom_call" | custom-call | tf_op jit(solution)/shard_map/pack_rest/pallas_call | solution.py:316
  3.2 0.6 collective-permute-start
  3.7 0.7 %collective-permute-start.1 = (s32[32,8,512]{2,1,0:T(8,128)S(1)}, s32[32,8,512]{2,1,0:T(8,128)S(1)}, u32[]{:S(2)}, u32[]{:S(2)}) collective-permute-start(s32[32,8,512]{2,1,0:T(8,128)S(1)} %get-tuple-element.14), channel_id=1, source_target_pairs={{8,16},{16,8},{9,17},{17,9},{10,18},{18,10},{11,19},{19,11},{12,20... | collective-permute-start | bytes 1572872 | tf_op jit(solution)/shard_map/ppermute | solution.py:385
  4.4 2.3 %pack_edges.1 = (s32[5,16,512]{2,1,0:T(8,128)}, s32[5,16,512]{2,1,0:T(8,128)}) custom-call(s32[4]{0:T(128)S(1)} %pad_add_fusion.1.where, s32[32,64,512]{2,1,0:T(8,128)} %c.3), custom_call_target="tpu_custom_call" | custom-call | tf_op jit(solution)/shard_map/pack_edges/pallas_call | solution.py:301
  6.7 2.6 %collective-permute-start.2 = (s32[5,16,512]{2,1,0:T(8,128)}, s32[5,16,512]{2,1,0:T(8,128)S(1)}, u32[]{:S(2)}, u32[]{:S(2)}) collective-permute-start(s32[5,16,512]{2,1,0:T(8,128)} %get-tuple-element.16), channel_id=1, source_target_pairs={{0,1},{1,0},{2,3},{3,2},{4,5},{5,4},{6,7},{7,6},{8,9},{9,8},{10,11... | collective-permute-start | bytes 491528 | tf_op jit(solution)/shard_map/ppermute | solution.py:385
  9.3 0.1 collective-permute-start.4
  9.4 0.7 collective-permute-start.3
  10.1 2.7 %collective-permute-done.2.edge_a = s32[5,16,512]{2,1,0:T(8,128)S(1)} collective-permute-done((s32[5,16,512]{2,1,0:T(8,128)}, s32[5,16,512]{2,1,0:T(8,128)S(1)}, u32[]{:S(2)}, u32[]{:S(2)}) %collective-permute-start.2) | collective-permute-done | bytes 163872 | tf_op jit(solution)/shard_map/ppermute | solution.py:385
  12.8 0.7 collective-permute-start.5
  13.5 0.1 add_convert_fusion.flags
  13.6 12.1 %collective-permute-start.6 = (s32[10,8,512]{2,1,0:T(8,128)S(1)}, s32[10,8,512]{2,1,0:T(8,128)S(1)}, u32[]{:S(2)}, u32[]{:S(2)}) collective-permute-start(s32[10,8,512]{2,1,0:T(8,128)S(1)} %get-tuple-element.27), channel_id=1, source_target_pairs={{0,8},{8,0},{16,24},{24,16},{1,9},{9,1},{17,25},{25,17},{2,10},{10... | collective-permute-start | bytes 491528 | tf_op jit(solution)/shard_map/ppermute | solution.py:385
  25.7 0.7 collective-permute-start.7
  26.4 7.5 %smooth.1.plane = f32[32,80,512]{2,1,0:T(8,128)S(1)} custom-call(s32[2]{0:T(128)S(1)} %pad_add_fusion.order, s32[32,64,512]{2,1,0:T(8,128)} %c.3, s32[32,8,512]{2,1,0:T(8,128)S(1)} %collective-permute-done.xa, s32[32,8,512]{2,1,0:T(8,128)S(1)} %collective-permute-done.1.xb, bf16[1024,512]{1,0:T(8,128)(2,1)S(1)} %copy-done, bf16[2,80,240]{2,1,0:T(8,128)(2,1)S(1)} %copy-done.1), custom_call_target="tpu_custom_call" | custom-call | flops 1000000000 | bytes 4000000 | tf_op jit(solution)/shard_map/smooth/pallas_call | solution.py:331
  34.0 7.3 %interior.1 = (f32[4,64,512]{2,1,0:T(8,128)S(1)}, f32[24,80,512]{2,1,0:T(8,128)S(1)}) custom-call(f32[4]{0:T(128)S(1)} %add_convert_fusion.flags, f32[32,80,512]{2,1,0:T(8,128)S(1)} %smooth.1.plane), custom_call_target="tpu_custom_call" | custom-call | flops 1000000000 | bytes 4000000 | tf_op jit(solution)/shard_map/interior/pallas_call | solution.py:348
  41.3 5.2 %edges.1 = f32[4,64,512]{2,1,0:T(8,128)S(1)} custom-call(f32[4]{0:T(128)S(1)} %add_convert_fusion.flags, s32[2]{0:T(128)S(1)} %pad_add_fusion.order, f32[32,80,512]{2,1,0:T(8,128)S(1)} %smooth.1.plane, f32[24,80,512]{2,1,0:T(8,128)S(1)} %get-tuple-element.15.smoothed, s32[5,16,512]{2,1,0:T(8,128)S(1)} %collective-permute-done.2.edge_a, ...), custom_call_target="tpu_custom_call" | custom-call | flops 300000000 | bytes 4000000 | tf_op jit(solution)/shard_map/edges/pallas_call | solution.py:365
  46.6 5.1 %collective-permute-start.8 = (f32[4,4,8,512]{3,2,1,0:T(8,128)S(1)}, f32[4,4,8,512]{3,2,1,0:T(8,128)S(1)}, u32[]{:S(2)}, u32[]{:S(2)}) collective-permute-start(f32[4,4,8,512]{3,2,1,0:T(8,128)S(1)} %dynamic-slice_bitcast_fusion), channel_id=1, source_target_pairs={{0,1},{1,0},{2,3},{3,2},{4,5},{5,4},{6,7},{7,6},{8,9},{9,8},{10,11... | collective-permute-start | bytes 786440 | tf_op jit(solution)/shard_map/ppermute | solution.py:403
  51.6 4.9 %collective-permute-done.8 = f32[4,4,8,512]{3,2,1,0:T(8,128)S(1)} collective-permute-done((f32[4,4,8,512]{3,2,1,0:T(8,128)S(1)}, f32[4,4,8,512]{3,2,1,0:T(8,128)S(1)}, u32[]{:S(2)}, u32[]{:S(2)}) %collective-permute-start.8) | collective-permute-done | bytes 262176 | tf_op jit(solution)/shard_map/ppermute | solution.py:403
  56.6 3.3 %collective-permute-start.10 = (f32[4,8,512]{2,1,0:T(8,128)S(1)}, f32[4,8,512]{2,1,0:T(8,128)S(1)}, u32[]{:S(2)}, u32[]{:S(2)}) collective-permute-start(f32[4,8,512]{2,1,0:T(8,128)S(1)} %get-tuple-element.30), channel_id=1, source_target_pairs={{0,4},{1,5},{2,6},{3,7},{4,0},{5,1},{6,2},{7,3},{8,12},{9,13},{10,... | collective-permute-start | bytes 196616 | tf_op jit(solution)/shard_map/ppermute | solution.py:409
  59.9 1.3 %collective-permute-start.11 = (f32[4,8,512]{2,1,0:T(8,128)S(1)}, f32[4,8,512]{2,1,0:T(8,128)S(1)}, u32[]{:S(2)}, u32[]{:S(2)}) collective-permute-start(f32[4,8,512]{2,1,0:T(8,128)S(1)} %get-tuple-element.29), channel_id=1, source_target_pairs={{0,6},{1,7},{2,4},{3,5},{4,2},{5,3},{6,0},{7,1},{8,14},{9,15},{10,... | collective-permute-start | bytes 196616 | tf_op jit(solution)/shard_map/ppermute | solution.py:409
  61.3 0.2 collective-permute-start.9
  61.5 0.7 collective-permute-done.10
  62.2 4.0 %collective-permute-done.11 = f32[4,8,512]{2,1,0:T(8,128)S(1)} collective-permute-done((f32[4,8,512]{2,1,0:T(8,128)S(1)}, f32[4,8,512]{2,1,0:T(8,128)S(1)}, u32[]{:S(2)}, u32[]{:S(2)}) %collective-permute-start.11) | collective-permute-done | bytes 65568 | tf_op jit(solution)/shard_map/ppermute | solution.py:409
  66.2 1.2 %collective-permute-done.9 = f32[4,8,512]{2,1,0:T(8,128)S(1)} collective-permute-done((f32[4,8,512]{2,1,0:T(8,128)S(1)}, f32[4,8,512]{2,1,0:T(8,128)S(1)}, u32[]{:S(2)}, u32[]{:S(2)}) %collective-permute-start.9) | collective-permute-done | bytes 65568 | tf_op jit(solution)/shard_map/ppermute | solution.py:409
  67.5 0.6 pad_maximum_fusion.2
  (26 shorter events, 0.5 us)
Async XLA Ops:
  0.1 26.3 %copy-start = (bf16[1024,512]{1,0:T(8,128)(2,1)S(1)}, bf16[1024,512]{1,0:T(8,128)(2,1)}, u32[]{:S(2)}) copy-start(bf16[1024,512]{1,0:T(8,128)(2,1)} %constant.80.clone.by) | copy-start | bytes 3145732
  0.1 26.3 %copy-start.1 = (bf16[2,80,240]{2,1,0:T(8,128)(2,1)S(1)}, bf16[2,80,240]{2,1,0:T(8,128)(2,1)}, u32[]{:S(2)}) copy-start(bf16[2,80,240]{2,1,0:T(8,128)(2,1)} %constant.81.clone.lx) | copy-start | bytes 230404
  3.1 6.9 %copy-start.2 = (s32[5,48,512]{2,1,0:T(8,128)}, s32[5,48,512]{2,1,0:T(8,128)S(1)}, u32[]{:S(2)}) copy-start(s32[5,48,512]{2,1,0:T(8,128)S(1)} %get-tuple-element.19) | copy-start | bytes 1474564
  3.2 22.6 %collective-permute-start = (s32[32,8,512]{2,1,0:T(8,128)}, s32[32,8,512]{2,1,0:T(8,128)S(1)}, u32[]{:S(2)}, u32[]{:S(2)}) collective-permute-start(s32[32,8,512]{2,1,0:T(8,128)} %get-tuple-element.13), channel_id=1, source_target_pairs={{0,8},{8,0},{16,24},{24,16},{1,9},{9,1},{17,25},{25,17},{2,10},{10... | collective-permute-start | bytes 1572872 | tf_op jit(solution)/shard_map/ppermute | solution.py:385
  3.7 22.7 %collective-permute-start.1 = (s32[32,8,512]{2,1,0:T(8,128)S(1)}, s32[32,8,512]{2,1,0:T(8,128)S(1)}, u32[]{:S(2)}, u32[]{:S(2)}) collective-permute-start(s32[32,8,512]{2,1,0:T(8,128)S(1)} %get-tuple-element.14), channel_id=1, source_target_pairs={{8,16},{16,8},{9,17},{17,9},{10,18},{18,10},{11,19},{19,11},{12,20... | collective-permute-start | bytes 1572872 | tf_op jit(solution)/shard_map/ppermute | solution.py:385
  6.7 6.1 %collective-permute-start.2 = (s32[5,16,512]{2,1,0:T(8,128)}, s32[5,16,512]{2,1,0:T(8,128)S(1)}, u32[]{:S(2)}, u32[]{:S(2)}) collective-permute-start(s32[5,16,512]{2,1,0:T(8,128)} %get-tuple-element.16), channel_id=1, source_target_pairs={{0,1},{1,0},{2,3},{3,2},{4,5},{5,4},{6,7},{7,6},{8,9},{9,8},{10,11... | collective-permute-start | bytes 491528 | tf_op jit(solution)/shard_map/ppermute | solution.py:385
  9.3 32.0 %collective-permute-start.4 = (s32[5,48,512]{2,1,0:T(8,128)}, s32[5,48,512]{2,1,0:T(8,128)S(1)}, u32[]{:S(2)}, u32[]{:S(2)}) collective-permute-start(s32[5,48,512]{2,1,0:T(8,128)} %get-tuple-element.18), channel_id=1, source_target_pairs={{0,1},{1,0},{2,3},{3,2},{4,5},{5,4},{6,7},{7,6},{8,9},{9,8},{10,11... | collective-permute-start | bytes 1474568 | tf_op jit(solution)/shard_map/ppermute | solution.py:385
  9.4 4.2 %collective-permute-start.3 = (s32[5,16,512]{2,1,0:T(8,128)}, s32[5,16,512]{2,1,0:T(8,128)S(1)}, u32[]{:S(2)}, u32[]{:S(2)}) collective-permute-start(s32[5,16,512]{2,1,0:T(8,128)} %get-tuple-element.17), channel_id=1, source_target_pairs={{1,2},{2,1},{3,4},{4,3},{5,6},{6,5},{9,10},{10,9},{11,12},{12,11},... | collective-permute-start | bytes 491528 | tf_op jit(solution)/shard_map/ppermute | solution.py:385
  12.8 28.5 %collective-permute-start.5 = (s32[5,48,512]{2,1,0:T(8,128)}, s32[5,48,512]{2,1,0:T(8,128)S(1)}, u32[]{:S(2)}, u32[]{:S(2)}) collective-permute-start(s32[5,48,512]{2,1,0:T(8,128)} %copy-done.2), channel_id=1, source_target_pairs={{1,2},{2,1},{3,4},{4,3},{5,6},{6,5},{9,10},{10,9},{11,12},{12,11},... | collective-permute-start | bytes 1474568 | tf_op jit(solution)/shard_map/ppermute | solution.py:385
  13.6 27.7 %collective-permute-start.6 = (s32[10,8,512]{2,1,0:T(8,128)S(1)}, s32[10,8,512]{2,1,0:T(8,128)S(1)}, u32[]{:S(2)}, u32[]{:S(2)}) collective-permute-start(s32[10,8,512]{2,1,0:T(8,128)S(1)} %get-tuple-element.27), channel_id=1, source_target_pairs={{0,8},{8,0},{16,24},{24,16},{1,9},{9,1},{17,25},{25,17},{2,10},{10... | collective-permute-start | bytes 491528 | tf_op jit(solution)/shard_map/ppermute | solution.py:385
  25.7 15.6 %collective-permute-start.7 = (s32[10,8,512]{2,1,0:T(8,128)S(1)}, s32[10,8,512]{2,1,0:T(8,128)S(1)}, u32[]{:S(2)}, u32[]{:S(2)}) collective-permute-start(s32[10,8,512]{2,1,0:T(8,128)S(1)} %get-tuple-element.26), channel_id=1, source_target_pairs={{8,16},{16,8},{9,17},{17,9},{10,18},{18,10},{11,19},{19,11},{12,20... | collective-permute-start | bytes 491528 | tf_op jit(solution)/shard_map/ppermute | solution.py:385
  46.6 9.9 %collective-permute-start.8 = (f32[4,4,8,512]{3,2,1,0:T(8,128)S(1)}, f32[4,4,8,512]{3,2,1,0:T(8,128)S(1)}, u32[]{:S(2)}, u32[]{:S(2)}) collective-permute-start(f32[4,4,8,512]{3,2,1,0:T(8,128)S(1)} %dynamic-slice_bitcast_fusion), channel_id=1, source_target_pairs={{0,1},{1,0},{2,3},{3,2},{4,5},{5,4},{6,7},{7,6},{8,9},{9,8},{10,11... | collective-permute-start | bytes 786440 | tf_op jit(solution)/shard_map/ppermute | solution.py:403
  56.6 5.5 %collective-permute-start.10 = (f32[4,8,512]{2,1,0:T(8,128)S(1)}, f32[4,8,512]{2,1,0:T(8,128)S(1)}, u32[]{:S(2)}, u32[]{:S(2)}) collective-permute-start(f32[4,8,512]{2,1,0:T(8,128)S(1)} %get-tuple-element.30), channel_id=1, source_target_pairs={{0,4},{1,5},{2,6},{3,7},{4,0},{5,1},{6,2},{7,3},{8,12},{9,13},{10,... | collective-permute-start | bytes 196616 | tf_op jit(solution)/shard_map/ppermute | solution.py:409
  59.9 6.3 %collective-permute-start.11 = (f32[4,8,512]{2,1,0:T(8,128)S(1)}, f32[4,8,512]{2,1,0:T(8,128)S(1)}, u32[]{:S(2)}, u32[]{:S(2)}) collective-permute-start(f32[4,8,512]{2,1,0:T(8,128)S(1)} %get-tuple-element.29), channel_id=1, source_target_pairs={{0,6},{1,7},{2,4},{3,5},{4,2},{5,3},{6,0},{7,1},{8,14},{9,15},{10,... | collective-permute-start | bytes 196616 | tf_op jit(solution)/shard_map/ppermute | solution.py:409
  61.3 6.1 %collective-permute-start.9 = (f32[4,8,512]{2,1,0:T(8,128)S(1)}, f32[4,8,512]{2,1,0:T(8,128)S(1)}, u32[]{:S(2)}, u32[]{:S(2)}) collective-permute-start(f32[4,8,512]{2,1,0:T(8,128)S(1)} %get-tuple-element.28), channel_id=1, source_target_pairs={{0,2},{1,3},{2,0},{3,1},{4,6},{5,7},{6,4},{7,5},{8,10},{9,11},{10,... | collective-permute-start | bytes 196616 | tf_op jit(solution)/shard_map/ppermute | solution.py:409

commit v4 on v3

--- a/solution.py
+++ b/solution.py
@@ -138,35 +138,24 @@
         ref[n, rows, :] = value
 
 
-def run_copies(copies):
+def pack_kernel(where, c, edge_a, side_b, edge_b, side_a, middle_a, middle_b, sems):
+    rows = c.shape[1]
+    copies = []
+
+    def add(source, target):
+        copies.append(pltpu.make_async_copy(source, target, sems.at[len(copies)]))
+
+    sides = (side_a, side_b)
+    for n, (edge, middle) in enumerate(((edge_a, middle_a), (edge_b, middle_b))):
+        layers = pl.ds(where[n], REACH)
+        add(c.at[layers, pl.ds(0, PAD)], edge.at[:, pl.ds(0, PAD)])
+        add(c.at[layers, pl.ds(rows - PAD, PAD)], edge.at[:, pl.ds(PAD, PAD)])
+        add(c.at[layers, pl.ds(PAD, rows - 2 * PAD)], middle)
+        add(c.at[:, pl.ds(pl.multiple_of(where[2 + n], PAD), PAD)], sides[n])
     for copy in copies:
         copy.start()
     for copy in copies:
         copy.wait()
-
-
-def pack_edges_kernel(where, c, edge_a, edge_b, sems):
-    rows = c.shape[1]
-    copies = []
-    for n, target in enumerate((edge_a, edge_b)):
-        layers = pl.ds(where[n], REACH)
-        for half, start in enumerate((0, rows - PAD)):
-            source = c.at[layers, pl.ds(start, PAD)]
-            part = target.at[:, pl.ds(half * PAD, PAD)]
-            copies.append(pltpu.make_async_copy(source, part, sems.at[2 * n + half]))
-    run_copies(copies)
-
-
-def pack_rest_kernel(where, c, side_a, side_b, middle_a, middle_b, sems):
-    rows = c.shape[1]
-    copies = []
-    for n, target in enumerate((side_a, side_b)):
-        source = c.at[:, pl.ds(pl.multiple_of(where[2 + n], PAD), PAD)]
-        copies.append(pltpu.make_async_copy(source, target, sems.at[n]))
-    for n, target in enumerate((middle_a, middle_b)):
-        source = c.at[pl.ds(where[n], REACH), pl.ds(PAD, rows - 2 * PAD)]
-        copies.append(pltpu.make_async_copy(source, target, sems.at[2 + n]))
-    run_copies(copies)
 
 
 def smooth_kernel(group, order, c_hbm, xa, xb, by, lx, plane, c, sems):
@@ -217,59 +206,49 @@
 
 
 def edge_kernel(
-    scale, flags, order, plane, smoothed, edge_a, edge_b, mid_a, mid_b, ca, cb, by, lx, inner,
+    scale, turn, flags, order, plane, smoothed, edge, middle, ca, cb, by, lx, behind,
     image, halo, ends,
 ):
     layers, ext, columns = plane.shape
-    rows_of, depth_of = order[0], order[1]
-    counts = []
-    for n, (edge, middle) in enumerate(((edge_a, mid_a), (edge_b, mid_b))):
-        for j in range(REACH):
-            at = n * REACH + j
-            counts.append(
-                jnp.concatenate([ca[at], edge[j, :PAD], middle[j], edge[j, PAD:], cb[at]], 0)
-            )
-    for at, value in enumerate(smooth_plane(counts, by, lx[rows_of])):
-        slot = jnp.where(depth_of == 1, at, (at + REACH) % (2 * REACH))
-        halo[slot] = value
-
-    def counted(k, rows):
-        if k < 0:
-            return halo[k + REACH, rows, :]
-        if k >= layers:
-            return halo[k - layers + REACH, rows, :]
-        return plane[k, rows, :]
-
-    front_layers = range(-1, 4)
-    back_layers = range(layers - 4, layers + 1)
-    for j, k in enumerate([*front_layers, *back_layers]):
-
-        def write(rows, value, j=j, k=k):
-            if k < 0:
-                value = value * flags[2]
-            if k >= layers:
-                value = value * flags[3]
-            ends[j, rows, :] = value
-
-        smooth_depth_layer(flags, counted, k, ext // 8, write)
-
-    def layer(k, rows):
-        if k < 4:
-            return ends[k + 1, rows, :]
-        if k >= layers - 4:
-            return ends[k - (layers - 4) + REACH, rows, :]
-        return smoothed[k - 4, rows, :]
+    rows_of = order[0]
+    is_front = order[1] == 1 - turn
+    sign = jnp.where(is_front, 1, -1)
+    counts = [
+        jnp.concatenate([ca[j], edge[j, :PAD], middle[j], edge[j, PAD:], cb[j]], 0)
+        for j in range(REACH)
+    ]
+    for j, value in enumerate(smooth_plane(counts, by, lx[rows_of])):
+        halo[j] = value
+    plane_face = jnp.where(is_front, 0, layers - 1)
+    halo_face = jnp.where(is_front, REACH, -1)
+    ends_face = jnp.where(is_front, 1, REACH)
+    smoothed_face = jnp.where(is_front, -4, layers - 5)
+    on_grid = jnp.where(is_front, flags[2], flags[3])
+
+    def counted(v, rows):
+        if v < 0:
+            return halo[halo_face + sign * v, rows, :]
+        return plane[plane_face + sign * v, rows, :]
+
+    for v in range(-1, 4):
+
+        def write(rows, value, v=v):
+            ends[ends_face + sign * v, rows, :] = value * on_grid if v < 0 else value
+
+        smooth_depth_layer(flags, counted, v, ext // 8, write)
+    for v in (4, 5):
+        ends[ends_face + sign * v] = smoothed[smoothed_face + sign * v]
 
     def one_tile(tile, _):
         base = pl.multiple_of(tile * 8 + 8, 8)
         carry = empty_carry(columns)
-        for k in range(REACH):
-            carry = render_layer(layer, k, base, carry, scale)
-        behind = read_tile(inner, tile)
-        carry = tuple(carry[n] + carry[3] * behind[n] for n in range(3)) + (carry[3] * behind[3],)
-        for k in range(layers - REACH, layers):
-            carry = render_layer(layer, k, base, carry, scale)
-        store_tile(image, tile, carry)
+        for k in range(1, REACH + 1):
+            carry = render_layer(lambda k, rows: ends[k, rows, :], k, base, carry, scale)
+        other = read_tile(behind, tile)
+        front = [jnp.where(is_front, x, y) for x, y in zip(carry, other)]
+        back = [jnp.where(is_front, y, x) for x, y in zip(carry, other)]
+        colors = [front[n] + front[3] * back[n] for n in range(3)]
+        store_tile(image, tile, colors + [front[3] * back[3]])
         return 0
 
     lax.fori_loop(0, ext // 8 - 2, one_tile, 0)
@@ -295,32 +274,19 @@
     return pl.CostEstimate(flops=flops, transcendentals=0, bytes_accessed=4_000_000)
 
 
-def call_pack_edges(where, c):
-    _, _, columns = c.shape
-    shape = jax.ShapeDtypeStruct((REACH, 2 * PAD, columns), c.dtype)
+def call_pack(where, c):
+    layers, rows, columns = c.shape
+    edge = pltpu.VMEM((REACH, 2 * PAD, columns), c.dtype)
+    side = pltpu.VMEM((layers, PAD, columns), c.dtype)
+    middle = pltpu.VMEM((REACH, rows - 2 * PAD, columns), c.dtype)
     return pl.pallas_call(
-        pack_edges_kernel,
-        out_shape=(shape, shape),
+        pack_kernel,
+        out_shape=(edge, side, edge, side, middle, middle),
         in_specs=[smem(), in_hbm()],
-        out_specs=tuple(whole(2)),
-        scratch_shapes=[pltpu.SemaphoreType.DMA((4,))],
+        out_specs=tuple(whole(6)),
+        scratch_shapes=[pltpu.SemaphoreType.DMA((8,))],
         compiler_params=params(8),
-        name="pack_edges",
-    )(where, c)
-
-
-def call_pack_rest(where, c):
-    layers, rows, columns = c.shape
-    side = jax.ShapeDtypeStruct((layers, PAD, columns), c.dtype)
-    middle = jax.ShapeDtypeStruct((REACH, rows - 2 * PAD, columns), c.dtype)
-    return pl.pallas_call(
-        pack_rest_kernel,
-        out_shape=(side, side, middle, middle),
-        in_specs=[smem(), in_hbm()],
-        out_specs=tuple(whole(4)),
-        scratch_shapes=[pltpu.SemaphoreType.DMA((4,))],
-        compiler_params=params(8),
-        name="pack_rest",
+        name="pack",
     )(where, c)
 
 
@@ -359,21 +325,20 @@
     )(flags, plane)
 
 
-def call_edge(scale, flags, order, plane, *operands):
+def call_edge(scale, turn, flags, order, plane, *operands):
     _, ext, columns = plane.shape
     f32 = jnp.float32
     return pl.pallas_call(
-        functools.partial(edge_kernel, scale),
+        functools.partial(edge_kernel, scale, turn),
         out_shape=jax.ShapeDtypeStruct((4, ext - 2 * PAD, columns), f32),
         in_specs=[smem(), smem()] + whole(1 + len(operands)),
         out_specs=whole(1)[0],
         scratch_shapes=[
-            pltpu.VMEM((2 * REACH, ext, columns), f32),
-            pltpu.VMEM((2 * REACH, ext, columns), f32),
+            pltpu.VMEM((REACH, ext, columns), f32),
+            pltpu.VMEM((REACH + 2, ext, columns), f32),
         ],
-        compiler_params=params(32),
+        compiler_params=params(24),
         cost_estimate=cost(300_000_000),
-        name="edges",
     )(flags, order, plane, *operands)
 
 
@@ -438,8 +403,7 @@
     by = jnp.asarray(column_matrix(columns))
     lx = jnp.asarray(row_matrices(rows))
     held = pltpu.with_memory_space_constraint(counts, pltpu.HBM)
-    edge_a, edge_b = call_pack_edges(where, held)
-    side_a, side_b, mid_a, mid_b = call_pack_rest(where, held)
+    edge_a, side_b, edge_b, side_a, mid_a, mid_b = call_pack(where, held)
     edge_a = swap(edge_a, "depth", 0)
     edge_b = swap(edge_b, "depth", 1)
     xa = swap(side_a, "img", 0)
@@ -453,8 +417,12 @@
     cb = swap(corner_b, "img", 1)
     plane = call_smooth(order, held, xa, xb, by, lx)
     inner, smoothed = call_interior(scale, flags, plane)
+    common = (flags, order, plane, smoothed)
     layers = call_edge(
-        scale, flags, order, plane, smoothed, edge_a, edge_b, mid_a, mid_b, ca, cb, by, lx, inner
+        scale, 0, *common, edge_a, mid_a, ca[:REACH], cb[:REACH], by, lx, inner
+    )
+    layers = call_edge(
+        scale, 1, *common, edge_b, mid_b, ca[REACH:], cb[REACH:], by, lx, layers
     )
     return exchange(layers)
 

time: 68.4 us -> 74.1 us (1.083)
  the two profiles are of different devices: /device:TPU:0 before, /device:TPU:4 now
where the time goes in v4:
time: 74.1 us; the launch traced here: 73.9 us
  Pallas kernels  25 us (34%)
  waiting for transfers between devices  23.8 us (32%)
  starting transfers between devices  22 us (30%)
  local copies, waits for them, and re-layouts  1.78 us (2%)
  other arithmetic  1.05 us (1%)
    ppermute x8, waiting for transfers between devices, swap(): return lax.ppermute(value, axis, pairs)  14.9 us
    ppermute x8, starting transfers between devices, swap(): return lax.ppermute(value, axis, pairs)  14.7 us
    pallas_call x1, Pallas kernels, call_smooth(): pl.pallas_call(functools.partial(smooth_kernel, group), out_shape=jax.Sha...  7.54 us
    pallas_call x1, Pallas kernels, call_interior(): pl.pallas_call(functools.partial(interior_kernel, scale), out_shape=(jax....  7.31 us
    pallas_call x2, Pallas kernels, call_edge(): pl.pallas_call(functools.partial(edge_kernel, scale, turn), out_shape=jax...  6.65 us
    ppermute x3, starting transfers between devices, exchange(): lax.ppermute(piece, 'depth', [(i, i ^ 2 * step) for i in range(count)])  4.84 us
    ppermute x3, waiting for transfers between devices, exchange(): lax.ppermute(piece, 'depth', [(i, i ^ 2 * step) for i in range(count)])  4.52 us
    ppermute x1, waiting for transfers between devices, exchange(): got = lax.ppermute(send, 'depth', [(i, i ^ 1) for i in range(count)])  4.35 us
  transfers between devices with their start and end apart: 12, of which 6 were waited for; matrix products, arithmetic and copies ran while one was open for 3% of the time, Pallas kernels for 25%

profile of v4, /device:TPU:4, one launch (start us, length us, event | category | flops | bytes accessed | tf_op | source)
XLA Modules:
  0.0 73.9 jit_solution(6662688842257467152)
XLA Ops:
  0.1 3.5 %pack.1 = (s32[5,16,512]{2,1,0:T(8,128)}, s32[32,8,512]{2,1,0:T(8,128)}, s32[5,16,512]{2,1,0:T(8,128)}, s32[32,8,512]{2,1,0:T(8,128)}, s32[5,48,512]{2,1,0:T(8,128)S(1)}, /*index=5*/s32[5,48,512]{2,1,0:T(8,128)}) custom-call(s32[4]{0:T(128)S(1)} %pad_add_fusion.1.where, s32[32,64,512]{2,1,0:T(8,128)} %c_hbm.1), custom_call_target="tpu_custom_call" | custom-call | tf_op jit(solution)/shard_map/pack/pallas_call | solution.py:282
  3.6 0.7 collective-permute-start.2
  4.3 4.3 %collective-permute-start.4 = (s32[5,16,512]{2,1,0:T(8,128)}, s32[5,16,512]{2,1,0:T(8,128)S(1)}, u32[]{:S(2)}, u32[]{:S(2)}) collective-permute-start(s32[5,16,512]{2,1,0:T(8,128)} %get-tuple-element.18), channel_id=1, source_target_pairs={{0,1},{1,0},{2,3},{3,2},{4,5},{5,4},{6,7},{7,6},{8,9},{9,8},{10,11... | collective-permute-start | bytes 491528 | tf_op jit(solution)/shard_map/ppermute | solution.py:350
  8.7 2.5 %collective-permute-start.1 = (s32[32,8,512]{2,1,0:T(8,128)}, s32[32,8,512]{2,1,0:T(8,128)S(1)}, u32[]{:S(2)}, u32[]{:S(2)}) collective-permute-start(s32[32,8,512]{2,1,0:T(8,128)} %get-tuple-element.14), channel_id=1, source_target_pairs={{8,16},{16,8},{9,17},{17,9},{10,18},{18,10},{11,19},{19,11},{12,20... | collective-permute-start | bytes 1572872 | tf_op jit(solution)/shard_map/ppermute | solution.py:350
  11.2 0.7 collective-permute-start.3
  11.9 4.3 %collective-permute-start.7 = (s32[5,48,512]{2,1,0:T(8,128)S(1)}, s32[5,48,512]{2,1,0:T(8,128)}, u32[]{:S(2)}, u32[]{:S(2)}) collective-permute-start(s32[5,48,512]{2,1,0:T(8,128)S(1)} %get-tuple-element.19), channel_id=1, source_target_pairs={{0,1},{1,0},{2,3},{3,2},{4,5},{5,4},{6,7},{7,6},{8,9},{9,8},{10,11... | collective-permute-start | bytes 1474568 | tf_op jit(solution)/shard_map/ppermute | solution.py:350
  16.2 9.6 %collective-permute-done.4.edge = s32[5,16,512]{2,1,0:T(8,128)S(1)} collective-permute-done((s32[5,16,512]{2,1,0:T(8,128)}, s32[5,16,512]{2,1,0:T(8,128)S(1)}, u32[]{:S(2)}, u32[]{:S(2)}) %collective-permute-start.4) | collective-permute-done | bytes 163872 | tf_op jit(solution)/shard_map/ppermute | solution.py:350
  25.9 0.8 %dynamic-slice_bitcast_fusion.2 = (s32[10,8,512]{2,1,0:T(8,128)}, s32[10,8,512]{2,1,0:T(8,128)}) fusion(s32[10,2,8,512]{3,2,1,0:T(8,128)S(1)} %add_bitcast_fusion, s32[]{:T(128)S(6)} %select_n.156, s32[]{:T(128)S(6)} %select_n.155), kind=kLoop, calls=%fused_computation.8 | loop fusion | bytes 655368 | tf_op jit(solution)/shard_map/jit(dynamic_index_in_dim)/squeeze | solution.py:415
  26.7 0.1 add_convert_fusion.flags
  26.8 1.6 %collective-permute-done.5 = s32[10,8,512]{2,1,0:T(8,128)} collective-permute-done((s32[10,8,512]{2,1,0:T(8,128)}, s32[10,8,512]{2,1,0:T(8,128)}, u32[]{:S(2)}, u32[]{:S(2)}) %collective-permute-start.5) | collective-permute-done | bytes 163872 | tf_op jit(solution)/shard_map/ppermute | solution.py:350
  28.4 2.2 %collective-permute-start.6 = (s32[10,8,512]{2,1,0:T(8,128)}, s32[10,8,512]{2,1,0:T(8,128)S(1)}, u32[]{:S(2)}, u32[]{:S(2)}) collective-permute-start(s32[10,8,512]{2,1,0:T(8,128)} %get-tuple-element.26), channel_id=1, source_target_pairs={{8,16},{16,8},{9,17},{17,9},{10,18},{18,10},{11,19},{19,11},{12,20... | collective-permute-start | bytes 491528 | tf_op jit(solution)/shard_map/ppermute | solution.py:350
  30.5 0.9 %fusion.6 = (s32[5,8,512]{2,1,0:T(8,128)S(1)}, s32[5,8,512]{2,1,0:T(8,128)S(1)}) fusion(s32[10,8,512]{2,1,0:T(8,128)} %collective-permute-done.5), kind=kLoop, calls=%fused_computation.35 | loop fusion | bytes 327680 | tf_op jit(solution)/shard_map/slice | solution.py:422
  31.5 3.7 %collective-permute-done.6 = s32[10,8,512]{2,1,0:T(8,128)S(1)} collective-permute-done((s32[10,8,512]{2,1,0:T(8,128)}, s32[10,8,512]{2,1,0:T(8,128)S(1)}, u32[]{:S(2)}, u32[]{:S(2)}) %collective-permute-start.6) | collective-permute-done | bytes 163872 | tf_op jit(solution)/shard_map/ppermute | solution.py:350
  35.2 7.5 %smooth.1.plane = f32[32,80,512]{2,1,0:T(8,128)S(1)} custom-call(s32[2]{0:T(128)S(1)} %pad_add_fusion.order, s32[32,64,512]{2,1,0:T(8,128)} %c_hbm.1, s32[32,8,512]{2,1,0:T(8,128)S(1)} %collective-permute-done.xa, s32[32,8,512]{2,1,0:T(8,128)S(1)} %collective-permute-done.1.xb, bf16[1024,512]{1,0:T(8,128)(2,1)S(1)} %copy-done, bf16[2,80,240]{2,1,0:T(8,128)(2,1)S(1)} %copy-done.1), custom_call_target="tpu_custom_call" | custom-call | flops 1000000000 | bytes 4000000 | tf_op jit(solution)/shard_map/smooth/pallas_call | solution.py:297
  42.8 7.3 %interior.1 = (f32[4,64,512]{2,1,0:T(8,128)S(1)}, f32[24,80,512]{2,1,0:T(8,128)S(1)}) custom-call(f32[4]{0:T(128)S(1)} %add_convert_fusion.flags, f32[32,80,512]{2,1,0:T(8,128)S(1)} %smooth.1.plane), custom_call_target="tpu_custom_call" | custom-call | flops 1000000000 | bytes 4000000 | tf_op jit(solution)/shard_map/interior/pallas_call | solution.py:314
  50.1 3.6 %shard_map.37.behind = f32[4,64,512]{2,1,0:T(8,128)S(1)} custom-call(f32[4]{0:T(128)S(1)} %add_convert_fusion.flags, s32[2]{0:T(128)S(1)} %pad_add_fusion.order, f32[32,80,512]{2,1,0:T(8,128)S(1)} %smooth.1.plane, f32[24,80,512]{2,1,0:T(8,128)S(1)} %get-tuple-element.15.smoothed, s32[5,16,512]{2,1,0:T(8,128)S(1)} %collective-permute-done.4.edge, ...), custom_call_target="tpu_custom_call" | custom-call | flops 300000000 | bytes 4000000 | tf_op jit(solution)/shard_map/pallas_call | solution.py:331
  53.7 3.1 %shard_map.38 = f32[4,64,512]{2,1,0:T(8,128)S(1)} custom-call(f32[4]{0:T(128)S(1)} %add_convert_fusion.flags, s32[2]{0:T(128)S(1)} %pad_add_fusion.order, f32[32,80,512]{2,1,0:T(8,128)S(1)} %smooth.1.plane, f32[24,80,512]{2,1,0:T(8,128)S(1)} %get-tuple-element.15.smoothed, s32[5,16,512]{2,1,0:T(8,128)S(1)} %collective-permute-done.2.edge, ...), custom_call_target="tpu_custom_call" | custom-call | flops 300000000 | bytes 4000000 | tf_op jit(solution)/shard_map/pallas_call | solution.py:331
  56.8 2.4 %collective-permute-start.8 = (f32[4,4,8,512]{3,2,1,0:T(8,128)S(1)}, f32[4,4,8,512]{3,2,1,0:T(8,128)S(1)}, u32[]{:S(2)}, u32[]{:S(2)}) collective-permute-start(f32[4,4,8,512]{3,2,1,0:T(8,128)S(1)} %dynamic-slice_bitcast_fusion), channel_id=1, source_target_pairs={{0,1},{1,0},{2,3},{3,2},{4,5},{5,4},{6,7},{7,6},{8,9},{9,8},{10,11... | collective-permute-start | bytes 786440 | tf_op jit(solution)/shard_map/ppermute | solution.py:368
  59.3 4.3 %collective-permute-done.8 = f32[4,4,8,512]{3,2,1,0:T(8,128)S(1)} collective-permute-done((f32[4,4,8,512]{3,2,1,0:T(8,128)S(1)}, f32[4,4,8,512]{3,2,1,0:T(8,128)S(1)}, u32[]{:S(2)}, u32[]{:S(2)}) %collective-permute-start.8) | collective-permute-done | bytes 262176 | tf_op jit(solution)/shard_map/ppermute | solution.py:368
  63.8 4.2 %collective-permute-start.11 = (f32[4,8,512]{2,1,0:T(8,128)S(1)}, f32[4,8,512]{2,1,0:T(8,128)S(1)}, u32[]{:S(2)}, u32[]{:S(2)}) collective-permute-start(f32[4,8,512]{2,1,0:T(8,128)S(1)} %get-tuple-element.29), channel_id=1, source_target_pairs={{0,6},{1,7},{2,4},{3,5},{4,2},{5,3},{6,0},{7,1},{8,14},{9,15},{10,... | collective-permute-start | bytes 196616 | tf_op jit(solution)/shard_map/ppermute | solution.py:374
  68.0 0.6 collective-permute-start.9
  68.6 1.7 %collective-permute-done.11 = f32[4,8,512]{2,1,0:T(8,128)S(1)} collective-permute-done((f32[4,8,512]{2,1,0:T(8,128)S(1)}, f32[4,8,512]{2,1,0:T(8,128)S(1)}, u32[]{:S(2)}, u32[]{:S(2)}) %collective-permute-start.11) | collective-permute-done | bytes 65568 | tf_op jit(solution)/shard_map/ppermute | solution.py:374
  70.3 2.8 %collective-permute-done.10 = f32[4,8,512]{2,1,0:T(8,128)S(1)} collective-permute-done((f32[4,8,512]{2,1,0:T(8,128)S(1)}, f32[4,8,512]{2,1,0:T(8,128)S(1)}, u32[]{:S(2)}, u32[]{:S(2)}) %collective-permute-start.10) | collective-permute-done | bytes 65568 | tf_op jit(solution)/shard_map/ppermute | solution.py:374
  73.2 0.6 pad_maximum_fusion.2
  (26 shorter events, 0.4 us)
Async XLA Ops:
  0.0 35.2 %copy-start = (bf16[1024,512]{1,0:T(8,128)(2,1)S(1)}, bf16[1024,512]{1,0:T(8,128)(2,1)}, u32[]{:S(2)}) copy-start(bf16[1024,512]{1,0:T(8,128)(2,1)} %constant.80.clone.by) | copy-start | bytes 3145732
  0.0 35.2 %copy-start.1 = (bf16[2,80,240]{2,1,0:T(8,128)(2,1)S(1)}, bf16[2,80,240]{2,1,0:T(8,128)(2,1)}, u32[]{:S(2)}) copy-start(bf16[2,80,240]{2,1,0:T(8,128)(2,1)} %constant.81.clone.lx) | copy-start | bytes 230404
  3.6 8.3 %collective-permute-start.2 = (s32[5,16,512]{2,1,0:T(8,128)}, s32[5,16,512]{2,1,0:T(8,128)S(1)}, u32[]{:S(2)}, u32[]{:S(2)}) collective-permute-start(s32[5,16,512]{2,1,0:T(8,128)} %get-tuple-element.16), channel_id=1, source_target_pairs={{1,2},{2,1},{3,4},{4,3},{5,6},{6,5},{9,10},{10,9},{11,12},{12,11},... | collective-permute-start | bytes 491528 | tf_op jit(solution)/shard_map/ppermute | solution.py:350
  4.3 21.5 %collective-permute-start.4 = (s32[5,16,512]{2,1,0:T(8,128)}, s32[5,16,512]{2,1,0:T(8,128)S(1)}, u32[]{:S(2)}, u32[]{:S(2)}) collective-permute-start(s32[5,16,512]{2,1,0:T(8,128)} %get-tuple-element.18), channel_id=1, source_target_pairs={{0,1},{1,0},{2,3},{3,2},{4,5},{5,4},{6,7},{7,6},{8,9},{9,8},{10,11... | collective-permute-start | bytes 491528 | tf_op jit(solution)/shard_map/ppermute | solution.py:350
  8.7 26.6 %collective-permute-start = (s32[32,8,512]{2,1,0:T(8,128)}, s32[32,8,512]{2,1,0:T(8,128)S(1)}, u32[]{:S(2)}, u32[]{:S(2)}) collective-permute-start(s32[32,8,512]{2,1,0:T(8,128)} %get-tuple-element.13), channel_id=1, source_target_pairs={{0,8},{8,0},{16,24},{24,16},{1,9},{9,1},{17,25},{25,17},{2,10},{10... | collective-permute-start | bytes 1572872 | tf_op jit(solution)/shard_map/ppermute | solution.py:350
  8.7 26.6 %collective-permute-start.1 = (s32[32,8,512]{2,1,0:T(8,128)}, s32[32,8,512]{2,1,0:T(8,128)S(1)}, u32[]{:S(2)}, u32[]{:S(2)}) collective-permute-start(s32[32,8,512]{2,1,0:T(8,128)} %get-tuple-element.14), channel_id=1, source_target_pairs={{8,16},{16,8},{9,17},{17,9},{10,18},{18,10},{11,19},{19,11},{12,20... | collective-permute-start | bytes 1572872 | tf_op jit(solution)/shard_map/ppermute | solution.py:350
  11.2 42.5 %collective-permute-start.3 = (s32[5,48,512]{2,1,0:T(8,128)}, s32[5,48,512]{2,1,0:T(8,128)S(1)}, u32[]{:S(2)}, u32[]{:S(2)}) collective-permute-start(s32[5,48,512]{2,1,0:T(8,128)} %get-tuple-element.17), channel_id=1, source_target_pairs={{1,2},{2,1},{3,4},{4,3},{5,6},{6,5},{9,10},{10,9},{11,12},{12,11},... | collective-permute-start | bytes 1474568 | tf_op jit(solution)/shard_map/ppermute | solution.py:350
  11.9 38.2 %collective-permute-start.7 = (s32[5,48,512]{2,1,0:T(8,128)S(1)}, s32[5,48,512]{2,1,0:T(8,128)}, u32[]{:S(2)}, u32[]{:S(2)}) collective-permute-start(s32[5,48,512]{2,1,0:T(8,128)S(1)} %get-tuple-element.19), channel_id=1, source_target_pairs={{0,1},{1,0},{2,3},{3,2},{4,5},{5,4},{6,7},{7,6},{8,9},{9,8},{10,11... | collective-permute-start | bytes 1474568 | tf_op jit(solution)/shard_map/ppermute | solution.py:350
  26.6 1.7 %collective-permute-start.5 = (s32[10,8,512]{2,1,0:T(8,128)}, s32[10,8,512]{2,1,0:T(8,128)}, u32[]{:S(2)}, u32[]{:S(2)}) collective-permute-start(s32[10,8,512]{2,1,0:T(8,128)} %get-tuple-element.27), channel_id=1, source_target_pairs={{0,8},{8,0},{16,24},{24,16},{1,9},{9,1},{17,25},{25,17},{2,10},{10... | collective-permute-start | bytes 491528 | tf_op jit(solution)/shard_map/ppermute | solution.py:350
  28.4 6.8 %collective-permute-start.6 = (s32[10,8,512]{2,1,0:T(8,128)}, s32[10,8,512]{2,1,0:T(8,128)S(1)}, u32[]{:S(2)}, u32[]{:S(2)}) collective-permute-start(s32[10,8,512]{2,1,0:T(8,128)} %get-tuple-element.26), channel_id=1, source_target_pairs={{8,16},{16,8},{9,17},{17,9},{10,18},{18,10},{11,19},{19,11},{12,20... | collective-permute-start | bytes 491528 | tf_op jit(solution)/shard_map/ppermute | solution.py:350
  56.8 6.8 %collective-permute-start.8 = (f32[4,4,8,512]{3,2,1,0:T(8,128)S(1)}, f32[4,4,8,512]{3,2,1,0:T(8,128)S(1)}, u32[]{:S(2)}, u32[]{:S(2)}) collective-permute-start(f32[4,4,8,512]{3,2,1,0:T(8,128)S(1)} %dynamic-slice_bitcast_fusion), channel_id=1, source_target_pairs={{0,1},{1,0},{2,3},{3,2},{4,5},{5,4},{6,7},{7,6},{8,9},{9,8},{10,11... | collective-permute-start | bytes 786440 | tf_op jit(solution)/shard_map/ppermute | solution.py:368
  63.8 6.5 %collective-permute-start.11 = (f32[4,8,512]{2,1,0:T(8,128)S(1)}, f32[4,8,512]{2,1,0:T(8,128)S(1)}, u32[]{:S(2)}, u32[]{:S(2)}) collective-permute-start(f32[4,8,512]{2,1,0:T(8,128)S(1)} %get-tuple-element.29), channel_id=1, source_target_pairs={{0,6},{1,7},{2,4},{3,5},{4,2},{5,3},{6,0},{7,1},{8,14},{9,15},{10,... | collective-permute-start | bytes 196616 | tf_op jit(solution)/shard_map/ppermute | solution.py:374
  68.0 5.2 %collective-permute-start.10 = (f32[4,8,512]{2,1,0:T(8,128)S(1)}, f32[4,8,512]{2,1,0:T(8,128)S(1)}, u32[]{:S(2)}, u32[]{:S(2)}) collective-permute-start(f32[4,8,512]{2,1,0:T(8,128)S(1)} %get-tuple-element.30), channel_id=1, source_target_pairs={{0,4},{1,5},{2,6},{3,7},{4,0},{5,1},{6,2},{7,3},{8,12},{9,13},{10,... | collective-permute-start | bytes 196616 | tf_op jit(solution)/shard_map/ppermute | solution.py:374
  68.0 5.2 %collective-permute-start.9 = (f32[4,8,512]{2,1,0:T(8,128)S(1)}, f32[4,8,512]{2,1,0:T(8,128)S(1)}, u32[]{:S(2)}, u32[]{:S(2)}) collective-permute-start(f32[4,8,512]{2,1,0:T(8,128)S(1)} %get-tuple-element.28), channel_id=1, source_target_pairs={{0,2},{1,3},{2,0},{3,1},{4,6},{5,7},{6,4},{7,5},{8,10},{9,11},{10,... | collective-permute-start | bytes 196616 | tf_op jit(solution)/shard_map/ppermute | solution.py:374

commit v5 on v4

--- a/solution.py
+++ b/solution.py
@@ -18,6 +18,7 @@
 light_z = 0.48
 light_x = 0.6
 light_y = 0.64
+
 
 REACH = 5
 PAD = 8
@@ -138,20 +139,18 @@
         ref[n, rows, :] = value
 
 
-def pack_kernel(where, c, edge_a, side_b, edge_b, side_a, middle_a, middle_b, sems):
+def pack_kernel(where, c, edge_a, side_b, edge_b, side_a, sems):
     rows = c.shape[1]
     copies = []
 
     def add(source, target):
         copies.append(pltpu.make_async_copy(source, target, sems.at[len(copies)]))
 
-    sides = (side_a, side_b)
-    for n, (edge, middle) in enumerate(((edge_a, middle_a), (edge_b, middle_b))):
+    for n, (edge, side) in enumerate(((edge_a, side_a), (edge_b, side_b))):
         layers = pl.ds(where[n], REACH)
         add(c.at[layers, pl.ds(0, PAD)], edge.at[:, pl.ds(0, PAD)])
         add(c.at[layers, pl.ds(rows - PAD, PAD)], edge.at[:, pl.ds(PAD, PAD)])
-        add(c.at[layers, pl.ds(PAD, rows - 2 * PAD)], middle)
-        add(c.at[:, pl.ds(pl.multiple_of(where[2 + n], PAD), PAD)], sides[n])
+        add(c.at[:, pl.ds(pl.multiple_of(where[2 + n], PAD), PAD)], side)
     for copy in copies:
         copy.start()
     for copy in copies:
@@ -205,11 +204,8 @@
     lax.fori_loop(0, ext // 8 - 2, one_tile, 0)
 
 
-def edge_kernel(
-    scale, turn, flags, order, plane, smoothed, edge, middle, ca, cb, by, lx, behind,
-    image, halo, ends,
-):
-    layers, ext, columns = plane.shape
+def edge_smooth(turn, flags, order, plane, smoothed, edge, middle, ca, cb, by, lx, ends, halo):
+    layers, ext, _ = plane.shape
     rows_of = order[0]
     is_front = order[1] == 1 - turn
     sign = jnp.where(is_front, 1, -1)
@@ -239,7 +235,12 @@
     for v in (4, 5):
         ends[ends_face + sign * v] = smoothed[smoothed_face + sign * v]
 
-    def one_tile(tile, _):
+
+def edge_render(scale, is_front, ends, behind, image, tiles, tile_of):
+    columns = ends.shape[2]
+
+    def one_tile(place, _):
+        tile = tile_of(place)
         base = pl.multiple_of(tile * 8 + 8, 8)
         carry = empty_carry(columns)
         for k in range(1, REACH + 1):
@@ -248,10 +249,40 @@
         front = [jnp.where(is_front, x, y) for x, y in zip(carry, other)]
         back = [jnp.where(is_front, y, x) for x, y in zip(carry, other)]
         colors = [front[n] + front[3] * back[n] for n in range(3)]
-        store_tile(image, tile, colors + [front[3] * back[3]])
+        store_tile(image, place, colors + [front[3] * back[3]])
         return 0
 
-    lax.fori_loop(0, ext // 8 - 2, one_tile, 0)
+    lax.fori_loop(0, tiles, one_tile, 0)
+
+
+def half_tiles(owner_tiles, wanted):
+    def tile_of(place):
+        return (place // owner_tiles * 2 + wanted) * owner_tiles + place % owner_tiles
+
+    return tile_of
+
+
+def first_edge_kernel(scale, flags, order, plane, smoothed, edge, middle, ca, cb, by, lx, behind,
+                      image, ends, halo):
+    edge_smooth(0, flags, order, plane, smoothed, edge, middle, ca, cb, by, lx, ends, halo)
+    tiles = plane.shape[1] // 8 - 2
+    edge_render(scale, order[1] == 1, ends, behind, image, tiles, lambda place: place)
+
+
+def last_edge_kernel(scale, owner_tiles, flags, order, plane, smoothed, edge, middle, ca, cb, by,
+                     lx, behind, image, ends, halo):
+    edge_smooth(1, flags, order, plane, smoothed, edge, middle, ca, cb, by, lx, ends, halo)
+    tiles = plane.shape[1] // 8 - 2
+    tile_of = lambda place: place
+    if owner_tiles:
+        tiles, tile_of = tiles // 2, half_tiles(owner_tiles, 1 - order[1])
+    edge_render(scale, order[1] == 0, ends, behind, image, tiles, tile_of)
+
+
+def kept_edge_kernel(scale, owner_tiles, order, ends, behind, image):
+    tiles = ends.shape[1] // 8 - 2
+    tile_of = half_tiles(owner_tiles, order[1])
+    edge_render(scale, order[1] == 0, ends, behind, image, tiles // 2, tile_of)
 
 
 def whole(count):
@@ -275,16 +306,15 @@
 
 
 def call_pack(where, c):
-    layers, rows, columns = c.shape
+    layers, _, columns = c.shape
     edge = pltpu.VMEM((REACH, 2 * PAD, columns), c.dtype)
     side = pltpu.VMEM((layers, PAD, columns), c.dtype)
-    middle = pltpu.VMEM((REACH, rows - 2 * PAD, columns), c.dtype)
     return pl.pallas_call(
         pack_kernel,
-        out_shape=(edge, side, edge, side, middle, middle),
+        out_shape=(edge, side, edge, side),
         in_specs=[smem(), in_hbm()],
-        out_specs=tuple(whole(6)),
-        scratch_shapes=[pltpu.SemaphoreType.DMA((8,))],
+        out_specs=tuple(whole(4)),
+        scratch_shapes=[pltpu.SemaphoreType.DMA((6,))],
         compiler_params=params(8),
         name="pack",
     )(where, c)
@@ -293,7 +323,7 @@
 def call_smooth(order, c, xa, xb, by, lx):
     layers, rows, columns = c.shape
     ext = rows + 2 * PAD
-    group = 4
+    group = 8
     return pl.pallas_call(
         functools.partial(smooth_kernel, group),
         out_shape=jax.ShapeDtypeStruct((layers, ext, columns), jnp.float32),
@@ -325,21 +355,54 @@
     )(flags, plane)
 
 
-def call_edge(scale, turn, flags, order, plane, *operands):
+def call_first_edge(scale, flags, order, plane, *operands):
     _, ext, columns = plane.shape
     f32 = jnp.float32
     return pl.pallas_call(
-        functools.partial(edge_kernel, scale, turn),
+        functools.partial(first_edge_kernel, scale),
         out_shape=jax.ShapeDtypeStruct((4, ext - 2 * PAD, columns), f32),
         in_specs=[smem(), smem()] + whole(1 + len(operands)),
         out_specs=whole(1)[0],
         scratch_shapes=[
+            pltpu.VMEM((REACH + 2, ext, columns), f32),
             pltpu.VMEM((REACH, ext, columns), f32),
-            pltpu.VMEM((REACH + 2, ext, columns), f32),
         ],
         compiler_params=params(24),
         cost_estimate=cost(300_000_000),
+        name="first_edge",
     )(flags, order, plane, *operands)
+
+
+def call_last_edge(scale, owner_tiles, flags, order, plane, *operands):
+    _, ext, columns = plane.shape
+    f32 = jnp.float32
+    rows = (ext - 2 * PAD) // (2 if owner_tiles else 1)
+    return pl.pallas_call(
+        functools.partial(last_edge_kernel, scale, owner_tiles),
+        out_shape=(
+            jax.ShapeDtypeStruct((4, rows, columns), f32),
+            jax.ShapeDtypeStruct((REACH + 2, ext, columns), f32),
+        ),
+        in_specs=[smem(), smem()] + whole(1 + len(operands)),
+        out_specs=tuple(whole(2)),
+        scratch_shapes=[pltpu.VMEM((REACH, ext, columns), f32)],
+        compiler_params=params(24),
+        cost_estimate=cost(300_000_000),
+        name="last_edge",
+    )(flags, order, plane, *operands)
+
+
+def call_kept_edge(scale, owner_tiles, order, ends, behind):
+    _, ext, columns = ends.shape
+    return pl.pallas_call(
+        functools.partial(kept_edge_kernel, scale, owner_tiles),
+        out_shape=jax.ShapeDtypeStruct((4, (ext - 2 * PAD) // 2, columns), jnp.float32),
+        in_specs=[smem()] + whole(2),
+        out_specs=whole(1)[0],
+        compiler_params=params(24),
+        cost_estimate=cost(200_000_000),
+        name="kept_edge",
+    )(order, ends, behind)
 
 
 def swap(value, axis, first):
@@ -355,17 +418,24 @@
     return jnp.concatenate([front[:3] + through * back[:3], through * back[3:]], 0)
 
 
-def exchange(layers):
+def halves_of(layers):
+    count = lax.axis_size("depth")
+    parity = lax.axis_index("depth") % 2
+    _, rows, columns = layers.shape
+    pieces = layers.reshape(4, count // 2, 2, rows // count, columns)
+    send = lax.dynamic_index_in_dim(pieces, 1 - parity, 2, keepdims=False)
+    keep = lax.dynamic_index_in_dim(pieces, parity, 2, keepdims=False)
+    return send, keep
+
+
+def exchange(send, keep):
     count = lax.axis_size("depth")
     me = lax.axis_index("depth")
-    _, rows, columns = layers.shape
-    owned = rows // count
     parity, pair = me % 2, me // 2
     pairs = count // 2
-    pieces = layers.reshape(4, pairs, 2, owned, columns)
-    send = lax.dynamic_index_in_dim(pieces, 1 - parity, 2, keepdims=False)
-    keep = lax.dynamic_index_in_dim(pieces, parity, 2, keepdims=False)
-    got = lax.ppermute(send, "depth", [(i, i ^ 1) for i in range(count)])
+    send, keep = (value.reshape(4, pairs, -1, value.shape[-1]) for value in (send, keep))
+    owned, columns = send.shape[2:]
+    got = swap(send, "depth", 0)
     joined = jnp.where(parity == 0, over(keep, got), over(got, keep))
     parts = []
     for step in range(pairs):
@@ -403,7 +473,10 @@
     by = jnp.asarray(column_matrix(columns))
     lx = jnp.asarray(row_matrices(rows))
     held = pltpu.with_memory_space_constraint(counts, pltpu.HBM)
-    edge_a, side_b, edge_b, side_a, mid_a, mid_b = call_pack(where, held)
+    mid_a = lax.dynamic_slice(counts, (first_a, PAD, 0), (REACH, rows - 2 * PAD, columns))
+    edge_a, side_b, edge_b, side_a = call_pack(where, held)
+    later, edge_a = lax.optimization_barrier((counts, edge_a))
+    mid_b = lax.dynamic_slice(later, (first_b, PAD, 0), (REACH, rows - 2 * PAD, columns))
     edge_a = swap(edge_a, "depth", 0)
     edge_b = swap(edge_b, "depth", 1)
     xa = swap(side_a, "img", 0)
@@ -417,14 +490,20 @@
     cb = swap(corner_b, "img", 1)
     plane = call_smooth(order, held, xa, xb, by, lx)
     inner, smoothed = call_interior(scale, flags, plane)
+    owned = rows // depths
+    owner_tiles = owned // 8 if owned % 8 == 0 else 0
     common = (flags, order, plane, smoothed)
-    layers = call_edge(
-        scale, 0, *common, edge_a, mid_a, ca[:REACH], cb[:REACH], by, lx, inner
+    layers = call_first_edge(
+        scale, *common, edge_a, mid_a, ca[:REACH], cb[:REACH], by, lx, inner
     )
-    layers = call_edge(
-        scale, 1, *common, edge_b, mid_b, ca[REACH:], cb[REACH:], by, lx, layers
+    send, ends = call_last_edge(
+        scale, owner_tiles, *common, edge_b, mid_b, ca[REACH:], cb[REACH:], by, lx, layers
     )
-    return exchange(layers)
+    if owner_tiles:
+        keep = call_kept_edge(scale, owner_tiles, order, ends, layers)
+    else:
+        send, keep = halves_of(send)
+    return exchange(send, keep)
 
 
 def solution(mesh):

time: 74.1 us -> 67.4 us (0.910)
  the two profiles are of different devices: /device:TPU:4 before, /device:TPU:0 now
where the time goes in v5:
time: 67.4 us; the launch traced here: 67 us
  starting transfers between devices  26.4 us (39%)
  Pallas kernels  23.9 us (35%)
  waiting for transfers between devices  11.7 us (17%)
  local copies, waits for them, and re-layouts  3.84 us (6%)
  other arithmetic  1.04 us (2%)
    ppermute x9, starting transfers between devices, swap(): return lax.ppermute(value, axis, pairs)  22.4 us
    pallas_call x1, Pallas kernels, call_interior(): pl.pallas_call(functools.partial(interior_kernel, scale), out_shape=(jax....  7.31 us
    ppermute x9, waiting for transfers between devices, swap(): return lax.ppermute(value, axis, pairs)  6.66 us
    pallas_call x1, Pallas kernels, call_smooth(): pl.pallas_call(functools.partial(smooth_kernel, group), out_shape=jax.Sha...  6.45 us
    ppermute x3, waiting for transfers between devices, exchange(): lax.ppermute(piece, 'depth', [(i, i ^ 2 * step) for i in range(count)])  5.02 us
    ppermute x3, starting transfers between devices, exchange(): lax.ppermute(piece, 'depth', [(i, i ^ 2 * step) for i in range(count)])  4.01 us
    pallas_call x1, Pallas kernels, call_first_edge(): pl.pallas_call(functools.partial(first_edge_kernel, scale), out_shape=jax...  3.09 us
    pallas_call x1, Pallas kernels, call_last_edge(): pl.pallas_call(functools.partial(last_edge_kernel, scale, owner_tiles), o...  2.95 us
  transfers between devices with their start and end apart: 12, of which 4 were waited for; matrix products, arithmetic and copies ran while one was open for 6% of the time, Pallas kernels for 27%

profile of v5, /device:TPU:0, one launch (start us, length us, event | category | flops | bytes accessed | tf_op | source)
XLA Modules:
  0.0 67.0 jit_solution(15205199547887014050)
XLA Ops:
  0.1 2.9 %pack.1 = (s32[5,16,512]{2,1,0:T(8,128)S(1)}, s32[32,8,512]{2,1,0:T(8,128)}, s32[5,16,512]{2,1,0:T(8,128)S(1)}, s32[32,8,512]{2,1,0:T(8,128)}) custom-call(s32[4]{0:T(128)S(1)} %pad_add_fusion.1.where, s32[32,64,512]{2,1,0:T(8,128)} %c_hbm.1), custom_call_target="tpu_custom_call" | custom-call | tf_op jit(solution)/shard_map/pack/pallas_call | solution.py:312
  3.0 0.6 collective-permute-start
  3.6 0.7 %collective-permute-start.1 = (s32[32,8,512]{2,1,0:T(8,128)}, s32[32,8,512]{2,1,0:T(8,128)S(1)}, u32[]{:S(2)}, u32[]{:S(2)}) collective-permute-start(s32[32,8,512]{2,1,0:T(8,128)} %get-tuple-element.16), channel_id=1, source_target_pairs={{8,16},{16,8},{9,17},{17,9},{10,18},{18,10},{11,19},{19,11},{12,20... | collective-permute-start | bytes 1572872 | tf_op jit(solution)/shard_map/ppermute | solution.py:413
  4.3 2.6 %collective-permute-start.4 = (s32[5,16,512]{2,1,0:T(8,128)S(1)}, s32[5,16,512]{2,1,0:T(8,128)S(1)}, u32[]{:S(2)}, u32[]{:S(2)}) collective-permute-start(s32[5,16,512]{2,1,0:T(8,128)S(1)} %get-tuple-element.21), channel_id=1, source_target_pairs={{0,1},{1,0},{2,3},{3,2},{4,5},{5,4},{6,7},{7,6},{8,9},{9,8},{10,11... | collective-permute-start | bytes 491528 | tf_op jit(solution)/shard_map/ppermute | solution.py:413
  6.8 0.7 collective-permute-start.2
  7.5 1.9 %constant_dynamic-slice_fusion = s32[5,48,512]{2,1,0:T(8,128)} fusion(s32[32,64,512]{2,1,0:T(8,128)} %c_hbm.1, s32[]{:T(128)S(6)} %select_n.157), kind=kLoop, calls=%fused_computation.30 | loop fusion | bytes 983044 | tf_op jit(solution)/shard_map/dynamic_slice | solution.py:476
  9.4 4.3 %collective-permute-start.7 = (s32[5,48,512]{2,1,0:T(8,128)}, s32[5,48,512]{2,1,0:T(8,128)S(1)}, u32[]{:S(2)}, u32[]{:S(2)}) collective-permute-start(s32[5,48,512]{2,1,0:T(8,128)} %constant_dynamic-slice_fusion), channel_id=1, source_target_pairs={{0,1},{1,0},{2,3},{3,2},{4,5},{5,4},{6,7},{7,6},{8,9},{9,8},{10,11... | collective-permute-start | bytes 1474568 | tf_op jit(solution)/shard_map/ppermute | solution.py:413
  13.6 1.9 %constant_dynamic-slice_fusion.1 = s32[5,48,512]{2,1,0:T(8,128)} fusion(s32[32,64,512]{2,1,0:T(8,128)} %c_hbm.1, s32[]{:T(128)S(6)} %select_n.154), kind=kLoop, calls=%fused_computation.31 | loop fusion | bytes 983044 | tf_op jit(solution)/shard_map/dynamic_slice | solution.py:479
  15.5 1.5 %collective-permute-start.3 = (s32[5,48,512]{2,1,0:T(8,128)}, s32[5,48,512]{2,1,0:T(8,128)}, u32[]{:S(2)}, u32[]{:S(2)}) collective-permute-start(s32[5,48,512]{2,1,0:T(8,128)} %constant_dynamic-slice_fusion.1), channel_id=1, source_target_pairs={{1,2},{2,1},{3,4},{4,3},{5,6},{6,5},{9,10},{10,9},{11,12},{12,11},... | collective-permute-start | bytes 1474568 | tf_op jit(solution)/shard_map/ppermute | solution.py:413
  17.1 0.7 %collective-permute-start.6 = (s32[10,8,512]{2,1,0:T(8,128)S(1)}, s32[10,8,512]{2,1,0:T(8,128)S(1)}, u32[]{:S(2)}, u32[]{:S(2)}) collective-permute-start(s32[10,8,512]{2,1,0:T(8,128)S(1)} %get-tuple-element.30), channel_id=1, source_target_pairs={{8,16},{16,8},{9,17},{17,9},{10,18},{18,10},{11,19},{19,11},{12,20... | collective-permute-start | bytes 491528 | tf_op jit(solution)/shard_map/ppermute | solution.py:413
  17.9 7.8 %collective-permute-start.5 = (s32[10,8,512]{2,1,0:T(8,128)S(1)}, s32[10,8,512]{2,1,0:T(8,128)S(1)}, u32[]{:S(2)}, u32[]{:S(2)}) collective-permute-start(s32[10,8,512]{2,1,0:T(8,128)S(1)} %get-tuple-element.31), channel_id=1, source_target_pairs={{0,8},{8,0},{16,24},{24,16},{1,9},{9,1},{17,25},{25,17},{2,10},{10... | collective-permute-start | bytes 491528 | tf_op jit(solution)/shard_map/ppermute | solution.py:413
  25.7 1.0 %collective-permute-done.5 = s32[10,8,512]{2,1,0:T(8,128)S(1)} collective-permute-done((s32[10,8,512]{2,1,0:T(8,128)S(1)}, s32[10,8,512]{2,1,0:T(8,128)S(1)}, u32[]{:S(2)}, u32[]{:S(2)}) %collective-permute-start.5) | collective-permute-done | bytes 163872 | tf_op jit(solution)/shard_map/ppermute | solution.py:413
  26.8 6.5 %smooth.1.plane = f32[32,80,512]{2,1,0:T(8,128)S(1)} custom-call(s32[2]{0:T(128)S(1)} %pad_add_fusion.order, s32[32,64,512]{2,1,0:T(8,128)} %c_hbm.1, s32[32,8,512]{2,1,0:T(8,128)S(1)} %collective-permute-done.xa, s32[32,8,512]{2,1,0:T(8,128)S(1)} %collective-permute-done.1.xb, bf16[1024,512]{1,0:T(8,128)(2,1)S(1)} %copy-done, bf16[2,80,240]{2,1,0:T(8,128)(2,1)S(1)} %copy-done.1), custom_call_target="tpu_custom_call" | custom-call | flops 1000000000 | bytes 4000000 | tf_op jit(solution)/shard_map/smooth/pallas_call | solution.py:327
  33.3 7.3 %interior.1 = (f32[4,64,512]{2,1,0:T(8,128)S(1)}, f32[24,80,512]{2,1,0:T(8,128)S(1)}) custom-call(f32[4]{0:T(128)S(1)} %add_convert_fusion.flags, f32[32,80,512]{2,1,0:T(8,128)S(1)} %smooth.1.plane), custom_call_target="tpu_custom_call" | custom-call | flops 1000000000 | bytes 4000000 | tf_op jit(solution)/shard_map/interior/pallas_call | solution.py:344
  40.6 3.1 %first_edge.1.behind = f32[4,64,512]{2,1,0:T(8,128)S(1)} custom-call(f32[4]{0:T(128)S(1)} %add_convert_fusion.flags, s32[2]{0:T(128)S(1)} %pad_add_fusion.order, f32[32,80,512]{2,1,0:T(8,128)S(1)} %smooth.1.plane, f32[24,80,512]{2,1,0:T(8,128)S(1)} %get-tuple-element.17.smoothed, s32[5,16,512]{2,1,0:T(8,128)S(1)} %collective-permute-done.4.edge, ...), custom_call_target="tpu_custom_call" | custom-call | flops 300000000 | bytes 4000000 | tf_op jit(solution)/shard_map/first_edge/pallas_call | solution.py:361
  43.7 3.0 %last_edge.1 = (f32[4,32,512]{2,1,0:T(8,128)S(1)}, f32[7,80,512]{2,1,0:T(8,128)S(1)}) custom-call(f32[4]{0:T(128)S(1)} %add_convert_fusion.flags, s32[2]{0:T(128)S(1)} %pad_add_fusion.order, f32[32,80,512]{2,1,0:T(8,128)S(1)} %smooth.1.plane, f32[24,80,512]{2,1,0:T(8,128)S(1)} %get-tuple-element.17.smoothed, s32[5,16,512]{2,1,0:T(8,128)S(1)} %collective-permute-done.2.edge, ...), custom_call_target="tpu_custom_call" | custom-call | flops 300000000 | bytes 4000000 | tf_op jit(solution)/shard_map/last_edge/pallas_call | solution.py:380
  46.6 3.7 %collective-permute-start.8 = (f32[4,4,8,512]{3,2,1,0:T(8,128)S(1)}, f32[4,4,8,512]{3,2,1,0:T(8,128)S(1)}, u32[]{:S(2)}, u32[]{:S(2)}) collective-permute-start(f32[4,4,8,512]{3,2,1,0:T(8,128)S(1)} %bitcast.63), channel_id=1, source_target_pairs={{0,1},{1,0},{2,3},{3,2},{4,5},{5,4},{6,7},{7,6},{8,9},{9,8},{10,11... | collective-permute-start | bytes 786440 | tf_op jit(solution)/shard_map/ppermute | solution.py:413
  50.3 1.2 %kept_edge.1 = f32[4,32,512]{2,1,0:T(8,128)S(1)} custom-call(s32[2]{0:T(128)S(1)} %pad_add_fusion.order, f32[7,80,512]{2,1,0:T(8,128)S(1)} %get-tuple-element.23.ends, f32[4,64,512]{2,1,0:T(8,128)S(1)} %first_edge.1.behind), custom_call_target="tpu_custom_call" | custom-call | flops 200000000 | bytes 4000000 | tf_op jit(solution)/shard_map/kept_edge/pallas_call | solution.py:397
  51.5 5.6 %collective-permute-done.8 = f32[4,4,8,512]{3,2,1,0:T(8,128)S(1)} collective-permute-done((f32[4,4,8,512]{3,2,1,0:T(8,128)S(1)}, f32[4,4,8,512]{3,2,1,0:T(8,128)S(1)}, u32[]{:S(2)}, u32[]{:S(2)}) %collective-permute-start.8) | collective-permute-done | bytes 262176 | tf_op jit(solution)/shard_map/ppermute | solution.py:413
  57.3 1.6 %collective-permute-start.10 = (f32[4,8,512]{2,1,0:T(8,128)S(1)}, f32[4,8,512]{2,1,0:T(8,128)S(1)}, u32[]{:S(2)}, u32[]{:S(2)}) collective-permute-start(f32[4,8,512]{2,1,0:T(8,128)S(1)} %get-tuple-element.34), channel_id=1, source_target_pairs={{0,4},{1,5},{2,6},{3,7},{4,0},{5,1},{6,2},{7,3},{8,12},{9,13},{10,... | collective-permute-start | bytes 196616 | tf_op jit(solution)/shard_map/ppermute | solution.py:444
  58.9 2.4 %collective-permute-start.11 = (f32[4,8,512]{2,1,0:T(8,128)S(1)}, f32[4,8,512]{2,1,0:T(8,128)S(1)}, u32[]{:S(2)}, u32[]{:S(2)}) collective-permute-start(f32[4,8,512]{2,1,0:T(8,128)S(1)} %get-tuple-element.33), channel_id=1, source_target_pairs={{0,6},{1,7},{2,4},{3,5},{4,2},{5,3},{6,0},{7,1},{8,14},{9,15},{10,... | collective-permute-start | bytes 196616 | tf_op jit(solution)/shard_map/ppermute | solution.py:444
  61.3 4.5 %collective-permute-done.10 = f32[4,8,512]{2,1,0:T(8,128)S(1)} collective-permute-done((f32[4,8,512]{2,1,0:T(8,128)S(1)}, f32[4,8,512]{2,1,0:T(8,128)S(1)}, u32[]{:S(2)}, u32[]{:S(2)}) %collective-permute-start.10) | collective-permute-done | bytes 65568 | tf_op jit(solution)/shard_map/ppermute | solution.py:444
  65.9 0.5 collective-permute-done.9
  66.4 0.6 pad_maximum_fusion.2
  (28 shorter events, 0.5 us)
Async XLA Ops:
  0.0 26.8 %copy-start = (bf16[1024,512]{1,0:T(8,128)(2,1)S(1)}, bf16[1024,512]{1,0:T(8,128)(2,1)}, u32[]{:S(2)}) copy-start(bf16[1024,512]{1,0:T(8,128)(2,1)} %constant.77.clone.by) | copy-start | bytes 3145732
  0.0 26.8 %copy-start.1 = (bf16[2,80,240]{2,1,0:T(8,128)(2,1)S(1)}, bf16[2,80,240]{2,1,0:T(8,128)(2,1)}, u32[]{:S(2)}) copy-start(bf16[2,80,240]{2,1,0:T(8,128)(2,1)} %constant.78.clone.lx) | copy-start | bytes 230404
  3.0 23.7 %collective-permute-start = (s32[32,8,512]{2,1,0:T(8,128)}, s32[32,8,512]{2,1,0:T(8,128)S(1)}, u32[]{:S(2)}, u32[]{:S(2)}) collective-permute-start(s32[32,8,512]{2,1,0:T(8,128)} %get-tuple-element.15), channel_id=1, source_target_pairs={{0,8},{8,0},{16,24},{24,16},{1,9},{9,1},{17,25},{25,17},{2,10},{10... | collective-permute-start | bytes 1572872 | tf_op jit(solution)/shard_map/ppermute | solution.py:413
  3.6 23.2 %collective-permute-start.1 = (s32[32,8,512]{2,1,0:T(8,128)}, s32[32,8,512]{2,1,0:T(8,128)S(1)}, u32[]{:S(2)}, u32[]{:S(2)}) collective-permute-start(s32[32,8,512]{2,1,0:T(8,128)} %get-tuple-element.16), channel_id=1, source_target_pairs={{8,16},{16,8},{9,17},{17,9},{10,18},{18,10},{11,19},{19,11},{12,20... | collective-permute-start | bytes 1572872 | tf_op jit(solution)/shard_map/ppermute | solution.py:413
  4.3 11.3 %collective-permute-start.4 = (s32[5,16,512]{2,1,0:T(8,128)S(1)}, s32[5,16,512]{2,1,0:T(8,128)S(1)}, u32[]{:S(2)}, u32[]{:S(2)}) collective-permute-start(s32[5,16,512]{2,1,0:T(8,128)S(1)} %get-tuple-element.21), channel_id=1, source_target_pairs={{0,1},{1,0},{2,3},{3,2},{4,5},{5,4},{6,7},{7,6},{8,9},{9,8},{10,11... | collective-permute-start | bytes 491528 | tf_op jit(solution)/shard_map/ppermute | solution.py:413
  6.8 10.2 %collective-permute-start.2 = (s32[5,16,512]{2,1,0:T(8,128)S(1)}, s32[5,16,512]{2,1,0:T(8,128)S(1)}, u32[]{:S(2)}, u32[]{:S(2)}) collective-permute-start(s32[5,16,512]{2,1,0:T(8,128)S(1)} %get-tuple-element.18), channel_id=1, source_target_pairs={{1,2},{2,1},{3,4},{4,3},{5,6},{6,5},{9,10},{10,9},{11,12},{12,11},... | collective-permute-start | bytes 491528 | tf_op jit(solution)/shard_map/ppermute | solution.py:413
  9.4 31.2 %collective-permute-start.7 = (s32[5,48,512]{2,1,0:T(8,128)}, s32[5,48,512]{2,1,0:T(8,128)S(1)}, u32[]{:S(2)}, u32[]{:S(2)}) collective-permute-start(s32[5,48,512]{2,1,0:T(8,128)} %constant_dynamic-slice_fusion), channel_id=1, source_target_pairs={{0,1},{1,0},{2,3},{3,2},{4,5},{5,4},{6,7},{7,6},{8,9},{9,8},{10,11... | collective-permute-start | bytes 1474568 | tf_op jit(solution)/shard_map/ppermute | solution.py:413
  15.5 28.1 %collective-permute-start.3 = (s32[5,48,512]{2,1,0:T(8,128)}, s32[5,48,512]{2,1,0:T(8,128)}, u32[]{:S(2)}, u32[]{:S(2)}) collective-permute-start(s32[5,48,512]{2,1,0:T(8,128)} %constant_dynamic-slice_fusion.1), channel_id=1, source_target_pairs={{1,2},{2,1},{3,4},{4,3},{5,6},{6,5},{9,10},{10,9},{11,12},{12,11},... | collective-permute-start | bytes 1474568 | tf_op jit(solution)/shard_map/ppermute | solution.py:413
  17.1 0.8 %collective-permute-start.6 = (s32[10,8,512]{2,1,0:T(8,128)S(1)}, s32[10,8,512]{2,1,0:T(8,128)S(1)}, u32[]{:S(2)}, u32[]{:S(2)}) collective-permute-start(s32[10,8,512]{2,1,0:T(8,128)S(1)} %get-tuple-element.30), channel_id=1, source_target_pairs={{8,16},{16,8},{9,17},{17,9},{10,18},{18,10},{11,19},{19,11},{12,20... | collective-permute-start | bytes 491528 | tf_op jit(solution)/shard_map/ppermute | solution.py:413
  17.9 8.8 %collective-permute-start.5 = (s32[10,8,512]{2,1,0:T(8,128)S(1)}, s32[10,8,512]{2,1,0:T(8,128)S(1)}, u32[]{:S(2)}, u32[]{:S(2)}) collective-permute-start(s32[10,8,512]{2,1,0:T(8,128)S(1)} %get-tuple-element.31), channel_id=1, source_target_pairs={{0,8},{8,0},{16,24},{24,16},{1,9},{9,1},{17,25},{25,17},{2,10},{10... | collective-permute-start | bytes 491528 | tf_op jit(solution)/shard_map/ppermute | solution.py:413
  46.6 10.5 %collective-permute-start.8 = (f32[4,4,8,512]{3,2,1,0:T(8,128)S(1)}, f32[4,4,8,512]{3,2,1,0:T(8,128)S(1)}, u32[]{:S(2)}, u32[]{:S(2)}) collective-permute-start(f32[4,4,8,512]{3,2,1,0:T(8,128)S(1)} %bitcast.63), channel_id=1, source_target_pairs={{0,1},{1,0},{2,3},{3,2},{4,5},{5,4},{6,7},{7,6},{8,9},{9,8},{10,11... | collective-permute-start | bytes 786440 | tf_op jit(solution)/shard_map/ppermute | solution.py:413
  57.3 8.5 %collective-permute-start.10 = (f32[4,8,512]{2,1,0:T(8,128)S(1)}, f32[4,8,512]{2,1,0:T(8,128)S(1)}, u32[]{:S(2)}, u32[]{:S(2)}) collective-permute-start(f32[4,8,512]{2,1,0:T(8,128)S(1)} %get-tuple-element.34), channel_id=1, source_target_pairs={{0,4},{1,5},{2,6},{3,7},{4,0},{5,1},{6,2},{7,3},{8,12},{9,13},{10,... | collective-permute-start | bytes 196616 | tf_op jit(solution)/shard_map/ppermute | solution.py:444
  58.9 6.9 %collective-permute-start.11 = (f32[4,8,512]{2,1,0:T(8,128)S(1)}, f32[4,8,512]{2,1,0:T(8,128)S(1)}, u32[]{:S(2)}, u32[]{:S(2)}) collective-permute-start(f32[4,8,512]{2,1,0:T(8,128)S(1)} %get-tuple-element.33), channel_id=1, source_target_pairs={{0,6},{1,7},{2,4},{3,5},{4,2},{5,3},{6,0},{7,1},{8,14},{9,15},{10,... | collective-permute-start | bytes 196616 | tf_op jit(solution)/shard_map/ppermute | solution.py:444
  61.3 5.0 %collective-permute-start.9 = (f32[4,8,512]{2,1,0:T(8,128)S(1)}, f32[4,8,512]{2,1,0:T(8,128)S(1)}, u32[]{:S(2)}, u32[]{:S(2)}) collective-permute-start(f32[4,8,512]{2,1,0:T(8,128)S(1)} %get-tuple-element.32), channel_id=1, source_target_pairs={{0,2},{1,3},{2,0},{3,1},{4,6},{5,7},{6,4},{7,5},{8,10},{9,11},{10,... | collective-permute-start | bytes 196616 | tf_op jit(solution)/shard_map/ppermute | solution.py:444

commit v6 on v5

--- a/solution.py
+++ b/solution.py
@@ -139,18 +139,20 @@
         ref[n, rows, :] = value
 
 
-def pack_kernel(where, c, edge_a, side_b, edge_b, side_a, sems):
+def pack_kernel(where, c, edge_a, side_b, edge_b, side_a, middle_a, middle_b, sems):
     rows = c.shape[1]
     copies = []
 
     def add(source, target):
         copies.append(pltpu.make_async_copy(source, target, sems.at[len(copies)]))
 
-    for n, (edge, side) in enumerate(((edge_a, side_a), (edge_b, side_b))):
+    blocks = ((edge_a, side_a, middle_a), (edge_b, side_b, middle_b))
+    for n, (edge, side, middle) in enumerate(blocks):
         layers = pl.ds(where[n], REACH)
         add(c.at[layers, pl.ds(0, PAD)], edge.at[:, pl.ds(0, PAD)])
         add(c.at[layers, pl.ds(rows - PAD, PAD)], edge.at[:, pl.ds(PAD, PAD)])
         add(c.at[:, pl.ds(pl.multiple_of(where[2 + n], PAD), PAD)], side)
+        add(c.at[layers, pl.ds(PAD, rows - 2 * PAD)], middle)
     for copy in copies:
         copy.start()
     for copy in copies:
@@ -306,15 +308,16 @@
 
 
 def call_pack(where, c):
-    layers, _, columns = c.shape
+    layers, rows, columns = c.shape
     edge = pltpu.VMEM((REACH, 2 * PAD, columns), c.dtype)
     side = pltpu.VMEM((layers, PAD, columns), c.dtype)
+    middle = pltpu.VMEM((REACH, rows - 2 * PAD, columns), c.dtype)
     return pl.pallas_call(
         pack_kernel,
-        out_shape=(edge, side, edge, side),
+        out_shape=(edge, side, edge, side, middle, middle),
         in_specs=[smem(), in_hbm()],
-        out_specs=tuple(whole(4)),
-        scratch_shapes=[pltpu.SemaphoreType.DMA((6,))],
+        out_specs=tuple(whole(6)),
+        scratch_shapes=[pltpu.SemaphoreType.DMA((8,))],
         compiler_params=params(8),
         name="pack",
     )(where, c)
@@ -473,10 +476,7 @@
     by = jnp.asarray(column_matrix(columns))
     lx = jnp.asarray(row_matrices(rows))
     held = pltpu.with_memory_space_constraint(counts, pltpu.HBM)
-    mid_a = lax.dynamic_slice(counts, (first_a, PAD, 0), (REACH, rows - 2 * PAD, columns))
-    edge_a, side_b, edge_b, side_a = call_pack(where, held)
-    later, edge_a = lax.optimization_barrier((counts, edge_a))
-    mid_b = lax.dynamic_slice(later, (first_b, PAD, 0), (REACH, rows - 2 * PAD, columns))
+    edge_a, side_b, edge_b, side_a, mid_a, mid_b = call_pack(where, held)
     edge_a = swap(edge_a, "depth", 0)
     edge_b = swap(edge_b, "depth", 1)
     xa = swap(side_a, "img", 0)

time: 67.4 us -> 65.1 us (0.966)
  waiting for transfers between devices: 11.7 us -> 15.6 us
  starting transfers between devices: 26.4 us -> 22.8 us
  local copies, waits for them, and re-layouts: 3.84 us -> 0.83 us
    ppermute x9, waiting for transfers between devices: 6.66 us -> 10.9 us  [swap(): return lax.ppermute(value, axis, pairs)]
    ppermute x9, starting transfers between devices: 22.4 us -> 18.3 us  [swap(): return lax.ppermute(value, axis, pairs)]
    dynamic_slice x2 -> x0, local copies, waits for them, and re-layouts: 3.75 us -> none  [the longest x1 1.89 us: local(): lax.dynamic_slice(later, (first_b, PAD, 0), (REACH, rows - 2 * PAD, colum...]
    squeeze x1, local copies, waits for them, and re-layouts: 0.03 us -> 0.77 us  [local(): corner_b = lax.dynamic_index_in_dim(halves, row_odd, 1, keepdims=False)]
  transfers between devices with their start and end apart: 12 -> 12, of which waited for: 4 -> 6; matrix products, arithmetic and copies ran while one was open for 6% -> 2% of each run, Pallas kernels for 27% -> 28%
where the time goes in v6:
time: 65.1 us; the launch traced here: 64.8 us
  Pallas kernels  24.4 us (37%)
  starting transfers between devices  22.8 us (35%)
  waiting for transfers between devices  15.6 us (24%)
  other arithmetic  1.04 us (2%)
  local copies, waits for them, and re-layouts  0.83 us (1%)
    ppermute x9, starting transfers between devices, swap(): return lax.ppermute(value, axis, pairs)  18.3 us
    ppermute x9, waiting for transfers between devices, swap(): return lax.ppermute(value, axis, pairs)  10.9 us
    pallas_call x1, Pallas kernels, call_interior(): pl.pallas_call(functools.partial(interior_kernel, scale), out_shape=(jax....  7.31 us
    pallas_call x1, Pallas kernels, call_smooth(): pl.pallas_call(functools.partial(smooth_kernel, group), out_shape=jax.Sha...  6.45 us
    ppermute x3, waiting for transfers between devices, exchange(): lax.ppermute(piece, 'depth', [(i, i ^ 2 * step) for i in range(count)])  4.74 us
    ppermute x3, starting transfers between devices, exchange(): lax.ppermute(piece, 'depth', [(i, i ^ 2 * step) for i in range(count)])  4.48 us
    pallas_call x1, Pallas kernels, call_pack(): pl.pallas_call(pack_kernel, out_shape=(edge, side, edge, side, middle, mi...  3.4 us
    pallas_call x1, Pallas kernels, call_first_edge(): pl.pallas_call(functools.partial(first_edge_kernel, scale), out_shape=jax...  3.08 us
  transfers between devices with their start and end apart: 12, of which 6 were waited for; matrix products, arithmetic and copies ran while one was open for 2% of the time, Pallas kernels for 28%

profile of v6, /device:TPU:0, one launch (start us, length us, event | category | flops | bytes accessed | tf_op | source)
XLA Modules:
  0.0 64.8 jit_solution(2334635529446512836)
XLA Ops:
  0.1 3.4 %pack.1 = (s32[5,16,512]{2,1,0:T(8,128)S(1)}, s32[32,8,512]{2,1,0:T(8,128)}, s32[5,16,512]{2,1,0:T(8,128)S(1)}, s32[32,8,512]{2,1,0:T(8,128)}, s32[5,48,512]{2,1,0:T(8,128)}, /*index=5*/s32[5,48,512]{2,1,0:T(8,128)S(1)}) custom-call(s32[4]{0:T(128)S(1)} %pad_add_fusion.1.where, s32[32,64,512]{2,1,0:T(8,128)} %c_hbm.1), custom_call_target="tpu_custom_call" | custom-call | tf_op jit(solution)/shard_map/pack/pallas_call | solution.py:315
  3.5 0.7 %collective-permute-start.2 = (s32[5,16,512]{2,1,0:T(8,128)S(1)}, s32[5,16,512]{2,1,0:T(8,128)S(1)}, u32[]{:S(2)}, u32[]{:S(2)}) collective-permute-start(s32[5,16,512]{2,1,0:T(8,128)S(1)} %get-tuple-element.18), channel_id=1, source_target_pairs={{1,2},{2,1},{3,4},{4,3},{5,6},{6,5},{9,10},{10,9},{11,12},{12,11},... | collective-permute-start | bytes 491528 | tf_op jit(solution)/shard_map/ppermute | solution.py:416
  4.2 5.8 %collective-permute-start.4 = (s32[5,16,512]{2,1,0:T(8,128)S(1)}, s32[5,16,512]{2,1,0:T(8,128)S(1)}, u32[]{:S(2)}, u32[]{:S(2)}) collective-permute-start(s32[5,16,512]{2,1,0:T(8,128)S(1)} %get-tuple-element.20), channel_id=1, source_target_pairs={{0,1},{1,0},{2,3},{3,2},{4,5},{5,4},{6,7},{7,6},{8,9},{9,8},{10,11... | collective-permute-start | bytes 491528 | tf_op jit(solution)/shard_map/ppermute | solution.py:416
  10.0 0.7 %collective-permute-start.1 = (s32[32,8,512]{2,1,0:T(8,128)}, s32[32,8,512]{2,1,0:T(8,128)S(1)}, u32[]{:S(2)}, u32[]{:S(2)}) collective-permute-start(s32[32,8,512]{2,1,0:T(8,128)} %get-tuple-element.16), channel_id=1, source_target_pairs={{8,16},{16,8},{9,17},{17,9},{10,18},{18,10},{11,19},{19,11},{12,20... | collective-permute-start | bytes 1572872 | tf_op jit(solution)/shard_map/ppermute | solution.py:416
  10.7 0.2 collective-permute-start.7
  10.9 1.4 %collective-permute-start.3 = (s32[5,48,512]{2,1,0:T(8,128)}, s32[5,48,512]{2,1,0:T(8,128)}, u32[]{:S(2)}, u32[]{:S(2)}) collective-permute-start(s32[5,48,512]{2,1,0:T(8,128)} %copy-done.2), channel_id=1, source_target_pairs={{1,2},{2,1},{3,4},{4,3},{5,6},{6,5},{9,10},{10,9},{11,12},{12,11},... | collective-permute-start | bytes 1474568 | tf_op jit(solution)/shard_map/ppermute | solution.py:416
  12.3 4.0 %collective-permute-done.4.edge = s32[5,16,512]{2,1,0:T(8,128)S(1)} collective-permute-done((s32[5,16,512]{2,1,0:T(8,128)S(1)}, s32[5,16,512]{2,1,0:T(8,128)S(1)}, u32[]{:S(2)}, u32[]{:S(2)}) %collective-permute-start.4) | collective-permute-done | bytes 163872 | tf_op jit(solution)/shard_map/ppermute | solution.py:416
  16.3 0.8 %dynamic-slice_bitcast_fusion = (s32[10,8,512]{2,1,0:T(8,128)}, s32[10,8,512]{2,1,0:T(8,128)}) fusion(s32[10,2,8,512]{3,2,1,0:T(8,128)S(1)} %add_bitcast_fusion, s32[]{:T(128)S(6)} %select_n.149, s32[]{:T(128)S(6)} %select_n.148), kind=kLoop, calls=%fused_computation.7 | loop fusion | bytes 655368 | tf_op jit(solution)/shard_map/jit(dynamic_index_in_dim)/squeeze | solution.py:488
  17.1 0.7 %collective-permute-start.6 = (s32[10,8,512]{2,1,0:T(8,128)}, s32[10,8,512]{2,1,0:T(8,128)S(1)}, u32[]{:S(2)}, u32[]{:S(2)}) collective-permute-start(s32[10,8,512]{2,1,0:T(8,128)} %get-tuple-element.30), channel_id=1, source_target_pairs={{8,16},{16,8},{9,17},{17,9},{10,18},{18,10},{11,19},{19,11},{12,20... | collective-permute-start | bytes 491528 | tf_op jit(solution)/shard_map/ppermute | solution.py:416
  17.9 5.9 %collective-permute-start.5 = (s32[10,8,512]{2,1,0:T(8,128)}, s32[10,8,512]{2,1,0:T(8,128)S(1)}, u32[]{:S(2)}, u32[]{:S(2)}) collective-permute-start(s32[10,8,512]{2,1,0:T(8,128)} %get-tuple-element.31), channel_id=1, source_target_pairs={{0,8},{8,0},{16,24},{24,16},{1,9},{9,1},{17,25},{25,17},{2,10},{10... | collective-permute-start | bytes 491528 | tf_op jit(solution)/shard_map/ppermute | solution.py:416
  23.9 1.2 %collective-permute-done.5 = s32[10,8,512]{2,1,0:T(8,128)S(1)} collective-permute-done((s32[10,8,512]{2,1,0:T(8,128)}, s32[10,8,512]{2,1,0:T(8,128)S(1)}, u32[]{:S(2)}, u32[]{:S(2)}) %collective-permute-start.5) | collective-permute-done | bytes 163872 | tf_op jit(solution)/shard_map/ppermute | solution.py:416
  25.2 6.4 %smooth.1.plane = f32[32,80,512]{2,1,0:T(8,128)S(1)} custom-call(s32[2]{0:T(128)S(1)} %pad_add_fusion.order, s32[32,64,512]{2,1,0:T(8,128)} %c_hbm.1, s32[32,8,512]{2,1,0:T(8,128)S(1)} %collective-permute-done.xa, s32[32,8,512]{2,1,0:T(8,128)S(1)} %collective-permute-done.1.xb, bf16[1024,512]{1,0:T(8,128)(2,1)S(1)} %copy-done, bf16[2,80,240]{2,1,0:T(8,128)(2,1)S(1)} %copy-done.1), custom_call_target="tpu_custom_call" | custom-call | flops 1000000000 | bytes 4000000 | tf_op jit(solution)/shard_map/smooth/pallas_call | solution.py:330
  31.6 7.3 %interior.1 = (f32[4,64,512]{2,1,0:T(8,128)S(1)}, f32[24,80,512]{2,1,0:T(8,128)S(1)}) custom-call(f32[4]{0:T(128)S(1)} %add_convert_fusion.flags, f32[32,80,512]{2,1,0:T(8,128)S(1)} %smooth.1.plane), custom_call_target="tpu_custom_call" | custom-call | flops 1000000000 | bytes 4000000 | tf_op jit(solution)/shard_map/interior/pallas_call | solution.py:347
  38.9 3.1 %first_edge.1.behind = f32[4,64,512]{2,1,0:T(8,128)S(1)} custom-call(f32[4]{0:T(128)S(1)} %add_convert_fusion.flags, s32[2]{0:T(128)S(1)} %pad_add_fusion.order, f32[32,80,512]{2,1,0:T(8,128)S(1)} %smooth.1.plane, f32[24,80,512]{2,1,0:T(8,128)S(1)} %get-tuple-element.17.smoothed, s32[5,16,512]{2,1,0:T(8,128)S(1)} %collective-permute-done.4.edge, ...), custom_call_target="tpu_custom_call" | custom-call | flops 300000000 | bytes 4000000 | tf_op jit(solution)/shard_map/first_edge/pallas_call | solution.py:364
  42.0 3.0 %last_edge.1 = (f32[4,32,512]{2,1,0:T(8,128)S(1)}, f32[7,80,512]{2,1,0:T(8,128)S(1)}) custom-call(f32[4]{0:T(128)S(1)} %add_convert_fusion.flags, s32[2]{0:T(128)S(1)} %pad_add_fusion.order, f32[32,80,512]{2,1,0:T(8,128)S(1)} %smooth.1.plane, f32[24,80,512]{2,1,0:T(8,128)S(1)} %get-tuple-element.17.smoothed, s32[5,16,512]{2,1,0:T(8,128)S(1)} %collective-permute-done.2.edge, ...), custom_call_target="tpu_custom_call" | custom-call | flops 300000000 | bytes 4000000 | tf_op jit(solution)/shard_map/last_edge/pallas_call | solution.py:383
  45.0 2.9 %collective-permute-start.8 = (f32[4,4,8,512]{3,2,1,0:T(8,128)S(1)}, f32[4,4,8,512]{3,2,1,0:T(8,128)S(1)}, u32[]{:S(2)}, u32[]{:S(2)}) collective-permute-start(f32[4,4,8,512]{3,2,1,0:T(8,128)S(1)} %bitcast.63), channel_id=1, source_target_pairs={{0,1},{1,0},{2,3},{3,2},{4,5},{5,4},{6,7},{7,6},{8,9},{9,8},{10,11... | collective-permute-start | bytes 786440 | tf_op jit(solution)/shard_map/ppermute | solution.py:416
  47.9 1.2 %kept_edge.1 = f32[4,32,512]{2,1,0:T(8,128)S(1)} custom-call(s32[2]{0:T(128)S(1)} %pad_add_fusion.order, f32[7,80,512]{2,1,0:T(8,128)S(1)} %get-tuple-element.23.ends, f32[4,64,512]{2,1,0:T(8,128)S(1)} %first_edge.1.behind), custom_call_target="tpu_custom_call" | custom-call | flops 200000000 | bytes 4000000 | tf_op jit(solution)/shard_map/kept_edge/pallas_call | solution.py:400
  49.1 5.6 %collective-permute-done.8 = f32[4,4,8,512]{3,2,1,0:T(8,128)S(1)} collective-permute-done((f32[4,4,8,512]{3,2,1,0:T(8,128)S(1)}, f32[4,4,8,512]{3,2,1,0:T(8,128)S(1)}, u32[]{:S(2)}, u32[]{:S(2)}) %collective-permute-start.8) | collective-permute-done | bytes 262176 | tf_op jit(solution)/shard_map/ppermute | solution.py:416
  54.9 2.9 %collective-permute-start.10 = (f32[4,8,512]{2,1,0:T(8,128)S(1)}, f32[4,8,512]{2,1,0:T(8,128)S(1)}, u32[]{:S(2)}, u32[]{:S(2)}) collective-permute-start(f32[4,8,512]{2,1,0:T(8,128)S(1)} %get-tuple-element.34), channel_id=1, source_target_pairs={{0,4},{1,5},{2,6},{3,7},{4,0},{5,1},{6,2},{7,3},{8,12},{9,13},{10,... | collective-permute-start | bytes 196616 | tf_op jit(solution)/shard_map/ppermute | solution.py:447
  57.8 1.3 %collective-permute-start.11 = (f32[4,8,512]{2,1,0:T(8,128)S(1)}, f32[4,8,512]{2,1,0:T(8,128)S(1)}, u32[]{:S(2)}, u32[]{:S(2)}) collective-permute-start(f32[4,8,512]{2,1,0:T(8,128)S(1)} %get-tuple-element.33), channel_id=1, source_target_pairs={{0,6},{1,7},{2,4},{3,5},{4,2},{5,3},{6,0},{7,1},{8,14},{9,15},{10,... | collective-permute-start | bytes 196616 | tf_op jit(solution)/shard_map/ppermute | solution.py:447
  59.1 0.2 collective-permute-start.9
  59.4 1.2 %collective-permute-done.10 = f32[4,8,512]{2,1,0:T(8,128)S(1)} collective-permute-done((f32[4,8,512]{2,1,0:T(8,128)S(1)}, f32[4,8,512]{2,1,0:T(8,128)S(1)}, u32[]{:S(2)}, u32[]{:S(2)}) %collective-permute-start.10) | collective-permute-done | bytes 65568 | tf_op jit(solution)/shard_map/ppermute | solution.py:447
  60.6 3.4 %collective-permute-done.11 = f32[4,8,512]{2,1,0:T(8,128)S(1)} collective-permute-done((f32[4,8,512]{2,1,0:T(8,128)S(1)}, f32[4,8,512]{2,1,0:T(8,128)S(1)}, u32[]{:S(2)}, u32[]{:S(2)}) %collective-permute-start.11) | collective-permute-done | bytes 65568 | tf_op jit(solution)/shard_map/ppermute | solution.py:447
  64.2 0.6 pad_maximum_fusion.2
  (28 shorter events, 0.6 us)
Async XLA Ops:
  0.0 25.1 %copy-start = (bf16[1024,512]{1,0:T(8,128)(2,1)S(1)}, bf16[1024,512]{1,0:T(8,128)(2,1)}, u32[]{:S(2)}) copy-start(bf16[1024,512]{1,0:T(8,128)(2,1)} %constant.73.clone.by) | copy-start | bytes 3145732
  0.0 25.2 %copy-start.1 = (bf16[2,80,240]{2,1,0:T(8,128)(2,1)S(1)}, bf16[2,80,240]{2,1,0:T(8,128)(2,1)}, u32[]{:S(2)}) copy-start(bf16[2,80,240]{2,1,0:T(8,128)(2,1)} %constant.74.clone.lx) | copy-start | bytes 230404
  3.5 6.5 %copy-start.2 = (s32[5,48,512]{2,1,0:T(8,128)}, s32[5,48,512]{2,1,0:T(8,128)S(1)}, u32[]{:S(2)}) copy-start(s32[5,48,512]{2,1,0:T(8,128)S(1)} %get-tuple-element.19) | copy-start | bytes 1474564
  3.5 7.4 %collective-permute-start.2 = (s32[5,16,512]{2,1,0:T(8,128)S(1)}, s32[5,16,512]{2,1,0:T(8,128)S(1)}, u32[]{:S(2)}, u32[]{:S(2)}) collective-permute-start(s32[5,16,512]{2,1,0:T(8,128)S(1)} %get-tuple-element.18), channel_id=1, source_target_pairs={{1,2},{2,1},{3,4},{4,3},{5,6},{6,5},{9,10},{10,9},{11,12},{12,11},... | collective-permute-start | bytes 491528 | tf_op jit(solution)/shard_map/ppermute | solution.py:416
  4.2 12.1 %collective-permute-start.4 = (s32[5,16,512]{2,1,0:T(8,128)S(1)}, s32[5,16,512]{2,1,0:T(8,128)S(1)}, u32[]{:S(2)}, u32[]{:S(2)}) collective-permute-start(s32[5,16,512]{2,1,0:T(8,128)S(1)} %get-tuple-element.20), channel_id=1, source_target_pairs={{0,1},{1,0},{2,3},{3,2},{4,5},{5,4},{6,7},{7,6},{8,9},{9,8},{10,11... | collective-permute-start | bytes 491528 | tf_op jit(solution)/shard_map/ppermute | solution.py:416
  10.0 15.1 %collective-permute-start = (s32[32,8,512]{2,1,0:T(8,128)}, s32[32,8,512]{2,1,0:T(8,128)S(1)}, u32[]{:S(2)}, u32[]{:S(2)}) collective-permute-start(s32[32,8,512]{2,1,0:T(8,128)} %get-tuple-element.15), channel_id=1, source_target_pairs={{0,8},{8,0},{16,24},{24,16},{1,9},{9,1},{17,25},{25,17},{2,10},{10... | collective-permute-start | bytes 1572872 | tf_op jit(solution)/shard_map/ppermute | solution.py:416
  10.0 15.1 %collective-permute-start.1 = (s32[32,8,512]{2,1,0:T(8,128)}, s32[32,8,512]{2,1,0:T(8,128)S(1)}, u32[]{:S(2)}, u32[]{:S(2)}) collective-permute-start(s32[32,8,512]{2,1,0:T(8,128)} %get-tuple-element.16), channel_id=1, source_target_pairs={{8,16},{16,8},{9,17},{17,9},{10,18},{18,10},{11,19},{19,11},{12,20... | collective-permute-start | bytes 1572872 | tf_op jit(solution)/shard_map/ppermute | solution.py:416
  10.7 28.2 %collective-permute-start.7 = (s32[5,48,512]{2,1,0:T(8,128)}, s32[5,48,512]{2,1,0:T(8,128)S(1)}, u32[]{:S(2)}, u32[]{:S(2)}) collective-permute-start(s32[5,48,512]{2,1,0:T(8,128)} %get-tuple-element.21), channel_id=1, source_target_pairs={{0,1},{1,0},{2,3},{3,2},{4,5},{5,4},{6,7},{7,6},{8,9},{9,8},{10,11... | collective-permute-start | bytes 1474568 | tf_op jit(solution)/shard_map/ppermute | solution.py:416
  10.9 31.2 %collective-permute-start.3 = (s32[5,48,512]{2,1,0:T(8,128)}, s32[5,48,512]{2,1,0:T(8,128)}, u32[]{:S(2)}, u32[]{:S(2)}) collective-permute-start(s32[5,48,512]{2,1,0:T(8,128)} %copy-done.2), channel_id=1, source_target_pairs={{1,2},{2,1},{3,4},{4,3},{5,6},{6,5},{9,10},{10,9},{11,12},{12,11},... | collective-permute-start | bytes 1474568 | tf_op jit(solution)/shard_map/ppermute | solution.py:416
  17.1 0.8 %collective-permute-start.6 = (s32[10,8,512]{2,1,0:T(8,128)}, s32[10,8,512]{2,1,0:T(8,128)S(1)}, u32[]{:S(2)}, u32[]{:S(2)}) collective-permute-start(s32[10,8,512]{2,1,0:T(8,128)} %get-tuple-element.30), channel_id=1, source_target_pairs={{8,16},{16,8},{9,17},{17,9},{10,18},{18,10},{11,19},{19,11},{12,20... | collective-permute-start | bytes 491528 | tf_op jit(solution)/shard_map/ppermute | solution.py:416
  17.9 7.2 %collective-permute-start.5 = (s32[10,8,512]{2,1,0:T(8,128)}, s32[10,8,512]{2,1,0:T(8,128)S(1)}, u32[]{:S(2)}, u32[]{:S(2)}) collective-permute-start(s32[10,8,512]{2,1,0:T(8,128)} %get-tuple-element.31), channel_id=1, source_target_pairs={{0,8},{8,0},{16,24},{24,16},{1,9},{9,1},{17,25},{25,17},{2,10},{10... | collective-permute-start | bytes 491528 | tf_op jit(solution)/shard_map/ppermute | solution.py:416
  45.0 9.7 %collective-permute-start.8 = (f32[4,4,8,512]{3,2,1,0:T(8,128)S(1)}, f32[4,4,8,512]{3,2,1,0:T(8,128)S(1)}, u32[]{:S(2)}, u32[]{:S(2)}) collective-permute-start(f32[4,4,8,512]{3,2,1,0:T(8,128)S(1)} %bitcast.63), channel_id=1, source_target_pairs={{0,1},{1,0},{2,3},{3,2},{4,5},{5,4},{6,7},{7,6},{8,9},{9,8},{10,11... | collective-permute-start | bytes 786440 | tf_op jit(solution)/shard_map/ppermute | solution.py:416
  54.9 5.7 %collective-permute-start.10 = (f32[4,8,512]{2,1,0:T(8,128)S(1)}, f32[4,8,512]{2,1,0:T(8,128)S(1)}, u32[]{:S(2)}, u32[]{:S(2)}) collective-permute-start(f32[4,8,512]{2,1,0:T(8,128)S(1)} %get-tuple-element.34), channel_id=1, source_target_pairs={{0,4},{1,5},{2,6},{3,7},{4,0},{5,1},{6,2},{7,3},{8,12},{9,13},{10,... | collective-permute-start | bytes 196616 | tf_op jit(solution)/shard_map/ppermute | solution.py:447
  57.8 6.2 %collective-permute-start.11 = (f32[4,8,512]{2,1,0:T(8,128)S(1)}, f32[4,8,512]{2,1,0:T(8,128)S(1)}, u32[]{:S(2)}, u32[]{:S(2)}) collective-permute-start(f32[4,8,512]{2,1,0:T(8,128)S(1)} %get-tuple-element.33), channel_id=1, source_target_pairs={{0,6},{1,7},{2,4},{3,5},{4,2},{5,3},{6,0},{7,1},{8,14},{9,15},{10,... | collective-permute-start | bytes 196616 | tf_op jit(solution)/shard_map/ppermute | solution.py:447
  59.1 5.0 %collective-permute-start.9 = (f32[4,8,512]{2,1,0:T(8,128)S(1)}, f32[4,8,512]{2,1,0:T(8,128)S(1)}, u32[]{:S(2)}, u32[]{:S(2)}) collective-permute-start(f32[4,8,512]{2,1,0:T(8,128)S(1)} %get-tuple-element.32), channel_id=1, source_target_pairs={{0,2},{1,3},{2,0},{3,1},{4,6},{5,7},{6,4},{7,5},{8,10},{9,11},{10,... | collective-permute-start | bytes 196616 | tf_op jit(solution)/shard_map/ppermute | solution.py:447

commit v7 on v6

--- a/solution.py
+++ b/solution.py
@@ -266,25 +266,25 @@
 
 def first_edge_kernel(scale, flags, order, plane, smoothed, edge, middle, ca, cb, by, lx, behind,
                       image, ends, halo):
-    edge_smooth(0, flags, order, plane, smoothed, edge, middle, ca, cb, by, lx, ends, halo)
+    edge_smooth(1, flags, order, plane, smoothed, edge, middle, ca, cb, by, lx, ends, halo)
     tiles = plane.shape[1] // 8 - 2
-    edge_render(scale, order[1] == 1, ends, behind, image, tiles, lambda place: place)
+    edge_render(scale, order[1] == 0, ends, behind, image, tiles, lambda place: place)
 
 
 def last_edge_kernel(scale, owner_tiles, flags, order, plane, smoothed, edge, middle, ca, cb, by,
                      lx, behind, image, ends, halo):
-    edge_smooth(1, flags, order, plane, smoothed, edge, middle, ca, cb, by, lx, ends, halo)
+    edge_smooth(0, flags, order, plane, smoothed, edge, middle, ca, cb, by, lx, ends, halo)
     tiles = plane.shape[1] // 8 - 2
     tile_of = lambda place: place
     if owner_tiles:
         tiles, tile_of = tiles // 2, half_tiles(owner_tiles, 1 - order[1])
-    edge_render(scale, order[1] == 0, ends, behind, image, tiles, tile_of)
+    edge_render(scale, order[1] == 1, ends, behind, image, tiles, tile_of)
 
 
 def kept_edge_kernel(scale, owner_tiles, order, ends, behind, image):
     tiles = ends.shape[1] // 8 - 2
     tile_of = half_tiles(owner_tiles, order[1])
-    edge_render(scale, order[1] == 0, ends, behind, image, tiles // 2, tile_of)
+    edge_render(scale, order[1] == 1, ends, behind, image, tiles // 2, tile_of)
 
 
 def whole(count):
@@ -494,10 +494,10 @@
     owner_tiles = owned // 8 if owned % 8 == 0 else 0
     common = (flags, order, plane, smoothed)
     layers = call_first_edge(
-        scale, *common, edge_a, mid_a, ca[:REACH], cb[:REACH], by, lx, inner
+        scale, *common, edge_b, mid_b, ca[REACH:], cb[REACH:], by, lx, inner
     )
     send, ends = call_last_edge(
-        scale, owner_tiles, *common, edge_b, mid_b, ca[REACH:], cb[REACH:], by, lx, layers
+        scale, owner_tiles, *common, edge_a, mid_a, ca[:REACH], cb[:REACH], by, lx, layers
     )
     if owner_tiles:
         keep = call_kept_edge(scale, owner_tiles, order, ends, layers)

time: 65.1 us -> 64.8 us (level)
  starting transfers between devices: 22.8 us -> 20 us
  waiting for transfers between devices: 15.6 us -> 18.1 us
    ppermute x9, starting transfers between devices: 18.3 us -> 16 us  [swap(): return lax.ppermute(value, axis, pairs)]
    ppermute x9, waiting for transfers between devices: 10.9 us -> 13.1 us  [swap(): return lax.ppermute(value, axis, pairs)]
where the time goes in v7:
time: 64.8 us; the launch traced here: 64.6 us
  Pallas kernels  24.4 us (38%)
  starting transfers between devices  20 us (31%)
  waiting for transfers between devices  18.1 us (28%)
  other arithmetic  1.04 us (2%)
  local copies, waits for them, and re-layouts  0.83 us (1%)
    ppermute x9, starting transfers between devices, swap(): return lax.ppermute(value, axis, pairs)  16 us
    ppermute x9, waiting for transfers between devices, swap(): return lax.ppermute(value, axis, pairs)  13.1 us
    pallas_call x1, Pallas kernels, call_interior(): pl.pallas_call(functools.partial(interior_kernel, scale), out_shape=(jax....  7.31 us
    pallas_call x1, Pallas kernels, call_smooth(): pl.pallas_call(functools.partial(smooth_kernel, group), out_shape=jax.Sha...  6.45 us
    ppermute x3, waiting for transfers between devices, exchange(): lax.ppermute(piece, 'depth', [(i, i ^ 2 * step) for i in range(count)])  4.96 us
    ppermute x3, starting transfers between devices, exchange(): lax.ppermute(piece, 'depth', [(i, i ^ 2 * step) for i in range(count)])  4.01 us
    pallas_call x1, Pallas kernels, call_pack(): pl.pallas_call(pack_kernel, out_shape=(edge, side, edge, side, middle, mi...  3.39 us
    pallas_call x1, Pallas kernels, call_first_edge(): pl.pallas_call(functools.partial(first_edge_kernel, scale), out_shape=jax...  3.08 us
  transfers between devices with their start and end apart: 12, of which 6 were waited for; matrix products, arithmetic and copies ran while one was open for 2% of the time, Pallas kernels for 28%

profile of v7, /device:TPU:0, one launch (start us, length us, event | category | flops | bytes accessed | tf_op | source)
XLA Modules:
  0.0 64.6 jit_solution(3057284649949463551)
XLA Ops:
  0.1 3.4 %pack.1 = (s32[5,16,512]{2,1,0:T(8,128)S(1)}, s32[32,8,512]{2,1,0:T(8,128)}, s32[5,16,512]{2,1,0:T(8,128)S(1)}, s32[32,8,512]{2,1,0:T(8,128)}, s32[5,48,512]{2,1,0:T(8,128)S(1)}, /*index=5*/s32[5,48,512]{2,1,0:T(8,128)}) custom-call(s32[4]{0:T(128)S(1)} %pad_add_fusion.1.where, s32[32,64,512]{2,1,0:T(8,128)} %c_hbm.1), custom_call_target="tpu_custom_call" | custom-call | tf_op jit(solution)/shard_map/pack/pallas_call | solution.py:315
  3.5 3.0 %collective-permute-start.2 = (s32[5,16,512]{2,1,0:T(8,128)S(1)}, s32[5,16,512]{2,1,0:T(8,128)S(1)}, u32[]{:S(2)}, u32[]{:S(2)}) collective-permute-start(s32[5,16,512]{2,1,0:T(8,128)S(1)} %get-tuple-element.18), channel_id=1, source_target_pairs={{0,1},{1,0},{2,3},{3,2},{4,5},{5,4},{6,7},{7,6},{8,9},{9,8},{10,11... | collective-permute-start | bytes 491528 | tf_op jit(solution)/shard_map/ppermute | solution.py:416
  6.5 0.7 %collective-permute-start.4 = (s32[5,16,512]{2,1,0:T(8,128)S(1)}, s32[5,16,512]{2,1,0:T(8,128)S(1)}, u32[]{:S(2)}, u32[]{:S(2)}) collective-permute-start(s32[5,16,512]{2,1,0:T(8,128)S(1)} %get-tuple-element.20), channel_id=1, source_target_pairs={{1,2},{2,1},{3,4},{4,3},{5,6},{6,5},{9,10},{10,9},{11,12},{12,11},... | collective-permute-start | bytes 491528 | tf_op jit(solution)/shard_map/ppermute | solution.py:416
  7.3 0.7 %collective-permute-start.1 = (s32[32,8,512]{2,1,0:T(8,128)}, s32[32,8,512]{2,1,0:T(8,128)S(1)}, u32[]{:S(2)}, u32[]{:S(2)}) collective-permute-start(s32[32,8,512]{2,1,0:T(8,128)} %get-tuple-element.16), channel_id=1, source_target_pairs={{8,16},{16,8},{9,17},{17,9},{10,18},{18,10},{11,19},{19,11},{12,20... | collective-permute-start | bytes 1572872 | tf_op jit(solution)/shard_map/ppermute | solution.py:416
  8.0 0.7 %collective-permute-start.7 = (s32[5,48,512]{2,1,0:T(8,128)}, s32[5,48,512]{2,1,0:T(8,128)S(1)}, u32[]{:S(2)}, u32[]{:S(2)}) collective-permute-start(s32[5,48,512]{2,1,0:T(8,128)} %get-tuple-element.21), channel_id=1, source_target_pairs={{1,2},{2,1},{3,4},{4,3},{5,6},{6,5},{9,10},{10,9},{11,12},{12,11},... | collective-permute-start | bytes 1474568 | tf_op jit(solution)/shard_map/ppermute | solution.py:416
  8.7 4.8 %collective-permute-done.2.edge = s32[5,16,512]{2,1,0:T(8,128)S(1)} collective-permute-done((s32[5,16,512]{2,1,0:T(8,128)S(1)}, s32[5,16,512]{2,1,0:T(8,128)S(1)}, u32[]{:S(2)}, u32[]{:S(2)}) %collective-permute-start.2) | collective-permute-done | bytes 163872 | tf_op jit(solution)/shard_map/ppermute | solution.py:416
  13.5 2.4 %collective-permute-start.3 = (s32[5,48,512]{2,1,0:T(8,128)}, s32[5,48,512]{2,1,0:T(8,128)}, u32[]{:S(2)}, u32[]{:S(2)}) collective-permute-start(s32[5,48,512]{2,1,0:T(8,128)} %copy-done.2), channel_id=1, source_target_pairs={{0,1},{1,0},{2,3},{3,2},{4,5},{5,4},{6,7},{7,6},{8,9},{9,8},{10,11... | collective-permute-start | bytes 1474568 | tf_op jit(solution)/shard_map/ppermute | solution.py:416
  16.0 0.8 %dynamic-slice_bitcast_fusion = (s32[10,8,512]{2,1,0:T(8,128)}, s32[10,8,512]{2,1,0:T(8,128)}) fusion(s32[10,2,8,512]{3,2,1,0:T(8,128)S(1)} %add_bitcast_fusion, s32[]{:T(128)S(6)} %select_n.149, s32[]{:T(128)S(6)} %select_n.148), kind=kLoop, calls=%fused_computation.7 | loop fusion | bytes 655368 | tf_op jit(solution)/shard_map/jit(dynamic_index_in_dim)/squeeze | solution.py:488
  16.8 0.7 %collective-permute-start.6 = (s32[10,8,512]{2,1,0:T(8,128)}, s32[10,8,512]{2,1,0:T(8,128)S(1)}, u32[]{:S(2)}, u32[]{:S(2)}) collective-permute-start(s32[10,8,512]{2,1,0:T(8,128)} %get-tuple-element.30), channel_id=1, source_target_pairs={{8,16},{16,8},{9,17},{17,9},{10,18},{18,10},{11,19},{19,11},{12,20... | collective-permute-start | bytes 491528 | tf_op jit(solution)/shard_map/ppermute | solution.py:416
  17.6 7.4 %collective-permute-start.5 = (s32[10,8,512]{2,1,0:T(8,128)}, s32[10,8,512]{2,1,0:T(8,128)S(1)}, u32[]{:S(2)}, u32[]{:S(2)}) collective-permute-start(s32[10,8,512]{2,1,0:T(8,128)} %get-tuple-element.31), channel_id=1, source_target_pairs={{0,8},{8,0},{16,24},{24,16},{1,9},{9,1},{17,25},{25,17},{2,10},{10... | collective-permute-start | bytes 491528 | tf_op jit(solution)/shard_map/ppermute | solution.py:416
  25.0 1.2 %collective-permute-done.5 = s32[10,8,512]{2,1,0:T(8,128)S(1)} collective-permute-done((s32[10,8,512]{2,1,0:T(8,128)}, s32[10,8,512]{2,1,0:T(8,128)S(1)}, u32[]{:S(2)}, u32[]{:S(2)}) %collective-permute-start.5) | collective-permute-done | bytes 163872 | tf_op jit(solution)/shard_map/ppermute | solution.py:416
  26.3 6.4 %smooth.1.plane = f32[32,80,512]{2,1,0:T(8,128)S(1)} custom-call(s32[2]{0:T(128)S(1)} %pad_add_fusion.order, s32[32,64,512]{2,1,0:T(8,128)} %c_hbm.1, s32[32,8,512]{2,1,0:T(8,128)S(1)} %collective-permute-done.xa, s32[32,8,512]{2,1,0:T(8,128)S(1)} %collective-permute-done.1.xb, bf16[1024,512]{1,0:T(8,128)(2,1)S(1)} %copy-done, bf16[2,80,240]{2,1,0:T(8,128)(2,1)S(1)} %copy-done.1), custom_call_target="tpu_custom_call" | custom-call | flops 1000000000 | bytes 4000000 | tf_op jit(solution)/shard_map/smooth/pallas_call | solution.py:330
  32.8 7.3 %interior.1 = (f32[4,64,512]{2,1,0:T(8,128)S(1)}, f32[24,80,512]{2,1,0:T(8,128)S(1)}) custom-call(f32[4]{0:T(128)S(1)} %add_convert_fusion.flags, f32[32,80,512]{2,1,0:T(8,128)S(1)} %smooth.1.plane), custom_call_target="tpu_custom_call" | custom-call | flops 1000000000 | bytes 4000000 | tf_op jit(solution)/shard_map/interior/pallas_call | solution.py:347
  40.1 3.1 %first_edge.1.behind = f32[4,64,512]{2,1,0:T(8,128)S(1)} custom-call(f32[4]{0:T(128)S(1)} %add_convert_fusion.flags, s32[2]{0:T(128)S(1)} %pad_add_fusion.order, f32[32,80,512]{2,1,0:T(8,128)S(1)} %smooth.1.plane, f32[24,80,512]{2,1,0:T(8,128)S(1)} %get-tuple-element.17.smoothed, s32[5,16,512]{2,1,0:T(8,128)S(1)} %collective-permute-done.4.edge, ...), custom_call_target="tpu_custom_call" | custom-call | flops 300000000 | bytes 4000000 | tf_op jit(solution)/shard_map/first_edge/pallas_call | solution.py:364
  43.2 3.0 %last_edge.1 = (f32[4,32,512]{2,1,0:T(8,128)S(1)}, f32[7,80,512]{2,1,0:T(8,128)S(1)}) custom-call(f32[4]{0:T(128)S(1)} %add_convert_fusion.flags, s32[2]{0:T(128)S(1)} %pad_add_fusion.order, f32[32,80,512]{2,1,0:T(8,128)S(1)} %smooth.1.plane, f32[24,80,512]{2,1,0:T(8,128)S(1)} %get-tuple-element.17.smoothed, s32[5,16,512]{2,1,0:T(8,128)S(1)} %collective-permute-done.2.edge, ...), custom_call_target="tpu_custom_call" | custom-call | flops 300000000 | bytes 4000000 | tf_op jit(solution)/shard_map/last_edge/pallas_call | solution.py:383
  46.1 0.4 collective-permute-start.8
  46.5 1.2 %kept_edge.1 = f32[4,32,512]{2,1,0:T(8,128)S(1)} custom-call(s32[2]{0:T(128)S(1)} %pad_add_fusion.order, f32[7,80,512]{2,1,0:T(8,128)S(1)} %get-tuple-element.23.ends, f32[4,64,512]{2,1,0:T(8,128)S(1)} %first_edge.1.behind), custom_call_target="tpu_custom_call" | custom-call | flops 200000000 | bytes 4000000 | tf_op jit(solution)/shard_map/kept_edge/pallas_call | solution.py:400
  47.7 7.0 %collective-permute-done.8 = f32[4,4,8,512]{3,2,1,0:T(8,128)S(1)} collective-permute-done((f32[4,4,8,512]{3,2,1,0:T(8,128)S(1)}, f32[4,4,8,512]{3,2,1,0:T(8,128)S(1)}, u32[]{:S(2)}, u32[]{:S(2)}) %collective-permute-start.8) | collective-permute-done | bytes 262176 | tf_op jit(solution)/shard_map/ppermute | solution.py:416
  54.9 2.7 %collective-permute-start.10 = (f32[4,8,512]{2,1,0:T(8,128)S(1)}, f32[4,8,512]{2,1,0:T(8,128)S(1)}, u32[]{:S(2)}, u32[]{:S(2)}) collective-permute-start(f32[4,8,512]{2,1,0:T(8,128)S(1)} %get-tuple-element.34), channel_id=1, source_target_pairs={{0,4},{1,5},{2,6},{3,7},{4,0},{5,1},{6,2},{7,3},{8,12},{9,13},{10,... | collective-permute-start | bytes 196616 | tf_op jit(solution)/shard_map/ppermute | solution.py:447
  57.5 1.3 %collective-permute-start.11 = (f32[4,8,512]{2,1,0:T(8,128)S(1)}, f32[4,8,512]{2,1,0:T(8,128)S(1)}, u32[]{:S(2)}, u32[]{:S(2)}) collective-permute-start(f32[4,8,512]{2,1,0:T(8,128)S(1)} %get-tuple-element.33), channel_id=1, source_target_pairs={{0,6},{1,7},{2,4},{3,5},{4,2},{5,3},{6,0},{7,1},{8,14},{9,15},{10,... | collective-permute-start | bytes 196616 | tf_op jit(solution)/shard_map/ppermute | solution.py:447
  58.9 3.0 %collective-permute-done.10 = f32[4,8,512]{2,1,0:T(8,128)S(1)} collective-permute-done((f32[4,8,512]{2,1,0:T(8,128)S(1)}, f32[4,8,512]{2,1,0:T(8,128)S(1)}, u32[]{:S(2)}, u32[]{:S(2)}) %collective-permute-start.10) | collective-permute-done | bytes 65568 | tf_op jit(solution)/shard_map/ppermute | solution.py:447
  61.9 1.8 %collective-permute-done.11 = f32[4,8,512]{2,1,0:T(8,128)S(1)} collective-permute-done((f32[4,8,512]{2,1,0:T(8,128)S(1)}, f32[4,8,512]{2,1,0:T(8,128)S(1)}, u32[]{:S(2)}, u32[]{:S(2)}) %collective-permute-start.11) | collective-permute-done | bytes 65568 | tf_op jit(solution)/shard_map/ppermute | solution.py:447
  63.7 0.1 collective-permute-done.9
  63.9 0.6 pad_maximum_fusion.2
  (28 shorter events, 0.6 us)
Async XLA Ops:
  0.0 26.3 %copy-start = (bf16[1024,512]{1,0:T(8,128)(2,1)S(1)}, bf16[1024,512]{1,0:T(8,128)(2,1)}, u32[]{:S(2)}) copy-start(bf16[1024,512]{1,0:T(8,128)(2,1)} %constant.73.clone.by) | copy-start | bytes 3145732
  0.0 26.3 %copy-start.1 = (bf16[2,80,240]{2,1,0:T(8,128)(2,1)S(1)}, bf16[2,80,240]{2,1,0:T(8,128)(2,1)}, u32[]{:S(2)}) copy-start(bf16[2,80,240]{2,1,0:T(8,128)(2,1)} %constant.74.clone.lx) | copy-start | bytes 230404
  3.5 4.5 %copy-start.2 = (s32[5,48,512]{2,1,0:T(8,128)}, s32[5,48,512]{2,1,0:T(8,128)S(1)}, u32[]{:S(2)}) copy-start(s32[5,48,512]{2,1,0:T(8,128)S(1)} %get-tuple-element.19) | copy-start | bytes 1474564
  3.5 10.0 %collective-permute-start.2 = (s32[5,16,512]{2,1,0:T(8,128)S(1)}, s32[5,16,512]{2,1,0:T(8,128)S(1)}, u32[]{:S(2)}, u32[]{:S(2)}) collective-permute-start(s32[5,16,512]{2,1,0:T(8,128)S(1)} %get-tuple-element.18), channel_id=1, source_target_pairs={{0,1},{1,0},{2,3},{3,2},{4,5},{5,4},{6,7},{7,6},{8,9},{9,8},{10,11... | collective-permute-start | bytes 491528 | tf_op jit(solution)/shard_map/ppermute | solution.py:416
  6.5 9.5 %collective-permute-start.4 = (s32[5,16,512]{2,1,0:T(8,128)S(1)}, s32[5,16,512]{2,1,0:T(8,128)S(1)}, u32[]{:S(2)}, u32[]{:S(2)}) collective-permute-start(s32[5,16,512]{2,1,0:T(8,128)S(1)} %get-tuple-element.20), channel_id=1, source_target_pairs={{1,2},{2,1},{3,4},{4,3},{5,6},{6,5},{9,10},{10,9},{11,12},{12,11},... | collective-permute-start | bytes 491528 | tf_op jit(solution)/shard_map/ppermute | solution.py:416
  7.2 19.1 %collective-permute-start = (s32[32,8,512]{2,1,0:T(8,128)}, s32[32,8,512]{2,1,0:T(8,128)S(1)}, u32[]{:S(2)}, u32[]{:S(2)}) collective-permute-start(s32[32,8,512]{2,1,0:T(8,128)} %get-tuple-element.15), channel_id=1, source_target_pairs={{0,8},{8,0},{16,24},{24,16},{1,9},{9,1},{17,25},{25,17},{2,10},{10... | collective-permute-start | bytes 1572872 | tf_op jit(solution)/shard_map/ppermute | solution.py:416
  7.3 19.0 %collective-permute-start.1 = (s32[32,8,512]{2,1,0:T(8,128)}, s32[32,8,512]{2,1,0:T(8,128)S(1)}, u32[]{:S(2)}, u32[]{:S(2)}) collective-permute-start(s32[32,8,512]{2,1,0:T(8,128)} %get-tuple-element.16), channel_id=1, source_target_pairs={{8,16},{16,8},{9,17},{17,9},{10,18},{18,10},{11,19},{19,11},{12,20... | collective-permute-start | bytes 1572872 | tf_op jit(solution)/shard_map/ppermute | solution.py:416
  8.0 32.1 %collective-permute-start.7 = (s32[5,48,512]{2,1,0:T(8,128)}, s32[5,48,512]{2,1,0:T(8,128)S(1)}, u32[]{:S(2)}, u32[]{:S(2)}) collective-permute-start(s32[5,48,512]{2,1,0:T(8,128)} %get-tuple-element.21), channel_id=1, source_target_pairs={{1,2},{2,1},{3,4},{4,3},{5,6},{6,5},{9,10},{10,9},{11,12},{12,11},... | collective-permute-start | bytes 1474568 | tf_op jit(solution)/shard_map/ppermute | solution.py:416
  13.5 29.6 %collective-permute-start.3 = (s32[5,48,512]{2,1,0:T(8,128)}, s32[5,48,512]{2,1,0:T(8,128)}, u32[]{:S(2)}, u32[]{:S(2)}) collective-permute-start(s32[5,48,512]{2,1,0:T(8,128)} %copy-done.2), channel_id=1, source_target_pairs={{0,1},{1,0},{2,3},{3,2},{4,5},{5,4},{6,7},{7,6},{8,9},{9,8},{10,11... | collective-permute-start | bytes 1474568 | tf_op jit(solution)/shard_map/ppermute | solution.py:416
  16.8 0.8 %collective-permute-start.6 = (s32[10,8,512]{2,1,0:T(8,128)}, s32[10,8,512]{2,1,0:T(8,128)S(1)}, u32[]{:S(2)}, u32[]{:S(2)}) collective-permute-start(s32[10,8,512]{2,1,0:T(8,128)} %get-tuple-element.30), channel_id=1, source_target_pairs={{8,16},{16,8},{9,17},{17,9},{10,18},{18,10},{11,19},{19,11},{12,20... | collective-permute-start | bytes 491528 | tf_op jit(solution)/shard_map/ppermute | solution.py:416
  17.6 8.6 %collective-permute-start.5 = (s32[10,8,512]{2,1,0:T(8,128)}, s32[10,8,512]{2,1,0:T(8,128)S(1)}, u32[]{:S(2)}, u32[]{:S(2)}) collective-permute-start(s32[10,8,512]{2,1,0:T(8,128)} %get-tuple-element.31), channel_id=1, source_target_pairs={{0,8},{8,0},{16,24},{24,16},{1,9},{9,1},{17,25},{25,17},{2,10},{10... | collective-permute-start | bytes 491528 | tf_op jit(solution)/shard_map/ppermute | solution.py:416
  46.1 8.6 %collective-permute-start.8 = (f32[4,4,8,512]{3,2,1,0:T(8,128)S(1)}, f32[4,4,8,512]{3,2,1,0:T(8,128)S(1)}, u32[]{:S(2)}, u32[]{:S(2)}) collective-permute-start(f32[4,4,8,512]{3,2,1,0:T(8,128)S(1)} %bitcast.63), channel_id=1, source_target_pairs={{0,1},{1,0},{2,3},{3,2},{4,5},{5,4},{6,7},{7,6},{8,9},{9,8},{10,11... | collective-permute-start | bytes 786440 | tf_op jit(solution)/shard_map/ppermute | solution.py:416
  54.9 7.1 %collective-permute-start.10 = (f32[4,8,512]{2,1,0:T(8,128)S(1)}, f32[4,8,512]{2,1,0:T(8,128)S(1)}, u32[]{:S(2)}, u32[]{:S(2)}) collective-permute-start(f32[4,8,512]{2,1,0:T(8,128)S(1)} %get-tuple-element.34), channel_id=1, source_target_pairs={{0,4},{1,5},{2,6},{3,7},{4,0},{5,1},{6,2},{7,3},{8,12},{9,13},{10,... | collective-permute-start | bytes 196616 | tf_op jit(solution)/shard_map/ppermute | solution.py:447
  57.5 6.2 %collective-permute-start.11 = (f32[4,8,512]{2,1,0:T(8,128)S(1)}, f32[4,8,512]{2,1,0:T(8,128)S(1)}, u32[]{:S(2)}, u32[]{:S(2)}) collective-permute-start(f32[4,8,512]{2,1,0:T(8,128)S(1)} %get-tuple-element.33), channel_id=1, source_target_pairs={{0,6},{1,7},{2,4},{3,5},{4,2},{5,3},{6,0},{7,1},{8,14},{9,15},{10,... | collective-permute-start | bytes 196616 | tf_op jit(solution)/shard_map/ppermute | solution.py:447
  58.9 5.0 %collective-permute-start.9 = (f32[4,8,512]{2,1,0:T(8,128)S(1)}, f32[4,8,512]{2,1,0:T(8,128)S(1)}, u32[]{:S(2)}, u32[]{:S(2)}) collective-permute-start(f32[4,8,512]{2,1,0:T(8,128)S(1)} %get-tuple-element.32), channel_id=1, source_target_pairs={{0,2},{1,3},{2,0},{3,1},{4,6},{5,7},{6,4},{7,5},{8,10},{9,11},{10,... | collective-permute-start | bytes 196616 | tf_op jit(solution)/shard_map/ppermute | solution.py:447

commit v8 on v7

--- a/solution.py
+++ b/solution.py
@@ -21,6 +21,7 @@
 
 
 REACH = 5
+BLOCK = 256
 PAD = 8
 
 
@@ -37,8 +38,14 @@
     return high, low
 
 
-def column_matrix(columns):
-    return np.concatenate(split_terms(band(columns)), 0)
+def column_matrices():
+    full = band(2 * BLOCK)
+    inside = full[:BLOCK, :BLOCK]
+    half = BLOCK // 2
+    across = full[half : 3 * half, half : 3 * half].copy()
+    across[:half, :half] = 0.0
+    across[half:, half:] = 0.0
+    return np.concatenate([*split_terms(inside), *split_terms(across)], 0)
 
 
 def row_matrices(rows):
@@ -51,13 +58,34 @@
     return np.stack(both)
 
 
+def two_terms(value, high, low):
+    return jnp.dot(value, high, preferred_element_type=jnp.float32) + jnp.dot(
+        value, low, preferred_element_type=jnp.float32
+    )
+
+
+def smooth_columns(exact, by):
+    rows, columns = exact.shape
+    half = BLOCK // 2
+    starts = range(0, columns, BLOCK)
+    stacked = jnp.concatenate([exact[:, at : at + BLOCK] for at in starts], 0)
+    inside = two_terms(stacked, by[:BLOCK], by[BLOCK : 2 * BLOCK])
+    parts = []
+    for n in range(len(starts)):
+        block = inside[n * rows : (n + 1) * rows]
+        parts += [block[:, :half], block[:, half:]]
+    for n, at in enumerate(starts[1:]):
+        window = exact[:, at - half : at + half]
+        across = two_terms(window, by[2 * BLOCK : 3 * BLOCK], by[3 * BLOCK :])
+        parts[2 * n + 1] = parts[2 * n + 1] + across[:, :half]
+        parts[2 * n + 2] = parts[2 * n + 2] + across[:, half:]
+    return jnp.concatenate(parts, 1)
+
+
 def smooth_plane(counts, by, lx):
     rows = counts[0].shape[0]
     exact = jnp.concatenate([c.astype(jnp.float32).astype(jnp.bfloat16) for c in counts], 0)
-    half = by.shape[0] // 2
-    wide = jnp.dot(exact, by[:half], preferred_element_type=jnp.float32) + jnp.dot(
-        exact, by[half:], preferred_element_type=jnp.float32
-    )
+    wide = smooth_columns(exact, by)
     high = wide.astype(jnp.bfloat16)
     low = (wide - high.astype(jnp.float32)).astype(jnp.bfloat16)
     planes = []
@@ -86,27 +114,23 @@
         write(rows, value)
 
 
-def shade_voxels(prev, mid, above, below, following, scale):
-    columns = mid.shape[1]
-    lane = lax.broadcasted_iota(jnp.int32, mid.shape, 1)
-    right = jnp.where(lane == columns - 1, 0.0, pltpu.roll(mid, columns - 1, 1))
-    left = jnp.where(lane == 0, 0.0, pltpu.roll(mid, 1, 1))
-    dz = following - prev
-    dx = below - above
-    dy = right - left
-    slope = (1.5 * light_z) * dz + (1.5 * light_x) * dx + (1.5 * light_y) * dy
-    shading = 0.55 + 0.45 * jnp.tanh(slope)
-    gradient_sq4 = dz * dz + dx * dx + dy * dy
-    square = mid * mid
-    optical = scale * (square / (1.0 + square)) * (1.0 + gradient_sq4)
-    centred = mid - 2.5
-    red_share = 0.5 + 0.5 * jnp.tanh(centred)
-    green_share = jnp.exp(-(centred * centred))
-    return optical, shading, red_share, green_share
+def beside(mid, step):
+    lanes = 128
+    lane = lax.broadcasted_iota(jnp.int32, (mid.shape[0], lanes), 1)
+    parts = [mid[:, at : at + lanes] for at in range(0, mid.shape[1], lanes)]
+    turned = [pltpu.roll(part, lanes - 1 if step == 1 else 1, 1) for part in parts]
+    zero = jnp.zeros_like(parts[0])
+    if step == 1:
+        return jnp.concatenate(
+            [jnp.where(lane == lanes - 1, y, x) for x, y in zip(turned, turned[1:] + [zero])], 1
+        )
+    return jnp.concatenate(
+        [jnp.where(lane == 0, y, x) for x, y in zip(turned, [zero] + turned[:-1])], 1
+    )
 
 
 def render_layer(layer, k, base, carry, scale):
-    red, green, blue, transmit = carry
+    total, tilted, green, transmit = carry
     rows = pl.ds(base, 8)
     mid = layer(k, rows)
     before = layer(k, pl.ds(base - 8, 8))
@@ -114,13 +138,24 @@
     sub = lax.broadcasted_iota(jnp.int32, mid.shape, 0)
     above = pltpu.roll(jnp.where(sub == 7, before, mid), 1, 0)
     below = pltpu.roll(jnp.where(sub == 0, after, mid), 7, 0)
-    optical, shading, red_share, green_share = shade_voxels(
-        layer(k - 1, rows), mid, above, below, layer(k + 1, rows), scale
+    dz = layer(k + 1, rows) - layer(k - 1, rows)
+    dx = below - above
+    dy = beside(mid, 1) - beside(mid, -1)
+    slope = (1.5 * light_z) * dz + (1.5 * light_x) * dx + (1.5 * light_y) * dy
+    shading = jnp.tanh(slope) + (0.55 / 0.45)
+    gradient_sq4 = dz * dz + dx * dx + dy * dy
+    square = mid * mid
+    optical = (square / (1.0 + square)) * (1.0 + gradient_sq4)
+    centred = mid - 2.5
+    log2e = math.log2(math.e)
+    remaining = transmit * jnp.exp2(optical * (-scale * log2e))
+    lit = (transmit - remaining) * shading
+    return (
+        total + lit,
+        tilted + lit * jnp.tanh(centred),
+        green + lit * jnp.exp2((centred * -log2e) * centred),
+        remaining,
     )
-    remaining = transmit * jnp.exp(-optical)
-    lit = (transmit - remaining) * shading
-    red_part = lit * red_share
-    return red + red_part, green + lit * green_share, blue + (lit - red_part), remaining
 
 
 def empty_carry(columns):
@@ -139,24 +174,39 @@
         ref[n, rows, :] = value
 
 
-def pack_kernel(where, c, edge_a, side_b, edge_b, side_a, middle_a, middle_b, sems):
-    rows = c.shape[1]
-    copies = []
-
-    def add(source, target):
-        copies.append(pltpu.make_async_copy(source, target, sems.at[len(copies)]))
-
-    blocks = ((edge_a, side_a, middle_a), (edge_b, side_b, middle_b))
-    for n, (edge, side, middle) in enumerate(blocks):
-        layers = pl.ds(where[n], REACH)
-        add(c.at[layers, pl.ds(0, PAD)], edge.at[:, pl.ds(0, PAD)])
-        add(c.at[layers, pl.ds(rows - PAD, PAD)], edge.at[:, pl.ds(PAD, PAD)])
-        add(c.at[:, pl.ds(pl.multiple_of(where[2 + n], PAD), PAD)], side)
-        add(c.at[layers, pl.ds(PAD, rows - 2 * PAD)], middle)
+def run_copies(copies):
     for copy in copies:
         copy.start()
     for copy in copies:
         copy.wait()
+
+
+def run_copies(pairs, sems):
+    copies = [pltpu.make_async_copy(*pair, sems.at[n]) for n, pair in enumerate(pairs)]
+    for copy in copies:
+        copy.start()
+    for copy in copies:
+        copy.wait()
+
+
+def pack_block_kernel(where, c, block, sems):
+    half = block.shape[1] // 2
+    layers = pl.ds(where[1], REACH)
+    parts = [pl.ds(n * half, half) for n in range(2)]
+    run_copies([(c.at[layers, part], block.at[:, part]) for part in parts], sems)
+
+
+def pack_rest_kernel(where, c, side_b, edge, middle, side_a, sems):
+    rows = c.shape[1]
+    layers = pl.ds(where[0], REACH)
+    pairs = [
+        (c.at[:, pl.ds(pl.multiple_of(where[2 + n], PAD), PAD)], side)
+        for n, side in enumerate((side_a, side_b))
+    ]
+    pairs.append((c.at[layers, pl.ds(0, PAD)], edge.at[:, pl.ds(0, PAD)]))
+    pairs.append((c.at[layers, pl.ds(rows - PAD, PAD)], edge.at[:, pl.ds(PAD, PAD)]))
+    pairs.append((c.at[layers, pl.ds(PAD, rows - 2 * PAD)], middle))
+    run_copies(pairs, sems)
 
 
 def smooth_kernel(group, order, c_hbm, xa, xb, by, lx, plane, c, sems):
@@ -206,15 +256,12 @@
     lax.fori_loop(0, ext // 8 - 2, one_tile, 0)
 
 
-def edge_smooth(turn, flags, order, plane, smoothed, edge, middle, ca, cb, by, lx, ends, halo):
+def edge_smooth(turn, flags, order, plane, smoothed, tile, ca, cb, by, lx, ends, halo):
     layers, ext, _ = plane.shape
     rows_of = order[0]
     is_front = order[1] == 1 - turn
     sign = jnp.where(is_front, 1, -1)
-    counts = [
-        jnp.concatenate([ca[j], edge[j, :PAD], middle[j], edge[j, PAD:], cb[j]], 0)
-        for j in range(REACH)
-    ]
+    counts = [jnp.concatenate([ca[j], tile(j), cb[j]], 0) for j in range(REACH)]
     for j, value in enumerate(smooth_plane(counts, by, lx[rows_of])):
         halo[j] = value
     plane_face = jnp.where(is_front, 0, layers - 1)
@@ -264,16 +311,19 @@
     return tile_of
 
 
-def first_edge_kernel(scale, flags, order, plane, smoothed, edge, middle, ca, cb, by, lx, behind,
-                      image, ends, halo):
-    edge_smooth(1, flags, order, plane, smoothed, edge, middle, ca, cb, by, lx, ends, halo)
+def first_edge_kernel(scale, flags, order, plane, smoothed, block, ca, cb, by, lx, behind, image,
+                      ends, halo):
+    tile = lambda j: block[j]
+    edge_smooth(1, flags, order, plane, smoothed, tile, ca, cb, by, lx, ends, halo)
     tiles = plane.shape[1] // 8 - 2
     edge_render(scale, order[1] == 0, ends, behind, image, tiles, lambda place: place)
 
 
-def last_edge_kernel(scale, owner_tiles, flags, order, plane, smoothed, edge, middle, ca, cb, by,
-                     lx, behind, image, ends, halo):
-    edge_smooth(0, flags, order, plane, smoothed, edge, middle, ca, cb, by, lx, ends, halo)
+def last_edge_kernel(scale, owner_tiles, flags, order, plane, smoothed, middle_any, edge, ca, cb,
+                     by, lx, behind, image, ends, halo, middle, sem):
+    run_copies([(middle_any, middle)], sem)
+    tile = lambda j: jnp.concatenate([edge[j, :PAD], middle[j], edge[j, PAD:]], 0)
+    edge_smooth(0, flags, order, plane, smoothed, tile, ca, cb, by, lx, ends, halo)
     tiles = plane.shape[1] // 8 - 2
     tile_of = lambda place: place
     if owner_tiles:
@@ -307,19 +357,32 @@
     return pl.CostEstimate(flops=flops, transcendentals=0, bytes_accessed=4_000_000)
 
 
-def call_pack(where, c):
+def call_pack_block(where, c):
+    _, rows, columns = c.shape
+    return pl.pallas_call(
+        pack_block_kernel,
+        out_shape=jax.ShapeDtypeStruct((REACH, rows, columns), c.dtype),
+        in_specs=[smem(), in_hbm()],
+        out_specs=whole(1)[0],
+        scratch_shapes=[pltpu.SemaphoreType.DMA((2,))],
+        compiler_params=params(8),
+        name="pack_block",
+    )(where, c)
+
+
+def call_pack_rest(where, c):
     layers, rows, columns = c.shape
-    edge = pltpu.VMEM((REACH, 2 * PAD, columns), c.dtype)
-    side = pltpu.VMEM((layers, PAD, columns), c.dtype)
-    middle = pltpu.VMEM((REACH, rows - 2 * PAD, columns), c.dtype)
-    return pl.pallas_call(
-        pack_kernel,
-        out_shape=(edge, side, edge, side, middle, middle),
+    edge = jax.ShapeDtypeStruct((REACH, 2 * PAD, columns), c.dtype)
+    side = jax.ShapeDtypeStruct((layers, PAD, columns), c.dtype)
+    middle = jax.ShapeDtypeStruct((REACH, rows - 2 * PAD, columns), c.dtype)
+    return pl.pallas_call(
+        pack_rest_kernel,
+        out_shape=(side, edge, middle, side),
         in_specs=[smem(), in_hbm()],
-        out_specs=tuple(whole(6)),
-        scratch_shapes=[pltpu.SemaphoreType.DMA((8,))],
+        out_specs=tuple(whole(4)),
+        scratch_shapes=[pltpu.SemaphoreType.DMA((5,))],
         compiler_params=params(8),
-        name="pack",
+        name="pack_rest",
     )(where, c)
 
 
@@ -386,9 +449,16 @@
             jax.ShapeDtypeStruct((4, rows, columns), f32),
             jax.ShapeDtypeStruct((REACH + 2, ext, columns), f32),
         ),
-        in_specs=[smem(), smem()] + whole(1 + len(operands)),
+        in_specs=[smem(), smem()]
+        + whole(2)
+        + [in_hbm()]
+        + whole(len(operands) - 2),
         out_specs=tuple(whole(2)),
-        scratch_shapes=[pltpu.VMEM((REACH, ext, columns), f32)],
+        scratch_shapes=[
+            pltpu.VMEM((REACH, ext, columns), f32),
+            pltpu.VMEM(operands[1].shape, operands[1].dtype),
+            pltpu.SemaphoreType.DMA((1,)),
+        ],
         compiler_params=params(24),
         cost_estimate=cost(300_000_000),
         name="last_edge",
@@ -456,11 +526,12 @@
                 ahead = ahead * jnp.where(nearer, parts[other][3:], 1.0)
         result = result + ahead * parts[step][:3]
         through = through * parts[step][3:]
-    return jnp.concatenate([result, 1.0 - through], 0)
+    total, tilted, green = 0.225 * result[:1], 0.225 * result[1:2], 0.45 * result[2:]
+    return jnp.concatenate([total + tilted, green, total - tilted, 1.0 - through], 0)
 
 
 def local(counts):
-    slab, rows, columns = counts.shape
+    slab, rows, _ = counts.shape
     img, depth = lax.axis_index("img"), lax.axis_index("depth")
     imgs, depths = lax.axis_size("img"), lax.axis_size("depth")
     scale = 1.5 / (slab * depths)
@@ -473,31 +544,35 @@
     flags = jnp.stack(
         [(img > 0) * one, (img < imgs - 1) * one, (depth > 0) * one, (depth < depths - 1) * one]
     )
-    by = jnp.asarray(column_matrix(columns))
+    by = jnp.asarray(column_matrices())
     lx = jnp.asarray(row_matrices(rows))
     held = pltpu.with_memory_space_constraint(counts, pltpu.HBM)
-    edge_a, side_b, edge_b, side_a, mid_a, mid_b = call_pack(where, held)
+    block_b = call_pack_block(where, held)
+    side_b, edge_a, mid_a, side_a = call_pack_rest(where, held)
+    block_b = swap(block_b, "depth", 1)
+    xb = swap(side_b, "img", 1)
     edge_a = swap(edge_a, "depth", 0)
-    edge_b = swap(edge_b, "depth", 1)
+    mid_a = swap(mid_a, "depth", 0)
     xa = swap(side_a, "img", 0)
-    xb = swap(side_b, "img", 1)
-    mid_a = swap(mid_a, "depth", 0)
-    mid_b = swap(mid_b, "depth", 1)
-    halves = jnp.concatenate([edge_a, edge_b], 0).reshape(2 * REACH, 2, PAD, columns)
-    corner_a = lax.dynamic_index_in_dim(halves, 1 - row_odd, 1, keepdims=False)
-    corner_b = lax.dynamic_index_in_dim(halves, row_odd, 1, keepdims=False)
-    ca = swap(corner_a, "img", 0)
-    cb = swap(corner_b, "img", 1)
+
+    def corner(far):
+        of_a = lax.dynamic_slice_in_dim(edge_a, far * PAD, PAD, 1)
+        of_b = lax.dynamic_slice_in_dim(block_b, far * (rows - PAD), PAD, 1)
+        return jnp.concatenate([of_a, of_b], 0)
+
+    ca = swap(corner(1 - row_odd), "img", 0)
+    cb = swap(corner(row_odd), "img", 1)
     plane = call_smooth(order, held, xa, xb, by, lx)
     inner, smoothed = call_interior(scale, flags, plane)
     owned = rows // depths
     owner_tiles = owned // 8 if owned % 8 == 0 else 0
     common = (flags, order, plane, smoothed)
     layers = call_first_edge(
-        scale, *common, edge_b, mid_b, ca[REACH:], cb[REACH:], by, lx, inner
+        scale, *common, block_b, ca[REACH:], cb[REACH:], by, lx, inner
     )
     send, ends = call_last_edge(
-        scale, owner_tiles, *common, edge_a, mid_a, ca[:REACH], cb[:REACH], by, lx, layers
+        scale, owner_tiles, *common, pltpu.with_memory_space_constraint(mid_a, pltpu.HBM), edge_a,
+        ca[:REACH], cb[:REACH], by, lx, layers
     )
     if owner_tiles:
         keep = call_kept_edge(scale, owner_tiles, order, ends, layers)

time: 64.8 us -> 70.1 us (1.082)
  waiting for transfers between devices: 18.1 us -> 23.2 us
  Pallas kernels: 24.4 us -> 26.4 us
  starting transfers between devices: 20 us -> 18.9 us
  local copies, waits for them, and re-layouts: 0.83 us -> 0.09 us
    ppermute x9 -> x8, waiting for transfers between devices: 13.1 us -> 18.6 us  [swap(): return lax.ppermute(value, axis, pairs)]
    ppermute x9 -> x8, starting transfers between devices: 16 us -> 14.3 us  [swap(): return lax.ppermute(value, axis, pairs)]
    pallas_call x1 -> x2, Pallas kernels: 3.39 us -> 4.78 us  [the longest x1 3.14 us: call_pack_rest(): pl.pallas_call(pack_rest_kernel, out_shape=(side, edge, middle, side), in...]
    pallas_call x1, Pallas kernels: 6.45 us -> 7.28 us  [call_smooth(): pl.pallas_call(functools.partial(smooth_kernel, group), out_shape=jax.Sha...]
    squeeze x1 -> x0, local copies, waits for them, and re-layouts: 0.77 us -> none  [local(): corner_b = lax.dynamic_index_in_dim(halves, row_odd, 1, keepdims=False)]
  transfers between devices with their start and end apart: 12 -> 11, of which waited for: 6 -> 6; matrix products, arithmetic and copies ran while one was open for 2% -> 0% of each run, Pallas kernels for 28% -> 30%
where the time goes in v8:
time: 70.1 us; the launch traced here: 69.9 us
  Pallas kernels  26.4 us (38%)
  waiting for transfers between devices  23.2 us (33%)
  starting transfers between devices  18.9 us (27%)
  other arithmetic  1.06 us (2%)
    ppermute x8, waiting for transfers between devices, swap(): return lax.ppermute(value, axis, pairs)  18.6 us
    ppermute x8, starting transfers between devices, swap(): return lax.ppermute(value, axis, pairs)  14.3 us
    pallas_call x1, Pallas kernels, call_smooth(): pl.pallas_call(functools.partial(smooth_kernel, group), out_shape=jax.Sha...  7.28 us
    pallas_call x1, Pallas kernels, call_interior(): pl.pallas_call(functools.partial(interior_kernel, scale), out_shape=(jax....  6.79 us
    ppermute x3, waiting for transfers between devices, exchange(): lax.ppermute(piece, 'depth', [(i, i ^ 2 * step) for i in range(count)])  4.66 us
    ppermute x3, starting transfers between devices, exchange(): lax.ppermute(piece, 'depth', [(i, i ^ 2 * step) for i in range(count)])  4.56 us
    pallas_call x1, Pallas kernels, call_last_edge(): pl.pallas_call(functools.partial(last_edge_kernel, scale, owner_tiles), o...  3.43 us
    pallas_call x1, Pallas kernels, call_pack_rest(): pl.pallas_call(pack_rest_kernel, out_shape=(side, edge, middle, side), in...  3.14 us
  transfers between devices with their start and end apart: 11, of which 6 were waited for; matrix products, arithmetic and copies ran while one was open for 0% of the time, Pallas kernels for 30%

profile of v8, /device:TPU:0, one launch (start us, length us, event | category | flops | bytes accessed | tf_op | source)
XLA Modules:
  0.0 69.9 jit_solution(18433394134170240781)
XLA Ops:
  0.1 1.6 %pack_block.1 = s32[5,64,512]{2,1,0:T(8,128)S(1)} custom-call(s32[4]{0:T(128)S(1)} %pad_add_fusion.3.where, s32[32,64,512]{2,1,0:T(8,128)} %c.3), custom_call_target="tpu_custom_call" | custom-call | tf_op jit(solution)/shard_map/pack_block/pallas_call | solution.py:362
  1.7 0.7 %collective-permute-start.4 = (s32[5,64,512]{2,1,0:T(8,128)S(1)}, s32[5,64,512]{2,1,0:T(8,128)S(1)}, u32[]{:S(2)}, u32[]{:S(2)}) collective-permute-start(s32[5,64,512]{2,1,0:T(8,128)S(1)} %pack_block.1), channel_id=1, source_target_pairs={{1,2},{2,1},{3,4},{4,3},{5,6},{6,5},{9,10},{10,9},{11,12},{12,11},... | collective-permute-start | bytes 1966088 | tf_op jit(solution)/shard_map/ppermute | solution.py:486
  2.4 3.1 %pack_rest.1 = (s32[32,8,512]{2,1,0:T(8,128)}, s32[5,16,512]{2,1,0:T(8,128)S(1)}, s32[5,48,512]{2,1,0:T(8,128)}, s32[32,8,512]{2,1,0:T(8,128)}) custom-call(s32[4]{0:T(128)S(1)} %pad_add_fusion.3.where, s32[32,64,512]{2,1,0:T(8,128)} %c.3), custom_call_target="tpu_custom_call" | custom-call | tf_op jit(solution)/shard_map/pack_rest/pallas_call | solution.py:378
  5.6 0.6 collective-permute-start
  6.1 1.5 %collective-permute-start.1 = (s32[32,8,512]{2,1,0:T(8,128)}, s32[32,8,512]{2,1,0:T(8,128)}, u32[]{:S(2)}, u32[]{:S(2)}) collective-permute-start(s32[32,8,512]{2,1,0:T(8,128)} %get-tuple-element.14), channel_id=1, source_target_pairs={{8,16},{16,8},{9,17},{17,9},{10,18},{18,10},{11,19},{19,11},{12,20... | collective-permute-start | bytes 1572872 | tf_op jit(solution)/shard_map/ppermute | solution.py:486
  7.6 5.3 %collective-permute-start.3 = (s32[5,16,512]{2,1,0:T(8,128)S(1)}, s32[5,16,512]{2,1,0:T(8,128)S(1)}, u32[]{:S(2)}, u32[]{:S(2)}) collective-permute-start(s32[5,16,512]{2,1,0:T(8,128)S(1)} %get-tuple-element.17), channel_id=1, source_target_pairs={{0,1},{1,0},{2,3},{3,2},{4,5},{5,4},{6,7},{7,6},{8,9},{9,8},{10,11... | collective-permute-start | bytes 491528 | tf_op jit(solution)/shard_map/ppermute | solution.py:486
  13.0 0.1 add_convert_fusion.flags
  13.0 11.8 %collective-permute-done.3.edge = s32[5,16,512]{2,1,0:T(8,128)S(1)} collective-permute-done((s32[5,16,512]{2,1,0:T(8,128)S(1)}, s32[5,16,512]{2,1,0:T(8,128)S(1)}, u32[]{:S(2)}, u32[]{:S(2)}) %collective-permute-start.3) | collective-permute-done | bytes 163872 | tf_op jit(solution)/shard_map/ppermute | solution.py:486
  24.9 7.3 %smooth.1.plane = f32[32,80,512]{2,1,0:T(8,128)S(1)} custom-call(s32[2]{0:T(128)S(1)} %pad_add_fusion.2.order, s32[32,64,512]{2,1,0:T(8,128)} %c.3, s32[32,8,512]{2,1,0:T(8,128)S(1)} %collective-permute-done.xa, s32[32,8,512]{2,1,0:T(8,128)} %collective-permute-done.1.xb, bf16[1024,256]{1,0:T(8,128)(2,1)S(1)} %copy-done, bf16[2,80,240]{2,1,0:T(8,128)(2,1)S(1)} %copy-done.1), custom_call_target="tpu_custom_call" | custom-call | flops 1000000000 | bytes 4000000 | tf_op jit(solution)/shard_map/smooth/pallas_call | solution.py:393
  32.3 0.7 collective-permute-start.6
  33.0 6.8 %interior.1 = (f32[4,64,512]{2,1,0:T(8,128)S(1)}, f32[24,80,512]{2,1,0:T(8,128)S(1)}) custom-call(f32[4]{0:T(128)S(1)} %add_convert_fusion.flags, f32[32,80,512]{2,1,0:T(8,128)S(1)} %smooth.1.plane), custom_call_target="tpu_custom_call" | custom-call | flops 1000000000 | bytes 4000000 | tf_op jit(solution)/shard_map/interior/pallas_call | solution.py:410
  39.8 3.1 %collective-permute-start.5 = (s32[10,8,512]{2,1,0:T(8,128)S(1)}, s32[10,8,512]{2,1,0:T(8,128)S(1)}, u32[]{:S(2)}, u32[]{:S(2)}) collective-permute-start(s32[10,8,512]{2,1,0:T(8,128)S(1)} %pad_add_fusion), channel_id=1, source_target_pairs={{0,8},{8,0},{16,24},{24,16},{1,9},{9,1},{17,25},{25,17},{2,10},{10... | collective-permute-start | bytes 491528 | tf_op jit(solution)/shard_map/ppermute | solution.py:486
  42.9 1.0 %collective-permute-done.5 = s32[10,8,512]{2,1,0:T(8,128)S(1)} collective-permute-done((s32[10,8,512]{2,1,0:T(8,128)S(1)}, s32[10,8,512]{2,1,0:T(8,128)S(1)}, u32[]{:S(2)}, u32[]{:S(2)}) %collective-permute-start.5) | collective-permute-done | bytes 163872 | tf_op jit(solution)/shard_map/ppermute | solution.py:486
  44.0 3.0 %first_edge.1.behind = f32[4,64,512]{2,1,0:T(8,128)S(1)} custom-call(f32[4]{0:T(128)S(1)} %add_convert_fusion.flags, s32[2]{0:T(128)S(1)} %pad_add_fusion.2.order, f32[32,80,512]{2,1,0:T(8,128)S(1)} %smooth.1.plane, f32[24,80,512]{2,1,0:T(8,128)S(1)} %get-tuple-element.15.smoothed, s32[5,64,512]{2,1,0:T(8,128)S(1)} %collective-permute-done.4.block, ...), custom_call_target="tpu_custom_call" | custom-call | flops 300000000 | bytes 4000000 | tf_op jit(solution)/shard_map/first_edge/pallas_call | solution.py:427
  46.9 3.4 %last_edge.1 = (f32[4,32,512]{2,1,0:T(8,128)S(1)}, f32[7,80,512]{2,1,0:T(8,128)S(1)}) custom-call(f32[4]{0:T(128)S(1)} %add_convert_fusion.flags, s32[2]{0:T(128)S(1)} %pad_add_fusion.2.order, f32[32,80,512]{2,1,0:T(8,128)S(1)} %smooth.1.plane, f32[24,80,512]{2,1,0:T(8,128)S(1)} %get-tuple-element.15.smoothed, ...), custom_call_target="tpu_custom_call" | custom-call | flops 300000000 | bytes 4000000 | tf_op jit(solution)/shard_map/last_edge/pallas_call | solution.py:446
  50.4 2.5 %collective-permute-start.7 = (f32[4,4,8,512]{3,2,1,0:T(8,128)S(1)}, f32[4,4,8,512]{3,2,1,0:T(8,128)S(1)}, u32[]{:S(2)}, u32[]{:S(2)}) collective-permute-start(f32[4,4,8,512]{3,2,1,0:T(8,128)S(1)} %bitcast.53), channel_id=1, source_target_pairs={{0,1},{1,0},{2,3},{3,2},{4,5},{5,4},{6,7},{7,6},{8,9},{9,8},{10,11... | collective-permute-start | bytes 786440 | tf_op jit(solution)/shard_map/ppermute | solution.py:486
  52.9 1.1 %kept_edge.1 = f32[4,32,512]{2,1,0:T(8,128)S(1)} custom-call(s32[2]{0:T(128)S(1)} %pad_add_fusion.2.order, f32[7,80,512]{2,1,0:T(8,128)S(1)} %get-tuple-element.19.ends, f32[4,64,512]{2,1,0:T(8,128)S(1)} %first_edge.1.behind), custom_call_target="tpu_custom_call" | custom-call | flops 200000000 | bytes 4000000 | tf_op jit(solution)/shard_map/kept_edge/pallas_call | solution.py:470
  54.1 5.7 %collective-permute-done.7 = f32[4,4,8,512]{3,2,1,0:T(8,128)S(1)} collective-permute-done((f32[4,4,8,512]{3,2,1,0:T(8,128)S(1)}, f32[4,4,8,512]{3,2,1,0:T(8,128)S(1)}, u32[]{:S(2)}, u32[]{:S(2)}) %collective-permute-start.7) | collective-permute-done | bytes 262176 | tf_op jit(solution)/shard_map/ppermute | solution.py:486
  59.9 3.9 %collective-permute-start.10 = (f32[4,8,512]{2,1,0:T(8,128)S(1)}, f32[4,8,512]{2,1,0:T(8,128)S(1)}, u32[]{:S(2)}, u32[]{:S(2)}) collective-permute-start(f32[4,8,512]{2,1,0:T(8,128)S(1)} %get-tuple-element.29), channel_id=1, source_target_pairs={{0,6},{1,7},{2,4},{3,5},{4,2},{5,3},{6,0},{7,1},{8,14},{9,15},{10,... | collective-permute-start | bytes 196616 | tf_op jit(solution)/shard_map/ppermute | solution.py:517
  63.8 0.6 collective-permute-start.9
  64.5 1.9 %collective-permute-done.10 = f32[4,8,512]{2,1,0:T(8,128)S(1)} collective-permute-done((f32[4,8,512]{2,1,0:T(8,128)S(1)}, f32[4,8,512]{2,1,0:T(8,128)S(1)}, u32[]{:S(2)}, u32[]{:S(2)}) %collective-permute-start.10) | collective-permute-done | bytes 65568 | tf_op jit(solution)/shard_map/ppermute | solution.py:517
  66.4 1.9 %collective-permute-done.8 = f32[4,8,512]{2,1,0:T(8,128)S(1)} collective-permute-done((f32[4,8,512]{2,1,0:T(8,128)S(1)}, f32[4,8,512]{2,1,0:T(8,128)S(1)}, u32[]{:S(2)}, u32[]{:S(2)}) %collective-permute-start.8) | collective-permute-done | bytes 65568 | tf_op jit(solution)/shard_map/ppermute | solution.py:517
  68.3 0.8 %collective-permute-done.9 = f32[4,8,512]{2,1,0:T(8,128)S(1)} collective-permute-done((f32[4,8,512]{2,1,0:T(8,128)S(1)}, f32[4,8,512]{2,1,0:T(8,128)S(1)}, u32[]{:S(2)}, u32[]{:S(2)}) %collective-permute-start.9) | collective-permute-done | bytes 65568 | tf_op jit(solution)/shard_map/ppermute | solution.py:517
  69.2 0.6 pad_maximum_fusion.2
  (28 shorter events, 0.5 us)
Async XLA Ops:
  0.1 24.8 %copy-start = (bf16[1024,256]{1,0:T(8,128)(2,1)S(1)}, bf16[1024,256]{1,0:T(8,128)(2,1)}, u32[]{:S(2)}) copy-start(bf16[1024,256]{1,0:T(8,128)(2,1)} %constant.76.clone.by) | copy-start | bytes 1572868
  0.1 24.9 %copy-start.1 = (bf16[2,80,240]{2,1,0:T(8,128)(2,1)S(1)}, bf16[2,80,240]{2,1,0:T(8,128)(2,1)}, u32[]{:S(2)}) copy-start(bf16[2,80,240]{2,1,0:T(8,128)(2,1)} %constant.77.clone.lx) | copy-start | bytes 230404
  1.7 30.5 %collective-permute-start.4 = (s32[5,64,512]{2,1,0:T(8,128)S(1)}, s32[5,64,512]{2,1,0:T(8,128)S(1)}, u32[]{:S(2)}, u32[]{:S(2)}) collective-permute-start(s32[5,64,512]{2,1,0:T(8,128)S(1)} %pack_block.1), channel_id=1, source_target_pairs={{1,2},{2,1},{3,4},{4,3},{5,6},{6,5},{9,10},{10,9},{11,12},{12,11},... | collective-permute-start | bytes 1966088 | tf_op jit(solution)/shard_map/ppermute | solution.py:486
  5.6 19.3 %collective-permute-start = (s32[32,8,512]{2,1,0:T(8,128)}, s32[32,8,512]{2,1,0:T(8,128)S(1)}, u32[]{:S(2)}, u32[]{:S(2)}) collective-permute-start(s32[32,8,512]{2,1,0:T(8,128)} %get-tuple-element.13), channel_id=1, source_target_pairs={{0,8},{8,0},{16,24},{24,16},{1,9},{9,1},{17,25},{25,17},{2,10},{10... | collective-permute-start | bytes 1572872 | tf_op jit(solution)/shard_map/ppermute | solution.py:486
  6.1 18.8 %collective-permute-start.1 = (s32[32,8,512]{2,1,0:T(8,128)}, s32[32,8,512]{2,1,0:T(8,128)}, u32[]{:S(2)}, u32[]{:S(2)}) collective-permute-start(s32[32,8,512]{2,1,0:T(8,128)} %get-tuple-element.14), channel_id=1, source_target_pairs={{8,16},{16,8},{9,17},{17,9},{10,18},{18,10},{11,19},{19,11},{12,20... | collective-permute-start | bytes 1572872 | tf_op jit(solution)/shard_map/ppermute | solution.py:486
  7.6 17.3 %collective-permute-start.3 = (s32[5,16,512]{2,1,0:T(8,128)S(1)}, s32[5,16,512]{2,1,0:T(8,128)S(1)}, u32[]{:S(2)}, u32[]{:S(2)}) collective-permute-start(s32[5,16,512]{2,1,0:T(8,128)S(1)} %get-tuple-element.17), channel_id=1, source_target_pairs={{0,1},{1,0},{2,3},{3,2},{4,5},{5,4},{6,7},{7,6},{8,9},{9,8},{10,11... | collective-permute-start | bytes 491528 | tf_op jit(solution)/shard_map/ppermute | solution.py:486
  12.9 34.1 %collective-permute-start.2 = (s32[5,48,512]{2,1,0:T(8,128)}, s32[5,48,512]{2,1,0:T(8,128)}, u32[]{:S(2)}, u32[]{:S(2)}) collective-permute-start(s32[5,48,512]{2,1,0:T(8,128)} %get-tuple-element.16), channel_id=1, source_target_pairs={{0,1},{1,0},{2,3},{3,2},{4,5},{5,4},{6,7},{7,6},{8,9},{9,8},{10,11... | collective-permute-start | bytes 1474568 | tf_op jit(solution)/shard_map/ppermute | solution.py:486
  32.3 10.6 %collective-permute-start.6 = (s32[10,8,512]{2,1,0:T(8,128)S(1)}, s32[10,8,512]{2,1,0:T(8,128)S(1)}, u32[]{:S(2)}, u32[]{:S(2)}) collective-permute-start(s32[10,8,512]{2,1,0:T(8,128)S(1)} %pad_add_fusion.1), channel_id=1, source_target_pairs={{8,16},{16,8},{9,17},{17,9},{10,18},{18,10},{11,19},{19,11},{12,20... | collective-permute-start | bytes 491528 | tf_op jit(solution)/shard_map/ppermute | solution.py:486
  39.8 4.2 %collective-permute-start.5 = (s32[10,8,512]{2,1,0:T(8,128)S(1)}, s32[10,8,512]{2,1,0:T(8,128)S(1)}, u32[]{:S(2)}, u32[]{:S(2)}) collective-permute-start(s32[10,8,512]{2,1,0:T(8,128)S(1)} %pad_add_fusion), channel_id=1, source_target_pairs={{0,8},{8,0},{16,24},{24,16},{1,9},{9,1},{17,25},{25,17},{2,10},{10... | collective-permute-start | bytes 491528 | tf_op jit(solution)/shard_map/ppermute | solution.py:486
  50.4 9.4 %collective-permute-start.7 = (f32[4,4,8,512]{3,2,1,0:T(8,128)S(1)}, f32[4,4,8,512]{3,2,1,0:T(8,128)S(1)}, u32[]{:S(2)}, u32[]{:S(2)}) collective-permute-start(f32[4,4,8,512]{3,2,1,0:T(8,128)S(1)} %bitcast.53), channel_id=1, source_target_pairs={{0,1},{1,0},{2,3},{3,2},{4,5},{5,4},{6,7},{7,6},{8,9},{9,8},{10,11... | collective-permute-start | bytes 786440 | tf_op jit(solution)/shard_map/ppermute | solution.py:486
  59.9 6.5 %collective-permute-start.10 = (f32[4,8,512]{2,1,0:T(8,128)S(1)}, f32[4,8,512]{2,1,0:T(8,128)S(1)}, u32[]{:S(2)}, u32[]{:S(2)}) collective-permute-start(f32[4,8,512]{2,1,0:T(8,128)S(1)} %get-tuple-element.29), channel_id=1, source_target_pairs={{0,6},{1,7},{2,4},{3,5},{4,2},{5,3},{6,0},{7,1},{8,14},{9,15},{10,... | collective-permute-start | bytes 196616 | tf_op jit(solution)/shard_map/ppermute | solution.py:517
  63.8 4.5 %collective-permute-start.8 = (f32[4,8,512]{2,1,0:T(8,128)S(1)}, f32[4,8,512]{2,1,0:T(8,128)S(1)}, u32[]{:S(2)}, u32[]{:S(2)}) collective-permute-start(f32[4,8,512]{2,1,0:T(8,128)S(1)} %get-tuple-element.28), channel_id=1, source_target_pairs={{0,2},{1,3},{2,0},{3,1},{4,6},{5,7},{6,4},{7,5},{8,10},{9,11},{10,... | collective-permute-start | bytes 196616 | tf_op jit(solution)/shard_map/ppermute | solution.py:517
  63.8 5.3 %collective-permute-start.9 = (f32[4,8,512]{2,1,0:T(8,128)S(1)}, f32[4,8,512]{2,1,0:T(8,128)S(1)}, u32[]{:S(2)}, u32[]{:S(2)}) collective-permute-start(f32[4,8,512]{2,1,0:T(8,128)S(1)} %get-tuple-element.30), channel_id=1, source_target_pairs={{0,4},{1,5},{2,6},{3,7},{4,0},{5,1},{6,2},{7,3},{8,12},{9,13},{10,... | collective-permute-start | bytes 196616 | tf_op jit(solution)/shard_map/ppermute | solution.py:517

commit v9 on v8

--- a/solution.py
+++ b/solution.py
@@ -21,7 +21,7 @@
 
 
 REACH = 5
-BLOCK = 256
+SIDE_GROUP = 4
 PAD = 8
 
 
@@ -38,23 +38,36 @@
     return high, low
 
 
-def column_matrices():
-    full = band(2 * BLOCK)
-    inside = full[:BLOCK, :BLOCK]
-    half = BLOCK // 2
-    across = full[half : 3 * half, half : 3 * half].copy()
-    across[:half, :half] = 0.0
-    across[half:, half:] = 0.0
-    return np.concatenate([*split_terms(inside), *split_terms(across)], 0)
-
-
-def row_matrices(rows):
-    high, low = split_terms(band(rows + 2 * PAD))
+def column_matrices(columns):
+    return np.concatenate(split_terms(band(columns)), 0)
+
+
+def row_terms(matrix):
+    high, low = split_terms(matrix)
+    return np.concatenate([high, high, low], 1)
+
+
+def row_orders(rows):
+    full = band(rows + 2 * PAD)
     order = np.arange(rows + 2 * PAD)
     swapped = np.concatenate([order[rows + PAD :], order[PAD : rows + PAD], order[:PAD]])
+    return [full[:, order], full[:, swapped]]
+
+
+def row_matrices(rows):
+    return np.stack([row_terms(matrix) for matrix in row_orders(rows)])
+
+
+def own_matrix(rows):
+    return row_terms(band(rows + 2 * PAD)[:, PAD : rows + PAD])
+
+
+def side_matrices(rows):
     both = []
-    for columns in (order, swapped):
-        both.append(np.concatenate([high[:, columns], high[:, columns], low[:, columns]], 1))
+    for matrix in row_orders(rows):
+        sides = np.concatenate([matrix[:, :PAD], matrix[:, rows + PAD :]], 1)
+        touched = np.concatenate([sides[: 2 * PAD], sides[rows:]], 0)
+        both.append(row_terms(np.kron(np.eye(SIDE_GROUP), touched)))
     return np.stack(both)
 
 
@@ -65,35 +78,27 @@
 
 
 def smooth_columns(exact, by):
-    rows, columns = exact.shape
-    half = BLOCK // 2
-    starts = range(0, columns, BLOCK)
-    stacked = jnp.concatenate([exact[:, at : at + BLOCK] for at in starts], 0)
-    inside = two_terms(stacked, by[:BLOCK], by[BLOCK : 2 * BLOCK])
-    parts = []
-    for n in range(len(starts)):
-        block = inside[n * rows : (n + 1) * rows]
-        parts += [block[:, :half], block[:, half:]]
-    for n, at in enumerate(starts[1:]):
-        window = exact[:, at - half : at + half]
-        across = two_terms(window, by[2 * BLOCK : 3 * BLOCK], by[3 * BLOCK :])
-        parts[2 * n + 1] = parts[2 * n + 1] + across[:, :half]
-        parts[2 * n + 2] = parts[2 * n + 2] + across[:, half:]
-    return jnp.concatenate(parts, 1)
-
-
-def smooth_plane(counts, by, lx):
-    rows = counts[0].shape[0]
+    half = by.shape[0] // 2
+    return two_terms(exact, by[:half], by[half:])
+
+
+def column_terms(counts, by):
     exact = jnp.concatenate([c.astype(jnp.float32).astype(jnp.bfloat16) for c in counts], 0)
     wide = smooth_columns(exact, by)
     high = wide.astype(jnp.bfloat16)
-    low = (wide - high.astype(jnp.float32)).astype(jnp.bfloat16)
-    planes = []
-    for n in range(len(counts)):
-        part = slice(n * rows, (n + 1) * rows)
-        stacked = jnp.concatenate([high[part], low[part], high[part]], 0)
-        planes.append(jnp.dot(lx, stacked, preferred_element_type=jnp.float32))
-    return planes
+    return high, (wide - high.astype(jnp.float32)).astype(jnp.bfloat16)
+
+
+def row_product(matrix, high, low):
+    stacked = jnp.concatenate([high, low, high], 0)
+    return jnp.dot(matrix, stacked, preferred_element_type=jnp.float32)
+
+
+def smooth_plane(counts, by, lx):
+    rows = counts[0].shape[0]
+    high, low = column_terms(counts, by)
+    parts = [slice(n * rows, (n + 1) * rows) for n in range(len(counts))]
+    return [row_product(lx, high[part], low[part]) for part in parts]
 
 
 def smooth_depth(read, k):
@@ -209,9 +214,8 @@
     run_copies(pairs, sems)
 
 
-def smooth_kernel(group, order, c_hbm, xa, xb, by, lx, plane, c, sems):
+def smooth_kernel(group, c_hbm, by, lx, plane, c, sems):
     groups = c.shape[0] // group
-    rows_of = order[0]
 
     def fetch(g):
         part = pl.ds(g * group, group)
@@ -223,18 +227,37 @@
     def smooth_group(g, _):
         first = g * group
         fetch(g).wait()
-        counts = [
-            jnp.concatenate([xa[first + n], c[first + n], xb[first + n]], 0) for n in range(group)
-        ]
-        for n, value in enumerate(smooth_plane(counts, by, lx[rows_of])):
+        counts = [c[first + n] for n in range(group)]
+        for n, value in enumerate(smooth_plane(counts, by, lx[...])):
             plane[first + n] = value
         return 0
 
     lax.fori_loop(0, groups, smooth_group, 0)
 
 
-def interior_kernel(scale, flags, plane, image, smoothed):
-    layers, ext, columns = plane.shape
+def depth_kernel(flags, order, partial, xa, xb, by, lx, plane, smoothed):
+    layers, ext, _ = plane.shape
+    group = 2 * SIDE_GROUP
+    edge = 2 * PAD
+    sides = lx[order[0]]
+
+    def add_sides(g, _):
+        first = g * group
+        counts = [jnp.concatenate([xa[first + n], xb[first + n]], 0) for n in range(group)]
+        high, low = column_terms(counts, by)
+        for half in range(2):
+            part = slice(half * SIDE_GROUP * edge, (half + 1) * SIDE_GROUP * edge)
+            added = row_product(sides, high[part], low[part])
+            for n in range(SIDE_GROUP):
+                k = first + half * SIDE_GROUP + n
+                at = n * 2 * edge
+                plane[k, :edge, :] = partial[k, :edge, :] + added[at : at + edge]
+                plane[k, ext - edge :, :] = (
+                    partial[k, ext - edge :, :] + added[at + edge : at + 2 * edge]
+                )
+        return 0
+
+    lax.fori_loop(0, layers // group, add_sides, 0)
 
     def one_layer(j, _):
         def write(rows, value):
@@ -245,10 +268,14 @@
 
     lax.fori_loop(0, layers - 8, one_layer, 0)
 
+
+def interior_kernel(scale, smoothed, image):
+    held, ext, columns = smoothed.shape
+
     def one_tile(tile, _):
         base = pl.multiple_of(tile * 8 + 8, 8)
         carry = empty_carry(columns)
-        for k in range(1, layers - 9):
+        for k in range(1, held - 1):
             carry = render_layer(lambda k, rows: smoothed[k, rows, :], k, base, carry, scale)
         store_tile(image, tile, carry)
         return 0
@@ -386,39 +413,53 @@
     )(where, c)
 
 
-def call_smooth(order, c, xa, xb, by, lx):
+def call_smooth(c, by, lx):
     layers, rows, columns = c.shape
     ext = rows + 2 * PAD
     group = 8
     return pl.pallas_call(
         functools.partial(smooth_kernel, group),
         out_shape=jax.ShapeDtypeStruct((layers, ext, columns), jnp.float32),
-        in_specs=[smem(), in_hbm()] + whole(4),
+        in_specs=[in_hbm()] + whole(2),
         out_specs=whole(1)[0],
         scratch_shapes=[
             pltpu.VMEM((layers, rows, columns), jnp.int32),
             pltpu.SemaphoreType.DMA((layers // group,)),
         ],
-        compiler_params=params(24),
+        compiler_params=params(16),
         cost_estimate=cost(1_000_000_000),
         name="smooth",
-    )(order, c, xa, xb, by, lx)
-
-
-def call_interior(scale, flags, plane):
-    layers, ext, columns = plane.shape
-    return pl.pallas_call(
-        functools.partial(interior_kernel, scale),
+    )(c, by, lx)
+
+
+def call_depth(flags, order, partial, *operands):
+    layers, ext, columns = partial.shape
+    return pl.pallas_call(
+        depth_kernel,
         out_shape=(
-            jax.ShapeDtypeStruct((4, ext - 2 * PAD, columns), jnp.float32),
+            jax.ShapeDtypeStruct(partial.shape, jnp.float32),
             jax.ShapeDtypeStruct((layers - 8, ext, columns), jnp.float32),
         ),
-        in_specs=[smem()] + whole(1),
+        in_specs=[smem(), smem()] + whole(1 + len(operands)),
         out_specs=tuple(whole(2)),
-        compiler_params=params(24),
+        input_output_aliases={2: 0},
+        compiler_params=params(12),
+        cost_estimate=cost(500_000_000),
+        name="depth",
+    )(flags, order, partial, *operands)
+
+
+def call_interior(scale, smoothed):
+    _, ext, columns = smoothed.shape
+    return pl.pallas_call(
+        functools.partial(interior_kernel, scale),
+        out_shape=jax.ShapeDtypeStruct((4, ext - 2 * PAD, columns), jnp.float32),
+        in_specs=whole(1),
+        out_specs=whole(1)[0],
+        compiler_params=params(12),
         cost_estimate=cost(1_000_000_000),
         name="interior",
-    )(flags, plane)
+    )(smoothed)
 
 
 def call_first_edge(scale, flags, order, plane, *operands):
@@ -531,7 +572,7 @@
 
 
 def local(counts):
-    slab, rows, _ = counts.shape
+    slab, rows, columns = counts.shape
     img, depth = lax.axis_index("img"), lax.axis_index("depth")
     imgs, depths = lax.axis_size("img"), lax.axis_size("depth")
     scale = 1.5 / (slab * depths)
@@ -544,7 +585,7 @@
     flags = jnp.stack(
         [(img > 0) * one, (img < imgs - 1) * one, (depth > 0) * one, (depth < depths - 1) * one]
     )
-    by = jnp.asarray(column_matrices())
+    by = jnp.asarray(column_matrices(columns))
     lx = jnp.asarray(row_matrices(rows))
     held = pltpu.with_memory_space_constraint(counts, pltpu.HBM)
     block_b = call_pack_block(where, held)
@@ -562,8 +603,11 @@
 
     ca = swap(corner(1 - row_odd), "img", 0)
     cb = swap(corner(row_odd), "img", 1)
-    plane = call_smooth(order, held, xa, xb, by, lx)
-    inner, smoothed = call_interior(scale, flags, plane)
+    partial = call_smooth(held, by, jnp.asarray(own_matrix(rows)))
+    plane, smoothed = call_depth(
+        flags, order, partial, xa, xb, by, jnp.asarray(side_matrices(rows))
+    )
+    inner = call_interior(scale, smoothed)
     owned = rows // depths
     owner_tiles = owned // 8 if owned % 8 == 0 else 0
     common = (flags, order, plane, smoothed)

time: 70.1 us -> 65.5 us (0.934)
  waiting for transfers between devices: 23.2 us -> 18 us
    ppermute x8, waiting for transfers between devices: 18.6 us -> 13.3 us  [swap(): return lax.ppermute(value, axis, pairs)]
    pallas_call x1 -> x2, Pallas kernels: 6.79 us -> 9.4 us  [the longest x1 5.22 us: call_depth(): pl.pallas_call(depth_kernel, out_shape=(jax.ShapeDtypeStruct(partial.shap...]
    pallas_call x1, Pallas kernels: 7.28 us -> 5.23 us  [call_smooth(): pl.pallas_call(functools.partial(smooth_kernel, group), out_shape=jax.Sha...]
  transfers between devices with their start and end apart: 11 -> 11, of which waited for: 6 -> 6; matrix products, arithmetic and copies ran while one was open for 0% -> 0% of each run, Pallas kernels for 30% -> 34%
where the time goes in v9:
time: 65.5 us; the launch traced here: 65.2 us
  Pallas kernels  26.9 us (41%)
  starting transfers between devices  18.9 us (29%)
  waiting for transfers between devices  18 us (27%)
  other arithmetic  1.06 us (2%)
    ppermute x8, starting transfers between devices, swap(): return lax.ppermute(value, axis, pairs)  14.3 us
    ppermute x8, waiting for transfers between devices, swap(): return lax.ppermute(value, axis, pairs)  13.3 us
    pallas_call x1, Pallas kernels, call_smooth(): pl.pallas_call(functools.partial(smooth_kernel, group), out_shape=jax.Sha...  5.23 us
    pallas_call x1, Pallas kernels, call_depth(): pl.pallas_call(depth_kernel, out_shape=(jax.ShapeDtypeStruct(partial.shap...  5.22 us
    ppermute x3, waiting for transfers between devices, exchange(): lax.ppermute(piece, 'depth', [(i, i ^ 2 * step) for i in range(count)])  4.67 us
    ppermute x3, starting transfers between devices, exchange(): lax.ppermute(piece, 'depth', [(i, i ^ 2 * step) for i in range(count)])  4.56 us
    pallas_call x1, Pallas kernels, call_interior(): pl.pallas_call(functools.partial(interior_kernel, scale), out_shape=jax.S...  4.19 us
    pallas_call x1, Pallas kernels, call_last_edge(): pl.pallas_call(functools.partial(last_edge_kernel, scale, owner_tiles), o...  3.43 us
  transfers between devices with their start and end apart: 11, of which 6 were waited for; matrix products, arithmetic and copies ran while one was open for 0% of the time, Pallas kernels for 34%

profile of v9, /device:TPU:0, one launch (start us, length us, event | category | flops | bytes accessed | tf_op | source)
XLA Modules:
  0.0 65.2 jit_solution(6239974663974694709)
XLA Ops:
  0.1 1.6 %pack_block.1 = s32[5,64,512]{2,1,0:T(8,128)S(1)} custom-call(s32[4]{0:T(128)S(1)} %pad_add_fusion.3.where, s32[32,64,512]{2,1,0:T(8,128)} %c.3), custom_call_target="tpu_custom_call" | custom-call | tf_op jit(solution)/shard_map/pack_block/pallas_call | solution.py:389
  1.7 0.7 %collective-permute-start.4 = (s32[5,64,512]{2,1,0:T(8,128)S(1)}, s32[5,64,512]{2,1,0:T(8,128)S(1)}, u32[]{:S(2)}, u32[]{:S(2)}) collective-permute-start(s32[5,64,512]{2,1,0:T(8,128)S(1)} %pack_block.1), channel_id=1, source_target_pairs={{1,2},{2,1},{3,4},{4,3},{5,6},{6,5},{9,10},{10,9},{11,12},{12,11},... | collective-permute-start | bytes 1966088 | tf_op jit(solution)/shard_map/ppermute | solution.py:527
  2.4 3.1 %pack_rest.1 = (s32[32,8,512]{2,1,0:T(8,128)}, s32[5,16,512]{2,1,0:T(8,128)S(1)}, s32[5,48,512]{2,1,0:T(8,128)}, s32[32,8,512]{2,1,0:T(8,128)}) custom-call(s32[4]{0:T(128)S(1)} %pad_add_fusion.3.where, s32[32,64,512]{2,1,0:T(8,128)} %c.3), custom_call_target="tpu_custom_call" | custom-call | tf_op jit(solution)/shard_map/pack_rest/pallas_call | solution.py:405
  5.6 0.6 collective-permute-start
  6.1 1.5 %collective-permute-start.1 = (s32[32,8,512]{2,1,0:T(8,128)}, s32[32,8,512]{2,1,0:T(8,128)}, u32[]{:S(2)}, u32[]{:S(2)}) collective-permute-start(s32[32,8,512]{2,1,0:T(8,128)} %get-tuple-element.14), channel_id=1, source_target_pairs={{8,16},{16,8},{9,17},{17,9},{10,18},{18,10},{11,19},{19,11},{12,20... | collective-permute-start | bytes 1572872 | tf_op jit(solution)/shard_map/ppermute | solution.py:527
  7.6 5.3 %collective-permute-start.3 = (s32[5,16,512]{2,1,0:T(8,128)S(1)}, s32[5,16,512]{2,1,0:T(8,128)S(1)}, u32[]{:S(2)}, u32[]{:S(2)}) collective-permute-start(s32[5,16,512]{2,1,0:T(8,128)S(1)} %get-tuple-element.18), channel_id=1, source_target_pairs={{0,1},{1,0},{2,3},{3,2},{4,5},{5,4},{6,7},{7,6},{8,9},{9,8},{10,11... | collective-permute-start | bytes 491528 | tf_op jit(solution)/shard_map/ppermute | solution.py:527
  13.0 5.2 %smooth.1.partial = f32[32,80,512]{2,1,0:T(8,128)S(1)} custom-call(s32[32,64,512]{2,1,0:T(8,128)} %c.3, bf16[1024,512]{1,0:T(8,128)(2,1)S(1)} %copy-done, bf16[80,192]{1,0:T(8,128)(2,1)S(1)} %copy-done.3), custom_call_target="tpu_custom_call" | custom-call | flops 1000000000 | bytes 4000000 | tf_op jit(solution)/shard_map/smooth/pallas_call | solution.py:420
  18.3 6.6 %collective-permute-done.3.edge = s32[5,16,512]{2,1,0:T(8,128)S(1)} collective-permute-done((s32[5,16,512]{2,1,0:T(8,128)S(1)}, s32[5,16,512]{2,1,0:T(8,128)S(1)}, u32[]{:S(2)}, u32[]{:S(2)}) %collective-permute-start.3) | collective-permute-done | bytes 163872 | tf_op jit(solution)/shard_map/ppermute | solution.py:527
  24.9 5.2 %depth.1 = (f32[32,80,512]{2,1,0:T(8,128)S(1)}, f32[24,80,512]{2,1,0:T(8,128)S(1)}) custom-call(f32[4]{0:T(128)S(1)} %add_convert_fusion.flags, s32[2]{0:T(128)S(1)} %pad_add_fusion.2.order, f32[32,80,512]{2,1,0:T(8,128)S(1)} %smooth.1.partial, s32[32,8,512]{2,1,0:T(8,128)S(1)} %collective-permute-done.xa, ...), custom_call_target="tpu_custom_call", output_to_operand_aliasing={{0}: (2, {})} | custom-call | flops 500000000 | bytes 4000000 | tf_op jit(solution)/shard_map/depth/pallas_call | solution.py:437
  30.2 0.7 %collective-permute-start.6 = (s32[10,8,512]{2,1,0:T(8,128)S(1)}, s32[10,8,512]{2,1,0:T(8,128)S(1)}, u32[]{:S(2)}, u32[]{:S(2)}) collective-permute-start(s32[10,8,512]{2,1,0:T(8,128)S(1)} %pad_add_fusion.1), channel_id=1, source_target_pairs={{8,16},{16,8},{9,17},{17,9},{10,18},{18,10},{11,19},{19,11},{12,20... | collective-permute-start | bytes 491528 | tf_op jit(solution)/shard_map/ppermute | solution.py:527
  30.9 4.2 %interior.1.behind = f32[4,64,512]{2,1,0:T(8,128)S(1)} custom-call(f32[24,80,512]{2,1,0:T(8,128)S(1)} %get-tuple-element.16.smoothed), custom_call_target="tpu_custom_call" | custom-call | flops 1000000000 | bytes 4000000 | tf_op jit(solution)/shard_map/interior/pallas_call | solution.py:454
  35.1 3.1 %collective-permute-start.5 = (s32[10,8,512]{2,1,0:T(8,128)S(1)}, s32[10,8,512]{2,1,0:T(8,128)S(1)}, u32[]{:S(2)}, u32[]{:S(2)}) collective-permute-start(s32[10,8,512]{2,1,0:T(8,128)S(1)} %pad_add_fusion), channel_id=1, source_target_pairs={{0,8},{8,0},{16,24},{24,16},{1,9},{9,1},{17,25},{25,17},{2,10},{10... | collective-permute-start | bytes 491528 | tf_op jit(solution)/shard_map/ppermute | solution.py:527
  38.3 1.0 %collective-permute-done.5 = s32[10,8,512]{2,1,0:T(8,128)S(1)} collective-permute-done((s32[10,8,512]{2,1,0:T(8,128)S(1)}, s32[10,8,512]{2,1,0:T(8,128)S(1)}, u32[]{:S(2)}, u32[]{:S(2)}) %collective-permute-start.5) | collective-permute-done | bytes 163872 | tf_op jit(solution)/shard_map/ppermute | solution.py:527
  39.3 3.0 %first_edge.1.behind = f32[4,64,512]{2,1,0:T(8,128)S(1)} custom-call(f32[4]{0:T(128)S(1)} %add_convert_fusion.flags, s32[2]{0:T(128)S(1)} %pad_add_fusion.2.order, f32[32,80,512]{2,1,0:T(8,128)S(1)} %get-tuple-element.15.plane, f32[24,80,512]{2,1,0:T(8,128)S(1)} %get-tuple-element.16.smoothed, s32[5,64,512]{2,1,0:T(8,128)S(1)} %collective-permute-done.4.block, ...), custom_call_target="tpu_custom_call" | custom-call | flops 300000000 | bytes 4000000 | tf_op jit(solution)/shard_map/first_edge/pallas_call | solution.py:468
  42.3 3.4 %last_edge.1 = (f32[4,32,512]{2,1,0:T(8,128)S(1)}, f32[7,80,512]{2,1,0:T(8,128)S(1)}) custom-call(f32[4]{0:T(128)S(1)} %add_convert_fusion.flags, s32[2]{0:T(128)S(1)} %pad_add_fusion.2.order, f32[32,80,512]{2,1,0:T(8,128)S(1)} %get-tuple-element.15.plane, f32[24,80,512]{2,1,0:T(8,128)S(1)} %get-tuple-element.16.smoothed, ...), custom_call_target="tpu_custom_call" | custom-call | flops 300000000 | bytes 4000000 | tf_op jit(solution)/shard_map/last_edge/pallas_call | solution.py:487
  45.7 2.5 %collective-permute-start.7 = (f32[4,4,8,512]{3,2,1,0:T(8,128)S(1)}, f32[4,4,8,512]{3,2,1,0:T(8,128)S(1)}, u32[]{:S(2)}, u32[]{:S(2)}) collective-permute-start(f32[4,4,8,512]{3,2,1,0:T(8,128)S(1)} %bitcast.53), channel_id=1, source_target_pairs={{0,1},{1,0},{2,3},{3,2},{4,5},{5,4},{6,7},{7,6},{8,9},{9,8},{10,11... | collective-permute-start | bytes 786440 | tf_op jit(solution)/shard_map/ppermute | solution.py:527
  48.3 1.1 %kept_edge.1 = f32[4,32,512]{2,1,0:T(8,128)S(1)} custom-call(s32[2]{0:T(128)S(1)} %pad_add_fusion.2.order, f32[7,80,512]{2,1,0:T(8,128)S(1)} %get-tuple-element.19.ends, f32[4,64,512]{2,1,0:T(8,128)S(1)} %first_edge.1.behind), custom_call_target="tpu_custom_call" | custom-call | flops 200000000 | bytes 4000000 | tf_op jit(solution)/shard_map/kept_edge/pallas_call | solution.py:511
  49.4 5.7 %collective-permute-done.7 = f32[4,4,8,512]{3,2,1,0:T(8,128)S(1)} collective-permute-done((f32[4,4,8,512]{3,2,1,0:T(8,128)S(1)}, f32[4,4,8,512]{3,2,1,0:T(8,128)S(1)}, u32[]{:S(2)}, u32[]{:S(2)}) %collective-permute-start.7) | collective-permute-done | bytes 262176 | tf_op jit(solution)/shard_map/ppermute | solution.py:527
  55.3 3.9 %collective-permute-start.10 = (f32[4,8,512]{2,1,0:T(8,128)S(1)}, f32[4,8,512]{2,1,0:T(8,128)S(1)}, u32[]{:S(2)}, u32[]{:S(2)}) collective-permute-start(f32[4,8,512]{2,1,0:T(8,128)S(1)} %get-tuple-element.29), channel_id=1, source_target_pairs={{0,6},{1,7},{2,4},{3,5},{4,2},{5,3},{6,0},{7,1},{8,14},{9,15},{10,... | collective-permute-start | bytes 196616 | tf_op jit(solution)/shard_map/ppermute | solution.py:558
  59.2 0.6 collective-permute-start.9
  59.8 1.9 %collective-permute-done.10 = f32[4,8,512]{2,1,0:T(8,128)S(1)} collective-permute-done((f32[4,8,512]{2,1,0:T(8,128)S(1)}, f32[4,8,512]{2,1,0:T(8,128)S(1)}, u32[]{:S(2)}, u32[]{:S(2)}) %collective-permute-start.10) | collective-permute-done | bytes 65568 | tf_op jit(solution)/shard_map/ppermute | solution.py:558
  61.8 1.9 %collective-permute-done.8 = f32[4,8,512]{2,1,0:T(8,128)S(1)} collective-permute-done((f32[4,8,512]{2,1,0:T(8,128)S(1)}, f32[4,8,512]{2,1,0:T(8,128)S(1)}, u32[]{:S(2)}, u32[]{:S(2)}) %collective-permute-start.8) | collective-permute-done | bytes 65568 | tf_op jit(solution)/shard_map/ppermute | solution.py:558
  63.7 0.8 %collective-permute-done.9 = f32[4,8,512]{2,1,0:T(8,128)S(1)} collective-permute-done((f32[4,8,512]{2,1,0:T(8,128)S(1)}, f32[4,8,512]{2,1,0:T(8,128)S(1)}, u32[]{:S(2)}, u32[]{:S(2)}) %collective-permute-start.9) | collective-permute-done | bytes 65568 | tf_op jit(solution)/shard_map/ppermute | solution.py:558
  64.6 0.6 pad_maximum_fusion.2
  (33 shorter events, 0.6 us)
Async XLA Ops:
  0.1 12.9 %copy-start = (bf16[1024,512]{1,0:T(8,128)(2,1)S(1)}, bf16[1024,512]{1,0:T(8,128)(2,1)}, u32[]{:S(2)}) copy-start(bf16[1024,512]{1,0:T(8,128)(2,1)} %constant.80.clone.by) | copy-start | bytes 3145732
  0.1 12.9 %copy-start.3 = (bf16[80,192]{1,0:T(8,128)(2,1)S(1)}, bf16[80,192]{1,0:T(8,128)(2,1)}, u32[]{:S(2)}) copy-start(bf16[80,192]{1,0:T(8,128)(2,1)} %constant.82.clone.lx) | copy-start | bytes 92164
  1.7 28.5 %collective-permute-start.4 = (s32[5,64,512]{2,1,0:T(8,128)S(1)}, s32[5,64,512]{2,1,0:T(8,128)S(1)}, u32[]{:S(2)}, u32[]{:S(2)}) collective-permute-start(s32[5,64,512]{2,1,0:T(8,128)S(1)} %pack_block.1), channel_id=1, source_target_pairs={{1,2},{2,1},{3,4},{4,3},{5,6},{6,5},{9,10},{10,9},{11,12},{12,11},... | collective-permute-start | bytes 1966088 | tf_op jit(solution)/shard_map/ppermute | solution.py:527
  5.6 19.3 %collective-permute-start = (s32[32,8,512]{2,1,0:T(8,128)}, s32[32,8,512]{2,1,0:T(8,128)S(1)}, u32[]{:S(2)}, u32[]{:S(2)}) collective-permute-start(s32[32,8,512]{2,1,0:T(8,128)} %get-tuple-element.13), channel_id=1, source_target_pairs={{0,8},{8,0},{16,24},{24,16},{1,9},{9,1},{17,25},{25,17},{2,10},{10... | collective-permute-start | bytes 1572872 | tf_op jit(solution)/shard_map/ppermute | solution.py:527
  6.1 18.8 %collective-permute-start.1 = (s32[32,8,512]{2,1,0:T(8,128)}, s32[32,8,512]{2,1,0:T(8,128)}, u32[]{:S(2)}, u32[]{:S(2)}) collective-permute-start(s32[32,8,512]{2,1,0:T(8,128)} %get-tuple-element.14), channel_id=1, source_target_pairs={{8,16},{16,8},{9,17},{17,9},{10,18},{18,10},{11,19},{19,11},{12,20... | collective-permute-start | bytes 1572872 | tf_op jit(solution)/shard_map/ppermute | solution.py:527
  7.6 17.3 %collective-permute-start.3 = (s32[5,16,512]{2,1,0:T(8,128)S(1)}, s32[5,16,512]{2,1,0:T(8,128)S(1)}, u32[]{:S(2)}, u32[]{:S(2)}) collective-permute-start(s32[5,16,512]{2,1,0:T(8,128)S(1)} %get-tuple-element.18), channel_id=1, source_target_pairs={{0,1},{1,0},{2,3},{3,2},{4,5},{5,4},{6,7},{7,6},{8,9},{9,8},{10,11... | collective-permute-start | bytes 491528 | tf_op jit(solution)/shard_map/ppermute | solution.py:527
  12.9 29.4 %collective-permute-start.2 = (s32[5,48,512]{2,1,0:T(8,128)}, s32[5,48,512]{2,1,0:T(8,128)}, u32[]{:S(2)}, u32[]{:S(2)}) collective-permute-start(s32[5,48,512]{2,1,0:T(8,128)} %get-tuple-element.17), channel_id=1, source_target_pairs={{0,1},{1,0},{2,3},{3,2},{4,5},{5,4},{6,7},{7,6},{8,9},{9,8},{10,11... | collective-permute-start | bytes 1474568 | tf_op jit(solution)/shard_map/ppermute | solution.py:527
  13.0 12.0 %copy-start.2 = (bf16[2,128,192]{2,1,0:T(8,128)(2,1)S(1)}, bf16[2,128,192]{2,1,0:T(8,128)(2,1)}, u32[]{:S(2)}) copy-start(bf16[2,128,192]{2,1,0:T(8,128)(2,1)} %constant.83.clone.lx) | copy-start | bytes 294916
  30.2 9.1 %copy-start.1 = (bf16[2,80,240]{2,1,0:T(8,128)(2,1)S(1)}, bf16[2,80,240]{2,1,0:T(8,128)(2,1)}, u32[]{:S(2)}) copy-start(bf16[2,80,240]{2,1,0:T(8,128)(2,1)} %constant.81.clone.lx) | copy-start | bytes 230404
  30.2 8.0 %collective-permute-start.6 = (s32[10,8,512]{2,1,0:T(8,128)S(1)}, s32[10,8,512]{2,1,0:T(8,128)S(1)}, u32[]{:S(2)}, u32[]{:S(2)}) collective-permute-start(s32[10,8,512]{2,1,0:T(8,128)S(1)} %pad_add_fusion.1), channel_id=1, source_target_pairs={{8,16},{16,8},{9,17},{17,9},{10,18},{18,10},{11,19},{19,11},{12,20... | collective-permute-start | bytes 491528 | tf_op jit(solution)/shard_map/ppermute | solution.py:527
  35.1 4.2 %collective-permute-start.5 = (s32[10,8,512]{2,1,0:T(8,128)S(1)}, s32[10,8,512]{2,1,0:T(8,128)S(1)}, u32[]{:S(2)}, u32[]{:S(2)}) collective-permute-start(s32[10,8,512]{2,1,0:T(8,128)S(1)} %pad_add_fusion), channel_id=1, source_target_pairs={{0,8},{8,0},{16,24},{24,16},{1,9},{9,1},{17,25},{25,17},{2,10},{10... | collective-permute-start | bytes 491528 | tf_op jit(solution)/shard_map/ppermute | solution.py:527
  45.7 9.4 %collective-permute-start.7 = (f32[4,4,8,512]{3,2,1,0:T(8,128)S(1)}, f32[4,4,8,512]{3,2,1,0:T(8,128)S(1)}, u32[]{:S(2)}, u32[]{:S(2)}) collective-permute-start(f32[4,4,8,512]{3,2,1,0:T(8,128)S(1)} %bitcast.53), channel_id=1, source_target_pairs={{0,1},{1,0},{2,3},{3,2},{4,5},{5,4},{6,7},{7,6},{8,9},{9,8},{10,11... | collective-permute-start | bytes 786440 | tf_op jit(solution)/shard_map/ppermute | solution.py:527
  55.3 6.5 %collective-permute-start.10 = (f32[4,8,512]{2,1,0:T(8,128)S(1)}, f32[4,8,512]{2,1,0:T(8,128)S(1)}, u32[]{:S(2)}, u32[]{:S(2)}) collective-permute-start(f32[4,8,512]{2,1,0:T(8,128)S(1)} %get-tuple-element.29), channel_id=1, source_target_pairs={{0,6},{1,7},{2,4},{3,5},{4,2},{5,3},{6,0},{7,1},{8,14},{9,15},{10,... | collective-permute-start | bytes 196616 | tf_op jit(solution)/shard_map/ppermute | solution.py:558
  59.2 4.5 %collective-permute-start.8 = (f32[4,8,512]{2,1,0:T(8,128)S(1)}, f32[4,8,512]{2,1,0:T(8,128)S(1)}, u32[]{:S(2)}, u32[]{:S(2)}) collective-permute-start(f32[4,8,512]{2,1,0:T(8,128)S(1)} %get-tuple-element.28), channel_id=1, source_target_pairs={{0,2},{1,3},{2,0},{3,1},{4,6},{5,7},{6,4},{7,5},{8,10},{9,11},{10,... | collective-permute-start | bytes 196616 | tf_op jit(solution)/shard_map/ppermute | solution.py:558
  59.2 5.3 %collective-permute-start.9 = (f32[4,8,512]{2,1,0:T(8,128)S(1)}, f32[4,8,512]{2,1,0:T(8,128)S(1)}, u32[]{:S(2)}, u32[]{:S(2)}) collective-permute-start(f32[4,8,512]{2,1,0:T(8,128)S(1)} %get-tuple-element.30), channel_id=1, source_target_pairs={{0,4},{1,5},{2,6},{3,7},{4,0},{5,1},{6,2},{7,3},{8,12},{9,13},{10,... | collective-permute-start | bytes 196616 | tf_op jit(solution)/shard_map/ppermute | solution.py:558

commit v10 on v9

--- a/solution.py
+++ b/solution.py
@@ -312,11 +312,11 @@
         ends[ends_face + sign * v] = smoothed[smoothed_face + sign * v]
 
 
-def edge_render(scale, is_front, ends, behind, image, tiles, tile_of):
+def edge_render(scale, is_front, ends, behind, image, tiles, tile_of, first=0):
     columns = ends.shape[2]
 
     def one_tile(place, _):
-        tile = tile_of(place)
+        tile = tile_of(place + first)
         base = pl.multiple_of(tile * 8 + 8, 8)
         carry = empty_carry(columns)
         for k in range(1, REACH + 1):
@@ -325,15 +325,21 @@
         front = [jnp.where(is_front, x, y) for x, y in zip(carry, other)]
         back = [jnp.where(is_front, y, x) for x, y in zip(carry, other)]
         colors = [front[n] + front[3] * back[n] for n in range(3)]
-        store_tile(image, place, colors + [front[3] * back[3]])
+        colors.append(front[3] * back[3])
+        if len(image.shape) == 3:
+            store_tile(image, place, colors)
+        else:
+            owner_tiles = image.shape[2] // 8
+            store_tile(image.at[place // owner_tiles], place % owner_tiles, colors)
         return 0
 
     lax.fori_loop(0, tiles, one_tile, 0)
 
 
-def half_tiles(owner_tiles, wanted):
+def half_tiles(order, pairs, owner_tiles, wanted):
     def tile_of(place):
-        return (place // owner_tiles * 2 + wanted) * owner_tiles + place % owner_tiles
+        pair = order[2] ^ (pairs - 1 - place // owner_tiles)
+        return (2 * pair + wanted) * owner_tiles + place % owner_tiles
 
     return tile_of
 
@@ -346,22 +352,30 @@
     edge_render(scale, order[1] == 0, ends, behind, image, tiles, lambda place: place)
 
 
-def last_edge_kernel(scale, owner_tiles, flags, order, plane, smoothed, middle_any, edge, ca, cb,
-                     by, lx, behind, image, ends, halo, middle, sem):
+def render_halves(scale, is_front, ends, behind, images, tile_of):
+    for n, image in enumerate(images):
+        places, _, owned, _ = image.shape
+        tiles = places * (owned // 8)
+        edge_render(scale, is_front, ends, behind, image, tiles, tile_of, n * tiles)
+
+
+def last_edge_kernel(scale, split, flags, order, plane, smoothed, middle_any, edge, ca, cb,
+                     by, lx, behind, *refs):
+    images, (ends, halo, middle, sem) = refs[:-4], refs[-4:]
     run_copies([(middle_any, middle)], sem)
     tile = lambda j: jnp.concatenate([edge[j, :PAD], middle[j], edge[j, PAD:]], 0)
     edge_smooth(0, flags, order, plane, smoothed, tile, ca, cb, by, lx, ends, halo)
-    tiles = plane.shape[1] // 8 - 2
-    tile_of = lambda place: place
-    if owner_tiles:
-        tiles, tile_of = tiles // 2, half_tiles(owner_tiles, 1 - order[1])
-    edge_render(scale, order[1] == 1, ends, behind, image, tiles, tile_of)
-
-
-def kept_edge_kernel(scale, owner_tiles, order, ends, behind, image):
-    tiles = ends.shape[1] // 8 - 2
-    tile_of = half_tiles(owner_tiles, order[1])
-    edge_render(scale, order[1] == 1, ends, behind, image, tiles // 2, tile_of)
+    if split:
+        tile_of = half_tiles(order, *split, 1 - order[1])
+        render_halves(scale, order[1] == 1, ends, behind, images, tile_of)
+    else:
+        tiles = plane.shape[1] // 8 - 2
+        edge_render(scale, order[1] == 1, ends, behind, images[0], tiles, lambda place: place)
+
+
+def kept_edge_kernel(scale, split, order, ends, behind, *images):
+    tile_of = half_tiles(order, *split, order[1])
+    render_halves(scale, order[1] == 1, ends, behind, images, tile_of)
 
 
 def whole(count):
@@ -480,40 +494,41 @@
     )(flags, order, plane, *operands)
 
 
-def call_last_edge(scale, owner_tiles, flags, order, plane, *operands):
+def half_shape(split, columns):
+    pairs, owner_tiles = split
+    return pairs // 2, 4, owner_tiles * 8, columns
+
+
+def call_last_edge(scale, split, flags, order, plane, *operands):
     _, ext, columns = plane.shape
     f32 = jnp.float32
-    rows = (ext - 2 * PAD) // (2 if owner_tiles else 1)
-    return pl.pallas_call(
-        functools.partial(last_edge_kernel, scale, owner_tiles),
-        out_shape=(
-            jax.ShapeDtypeStruct((4, rows, columns), f32),
-            jax.ShapeDtypeStruct((REACH + 2, ext, columns), f32),
-        ),
-        in_specs=[smem(), smem()]
-        + whole(2)
-        + [in_hbm()]
-        + whole(len(operands) - 2),
-        out_specs=tuple(whole(2)),
+    rows = ext - 2 * PAD
+    images = 2 * [half_shape(split, columns)] if split else [(4, rows, columns)]
+    shapes = [*images, (REACH + 2, ext, columns)]
+    return pl.pallas_call(
+        functools.partial(last_edge_kernel, scale, split),
+        out_shape=tuple(jax.ShapeDtypeStruct(shape, f32) for shape in shapes),
+        in_specs=[smem(), smem()] + whole(2) + [in_hbm()] + whole(len(operands) - 2),
+        out_specs=tuple(whole(len(shapes))),
         scratch_shapes=[
             pltpu.VMEM((REACH, ext, columns), f32),
             pltpu.VMEM(operands[1].shape, operands[1].dtype),
             pltpu.SemaphoreType.DMA((1,)),
         ],
-        compiler_params=params(24),
+        compiler_params=params(12),
         cost_estimate=cost(300_000_000),
         name="last_edge",
     )(flags, order, plane, *operands)
 
 
-def call_kept_edge(scale, owner_tiles, order, ends, behind):
-    _, ext, columns = ends.shape
-    return pl.pallas_call(
-        functools.partial(kept_edge_kernel, scale, owner_tiles),
-        out_shape=jax.ShapeDtypeStruct((4, (ext - 2 * PAD) // 2, columns), jnp.float32),
+def call_kept_edge(scale, split, order, ends, behind):
+    image = jax.ShapeDtypeStruct(half_shape(split, ends.shape[2]), jnp.float32)
+    return pl.pallas_call(
+        functools.partial(kept_edge_kernel, scale, split),
+        out_shape=(image, image),
         in_specs=[smem()] + whole(2),
-        out_specs=whole(1)[0],
-        compiler_params=params(24),
+        out_specs=tuple(whole(2)),
+        compiler_params=params(12),
         cost_estimate=cost(200_000_000),
         name="kept_edge",
     )(order, ends, behind)
@@ -528,35 +543,43 @@
 
 
 def over(front, back):
-    through = front[3:]
-    return jnp.concatenate([front[:3] + through * back[:3], through * back[3:]], 0)
+    through = front[:, 3:]
+    return jnp.concatenate([front[:, :3] + through * back[:, :3], through * back[:, 3:]], 1)
 
 
 def halves_of(layers):
     count = lax.axis_size("depth")
-    parity = lax.axis_index("depth") % 2
+    me = lax.axis_index("depth")
+    parity, pair, pairs = me % 2, me // 2, count // 2
     _, rows, columns = layers.shape
-    pieces = layers.reshape(4, count // 2, 2, rows // count, columns)
-    send = lax.dynamic_index_in_dim(pieces, 1 - parity, 2, keepdims=False)
-    keep = lax.dynamic_index_in_dim(pieces, parity, 2, keepdims=False)
-    return send, keep
-
-
-def exchange(send, keep):
+    pieces = layers.reshape(4, pairs, 2, rows // count, columns)
+    ordered = jnp.concatenate(
+        [lax.dynamic_slice_in_dim(pieces, pair ^ step, 1, 1) for step in reversed(range(pairs))], 1
+    )
+    both = []
+    for wanted in (1 - parity, parity):
+        chosen = lax.dynamic_index_in_dim(ordered, wanted, 2, keepdims=False)
+        chosen = jnp.moveaxis(chosen, 1, 0)
+        both.append((chosen[: pairs // 2], chosen[pairs // 2 :]))
+    return both
+
+
+def exchange(sends, keeps):
     count = lax.axis_size("depth")
     me = lax.axis_index("depth")
     parity, pair = me % 2, me // 2
     pairs = count // 2
-    send, keep = (value.reshape(4, pairs, -1, value.shape[-1]) for value in (send, keep))
-    owned, columns = send.shape[2:]
-    got = swap(send, "depth", 0)
-    joined = jnp.where(parity == 0, over(keep, got), over(got, keep))
-    parts = []
-    for step in range(pairs):
-        piece = lax.dynamic_index_in_dim(joined, pair ^ step, 1, keepdims=False)
-        if step:
-            piece = lax.ppermute(piece, "depth", [(i, i ^ (2 * step)) for i in range(count)])
-        parts.append(piece)
+    parts = [None] * pairs
+    for half, (send, keep) in enumerate(zip(sends, keeps)):
+        owned, columns = send.shape[2:]
+        got = swap(send, "depth", 0)
+        joined = jnp.where(parity == 0, over(keep, got), over(got, keep))
+        for place in range(pairs // 2):
+            step = pairs - 1 - half * (pairs // 2) - place
+            piece = joined[place]
+            if step:
+                piece = lax.ppermute(piece, "depth", [(i, i ^ (2 * step)) for i in range(count)])
+            parts[step] = piece
     result = jnp.zeros((3, owned, columns), jnp.float32)
     through = jnp.ones((1, owned, columns), jnp.float32)
     for step in range(pairs):
@@ -580,7 +603,7 @@
     first_a, first_b = (1 - depth_odd) * (slab - REACH), depth_odd * (slab - REACH)
     row_a, row_b = (1 - row_odd) * (rows - PAD), row_odd * (rows - PAD)
     where = jnp.stack([first_a, first_b, row_a, row_b])
-    order = jnp.stack([1 - row_odd, depth_odd])
+    order = jnp.stack([1 - row_odd, depth_odd, depth // 2])
     one = jnp.float32(1.0)
     flags = jnp.stack(
         [(img > 0) * one, (img < imgs - 1) * one, (depth > 0) * one, (depth < depths - 1) * one]
@@ -609,20 +632,20 @@
     )
     inner = call_interior(scale, smoothed)
     owned = rows // depths
-    owner_tiles = owned // 8 if owned % 8 == 0 else 0
+    split = (depths // 2, owned // 8) if owned % 8 == 0 else None
     common = (flags, order, plane, smoothed)
     layers = call_first_edge(
         scale, *common, block_b, ca[REACH:], cb[REACH:], by, lx, inner
     )
-    send, ends = call_last_edge(
-        scale, owner_tiles, *common, pltpu.with_memory_space_constraint(mid_a, pltpu.HBM), edge_a,
-        ca[:REACH], cb[:REACH], by, lx, layers
-    )
-    if owner_tiles:
-        keep = call_kept_edge(scale, owner_tiles, order, ends, layers)
+    mid_a = pltpu.with_memory_space_constraint(mid_a, pltpu.HBM)
+    *sends, ends = call_last_edge(
+        scale, split, *common, mid_a, edge_a, ca[:REACH], cb[:REACH], by, lx, layers
+    )
+    if split:
+        keeps = call_kept_edge(scale, split, order, ends, layers)
     else:
-        send, keep = halves_of(send)
-    return exchange(send, keep)
+        sends, keeps = halves_of(sends[0])
+    return exchange(sends, keeps)
 
 
 def solution(mesh):

time: 65.5 us -> 65.6 us (level)
    ppermute x8 -> x9, starting transfers between devices: 14.3 us -> 14.4 us  [swap(): return lax.ppermute(value, axis, pairs)]
    ppermute x8 -> x9, waiting for transfers between devices: 13.3 us -> 13.2 us  [swap(): return lax.ppermute(value, axis, pairs)]
  transfers between devices with their start and end apart: 11 -> 12, of which waited for: 6 -> 7; matrix products, arithmetic and copies ran while one was open for 0% -> 0% of each run, Pallas kernels for 34% -> 33%
where the time goes in v10:
time: 65.6 us; the launch traced here: 65.3 us
  Pallas kernels  26.9 us (41%)
  starting transfers between devices  19 us (29%)
  waiting for transfers between devices  18 us (27%)
  other arithmetic  1.06 us (2%)
    ppermute x9, starting transfers between devices, swap(): return lax.ppermute(value, axis, pairs)  14.4 us
    ppermute x9, waiting for transfers between devices, swap(): return lax.ppermute(value, axis, pairs)  13.2 us
    pallas_call x1, Pallas kernels, call_smooth(): pl.pallas_call(functools.partial(smooth_kernel, group), out_shape=jax.Sha...  5.23 us
    pallas_call x1, Pallas kernels, call_depth(): pl.pallas_call(depth_kernel, out_shape=(jax.ShapeDtypeStruct(partial.shap...  5.22 us
    ppermute x3, waiting for transfers between devices, exchange(): lax.ppermute(piece, 'depth', [(i, i ^ 2 * step) for i in range(count)])  4.73 us
    ppermute x3, starting transfers between devices, exchange(): lax.ppermute(piece, 'depth', [(i, i ^ 2 * step) for i in range(count)])  4.55 us
    pallas_call x1, Pallas kernels, call_interior(): pl.pallas_call(functools.partial(interior_kernel, scale), out_shape=jax.S...  4.19 us
    pallas_call x1, Pallas kernels, call_last_edge(): pl.pallas_call(functools.partial(last_edge_kernel, scale, split), out_sha...  3.43 us
  transfers between devices with their start and end apart: 12, of which 7 were waited for; matrix products, arithmetic and copies ran while one was open for 0% of the time, Pallas kernels for 33%

profile of v10, /device:TPU:0, one launch (start us, length us, event | category | flops | bytes accessed | tf_op | source)
XLA Modules:
  0.0 65.3 jit_solution(10947129459370480594)
XLA Ops:
  0.1 1.6 %pack_block.1 = s32[5,64,512]{2,1,0:T(8,128)S(1)} custom-call(s32[4]{0:T(128)S(1)} %pad_add_fusion.3.where, s32[32,64,512]{2,1,0:T(8,128)} %c.3), custom_call_target="tpu_custom_call" | custom-call | tf_op jit(solution)/shard_map/pack_block/pallas_call | solution.py:403
  1.7 0.7 %collective-permute-start.4 = (s32[5,64,512]{2,1,0:T(8,128)S(1)}, s32[5,64,512]{2,1,0:T(8,128)S(1)}, u32[]{:S(2)}, u32[]{:S(2)}) collective-permute-start(s32[5,64,512]{2,1,0:T(8,128)S(1)} %pack_block.1), channel_id=1, source_target_pairs={{1,2},{2,1},{3,4},{4,3},{5,6},{6,5},{9,10},{10,9},{11,12},{12,11},... | collective-permute-start | bytes 1966088 | tf_op jit(solution)/shard_map/ppermute | solution.py:542
  2.4 3.1 %pack_rest.1 = (s32[32,8,512]{2,1,0:T(8,128)}, s32[5,16,512]{2,1,0:T(8,128)S(1)}, s32[5,48,512]{2,1,0:T(8,128)}, s32[32,8,512]{2,1,0:T(8,128)}) custom-call(s32[4]{0:T(128)S(1)} %pad_add_fusion.3.where, s32[32,64,512]{2,1,0:T(8,128)} %c.3), custom_call_target="tpu_custom_call" | custom-call | tf_op jit(solution)/shard_map/pack_rest/pallas_call | solution.py:419
  5.6 0.6 collective-permute-start
  6.1 1.5 %collective-permute-start.1 = (s32[32,8,512]{2,1,0:T(8,128)}, s32[32,8,512]{2,1,0:T(8,128)}, u32[]{:S(2)}, u32[]{:S(2)}) collective-permute-start(s32[32,8,512]{2,1,0:T(8,128)} %get-tuple-element.17), channel_id=1, source_target_pairs={{8,16},{16,8},{9,17},{17,9},{10,18},{18,10},{11,19},{19,11},{12,20... | collective-permute-start | bytes 1572872 | tf_op jit(solution)/shard_map/ppermute | solution.py:542
  7.6 5.3 %collective-permute-start.3 = (s32[5,16,512]{2,1,0:T(8,128)S(1)}, s32[5,16,512]{2,1,0:T(8,128)S(1)}, u32[]{:S(2)}, u32[]{:S(2)}) collective-permute-start(s32[5,16,512]{2,1,0:T(8,128)S(1)} %get-tuple-element.21), channel_id=1, source_target_pairs={{0,1},{1,0},{2,3},{3,2},{4,5},{5,4},{6,7},{7,6},{8,9},{9,8},{10,11... | collective-permute-start | bytes 491528 | tf_op jit(solution)/shard_map/ppermute | solution.py:542
  13.0 5.2 %smooth.1.partial = f32[32,80,512]{2,1,0:T(8,128)S(1)} custom-call(s32[32,64,512]{2,1,0:T(8,128)} %c.3, bf16[1024,512]{1,0:T(8,128)(2,1)S(1)} %copy-done, bf16[80,192]{1,0:T(8,128)(2,1)S(1)} %copy-done.3), custom_call_target="tpu_custom_call" | custom-call | flops 1000000000 | bytes 4000000 | tf_op jit(solution)/shard_map/smooth/pallas_call | solution.py:434
  18.3 6.6 %collective-permute-done.3.edge = s32[5,16,512]{2,1,0:T(8,128)S(1)} collective-permute-done((s32[5,16,512]{2,1,0:T(8,128)S(1)}, s32[5,16,512]{2,1,0:T(8,128)S(1)}, u32[]{:S(2)}, u32[]{:S(2)}) %collective-permute-start.3) | collective-permute-done | bytes 163872 | tf_op jit(solution)/shard_map/ppermute | solution.py:542
  24.9 5.2 %depth.1 = (f32[32,80,512]{2,1,0:T(8,128)S(1)}, f32[24,80,512]{2,1,0:T(8,128)S(1)}) custom-call(f32[4]{0:T(128)S(1)} %add_convert_fusion.flags, s32[3]{0:T(128)S(1)} %pad_add_fusion.2.order, f32[32,80,512]{2,1,0:T(8,128)S(1)} %smooth.1.partial, s32[32,8,512]{2,1,0:T(8,128)S(1)} %collective-permute-done.xa, ...), custom_call_target="tpu_custom_call", output_to_operand_aliasing={{0}: (2, {})} | custom-call | flops 500000000 | bytes 4000000 | tf_op jit(solution)/shard_map/depth/pallas_call | solution.py:451
  30.2 0.7 %collective-permute-start.6 = (s32[10,8,512]{2,1,0:T(8,128)S(1)}, s32[10,8,512]{2,1,0:T(8,128)S(1)}, u32[]{:S(2)}, u32[]{:S(2)}) collective-permute-start(s32[10,8,512]{2,1,0:T(8,128)S(1)} %pad_add_fusion.1), channel_id=1, source_target_pairs={{8,16},{16,8},{9,17},{17,9},{10,18},{18,10},{11,19},{19,11},{12,20... | collective-permute-start | bytes 491528 | tf_op jit(solution)/shard_map/ppermute | solution.py:542
  30.9 4.2 %interior.1.behind = f32[4,64,512]{2,1,0:T(8,128)S(1)} custom-call(f32[24,80,512]{2,1,0:T(8,128)S(1)} %get-tuple-element.19.smoothed), custom_call_target="tpu_custom_call" | custom-call | flops 1000000000 | bytes 4000000 | tf_op jit(solution)/shard_map/interior/pallas_call | solution.py:468
  35.1 3.1 %collective-permute-start.5 = (s32[10,8,512]{2,1,0:T(8,128)S(1)}, s32[10,8,512]{2,1,0:T(8,128)S(1)}, u32[]{:S(2)}, u32[]{:S(2)}) collective-permute-start(s32[10,8,512]{2,1,0:T(8,128)S(1)} %pad_add_fusion), channel_id=1, source_target_pairs={{0,8},{8,0},{16,24},{24,16},{1,9},{9,1},{17,25},{25,17},{2,10},{10... | collective-permute-start | bytes 491528 | tf_op jit(solution)/shard_map/ppermute | solution.py:542
  38.3 1.0 %collective-permute-done.5 = s32[10,8,512]{2,1,0:T(8,128)S(1)} collective-permute-done((s32[10,8,512]{2,1,0:T(8,128)S(1)}, s32[10,8,512]{2,1,0:T(8,128)S(1)}, u32[]{:S(2)}, u32[]{:S(2)}) %collective-permute-start.5) | collective-permute-done | bytes 163872 | tf_op jit(solution)/shard_map/ppermute | solution.py:542
  39.3 3.0 %first_edge.1.behind = f32[4,64,512]{2,1,0:T(8,128)S(1)} custom-call(f32[4]{0:T(128)S(1)} %add_convert_fusion.flags, s32[3]{0:T(128)S(1)} %pad_add_fusion.2.order, f32[32,80,512]{2,1,0:T(8,128)S(1)} %get-tuple-element.18.plane, f32[24,80,512]{2,1,0:T(8,128)S(1)} %get-tuple-element.19.smoothed, s32[5,64,512]{2,1,0:T(8,128)S(1)} %collective-permute-done.4.block, ...), custom_call_target="tpu_custom_call" | custom-call | flops 300000000 | bytes 4000000 | tf_op jit(solution)/shard_map/first_edge/pallas_call | solution.py:482
  42.3 3.4 %last_edge.1 = (f32[2,4,8,512]{3,2,1,0:T(8,128)S(1)}, f32[2,4,8,512]{3,2,1,0:T(8,128)S(1)}, f32[7,80,512]{2,1,0:T(8,128)S(1)}) custom-call(f32[4]{0:T(128)S(1)} %add_convert_fusion.flags, s32[3]{0:T(128)S(1)} %pad_add_fusion.2.order, f32[32,80,512]{2,1,0:T(8,128)S(1)} %get-tuple-element.18.plane, f32[24,80,512]{2,1,0:T(8,128)S(1)} %get-tuple-element.19.smoothed, ...), custom_call_target="tpu_custom_call" | custom-call | flops 300000000 | bytes 4000000 | tf_op jit(solution)/shard_map/last_edge/pallas_call | solution.py:508
  45.7 2.5 %collective-permute-start.9 = (f32[2,4,8,512]{3,2,1,0:T(8,128)S(1)}, f32[2,4,8,512]{3,2,1,0:T(8,128)S(1)}, u32[]{:S(2)}, u32[]{:S(2)}) collective-permute-start(f32[2,4,8,512]{3,2,1,0:T(8,128)S(1)} %get-tuple-element.26), channel_id=1, source_target_pairs={{0,1},{1,0},{2,3},{3,2},{4,5},{5,4},{6,7},{7,6},{8,9},{9,8},{10,11... | collective-permute-start | bytes 393224 | tf_op jit(solution)/shard_map/ppermute | solution.py:542
  48.4 1.1 %kept_edge.1 = (f32[2,4,8,512]{3,2,1,0:T(8,128)S(1)}, f32[2,4,8,512]{3,2,1,0:T(8,128)S(1)}) custom-call(s32[3]{0:T(128)S(1)} %pad_add_fusion.2.order, f32[7,80,512]{2,1,0:T(8,128)S(1)} %get-tuple-element.22.ends, f32[4,64,512]{2,1,0:T(8,128)S(1)} %first_edge.1.behind), custom_call_target="tpu_custom_call" | custom-call | flops 200000000 | bytes 4000000 | tf_op jit(solution)/shard_map/kept_edge/pallas_call | solution.py:526
  49.5 3.1 %collective-permute-done.9 = f32[2,4,8,512]{3,2,1,0:T(8,128)S(1)} collective-permute-done((f32[2,4,8,512]{3,2,1,0:T(8,128)S(1)}, f32[2,4,8,512]{3,2,1,0:T(8,128)S(1)}, u32[]{:S(2)}, u32[]{:S(2)}) %collective-permute-start.9) | collective-permute-done | bytes 131104 | tf_op jit(solution)/shard_map/ppermute | solution.py:542
  52.6 2.5 %collective-permute-done.7 = f32[2,4,8,512]{3,2,1,0:T(8,128)S(1)} collective-permute-done((f32[2,4,8,512]{3,2,1,0:T(8,128)S(1)}, f32[2,4,8,512]{3,2,1,0:T(8,128)S(1)}, u32[]{:S(2)}, u32[]{:S(2)}) %collective-permute-start.7) | collective-permute-done | bytes 131104 | tf_op jit(solution)/shard_map/ppermute | solution.py:542
  55.2 2.9 %collective-permute-start.10 = (f32[4,8,512]{2,1,0:T(8,128)S(1)}, f32[4,8,512]{2,1,0:T(8,128)S(1)}, u32[]{:S(2)}, u32[]{:S(2)}) collective-permute-start(f32[4,8,512]{2,1,0:T(8,128)S(1)} %get-tuple-element.44), channel_id=1, source_target_pairs={{0,4},{1,5},{2,6},{3,7},{4,0},{5,1},{6,2},{7,3},{8,12},{9,13},{10,... | collective-permute-start | bytes 196616 | tf_op jit(solution)/shard_map/ppermute | solution.py:581
  58.1 1.3 %collective-permute-start.11 = (f32[4,8,512]{2,1,0:T(8,128)S(1)}, f32[4,8,512]{2,1,0:T(8,128)S(1)}, u32[]{:S(2)}, u32[]{:S(2)}) collective-permute-start(f32[4,8,512]{2,1,0:T(8,128)S(1)} %get-tuple-element.45), channel_id=1, source_target_pairs={{0,6},{1,7},{2,4},{3,5},{4,2},{5,3},{6,0},{7,1},{8,14},{9,15},{10,... | collective-permute-start | bytes 196616 | tf_op jit(solution)/shard_map/ppermute | solution.py:581
  59.8 1.2 %collective-permute-done.10 = f32[4,8,512]{2,1,0:T(8,128)S(1)} collective-permute-done((f32[4,8,512]{2,1,0:T(8,128)S(1)}, f32[4,8,512]{2,1,0:T(8,128)S(1)}, u32[]{:S(2)}, u32[]{:S(2)}) %collective-permute-start.10) | collective-permute-done | bytes 65568 | tf_op jit(solution)/shard_map/ppermute | solution.py:581
  61.0 3.3 %collective-permute-done.11 = f32[4,8,512]{2,1,0:T(8,128)S(1)} collective-permute-done((f32[4,8,512]{2,1,0:T(8,128)S(1)}, f32[4,8,512]{2,1,0:T(8,128)S(1)}, u32[]{:S(2)}, u32[]{:S(2)}) %collective-permute-start.11) | collective-permute-done | bytes 65568 | tf_op jit(solution)/shard_map/ppermute | solution.py:581
  64.6 0.6 pad_maximum_fusion.4
  (37 shorter events, 1.2 us)
Async XLA Ops:
  0.1 12.9 %copy-start = (bf16[1024,512]{1,0:T(8,128)(2,1)S(1)}, bf16[1024,512]{1,0:T(8,128)(2,1)}, u32[]{:S(2)}) copy-start(bf16[1024,512]{1,0:T(8,128)(2,1)} %constant.71.clone.by) | copy-start | bytes 3145732
  0.1 12.9 %copy-start.3 = (bf16[80,192]{1,0:T(8,128)(2,1)S(1)}, bf16[80,192]{1,0:T(8,128)(2,1)}, u32[]{:S(2)}) copy-start(bf16[80,192]{1,0:T(8,128)(2,1)} %constant.73.clone.lx) | copy-start | bytes 92164
  1.7 28.5 %collective-permute-start.4 = (s32[5,64,512]{2,1,0:T(8,128)S(1)}, s32[5,64,512]{2,1,0:T(8,128)S(1)}, u32[]{:S(2)}, u32[]{:S(2)}) collective-permute-start(s32[5,64,512]{2,1,0:T(8,128)S(1)} %pack_block.1), channel_id=1, source_target_pairs={{1,2},{2,1},{3,4},{4,3},{5,6},{6,5},{9,10},{10,9},{11,12},{12,11},... | collective-permute-start | bytes 1966088 | tf_op jit(solution)/shard_map/ppermute | solution.py:542
  5.6 19.3 %collective-permute-start = (s32[32,8,512]{2,1,0:T(8,128)}, s32[32,8,512]{2,1,0:T(8,128)S(1)}, u32[]{:S(2)}, u32[]{:S(2)}) collective-permute-start(s32[32,8,512]{2,1,0:T(8,128)} %get-tuple-element.16), channel_id=1, source_target_pairs={{0,8},{8,0},{16,24},{24,16},{1,9},{9,1},{17,25},{25,17},{2,10},{10... | collective-permute-start | bytes 1572872 | tf_op jit(solution)/shard_map/ppermute | solution.py:542
  6.1 18.8 %collective-permute-start.1 = (s32[32,8,512]{2,1,0:T(8,128)}, s32[32,8,512]{2,1,0:T(8,128)}, u32[]{:S(2)}, u32[]{:S(2)}) collective-permute-start(s32[32,8,512]{2,1,0:T(8,128)} %get-tuple-element.17), channel_id=1, source_target_pairs={{8,16},{16,8},{9,17},{17,9},{10,18},{18,10},{11,19},{19,11},{12,20... | collective-permute-start | bytes 1572872 | tf_op jit(solution)/shard_map/ppermute | solution.py:542
  7.6 17.3 %collective-permute-start.3 = (s32[5,16,512]{2,1,0:T(8,128)S(1)}, s32[5,16,512]{2,1,0:T(8,128)S(1)}, u32[]{:S(2)}, u32[]{:S(2)}) collective-permute-start(s32[5,16,512]{2,1,0:T(8,128)S(1)} %get-tuple-element.21), channel_id=1, source_target_pairs={{0,1},{1,0},{2,3},{3,2},{4,5},{5,4},{6,7},{7,6},{8,9},{9,8},{10,11... | collective-permute-start | bytes 491528 | tf_op jit(solution)/shard_map/ppermute | solution.py:542
  12.9 29.4 %collective-permute-start.2 = (s32[5,48,512]{2,1,0:T(8,128)}, s32[5,48,512]{2,1,0:T(8,128)}, u32[]{:S(2)}, u32[]{:S(2)}) collective-permute-start(s32[5,48,512]{2,1,0:T(8,128)} %get-tuple-element.20), channel_id=1, source_target_pairs={{0,1},{1,0},{2,3},{3,2},{4,5},{5,4},{6,7},{7,6},{8,9},{9,8},{10,11... | collective-permute-start | bytes 1474568 | tf_op jit(solution)/shard_map/ppermute | solution.py:542
  13.0 12.0 %copy-start.2 = (bf16[2,128,192]{2,1,0:T(8,128)(2,1)S(1)}, bf16[2,128,192]{2,1,0:T(8,128)(2,1)}, u32[]{:S(2)}) copy-start(bf16[2,128,192]{2,1,0:T(8,128)(2,1)} %constant.74.clone.lx) | copy-start | bytes 294916
  30.2 9.1 %copy-start.1 = (bf16[2,80,240]{2,1,0:T(8,128)(2,1)S(1)}, bf16[2,80,240]{2,1,0:T(8,128)(2,1)}, u32[]{:S(2)}) copy-start(bf16[2,80,240]{2,1,0:T(8,128)(2,1)} %constant.72.clone.lx) | copy-start | bytes 230404
  30.2 8.0 %collective-permute-start.6 = (s32[10,8,512]{2,1,0:T(8,128)S(1)}, s32[10,8,512]{2,1,0:T(8,128)S(1)}, u32[]{:S(2)}, u32[]{:S(2)}) collective-permute-start(s32[10,8,512]{2,1,0:T(8,128)S(1)} %pad_add_fusion.1), channel_id=1, source_target_pairs={{8,16},{16,8},{9,17},{17,9},{10,18},{18,10},{11,19},{19,11},{12,20... | collective-permute-start | bytes 491528 | tf_op jit(solution)/shard_map/ppermute | solution.py:542
  35.1 4.2 %collective-permute-start.5 = (s32[10,8,512]{2,1,0:T(8,128)S(1)}, s32[10,8,512]{2,1,0:T(8,128)S(1)}, u32[]{:S(2)}, u32[]{:S(2)}) collective-permute-start(s32[10,8,512]{2,1,0:T(8,128)S(1)} %pad_add_fusion), channel_id=1, source_target_pairs={{0,8},{8,0},{16,24},{24,16},{1,9},{9,1},{17,25},{25,17},{2,10},{10... | collective-permute-start | bytes 491528 | tf_op jit(solution)/shard_map/ppermute | solution.py:542
  45.7 6.9 %collective-permute-start.9 = (f32[2,4,8,512]{3,2,1,0:T(8,128)S(1)}, f32[2,4,8,512]{3,2,1,0:T(8,128)S(1)}, u32[]{:S(2)}, u32[]{:S(2)}) collective-permute-start(f32[2,4,8,512]{3,2,1,0:T(8,128)S(1)} %get-tuple-element.26), channel_id=1, source_target_pairs={{0,1},{1,0},{2,3},{3,2},{4,5},{5,4},{6,7},{7,6},{8,9},{9,8},{10,11... | collective-permute-start | bytes 393224 | tf_op jit(solution)/shard_map/ppermute | solution.py:542
  48.3 6.8 %collective-permute-start.7 = (f32[2,4,8,512]{3,2,1,0:T(8,128)S(1)}, f32[2,4,8,512]{3,2,1,0:T(8,128)S(1)}, u32[]{:S(2)}, u32[]{:S(2)}) collective-permute-start(f32[2,4,8,512]{3,2,1,0:T(8,128)S(1)} %get-tuple-element.24), channel_id=1, source_target_pairs={{0,1},{1,0},{2,3},{3,2},{4,5},{5,4},{6,7},{7,6},{8,9},{9,8},{10,11... | collective-permute-start | bytes 393224 | tf_op jit(solution)/shard_map/ppermute | solution.py:542
  55.2 5.7 %collective-permute-start.10 = (f32[4,8,512]{2,1,0:T(8,128)S(1)}, f32[4,8,512]{2,1,0:T(8,128)S(1)}, u32[]{:S(2)}, u32[]{:S(2)}) collective-permute-start(f32[4,8,512]{2,1,0:T(8,128)S(1)} %get-tuple-element.44), channel_id=1, source_target_pairs={{0,4},{1,5},{2,6},{3,7},{4,0},{5,1},{6,2},{7,3},{8,12},{9,13},{10,... | collective-permute-start | bytes 196616 | tf_op jit(solution)/shard_map/ppermute | solution.py:581
  58.1 6.2 %collective-permute-start.11 = (f32[4,8,512]{2,1,0:T(8,128)S(1)}, f32[4,8,512]{2,1,0:T(8,128)S(1)}, u32[]{:S(2)}, u32[]{:S(2)}) collective-permute-start(f32[4,8,512]{2,1,0:T(8,128)S(1)} %get-tuple-element.45), channel_id=1, source_target_pairs={{0,6},{1,7},{2,4},{3,5},{4,2},{5,3},{6,0},{7,1},{8,14},{9,15},{10,... | collective-permute-start | bytes 196616 | tf_op jit(solution)/shard_map/ppermute | solution.py:581
  59.5 5.0 %collective-permute-start.8 = (f32[4,8,512]{2,1,0:T(8,128)S(1)}, f32[4,8,512]{2,1,0:T(8,128)S(1)}, u32[]{:S(2)}, u32[]{:S(2)}) collective-permute-start(f32[4,8,512]{2,1,0:T(8,128)S(1)} %slice_bitcast_fusion.2), channel_id=1, source_target_pairs={{0,2},{1,3},{2,0},{3,1},{4,6},{5,7},{6,4},{7,5},{8,10},{9,11},{10,... | collective-permute-start | bytes 196616 | tf_op jit(solution)/shard_map/ppermute | solution.py:581

commit v11 on v10

--- a/solution.py
+++ b/solution.py
@@ -237,7 +237,7 @@
 
 def depth_kernel(flags, order, partial, xa, xb, by, lx, plane, smoothed):
     layers, ext, _ = plane.shape
-    group = 2 * SIDE_GROUP
+    group = 4 * SIDE_GROUP
     edge = 2 * PAD
     sides = lx[order[0]]
 
@@ -245,7 +245,7 @@
         first = g * group
         counts = [jnp.concatenate([xa[first + n], xb[first + n]], 0) for n in range(group)]
         high, low = column_terms(counts, by)
-        for half in range(2):
+        for half in range(4):
             part = slice(half * SIDE_GROUP * edge, (half + 1) * SIDE_GROUP * edge)
             added = row_product(sides, high[part], low[part])
             for n in range(SIDE_GROUP):
@@ -352,11 +352,10 @@
     edge_render(scale, order[1] == 0, ends, behind, image, tiles, lambda place: place)
 
 
-def render_halves(scale, is_front, ends, behind, images, tile_of):
-    for n, image in enumerate(images):
-        places, _, owned, _ = image.shape
-        tiles = places * (owned // 8)
-        edge_render(scale, is_front, ends, behind, image, tiles, tile_of, n * tiles)
+def render_half(scale, is_front, ends, behind, image, tile_of, half):
+    places, _, owned, _ = image.shape
+    tiles = places * (owned // 8)
+    edge_render(scale, is_front, ends, behind, image, tiles, tile_of, half * tiles)
 
 
 def last_edge_kernel(scale, split, flags, order, plane, smoothed, middle_any, edge, ca, cb,
@@ -367,15 +366,16 @@
     edge_smooth(0, flags, order, plane, smoothed, tile, ca, cb, by, lx, ends, halo)
     if split:
         tile_of = half_tiles(order, *split, 1 - order[1])
-        render_halves(scale, order[1] == 1, ends, behind, images, tile_of)
+        for half, image in enumerate(images):
+            render_half(scale, order[1] == 1, ends, behind, image, tile_of, half)
     else:
         tiles = plane.shape[1] // 8 - 2
         edge_render(scale, order[1] == 1, ends, behind, images[0], tiles, lambda place: place)
 
 
-def kept_edge_kernel(scale, split, order, ends, behind, *images):
+def kept_edge_kernel(scale, split, half, order, ends, behind, image):
     tile_of = half_tiles(order, *split, order[1])
-    render_halves(scale, order[1] == 1, ends, behind, images, tile_of)
+    render_half(scale, order[1] == 1, ends, behind, image, tile_of, half)
 
 
 def whole(count):
@@ -521,16 +521,15 @@
     )(flags, order, plane, *operands)
 
 
-def call_kept_edge(scale, split, order, ends, behind):
+def call_kept_edge(scale, split, half, order, ends, behind):
     image = jax.ShapeDtypeStruct(half_shape(split, ends.shape[2]), jnp.float32)
     return pl.pallas_call(
-        functools.partial(kept_edge_kernel, scale, split),
-        out_shape=(image, image),
+        functools.partial(kept_edge_kernel, scale, split, half),
+        out_shape=image,
         in_specs=[smem()] + whole(2),
-        out_specs=tuple(whole(2)),
+        out_specs=whole(1)[0],
         compiler_params=params(12),
         cost_estimate=cost(200_000_000),
-        name="kept_edge",
     )(order, ends, behind)
 
 
@@ -642,7 +641,7 @@
         scale, split, *common, mid_a, edge_a, ca[:REACH], cb[:REACH], by, lx, layers
     )
     if split:
-        keeps = call_kept_edge(scale, split, order, ends, layers)
+        keeps = [call_kept_edge(scale, split, half, order, ends, layers) for half in range(2)]
     else:
         sends, keeps = halves_of(sends[0])
     return exchange(sends, keeps)

time: 65.6 us -> 62.7 us (0.956)
  waiting for transfers between devices: 18 us -> 14.9 us
    ppermute x9, waiting for transfers between devices: 13.2 us -> 10.2 us  [swap(): return lax.ppermute(value, axis, pairs)]
    pallas_call x1, Pallas kernels: 5.22 us -> 4.54 us  [call_depth(): pl.pallas_call(depth_kernel, out_shape=(jax.ShapeDtypeStruct(partial.shap...]
    pallas_call x1 -> x2, Pallas kernels: 1.13 us -> 1.68 us  [call_kept_edge(): pl.pallas_call(functools.partial(kept_edge_kernel, scale, split, half), o...]
  transfers between devices with their start and end apart: 12 -> 12, of which waited for: 7 -> 6; matrix products, arithmetic and copies ran while one was open for 0% -> 1% of each run, Pallas kernels for 33% -> 35%
where the time goes in v11:
time: 62.7 us; the launch traced here: 62.4 us
  Pallas kernels  26.8 us (43%)
  starting transfers between devices  19.3 us (31%)
  waiting for transfers between devices  14.9 us (24%)
  other arithmetic  1.06 us (2%)
    ppermute x9, starting transfers between devices, swap(): return lax.ppermute(value, axis, pairs)  14.5 us
    ppermute x9, waiting for transfers between devices, swap(): return lax.ppermute(value, axis, pairs)  10.2 us
    pallas_call x1, Pallas kernels, call_smooth(): pl.pallas_call(functools.partial(smooth_kernel, group), out_shape=jax.Sha...  5.23 us
    ppermute x3, starting transfers between devices, exchange(): lax.ppermute(piece, 'depth', [(i, i ^ 2 * step) for i in range(count)])  4.82 us
    ppermute x3, waiting for transfers between devices, exchange(): lax.ppermute(piece, 'depth', [(i, i ^ 2 * step) for i in range(count)])  4.74 us
    pallas_call x1, Pallas kernels, call_depth(): pl.pallas_call(depth_kernel, out_shape=(jax.ShapeDtypeStruct(partial.shap...  4.54 us
    pallas_call x1, Pallas kernels, call_interior(): pl.pallas_call(functools.partial(interior_kernel, scale), out_shape=jax.S...  4.19 us
    pallas_call x1, Pallas kernels, call_last_edge(): pl.pallas_call(functools.partial(last_edge_kernel, scale, split), out_sha...  3.43 us
  transfers between devices with their start and end apart: 12, of which 6 were waited for; matrix products, arithmetic and copies ran while one was open for 1% of the time, Pallas kernels for 35%

profile of v11, /device:TPU:0, one launch (start us, length us, event | category | flops | bytes accessed | tf_op | source)
XLA Modules:
  0.0 62.4 jit_solution(17360718351496041273)
XLA Ops:
  0.1 1.6 %pack_block.1 = s32[5,64,512]{2,1,0:T(8,128)S(1)} custom-call(s32[4]{0:T(128)S(1)} %pad_add_fusion.3.where, s32[32,64,512]{2,1,0:T(8,128)} %c.3), custom_call_target="tpu_custom_call" | custom-call | tf_op jit(solution)/shard_map/pack_block/pallas_call | solution.py:403
  1.7 0.7 %collective-permute-start.4 = (s32[5,64,512]{2,1,0:T(8,128)S(1)}, s32[5,64,512]{2,1,0:T(8,128)S(1)}, u32[]{:S(2)}, u32[]{:S(2)}) collective-permute-start(s32[5,64,512]{2,1,0:T(8,128)S(1)} %pack_block.1), channel_id=1, source_target_pairs={{1,2},{2,1},{3,4},{4,3},{5,6},{6,5},{9,10},{10,9},{11,12},{12,11},... | collective-permute-start | bytes 1966088 | tf_op jit(solution)/shard_map/ppermute | solution.py:541
  2.4 3.1 %pack_rest.1 = (s32[32,8,512]{2,1,0:T(8,128)}, s32[5,16,512]{2,1,0:T(8,128)S(1)}, s32[5,48,512]{2,1,0:T(8,128)}, s32[32,8,512]{2,1,0:T(8,128)}) custom-call(s32[4]{0:T(128)S(1)} %pad_add_fusion.3.where, s32[32,64,512]{2,1,0:T(8,128)} %c.3), custom_call_target="tpu_custom_call" | custom-call | tf_op jit(solution)/shard_map/pack_rest/pallas_call | solution.py:419
  5.6 0.6 collective-permute-start
  6.1 1.5 %collective-permute-start.1 = (s32[32,8,512]{2,1,0:T(8,128)}, s32[32,8,512]{2,1,0:T(8,128)}, u32[]{:S(2)}, u32[]{:S(2)}) collective-permute-start(s32[32,8,512]{2,1,0:T(8,128)} %get-tuple-element.15), channel_id=1, source_target_pairs={{8,16},{16,8},{9,17},{17,9},{10,18},{18,10},{11,19},{19,11},{12,20... | collective-permute-start | bytes 1572872 | tf_op jit(solution)/shard_map/ppermute | solution.py:541
  7.6 5.3 %collective-permute-start.3 = (s32[5,16,512]{2,1,0:T(8,128)S(1)}, s32[5,16,512]{2,1,0:T(8,128)S(1)}, u32[]{:S(2)}, u32[]{:S(2)}) collective-permute-start(s32[5,16,512]{2,1,0:T(8,128)S(1)} %get-tuple-element.19), channel_id=1, source_target_pairs={{0,1},{1,0},{2,3},{3,2},{4,5},{5,4},{6,7},{7,6},{8,9},{9,8},{10,11... | collective-permute-start | bytes 491528 | tf_op jit(solution)/shard_map/ppermute | solution.py:541
  13.0 5.2 %smooth.1.partial = f32[32,80,512]{2,1,0:T(8,128)S(1)} custom-call(s32[32,64,512]{2,1,0:T(8,128)} %c.3, bf16[1024,512]{1,0:T(8,128)(2,1)S(1)} %copy-done, bf16[80,192]{1,0:T(8,128)(2,1)S(1)} %copy-done.3), custom_call_target="tpu_custom_call" | custom-call | flops 1000000000 | bytes 4000000 | tf_op jit(solution)/shard_map/smooth/pallas_call | solution.py:434
  18.3 6.6 %collective-permute-done.3.edge = s32[5,16,512]{2,1,0:T(8,128)S(1)} collective-permute-done((s32[5,16,512]{2,1,0:T(8,128)S(1)}, s32[5,16,512]{2,1,0:T(8,128)S(1)}, u32[]{:S(2)}, u32[]{:S(2)}) %collective-permute-start.3) | collective-permute-done | bytes 163872 | tf_op jit(solution)/shard_map/ppermute | solution.py:541
  24.9 4.5 %depth.1 = (f32[32,80,512]{2,1,0:T(8,128)S(1)}, f32[24,80,512]{2,1,0:T(8,128)S(1)}) custom-call(f32[4]{0:T(128)S(1)} %add_convert_fusion.flags, s32[3]{0:T(128)S(1)} %pad_add_fusion.2.order, f32[32,80,512]{2,1,0:T(8,128)S(1)} %smooth.1.partial, s32[32,8,512]{2,1,0:T(8,128)S(1)} %collective-permute-done.xa, ...), custom_call_target="tpu_custom_call", output_to_operand_aliasing={{0}: (2, {})} | custom-call | flops 500000000 | bytes 4000000 | tf_op jit(solution)/shard_map/depth/pallas_call | solution.py:451
  29.6 0.7 %collective-permute-start.6 = (s32[10,8,512]{2,1,0:T(8,128)S(1)}, s32[10,8,512]{2,1,0:T(8,128)S(1)}, u32[]{:S(2)}, u32[]{:S(2)}) collective-permute-start(s32[10,8,512]{2,1,0:T(8,128)S(1)} %pad_add_fusion.1), channel_id=1, source_target_pairs={{8,16},{16,8},{9,17},{17,9},{10,18},{18,10},{11,19},{19,11},{12,20... | collective-permute-start | bytes 491528 | tf_op jit(solution)/shard_map/ppermute | solution.py:541
  30.2 4.2 %interior.1.behind = f32[4,64,512]{2,1,0:T(8,128)S(1)} custom-call(f32[24,80,512]{2,1,0:T(8,128)S(1)} %get-tuple-element.17.smoothed), custom_call_target="tpu_custom_call" | custom-call | flops 1000000000 | bytes 4000000 | tf_op jit(solution)/shard_map/interior/pallas_call | solution.py:468
  34.4 3.1 %collective-permute-start.5 = (s32[10,8,512]{2,1,0:T(8,128)S(1)}, s32[10,8,512]{2,1,0:T(8,128)S(1)}, u32[]{:S(2)}, u32[]{:S(2)}) collective-permute-start(s32[10,8,512]{2,1,0:T(8,128)S(1)} %pad_add_fusion), channel_id=1, source_target_pairs={{0,8},{8,0},{16,24},{24,16},{1,9},{9,1},{17,25},{25,17},{2,10},{10... | collective-permute-start | bytes 491528 | tf_op jit(solution)/shard_map/ppermute | solution.py:541
  37.6 1.0 %collective-permute-done.5 = s32[10,8,512]{2,1,0:T(8,128)S(1)} collective-permute-done((s32[10,8,512]{2,1,0:T(8,128)S(1)}, s32[10,8,512]{2,1,0:T(8,128)S(1)}, u32[]{:S(2)}, u32[]{:S(2)}) %collective-permute-start.5) | collective-permute-done | bytes 163872 | tf_op jit(solution)/shard_map/ppermute | solution.py:541
  38.6 3.0 %first_edge.1.behind = f32[4,64,512]{2,1,0:T(8,128)S(1)} custom-call(f32[4]{0:T(128)S(1)} %add_convert_fusion.flags, s32[3]{0:T(128)S(1)} %pad_add_fusion.2.order, f32[32,80,512]{2,1,0:T(8,128)S(1)} %get-tuple-element.16.plane, f32[24,80,512]{2,1,0:T(8,128)S(1)} %get-tuple-element.17.smoothed, s32[5,64,512]{2,1,0:T(8,128)S(1)} %collective-permute-done.4.block, ...), custom_call_target="tpu_custom_call" | custom-call | flops 300000000 | bytes 4000000 | tf_op jit(solution)/shard_map/first_edge/pallas_call | solution.py:482
  41.6 3.4 %last_edge.1 = (f32[2,4,8,512]{3,2,1,0:T(8,128)S(1)}, f32[2,4,8,512]{3,2,1,0:T(8,128)S(1)}, f32[7,80,512]{2,1,0:T(8,128)S(1)}) custom-call(f32[4]{0:T(128)S(1)} %add_convert_fusion.flags, s32[3]{0:T(128)S(1)} %pad_add_fusion.2.order, f32[32,80,512]{2,1,0:T(8,128)S(1)} %get-tuple-element.16.plane, f32[24,80,512]{2,1,0:T(8,128)S(1)} %get-tuple-element.17.smoothed, ...), custom_call_target="tpu_custom_call" | custom-call | flops 300000000 | bytes 4000000 | tf_op jit(solution)/shard_map/last_edge/pallas_call | solution.py:508
  45.0 2.6 %collective-permute-start.9 = (f32[2,4,8,512]{3,2,1,0:T(8,128)S(1)}, f32[2,4,8,512]{3,2,1,0:T(8,128)S(1)}, u32[]{:S(2)}, u32[]{:S(2)}) collective-permute-start(f32[2,4,8,512]{3,2,1,0:T(8,128)S(1)} %get-tuple-element.22), channel_id=1, source_target_pairs={{0,1},{1,0},{2,3},{3,2},{4,5},{5,4},{6,7},{7,6},{8,9},{9,8},{10,11... | collective-permute-start | bytes 393224 | tf_op jit(solution)/shard_map/ppermute | solution.py:541
  47.7 0.8 %shard_map.56 = f32[2,4,8,512]{3,2,1,0:T(8,128)S(1)} custom-call(s32[3]{0:T(128)S(1)} %pad_add_fusion.2.order, f32[7,80,512]{2,1,0:T(8,128)S(1)} %get-tuple-element.20.ends, f32[4,64,512]{2,1,0:T(8,128)S(1)} %first_edge.1.behind), custom_call_target="tpu_custom_call" | custom-call | flops 200000000 | bytes 4000000 | tf_op jit(solution)/shard_map/pallas_call | solution.py:526
  48.5 0.8 %shard_map.55 = f32[2,4,8,512]{3,2,1,0:T(8,128)S(1)} custom-call(s32[3]{0:T(128)S(1)} %pad_add_fusion.2.order, f32[7,80,512]{2,1,0:T(8,128)S(1)} %get-tuple-element.20.ends, f32[4,64,512]{2,1,0:T(8,128)S(1)} %first_edge.1.behind), custom_call_target="tpu_custom_call" | custom-call | flops 200000000 | bytes 4000000 | tf_op jit(solution)/shard_map/pallas_call | solution.py:526
  49.4 2.6 %collective-permute-done.9 = f32[2,4,8,512]{3,2,1,0:T(8,128)S(1)} collective-permute-done((f32[2,4,8,512]{3,2,1,0:T(8,128)S(1)}, f32[2,4,8,512]{3,2,1,0:T(8,128)S(1)}, u32[]{:S(2)}, u32[]{:S(2)}) %collective-permute-start.9) | collective-permute-done | bytes 131104 | tf_op jit(solution)/shard_map/ppermute | solution.py:541
  52.0 3.2 %collective-permute-start.10 = (f32[4,8,512]{2,1,0:T(8,128)S(1)}, f32[4,8,512]{2,1,0:T(8,128)S(1)}, u32[]{:S(2)}, u32[]{:S(2)}) collective-permute-start(f32[4,8,512]{2,1,0:T(8,128)S(1)} %get-tuple-element.40), channel_id=1, source_target_pairs={{0,4},{1,5},{2,6},{3,7},{4,0},{5,1},{6,2},{7,3},{8,12},{9,13},{10,... | collective-permute-start | bytes 196616 | tf_op jit(solution)/shard_map/ppermute | solution.py:580
  55.2 1.3 %collective-permute-start.11 = (f32[4,8,512]{2,1,0:T(8,128)S(1)}, f32[4,8,512]{2,1,0:T(8,128)S(1)}, u32[]{:S(2)}, u32[]{:S(2)}) collective-permute-start(f32[4,8,512]{2,1,0:T(8,128)S(1)} %get-tuple-element.41), channel_id=1, source_target_pairs={{0,6},{1,7},{2,4},{3,5},{4,2},{5,3},{6,0},{7,1},{8,14},{9,15},{10,... | collective-permute-start | bytes 196616 | tf_op jit(solution)/shard_map/ppermute | solution.py:580
  56.9 0.5 collective-permute-done.10
  57.5 3.9 %collective-permute-done.11 = f32[4,8,512]{2,1,0:T(8,128)S(1)} collective-permute-done((f32[4,8,512]{2,1,0:T(8,128)S(1)}, f32[4,8,512]{2,1,0:T(8,128)S(1)}, u32[]{:S(2)}, u32[]{:S(2)}) %collective-permute-start.11) | collective-permute-done | bytes 65568 | tf_op jit(solution)/shard_map/ppermute | solution.py:580
  61.8 0.6 %pad_maximum_fusion.4 = f32[4,8,512]{2,1,0:T(8,128)} fusion(f32[1,8,512]{2,1,0:T(8,128)S(1)} %get-tuple-element.26, f32[1,8,512]{2,1,0:T(8,128)S(1)} %get-tuple-element.50, f32[1,8,512]{2,1,0:T(8,128)S(1)} %get-tuple-element.49, f32[1,8,512]{2,1,0:T(8,128)S(1)} %get-tuple-element.48), kind=kLoop, calls=%fused_computation.15 | loop fusion | flops 49152 | bytes 131072 | tf_op jit(solution)/shard_map/concatenate | solution.py:593
  (39 shorter events, 1.2 us)
Async XLA Ops:
  0.1 12.9 %copy-start = (bf16[1024,512]{1,0:T(8,128)(2,1)S(1)}, bf16[1024,512]{1,0:T(8,128)(2,1)}, u32[]{:S(2)}) copy-start(bf16[1024,512]{1,0:T(8,128)(2,1)} %constant.71.clone.by) | copy-start | bytes 3145732
  0.1 12.9 %copy-start.3 = (bf16[80,192]{1,0:T(8,128)(2,1)S(1)}, bf16[80,192]{1,0:T(8,128)(2,1)}, u32[]{:S(2)}) copy-start(bf16[80,192]{1,0:T(8,128)(2,1)} %constant.73.clone.lx) | copy-start | bytes 92164
  1.7 27.8 %collective-permute-start.4 = (s32[5,64,512]{2,1,0:T(8,128)S(1)}, s32[5,64,512]{2,1,0:T(8,128)S(1)}, u32[]{:S(2)}, u32[]{:S(2)}) collective-permute-start(s32[5,64,512]{2,1,0:T(8,128)S(1)} %pack_block.1), channel_id=1, source_target_pairs={{1,2},{2,1},{3,4},{4,3},{5,6},{6,5},{9,10},{10,9},{11,12},{12,11},... | collective-permute-start | bytes 1966088 | tf_op jit(solution)/shard_map/ppermute | solution.py:541
  5.6 19.3 %collective-permute-start = (s32[32,8,512]{2,1,0:T(8,128)}, s32[32,8,512]{2,1,0:T(8,128)S(1)}, u32[]{:S(2)}, u32[]{:S(2)}) collective-permute-start(s32[32,8,512]{2,1,0:T(8,128)} %get-tuple-element.14), channel_id=1, source_target_pairs={{0,8},{8,0},{16,24},{24,16},{1,9},{9,1},{17,25},{25,17},{2,10},{10... | collective-permute-start | bytes 1572872 | tf_op jit(solution)/shard_map/ppermute | solution.py:541
  6.1 18.8 %collective-permute-start.1 = (s32[32,8,512]{2,1,0:T(8,128)}, s32[32,8,512]{2,1,0:T(8,128)}, u32[]{:S(2)}, u32[]{:S(2)}) collective-permute-start(s32[32,8,512]{2,1,0:T(8,128)} %get-tuple-element.15), channel_id=1, source_target_pairs={{8,16},{16,8},{9,17},{17,9},{10,18},{18,10},{11,19},{19,11},{12,20... | collective-permute-start | bytes 1572872 | tf_op jit(solution)/shard_map/ppermute | solution.py:541
  7.6 17.3 %collective-permute-start.3 = (s32[5,16,512]{2,1,0:T(8,128)S(1)}, s32[5,16,512]{2,1,0:T(8,128)S(1)}, u32[]{:S(2)}, u32[]{:S(2)}) collective-permute-start(s32[5,16,512]{2,1,0:T(8,128)S(1)} %get-tuple-element.19), channel_id=1, source_target_pairs={{0,1},{1,0},{2,3},{3,2},{4,5},{5,4},{6,7},{7,6},{8,9},{9,8},{10,11... | collective-permute-start | bytes 491528 | tf_op jit(solution)/shard_map/ppermute | solution.py:541
  12.9 28.7 %collective-permute-start.2 = (s32[5,48,512]{2,1,0:T(8,128)}, s32[5,48,512]{2,1,0:T(8,128)}, u32[]{:S(2)}, u32[]{:S(2)}) collective-permute-start(s32[5,48,512]{2,1,0:T(8,128)} %get-tuple-element.18), channel_id=1, source_target_pairs={{0,1},{1,0},{2,3},{3,2},{4,5},{5,4},{6,7},{7,6},{8,9},{9,8},{10,11... | collective-permute-start | bytes 1474568 | tf_op jit(solution)/shard_map/ppermute | solution.py:541
  13.0 12.0 %copy-start.2 = (bf16[2,128,192]{2,1,0:T(8,128)(2,1)S(1)}, bf16[2,128,192]{2,1,0:T(8,128)(2,1)}, u32[]{:S(2)}) copy-start(bf16[2,128,192]{2,1,0:T(8,128)(2,1)} %constant.74.clone.lx) | copy-start | bytes 294916
  29.5 9.1 %copy-start.1 = (bf16[2,80,240]{2,1,0:T(8,128)(2,1)S(1)}, bf16[2,80,240]{2,1,0:T(8,128)(2,1)}, u32[]{:S(2)}) copy-start(bf16[2,80,240]{2,1,0:T(8,128)(2,1)} %constant.72.clone.lx) | copy-start | bytes 230404
  29.6 8.0 %collective-permute-start.6 = (s32[10,8,512]{2,1,0:T(8,128)S(1)}, s32[10,8,512]{2,1,0:T(8,128)S(1)}, u32[]{:S(2)}, u32[]{:S(2)}) collective-permute-start(s32[10,8,512]{2,1,0:T(8,128)S(1)} %pad_add_fusion.1), channel_id=1, source_target_pairs={{8,16},{16,8},{9,17},{17,9},{10,18},{18,10},{11,19},{19,11},{12,20... | collective-permute-start | bytes 491528 | tf_op jit(solution)/shard_map/ppermute | solution.py:541
  34.4 4.2 %collective-permute-start.5 = (s32[10,8,512]{2,1,0:T(8,128)S(1)}, s32[10,8,512]{2,1,0:T(8,128)S(1)}, u32[]{:S(2)}, u32[]{:S(2)}) collective-permute-start(s32[10,8,512]{2,1,0:T(8,128)S(1)} %pad_add_fusion), channel_id=1, source_target_pairs={{0,8},{8,0},{16,24},{24,16},{1,9},{9,1},{17,25},{25,17},{2,10},{10... | collective-permute-start | bytes 491528 | tf_op jit(solution)/shard_map/ppermute | solution.py:541
  45.0 6.9 %collective-permute-start.9 = (f32[2,4,8,512]{3,2,1,0:T(8,128)S(1)}, f32[2,4,8,512]{3,2,1,0:T(8,128)S(1)}, u32[]{:S(2)}, u32[]{:S(2)}) collective-permute-start(f32[2,4,8,512]{3,2,1,0:T(8,128)S(1)} %get-tuple-element.22), channel_id=1, source_target_pairs={{0,1},{1,0},{2,3},{3,2},{4,5},{5,4},{6,7},{7,6},{8,9},{9,8},{10,11... | collective-permute-start | bytes 393224 | tf_op jit(solution)/shard_map/ppermute | solution.py:541
  47.6 9.0 %collective-permute-start.7 = (f32[2,4,8,512]{3,2,1,0:T(8,128)S(1)}, f32[2,4,8,512]{3,2,1,0:T(8,128)S(1)}, u32[]{:S(2)}, u32[]{:S(2)}) collective-permute-start(f32[2,4,8,512]{3,2,1,0:T(8,128)S(1)} %get-tuple-element.21), channel_id=1, source_target_pairs={{0,1},{1,0},{2,3},{3,2},{4,5},{5,4},{6,7},{7,6},{8,9},{9,8},{10,11... | collective-permute-start | bytes 393224 | tf_op jit(solution)/shard_map/ppermute | solution.py:541
  52.0 5.4 %collective-permute-start.10 = (f32[4,8,512]{2,1,0:T(8,128)S(1)}, f32[4,8,512]{2,1,0:T(8,128)S(1)}, u32[]{:S(2)}, u32[]{:S(2)}) collective-permute-start(f32[4,8,512]{2,1,0:T(8,128)S(1)} %get-tuple-element.40), channel_id=1, source_target_pairs={{0,4},{1,5},{2,6},{3,7},{4,0},{5,1},{6,2},{7,3},{8,12},{9,13},{10,... | collective-permute-start | bytes 196616 | tf_op jit(solution)/shard_map/ppermute | solution.py:580
  55.2 6.2 %collective-permute-start.11 = (f32[4,8,512]{2,1,0:T(8,128)S(1)}, f32[4,8,512]{2,1,0:T(8,128)S(1)}, u32[]{:S(2)}, u32[]{:S(2)}) collective-permute-start(f32[4,8,512]{2,1,0:T(8,128)S(1)} %get-tuple-element.41), channel_id=1, source_target_pairs={{0,6},{1,7},{2,4},{3,5},{4,2},{5,3},{6,0},{7,1},{8,14},{9,15},{10,... | collective-permute-start | bytes 196616 | tf_op jit(solution)/shard_map/ppermute | solution.py:580
  56.6 5.0 %collective-permute-start.8 = (f32[4,8,512]{2,1,0:T(8,128)S(1)}, f32[4,8,512]{2,1,0:T(8,128)S(1)}, u32[]{:S(2)}, u32[]{:S(2)}) collective-permute-start(f32[4,8,512]{2,1,0:T(8,128)S(1)} %slice_bitcast_fusion.2), channel_id=1, source_target_pairs={{0,2},{1,3},{2,0},{3,1},{4,6},{5,7},{6,4},{7,5},{8,10},{9,11},{10,... | collective-permute-start | bytes 196616 | tf_op jit(solution)/shard_map/ppermute | solution.py:580

commit v12 on v11

--- a/solution.py
+++ b/solution.py
@@ -366,15 +366,14 @@
     edge_smooth(0, flags, order, plane, smoothed, tile, ca, cb, by, lx, ends, halo)
     if split:
         tile_of = half_tiles(order, *split, 1 - order[1])
-        for half, image in enumerate(images):
-            render_half(scale, order[1] == 1, ends, behind, image, tile_of, half)
+        render_half(scale, order[1] == 1, ends, behind, images[0], tile_of, 0)
     else:
         tiles = plane.shape[1] // 8 - 2
         edge_render(scale, order[1] == 1, ends, behind, images[0], tiles, lambda place: place)
 
 
-def kept_edge_kernel(scale, split, half, order, ends, behind, image):
-    tile_of = half_tiles(order, *split, order[1])
+def part_edge_kernel(scale, split, half, kept, order, ends, behind, image):
+    tile_of = half_tiles(order, *split, order[1] if kept else 1 - order[1])
     render_half(scale, order[1] == 1, ends, behind, image, tile_of, half)
 
 
@@ -503,7 +502,7 @@
     _, ext, columns = plane.shape
     f32 = jnp.float32
     rows = ext - 2 * PAD
-    images = 2 * [half_shape(split, columns)] if split else [(4, rows, columns)]
+    images = [half_shape(split, columns) if split else (4, rows, columns)]
     shapes = [*images, (REACH + 2, ext, columns)]
     return pl.pallas_call(
         functools.partial(last_edge_kernel, scale, split),
@@ -521,10 +520,10 @@
     )(flags, order, plane, *operands)
 
 
-def call_kept_edge(scale, split, half, order, ends, behind):
+def call_part_edge(scale, split, half, kept, order, ends, behind):
     image = jax.ShapeDtypeStruct(half_shape(split, ends.shape[2]), jnp.float32)
     return pl.pallas_call(
-        functools.partial(kept_edge_kernel, scale, split, half),
+        functools.partial(part_edge_kernel, scale, split, half, kept),
         out_shape=image,
         in_specs=[smem()] + whole(2),
         out_specs=whole(1)[0],
@@ -641,7 +640,9 @@
         scale, split, *common, mid_a, edge_a, ca[:REACH], cb[:REACH], by, lx, layers
     )
     if split:
-        keeps = [call_kept_edge(scale, split, half, order, ends, layers) for half in range(2)]
+        last = (order, ends, layers)
+        sends.append(call_part_edge(scale, split, 1, False, *last))
+        keeps = [call_part_edge(scale, split, half, True, *last) for half in range(2)]
     else:
         sends, keeps = halves_of(sends[0])
     return exchange(sends, keeps)

time: 62.7 us -> 62.4 us (level)
  waiting for transfers between devices: 14.9 us -> 14.1 us
    ppermute x9, waiting for transfers between devices: 10.2 us -> 9.36 us  [swap(): return lax.ppermute(value, axis, pairs)]
    pallas_call x2 -> x3, Pallas kernels: 1.68 us -> 2.51 us  [call_part_edge(): pl.pallas_call(functools.partial(part_edge_kernel, scale, split, half, ke...]
  transfers between devices with their start and end apart: 12 -> 12, of which waited for: 6 -> 6; matrix products, arithmetic and copies ran while one was open for 1% -> 1% of each run, Pallas kernels for 35% -> 36%
where the time goes in v12:
time: 62.4 us; the launch traced here: 62.1 us
  Pallas kernels  27.3 us (44%)
  starting transfers between devices  19.3 us (31%)
  waiting for transfers between devices  14.1 us (23%)
  other arithmetic  1.06 us (2%)
    ppermute x9, starting transfers between devices, swap(): return lax.ppermute(value, axis, pairs)  14.5 us
    ppermute x9, waiting for transfers between devices, swap(): return lax.ppermute(value, axis, pairs)  9.36 us
    pallas_call x1, Pallas kernels, call_smooth(): pl.pallas_call(functools.partial(smooth_kernel, group), out_shape=jax.Sha...  5.23 us
    ppermute x3, starting transfers between devices, exchange(): lax.ppermute(piece, 'depth', [(i, i ^ 2 * step) for i in range(count)])  4.81 us
    ppermute x3, waiting for transfers between devices, exchange(): lax.ppermute(piece, 'depth', [(i, i ^ 2 * step) for i in range(count)])  4.74 us
    pallas_call x1, Pallas kernels, call_depth(): pl.pallas_call(depth_kernel, out_shape=(jax.ShapeDtypeStruct(partial.shap...  4.54 us
    pallas_call x1, Pallas kernels, call_interior(): pl.pallas_call(functools.partial(interior_kernel, scale), out_shape=jax.S...  4.19 us
    pallas_call x1, Pallas kernels, call_last_edge(): pl.pallas_call(functools.partial(last_edge_kernel, scale, split), out_sha...  3.14 us
  transfers between devices with their start and end apart: 12, of which 6 were waited for; matrix products, arithmetic and copies ran while one was open for 1% of the time, Pallas kernels for 36%

profile of v12, /device:TPU:0, one launch (start us, length us, event | category | flops | bytes accessed | tf_op | source)
XLA Modules:
  0.0 62.1 jit_solution(1540855750654663470)
XLA Ops:
  0.1 1.6 %pack_block.1 = s32[5,64,512]{2,1,0:T(8,128)S(1)} custom-call(s32[4]{0:T(128)S(1)} %pad_add_fusion.3.where, s32[32,64,512]{2,1,0:T(8,128)} %c.3), custom_call_target="tpu_custom_call" | custom-call | tf_op jit(solution)/shard_map/pack_block/pallas_call | solution.py:402
  1.7 0.7 %collective-permute-start.4 = (s32[5,64,512]{2,1,0:T(8,128)S(1)}, s32[5,64,512]{2,1,0:T(8,128)S(1)}, u32[]{:S(2)}, u32[]{:S(2)}) collective-permute-start(s32[5,64,512]{2,1,0:T(8,128)S(1)} %pack_block.1), channel_id=1, source_target_pairs={{1,2},{2,1},{3,4},{4,3},{5,6},{6,5},{9,10},{10,9},{11,12},{12,11},... | collective-permute-start | bytes 1966088 | tf_op jit(solution)/shard_map/ppermute | solution.py:540
  2.4 3.1 %pack_rest.1 = (s32[32,8,512]{2,1,0:T(8,128)}, s32[5,16,512]{2,1,0:T(8,128)S(1)}, s32[5,48,512]{2,1,0:T(8,128)}, s32[32,8,512]{2,1,0:T(8,128)}) custom-call(s32[4]{0:T(128)S(1)} %pad_add_fusion.3.where, s32[32,64,512]{2,1,0:T(8,128)} %c.3), custom_call_target="tpu_custom_call" | custom-call | tf_op jit(solution)/shard_map/pack_rest/pallas_call | solution.py:418
  5.6 0.6 collective-permute-start
  6.1 1.5 %collective-permute-start.1 = (s32[32,8,512]{2,1,0:T(8,128)}, s32[32,8,512]{2,1,0:T(8,128)}, u32[]{:S(2)}, u32[]{:S(2)}) collective-permute-start(s32[32,8,512]{2,1,0:T(8,128)} %get-tuple-element.14), channel_id=1, source_target_pairs={{8,16},{16,8},{9,17},{17,9},{10,18},{18,10},{11,19},{19,11},{12,20... | collective-permute-start | bytes 1572872 | tf_op jit(solution)/shard_map/ppermute | solution.py:540
  7.6 5.3 %collective-permute-start.3 = (s32[5,16,512]{2,1,0:T(8,128)S(1)}, s32[5,16,512]{2,1,0:T(8,128)S(1)}, u32[]{:S(2)}, u32[]{:S(2)}) collective-permute-start(s32[5,16,512]{2,1,0:T(8,128)S(1)} %get-tuple-element.18), channel_id=1, source_target_pairs={{0,1},{1,0},{2,3},{3,2},{4,5},{5,4},{6,7},{7,6},{8,9},{9,8},{10,11... | collective-permute-start | bytes 491528 | tf_op jit(solution)/shard_map/ppermute | solution.py:540
  13.0 5.2 %smooth.1.partial = f32[32,80,512]{2,1,0:T(8,128)S(1)} custom-call(s32[32,64,512]{2,1,0:T(8,128)} %c.3, bf16[1024,512]{1,0:T(8,128)(2,1)S(1)} %copy-done, bf16[80,192]{1,0:T(8,128)(2,1)S(1)} %copy-done.3), custom_call_target="tpu_custom_call" | custom-call | flops 1000000000 | bytes 4000000 | tf_op jit(solution)/shard_map/smooth/pallas_call | solution.py:433
  18.3 6.6 %collective-permute-done.3.edge = s32[5,16,512]{2,1,0:T(8,128)S(1)} collective-permute-done((s32[5,16,512]{2,1,0:T(8,128)S(1)}, s32[5,16,512]{2,1,0:T(8,128)S(1)}, u32[]{:S(2)}, u32[]{:S(2)}) %collective-permute-start.3) | collective-permute-done | bytes 163872 | tf_op jit(solution)/shard_map/ppermute | solution.py:540
  24.9 4.5 %depth.1 = (f32[32,80,512]{2,1,0:T(8,128)S(1)}, f32[24,80,512]{2,1,0:T(8,128)S(1)}) custom-call(f32[4]{0:T(128)S(1)} %add_convert_fusion.flags, s32[3]{0:T(128)S(1)} %pad_add_fusion.2.order, f32[32,80,512]{2,1,0:T(8,128)S(1)} %smooth.1.partial, s32[32,8,512]{2,1,0:T(8,128)S(1)} %collective-permute-done.xa, ...), custom_call_target="tpu_custom_call", output_to_operand_aliasing={{0}: (2, {})} | custom-call | flops 500000000 | bytes 4000000 | tf_op jit(solution)/shard_map/depth/pallas_call | solution.py:450
  29.6 0.7 %collective-permute-start.6 = (s32[10,8,512]{2,1,0:T(8,128)S(1)}, s32[10,8,512]{2,1,0:T(8,128)S(1)}, u32[]{:S(2)}, u32[]{:S(2)}) collective-permute-start(s32[10,8,512]{2,1,0:T(8,128)S(1)} %pad_add_fusion.1), channel_id=1, source_target_pairs={{8,16},{16,8},{9,17},{17,9},{10,18},{18,10},{11,19},{19,11},{12,20... | collective-permute-start | bytes 491528 | tf_op jit(solution)/shard_map/ppermute | solution.py:540
  30.2 4.2 %interior.1.behind = f32[4,64,512]{2,1,0:T(8,128)S(1)} custom-call(f32[24,80,512]{2,1,0:T(8,128)S(1)} %get-tuple-element.16.smoothed), custom_call_target="tpu_custom_call" | custom-call | flops 1000000000 | bytes 4000000 | tf_op jit(solution)/shard_map/interior/pallas_call | solution.py:467
  34.4 3.1 %collective-permute-start.5 = (s32[10,8,512]{2,1,0:T(8,128)S(1)}, s32[10,8,512]{2,1,0:T(8,128)S(1)}, u32[]{:S(2)}, u32[]{:S(2)}) collective-permute-start(s32[10,8,512]{2,1,0:T(8,128)S(1)} %pad_add_fusion), channel_id=1, source_target_pairs={{0,8},{8,0},{16,24},{24,16},{1,9},{9,1},{17,25},{25,17},{2,10},{10... | collective-permute-start | bytes 491528 | tf_op jit(solution)/shard_map/ppermute | solution.py:540
  37.6 1.0 %collective-permute-done.5 = s32[10,8,512]{2,1,0:T(8,128)S(1)} collective-permute-done((s32[10,8,512]{2,1,0:T(8,128)S(1)}, s32[10,8,512]{2,1,0:T(8,128)S(1)}, u32[]{:S(2)}, u32[]{:S(2)}) %collective-permute-start.5) | collective-permute-done | bytes 163872 | tf_op jit(solution)/shard_map/ppermute | solution.py:540
  38.6 3.0 %first_edge.1.behind = f32[4,64,512]{2,1,0:T(8,128)S(1)} custom-call(f32[4]{0:T(128)S(1)} %add_convert_fusion.flags, s32[3]{0:T(128)S(1)} %pad_add_fusion.2.order, f32[32,80,512]{2,1,0:T(8,128)S(1)} %get-tuple-element.15.plane, f32[24,80,512]{2,1,0:T(8,128)S(1)} %get-tuple-element.16.smoothed, s32[5,64,512]{2,1,0:T(8,128)S(1)} %collective-permute-done.4.block, ...), custom_call_target="tpu_custom_call" | custom-call | flops 300000000 | bytes 4000000 | tf_op jit(solution)/shard_map/first_edge/pallas_call | solution.py:481
  41.6 3.1 %last_edge.1 = (f32[2,4,8,512]{3,2,1,0:T(8,128)S(1)}, f32[7,80,512]{2,1,0:T(8,128)S(1)}) custom-call(f32[4]{0:T(128)S(1)} %add_convert_fusion.flags, s32[3]{0:T(128)S(1)} %pad_add_fusion.2.order, f32[32,80,512]{2,1,0:T(8,128)S(1)} %get-tuple-element.15.plane, f32[24,80,512]{2,1,0:T(8,128)S(1)} %get-tuple-element.16.smoothed, ...), custom_call_target="tpu_custom_call" | custom-call | flops 300000000 | bytes 4000000 | tf_op jit(solution)/shard_map/last_edge/pallas_call | solution.py:507
  44.8 2.6 %collective-permute-start.9 = (f32[2,4,8,512]{3,2,1,0:T(8,128)S(1)}, f32[2,4,8,512]{3,2,1,0:T(8,128)S(1)}, u32[]{:S(2)}, u32[]{:S(2)}) collective-permute-start(f32[2,4,8,512]{3,2,1,0:T(8,128)S(1)} %get-tuple-element.20), channel_id=1, source_target_pairs={{0,1},{1,0},{2,3},{3,2},{4,5},{5,4},{6,7},{7,6},{8,9},{9,8},{10,11... | collective-permute-start | bytes 393224 | tf_op jit(solution)/shard_map/ppermute | solution.py:540
  47.3 0.8 %shard_map.56 = f32[2,4,8,512]{3,2,1,0:T(8,128)S(1)} custom-call(s32[3]{0:T(128)S(1)} %pad_add_fusion.2.order, f32[7,80,512]{2,1,0:T(8,128)S(1)} %get-tuple-element.19.ends, f32[4,64,512]{2,1,0:T(8,128)S(1)} %first_edge.1.behind), custom_call_target="tpu_custom_call" | custom-call | flops 200000000 | bytes 4000000 | tf_op jit(solution)/shard_map/pallas_call | solution.py:525
  48.2 0.8 %shard_map.57 = f32[2,4,8,512]{3,2,1,0:T(8,128)S(1)} custom-call(s32[3]{0:T(128)S(1)} %pad_add_fusion.2.order, f32[7,80,512]{2,1,0:T(8,128)S(1)} %get-tuple-element.19.ends, f32[4,64,512]{2,1,0:T(8,128)S(1)} %first_edge.1.behind), custom_call_target="tpu_custom_call" | custom-call | flops 200000000 | bytes 4000000 | tf_op jit(solution)/shard_map/pallas_call | solution.py:525
  49.1 0.8 %shard_map.55 = f32[2,4,8,512]{3,2,1,0:T(8,128)S(1)} custom-call(s32[3]{0:T(128)S(1)} %pad_add_fusion.2.order, f32[7,80,512]{2,1,0:T(8,128)S(1)} %get-tuple-element.19.ends, f32[4,64,512]{2,1,0:T(8,128)S(1)} %first_edge.1.behind), custom_call_target="tpu_custom_call" | custom-call | flops 200000000 | bytes 4000000 | tf_op jit(solution)/shard_map/pallas_call | solution.py:525
  49.9 1.7 %collective-permute-done.9 = f32[2,4,8,512]{3,2,1,0:T(8,128)S(1)} collective-permute-done((f32[2,4,8,512]{3,2,1,0:T(8,128)S(1)}, f32[2,4,8,512]{3,2,1,0:T(8,128)S(1)}, u32[]{:S(2)}, u32[]{:S(2)}) %collective-permute-start.9) | collective-permute-done | bytes 131104 | tf_op jit(solution)/shard_map/ppermute | solution.py:540
  51.7 3.2 %collective-permute-start.10 = (f32[4,8,512]{2,1,0:T(8,128)S(1)}, f32[4,8,512]{2,1,0:T(8,128)S(1)}, u32[]{:S(2)}, u32[]{:S(2)}) collective-permute-start(f32[4,8,512]{2,1,0:T(8,128)S(1)} %get-tuple-element.38), channel_id=1, source_target_pairs={{0,4},{1,5},{2,6},{3,7},{4,0},{5,1},{6,2},{7,3},{8,12},{9,13},{10,... | collective-permute-start | bytes 196616 | tf_op jit(solution)/shard_map/ppermute | solution.py:579
  54.9 1.3 %collective-permute-start.11 = (f32[4,8,512]{2,1,0:T(8,128)S(1)}, f32[4,8,512]{2,1,0:T(8,128)S(1)}, u32[]{:S(2)}, u32[]{:S(2)}) collective-permute-start(f32[4,8,512]{2,1,0:T(8,128)S(1)} %get-tuple-element.39), channel_id=1, source_target_pairs={{0,6},{1,7},{2,4},{3,5},{4,2},{5,3},{6,0},{7,1},{8,14},{9,15},{10,... | collective-permute-start | bytes 196616 | tf_op jit(solution)/shard_map/ppermute | solution.py:579
  57.2 3.9 %collective-permute-done.11 = f32[4,8,512]{2,1,0:T(8,128)S(1)} collective-permute-done((f32[4,8,512]{2,1,0:T(8,128)S(1)}, f32[4,8,512]{2,1,0:T(8,128)S(1)}, u32[]{:S(2)}, u32[]{:S(2)}) %collective-permute-start.11) | collective-permute-done | bytes 65568 | tf_op jit(solution)/shard_map/ppermute | solution.py:579
  61.5 0.6 %pad_maximum_fusion.4 = f32[4,8,512]{2,1,0:T(8,128)} fusion(f32[1,8,512]{2,1,0:T(8,128)S(1)} %get-tuple-element.24, f32[1,8,512]{2,1,0:T(8,128)S(1)} %get-tuple-element.48, f32[1,8,512]{2,1,0:T(8,128)S(1)} %get-tuple-element.47, f32[1,8,512]{2,1,0:T(8,128)S(1)} %get-tuple-element.46), kind=kLoop, calls=%fused_computation.15 | loop fusion | flops 49152 | bytes 131072 | tf_op jit(solution)/shard_map/concatenate | solution.py:592
  (40 shorter events, 1.8 us)
Async XLA Ops:
  0.1 12.9 %copy-start = (bf16[1024,512]{1,0:T(8,128)(2,1)S(1)}, bf16[1024,512]{1,0:T(8,128)(2,1)}, u32[]{:S(2)}) copy-start(bf16[1024,512]{1,0:T(8,128)(2,1)} %constant.71.clone.by) | copy-start | bytes 3145732
  0.1 12.9 %copy-start.3 = (bf16[80,192]{1,0:T(8,128)(2,1)S(1)}, bf16[80,192]{1,0:T(8,128)(2,1)}, u32[]{:S(2)}) copy-start(bf16[80,192]{1,0:T(8,128)(2,1)} %constant.73.clone.lx) | copy-start | bytes 92164
  1.7 27.8 %collective-permute-start.4 = (s32[5,64,512]{2,1,0:T(8,128)S(1)}, s32[5,64,512]{2,1,0:T(8,128)S(1)}, u32[]{:S(2)}, u32[]{:S(2)}) collective-permute-start(s32[5,64,512]{2,1,0:T(8,128)S(1)} %pack_block.1), channel_id=1, source_target_pairs={{1,2},{2,1},{3,4},{4,3},{5,6},{6,5},{9,10},{10,9},{11,12},{12,11},... | collective-permute-start | bytes 1966088 | tf_op jit(solution)/shard_map/ppermute | solution.py:540
  5.6 19.3 %collective-permute-start = (s32[32,8,512]{2,1,0:T(8,128)}, s32[32,8,512]{2,1,0:T(8,128)S(1)}, u32[]{:S(2)}, u32[]{:S(2)}) collective-permute-start(s32[32,8,512]{2,1,0:T(8,128)} %get-tuple-element.13), channel_id=1, source_target_pairs={{0,8},{8,0},{16,24},{24,16},{1,9},{9,1},{17,25},{25,17},{2,10},{10... | collective-permute-start | bytes 1572872 | tf_op jit(solution)/shard_map/ppermute | solution.py:540
  6.1 18.8 %collective-permute-start.1 = (s32[32,8,512]{2,1,0:T(8,128)}, s32[32,8,512]{2,1,0:T(8,128)}, u32[]{:S(2)}, u32[]{:S(2)}) collective-permute-start(s32[32,8,512]{2,1,0:T(8,128)} %get-tuple-element.14), channel_id=1, source_target_pairs={{8,16},{16,8},{9,17},{17,9},{10,18},{18,10},{11,19},{19,11},{12,20... | collective-permute-start | bytes 1572872 | tf_op jit(solution)/shard_map/ppermute | solution.py:540
  7.6 17.3 %collective-permute-start.3 = (s32[5,16,512]{2,1,0:T(8,128)S(1)}, s32[5,16,512]{2,1,0:T(8,128)S(1)}, u32[]{:S(2)}, u32[]{:S(2)}) collective-permute-start(s32[5,16,512]{2,1,0:T(8,128)S(1)} %get-tuple-element.18), channel_id=1, source_target_pairs={{0,1},{1,0},{2,3},{3,2},{4,5},{5,4},{6,7},{7,6},{8,9},{9,8},{10,11... | collective-permute-start | bytes 491528 | tf_op jit(solution)/shard_map/ppermute | solution.py:540
  12.9 28.7 %collective-permute-start.2 = (s32[5,48,512]{2,1,0:T(8,128)}, s32[5,48,512]{2,1,0:T(8,128)}, u32[]{:S(2)}, u32[]{:S(2)}) collective-permute-start(s32[5,48,512]{2,1,0:T(8,128)} %get-tuple-element.17), channel_id=1, source_target_pairs={{0,1},{1,0},{2,3},{3,2},{4,5},{5,4},{6,7},{7,6},{8,9},{9,8},{10,11... | collective-permute-start | bytes 1474568 | tf_op jit(solution)/shard_map/ppermute | solution.py:540
  13.0 12.0 %copy-start.2 = (bf16[2,128,192]{2,1,0:T(8,128)(2,1)S(1)}, bf16[2,128,192]{2,1,0:T(8,128)(2,1)}, u32[]{:S(2)}) copy-start(bf16[2,128,192]{2,1,0:T(8,128)(2,1)} %constant.74.clone.lx) | copy-start | bytes 294916
  29.5 9.1 %copy-start.1 = (bf16[2,80,240]{2,1,0:T(8,128)(2,1)S(1)}, bf16[2,80,240]{2,1,0:T(8,128)(2,1)}, u32[]{:S(2)}) copy-start(bf16[2,80,240]{2,1,0:T(8,128)(2,1)} %constant.72.clone.lx) | copy-start | bytes 230404
  29.6 8.0 %collective-permute-start.6 = (s32[10,8,512]{2,1,0:T(8,128)S(1)}, s32[10,8,512]{2,1,0:T(8,128)S(1)}, u32[]{:S(2)}, u32[]{:S(2)}) collective-permute-start(s32[10,8,512]{2,1,0:T(8,128)S(1)} %pad_add_fusion.1), channel_id=1, source_target_pairs={{8,16},{16,8},{9,17},{17,9},{10,18},{18,10},{11,19},{19,11},{12,20... | collective-permute-start | bytes 491528 | tf_op jit(solution)/shard_map/ppermute | solution.py:540
  34.4 4.2 %collective-permute-start.5 = (s32[10,8,512]{2,1,0:T(8,128)S(1)}, s32[10,8,512]{2,1,0:T(8,128)S(1)}, u32[]{:S(2)}, u32[]{:S(2)}) collective-permute-start(s32[10,8,512]{2,1,0:T(8,128)S(1)} %pad_add_fusion), channel_id=1, source_target_pairs={{0,8},{8,0},{16,24},{24,16},{1,9},{9,1},{17,25},{25,17},{2,10},{10... | collective-permute-start | bytes 491528 | tf_op jit(solution)/shard_map/ppermute | solution.py:540
  44.8 6.9 %collective-permute-start.9 = (f32[2,4,8,512]{3,2,1,0:T(8,128)S(1)}, f32[2,4,8,512]{3,2,1,0:T(8,128)S(1)}, u32[]{:S(2)}, u32[]{:S(2)}) collective-permute-start(f32[2,4,8,512]{3,2,1,0:T(8,128)S(1)} %get-tuple-element.20), channel_id=1, source_target_pairs={{0,1},{1,0},{2,3},{3,2},{4,5},{5,4},{6,7},{7,6},{8,9},{9,8},{10,11... | collective-permute-start | bytes 393224 | tf_op jit(solution)/shard_map/ppermute | solution.py:540
  48.1 8.1 %collective-permute-start.7 = (f32[2,4,8,512]{3,2,1,0:T(8,128)S(1)}, f32[2,4,8,512]{3,2,1,0:T(8,128)S(1)}, u32[]{:S(2)}, u32[]{:S(2)}) collective-permute-start(f32[2,4,8,512]{3,2,1,0:T(8,128)S(1)} %shard_map.56), channel_id=1, source_target_pairs={{0,1},{1,0},{2,3},{3,2},{4,5},{5,4},{6,7},{7,6},{8,9},{9,8},{10,11... | collective-permute-start | bytes 393224 | tf_op jit(solution)/shard_map/ppermute | solution.py:540
  51.7 5.4 %collective-permute-start.10 = (f32[4,8,512]{2,1,0:T(8,128)S(1)}, f32[4,8,512]{2,1,0:T(8,128)S(1)}, u32[]{:S(2)}, u32[]{:S(2)}) collective-permute-start(f32[4,8,512]{2,1,0:T(8,128)S(1)} %get-tuple-element.38), channel_id=1, source_target_pairs={{0,4},{1,5},{2,6},{3,7},{4,0},{5,1},{6,2},{7,3},{8,12},{9,13},{10,... | collective-permute-start | bytes 196616 | tf_op jit(solution)/shard_map/ppermute | solution.py:579
  54.9 6.2 %collective-permute-start.11 = (f32[4,8,512]{2,1,0:T(8,128)S(1)}, f32[4,8,512]{2,1,0:T(8,128)S(1)}, u32[]{:S(2)}, u32[]{:S(2)}) collective-permute-start(f32[4,8,512]{2,1,0:T(8,128)S(1)} %get-tuple-element.39), channel_id=1, source_target_pairs={{0,6},{1,7},{2,4},{3,5},{4,2},{5,3},{6,0},{7,1},{8,14},{9,15},{10,... | collective-permute-start | bytes 196616 | tf_op jit(solution)/shard_map/ppermute | solution.py:579
  56.3 5.0 %collective-permute-start.8 = (f32[4,8,512]{2,1,0:T(8,128)S(1)}, f32[4,8,512]{2,1,0:T(8,128)S(1)}, u32[]{:S(2)}, u32[]{:S(2)}) collective-permute-start(f32[4,8,512]{2,1,0:T(8,128)S(1)} %slice_bitcast_fusion.2), channel_id=1, source_target_pairs={{0,2},{1,3},{2,0},{3,1},{4,6},{5,7},{6,4},{7,5},{8,10},{9,11},{10,... | collective-permute-start | bytes 196616 | tf_op jit(solution)/shard_map/ppermute | solution.py:579

commit v13 on v12

--- a/solution.py
+++ b/solution.py
@@ -108,15 +108,16 @@
     return total
 
 
-def smooth_depth_layer(flags, read, k, tiles, write):
+def smooth_depth_layers(flags, read, ks, tiles, write):
     for tile in range(tiles):
         rows = pl.ds(tile * 8, 8)
-        value = smooth_depth(lambda j: read(j, rows), k)
-        if tile == 0:
-            value = value * flags[0]
-        if tile == tiles - 1:
-            value = value * flags[1]
-        write(rows, value)
+        for n, k in enumerate(ks):
+            value = smooth_depth(lambda j: read(j, rows), k)
+            if tile == 0:
+                value = value * flags[0]
+            if tile == tiles - 1:
+                value = value * flags[1]
+            write(n, rows, value)
 
 
 def beside(mid, step):
@@ -259,14 +260,19 @@
 
     lax.fori_loop(0, layers // group, add_sides, 0)
 
-    def one_layer(j, _):
-        def write(rows, value):
-            smoothed[j, rows, :] = value
-
-        smooth_depth_layer(flags, lambda k, rows: plane[k, rows, :], j + 4, ext // 8, write)
+    together = 2 if layers % 2 == 0 else 1
+
+    def some_layers(m, _):
+        first = m * together
+
+        def write(n, rows, value):
+            smoothed[first + n, rows, :] = value
+
+        ks = [first + n + 4 for n in range(together)]
+        smooth_depth_layers(flags, lambda k, rows: plane[k, rows, :], ks, ext // 8, write)
         return 0
 
-    lax.fori_loop(0, layers - 8, one_layer, 0)
+    lax.fori_loop(0, (layers - 8) // together, some_layers, 0)
 
 
 def interior_kernel(scale, smoothed, image):
@@ -283,13 +289,11 @@
     lax.fori_loop(0, ext // 8 - 2, one_tile, 0)
 
 
-def edge_smooth(turn, flags, order, plane, smoothed, tile, ca, cb, by, lx, ends, halo):
+def edge_smooth(turn, flags, order, plane, smoothed, planes, ends, halo):
     layers, ext, _ = plane.shape
-    rows_of = order[0]
     is_front = order[1] == 1 - turn
     sign = jnp.where(is_front, 1, -1)
-    counts = [jnp.concatenate([ca[j], tile(j), cb[j]], 0) for j in range(REACH)]
-    for j, value in enumerate(smooth_plane(counts, by, lx[rows_of])):
+    for j, value in enumerate(planes):
         halo[j] = value
     plane_face = jnp.where(is_front, 0, layers - 1)
     halo_face = jnp.where(is_front, REACH, -1)
@@ -302,12 +306,10 @@
             return halo[halo_face + sign * v, rows, :]
         return plane[plane_face + sign * v, rows, :]
 
-    for v in range(-1, 4):
-
-        def write(rows, value, v=v):
-            ends[ends_face + sign * v, rows, :] = value * on_grid if v < 0 else value
-
-        smooth_depth_layer(flags, counted, v, ext // 8, write)
+    def write(n, rows, value):
+        ends[ends_face + sign * (n - 1), rows, :] = value * on_grid if n == 0 else value
+
+    smooth_depth_layers(flags, counted, range(-1, 4), ext // 8, write)
     for v in (4, 5):
         ends[ends_face + sign * v] = smoothed[smoothed_face + sign * v]
 
@@ -315,7 +317,7 @@
 def edge_render(scale, is_front, ends, behind, image, tiles, tile_of, first=0):
     columns = ends.shape[2]
 
-    def one_tile(place, _):
+    def one_tile(place):
         tile = tile_of(place + first)
         base = pl.multiple_of(tile * 8 + 8, 8)
         carry = empty_carry(columns)
@@ -331,9 +333,15 @@
         else:
             owner_tiles = image.shape[2] // 8
             store_tile(image.at[place // owner_tiles], place % owner_tiles, colors)
+
+    together = 2 if tiles % 2 == 0 else 1
+
+    def some_tiles(n, _):
+        for m in range(together):
+            one_tile(n * together + m)
         return 0
 
-    lax.fori_loop(0, tiles, one_tile, 0)
+    lax.fori_loop(0, tiles // together, some_tiles, 0)
 
 
 def half_tiles(order, pairs, owner_tiles, wanted):
@@ -346,8 +354,9 @@
 
 def first_edge_kernel(scale, flags, order, plane, smoothed, block, ca, cb, by, lx, behind, image,
                       ends, halo):
-    tile = lambda j: block[j]
-    edge_smooth(1, flags, order, plane, smoothed, tile, ca, cb, by, lx, ends, halo)
+    counts = [jnp.concatenate([ca[j], block[j], cb[j]], 0) for j in range(REACH)]
+    planes = smooth_plane(counts, by, lx[order[0]])
+    edge_smooth(1, flags, order, plane, smoothed, planes, ends, halo)
     tiles = plane.shape[1] // 8 - 2
     edge_render(scale, order[1] == 0, ends, behind, image, tiles, lambda place: place)
 
@@ -361,9 +370,31 @@
 def last_edge_kernel(scale, split, flags, order, plane, smoothed, middle_any, edge, ca, cb,
                      by, lx, behind, *refs):
     images, (ends, halo, middle, sem) = refs[:-4], refs[-4:]
-    run_copies([(middle_any, middle)], sem)
-    tile = lambda j: jnp.concatenate([edge[j, :PAD], middle[j], edge[j, PAD:]], 0)
-    edge_smooth(0, flags, order, plane, smoothed, tile, ca, cb, by, lx, ends, halo)
+    fetch = pltpu.make_async_copy(middle_any, middle, sem.at[0])
+    fetch.start()
+    two = 2 * PAD
+    outer = [
+        jnp.concatenate([ca[j], edge[j, :PAD], edge[j, PAD:], cb[j]], 0) for j in range(REACH)
+    ]
+    outer = column_terms(outer, by)
+    fetch.wait()
+    inner = column_terms([middle[j] for j in range(REACH)], by)
+    rows = middle.shape[1]
+    planes = []
+    for j in range(REACH):
+        high, low = (
+            jnp.concatenate(
+                [
+                    out[2 * two * j : 2 * two * j + two],
+                    mid[rows * j : rows * (j + 1)],
+                    out[2 * two * j + two : 2 * two * (j + 1)],
+                ],
+                0,
+            )
+            for out, mid in zip(outer, inner)
+        )
+        planes.append(row_product(lx[order[0]], high, low))
+    edge_smooth(0, flags, order, plane, smoothed, planes, ends, halo)
     if split:
         tile_of = half_tiles(order, *split, 1 - order[1])
         render_half(scale, order[1] == 1, ends, behind, images[0], tile_of, 0)

time: 62.4 us -> 61.9 us (level)
  no operation moved by 1% of the time
where the time goes in v13:
time: 61.9 us; the launch traced here: 61.6 us
  Pallas kernels  26.7 us (43%)
  starting transfers between devices  19.3 us (31%)
  waiting for transfers between devices  14.2 us (23%)
  other arithmetic  1.06 us (2%)
    ppermute x9, starting transfers between devices, swap(): return lax.ppermute(value, axis, pairs)  14.5 us
    ppermute x9, waiting for transfers between devices, swap(): return lax.ppermute(value, axis, pairs)  9.46 us
    pallas_call x1, Pallas kernels, call_smooth(): pl.pallas_call(functools.partial(smooth_kernel, group), out_shape=jax.Sha...  5.23 us
    ppermute x3, starting transfers between devices, exchange(): lax.ppermute(piece, 'depth', [(i, i ^ 2 * step) for i in range(count)])  4.82 us
    ppermute x3, waiting for transfers between devices, exchange(): lax.ppermute(piece, 'depth', [(i, i ^ 2 * step) for i in range(count)])  4.74 us
    pallas_call x1, Pallas kernels, call_depth(): pl.pallas_call(depth_kernel, out_shape=(jax.ShapeDtypeStruct(partial.shap...  4.28 us
    pallas_call x1, Pallas kernels, call_interior(): pl.pallas_call(functools.partial(interior_kernel, scale), out_shape=jax.S...  4.19 us
    pallas_call x1, Pallas kernels, call_pack_rest(): pl.pallas_call(pack_rest_kernel, out_shape=(side, edge, middle, side), in...  3.12 us
  transfers between devices with their start and end apart: 12, of which 6 were waited for; matrix products, arithmetic and copies ran while one was open for 1% of the time, Pallas kernels for 36%

profile of v13, /device:TPU:0, one launch (start us, length us, event | category | flops | bytes accessed | tf_op | source)
XLA Modules:
  0.0 61.6 jit_solution(2444224959353770119)
XLA Ops:
  0.1 1.6 %pack_block.1 = s32[5,64,512]{2,1,0:T(8,128)S(1)} custom-call(s32[4]{0:T(128)S(1)} %pad_add_fusion.3.where, s32[32,64,512]{2,1,0:T(8,128)} %c.3), custom_call_target="tpu_custom_call" | custom-call | tf_op jit(solution)/shard_map/pack_block/pallas_call | solution.py:433
  1.7 0.7 %collective-permute-start.4 = (s32[5,64,512]{2,1,0:T(8,128)S(1)}, s32[5,64,512]{2,1,0:T(8,128)S(1)}, u32[]{:S(2)}, u32[]{:S(2)}) collective-permute-start(s32[5,64,512]{2,1,0:T(8,128)S(1)} %pack_block.1), channel_id=1, source_target_pairs={{1,2},{2,1},{3,4},{4,3},{5,6},{6,5},{9,10},{10,9},{11,12},{12,11},... | collective-permute-start | bytes 1966088 | tf_op jit(solution)/shard_map/ppermute | solution.py:571
  2.4 3.1 %pack_rest.1 = (s32[32,8,512]{2,1,0:T(8,128)}, s32[5,16,512]{2,1,0:T(8,128)S(1)}, s32[5,48,512]{2,1,0:T(8,128)}, s32[32,8,512]{2,1,0:T(8,128)}) custom-call(s32[4]{0:T(128)S(1)} %pad_add_fusion.3.where, s32[32,64,512]{2,1,0:T(8,128)} %c.3), custom_call_target="tpu_custom_call" | custom-call | tf_op jit(solution)/shard_map/pack_rest/pallas_call | solution.py:449
  5.6 0.6 collective-permute-start
  6.1 1.5 %collective-permute-start.1 = (s32[32,8,512]{2,1,0:T(8,128)}, s32[32,8,512]{2,1,0:T(8,128)}, u32[]{:S(2)}, u32[]{:S(2)}) collective-permute-start(s32[32,8,512]{2,1,0:T(8,128)} %get-tuple-element.14), channel_id=1, source_target_pairs={{8,16},{16,8},{9,17},{17,9},{10,18},{18,10},{11,19},{19,11},{12,20... | collective-permute-start | bytes 1572872 | tf_op jit(solution)/shard_map/ppermute | solution.py:571
  7.6 5.3 %collective-permute-start.3 = (s32[5,16,512]{2,1,0:T(8,128)S(1)}, s32[5,16,512]{2,1,0:T(8,128)S(1)}, u32[]{:S(2)}, u32[]{:S(2)}) collective-permute-start(s32[5,16,512]{2,1,0:T(8,128)S(1)} %get-tuple-element.18), channel_id=1, source_target_pairs={{0,1},{1,0},{2,3},{3,2},{4,5},{5,4},{6,7},{7,6},{8,9},{9,8},{10,11... | collective-permute-start | bytes 491528 | tf_op jit(solution)/shard_map/ppermute | solution.py:571
  13.0 5.2 %smooth.1.partial = f32[32,80,512]{2,1,0:T(8,128)S(1)} custom-call(s32[32,64,512]{2,1,0:T(8,128)} %c.3, bf16[1024,512]{1,0:T(8,128)(2,1)S(1)} %copy-done, bf16[80,192]{1,0:T(8,128)(2,1)S(1)} %copy-done.3), custom_call_target="tpu_custom_call" | custom-call | flops 1000000000 | bytes 4000000 | tf_op jit(solution)/shard_map/smooth/pallas_call | solution.py:464
  18.3 6.6 %collective-permute-done.3.edge = s32[5,16,512]{2,1,0:T(8,128)S(1)} collective-permute-done((s32[5,16,512]{2,1,0:T(8,128)S(1)}, s32[5,16,512]{2,1,0:T(8,128)S(1)}, u32[]{:S(2)}, u32[]{:S(2)}) %collective-permute-start.3) | collective-permute-done | bytes 163872 | tf_op jit(solution)/shard_map/ppermute | solution.py:571
  24.9 4.3 %depth.1 = (f32[32,80,512]{2,1,0:T(8,128)S(1)}, f32[24,80,512]{2,1,0:T(8,128)S(1)}) custom-call(f32[4]{0:T(128)S(1)} %add_convert_fusion.flags, s32[3]{0:T(128)S(1)} %pad_add_fusion.2.order, f32[32,80,512]{2,1,0:T(8,128)S(1)} %smooth.1.partial, s32[32,8,512]{2,1,0:T(8,128)S(1)} %collective-permute-done.xa, ...), custom_call_target="tpu_custom_call", output_to_operand_aliasing={{0}: (2, {})} | custom-call | flops 500000000 | bytes 4000000 | tf_op jit(solution)/shard_map/depth/pallas_call | solution.py:481
  29.3 0.7 %collective-permute-start.6 = (s32[10,8,512]{2,1,0:T(8,128)S(1)}, s32[10,8,512]{2,1,0:T(8,128)S(1)}, u32[]{:S(2)}, u32[]{:S(2)}) collective-permute-start(s32[10,8,512]{2,1,0:T(8,128)S(1)} %pad_add_fusion.1), channel_id=1, source_target_pairs={{8,16},{16,8},{9,17},{17,9},{10,18},{18,10},{11,19},{19,11},{12,20... | collective-permute-start | bytes 491528 | tf_op jit(solution)/shard_map/ppermute | solution.py:571
  30.0 4.2 %interior.1.behind = f32[4,64,512]{2,1,0:T(8,128)S(1)} custom-call(f32[24,80,512]{2,1,0:T(8,128)S(1)} %get-tuple-element.16.smoothed), custom_call_target="tpu_custom_call" | custom-call | flops 1000000000 | bytes 4000000 | tf_op jit(solution)/shard_map/interior/pallas_call | solution.py:498
  34.2 3.1 %collective-permute-start.5 = (s32[10,8,512]{2,1,0:T(8,128)S(1)}, s32[10,8,512]{2,1,0:T(8,128)S(1)}, u32[]{:S(2)}, u32[]{:S(2)}) collective-permute-start(s32[10,8,512]{2,1,0:T(8,128)S(1)} %pad_add_fusion), channel_id=1, source_target_pairs={{0,8},{8,0},{16,24},{24,16},{1,9},{9,1},{17,25},{25,17},{2,10},{10... | collective-permute-start | bytes 491528 | tf_op jit(solution)/shard_map/ppermute | solution.py:571
  37.3 1.0 %collective-permute-done.5 = s32[10,8,512]{2,1,0:T(8,128)S(1)} collective-permute-done((s32[10,8,512]{2,1,0:T(8,128)S(1)}, s32[10,8,512]{2,1,0:T(8,128)S(1)}, u32[]{:S(2)}, u32[]{:S(2)}) %collective-permute-start.5) | collective-permute-done | bytes 163872 | tf_op jit(solution)/shard_map/ppermute | solution.py:571
  38.4 2.8 %first_edge.1.behind = f32[4,64,512]{2,1,0:T(8,128)S(1)} custom-call(f32[4]{0:T(128)S(1)} %add_convert_fusion.flags, s32[3]{0:T(128)S(1)} %pad_add_fusion.2.order, f32[32,80,512]{2,1,0:T(8,128)S(1)} %get-tuple-element.15.plane, f32[24,80,512]{2,1,0:T(8,128)S(1)} %get-tuple-element.16.smoothed, s32[5,64,512]{2,1,0:T(8,128)S(1)} %collective-permute-done.4.block, ...), custom_call_target="tpu_custom_call" | custom-call | flops 300000000 | bytes 4000000 | tf_op jit(solution)/shard_map/first_edge/pallas_call | solution.py:512
  41.2 3.0 %last_edge.1 = (f32[2,4,8,512]{3,2,1,0:T(8,128)S(1)}, f32[7,80,512]{2,1,0:T(8,128)S(1)}) custom-call(f32[4]{0:T(128)S(1)} %add_convert_fusion.flags, s32[3]{0:T(128)S(1)} %pad_add_fusion.2.order, f32[32,80,512]{2,1,0:T(8,128)S(1)} %get-tuple-element.15.plane, f32[24,80,512]{2,1,0:T(8,128)S(1)} %get-tuple-element.16.smoothed, ...), custom_call_target="tpu_custom_call" | custom-call | flops 300000000 | bytes 4000000 | tf_op jit(solution)/shard_map/last_edge/pallas_call | solution.py:538
  44.2 2.6 %collective-permute-start.9 = (f32[2,4,8,512]{3,2,1,0:T(8,128)S(1)}, f32[2,4,8,512]{3,2,1,0:T(8,128)S(1)}, u32[]{:S(2)}, u32[]{:S(2)}) collective-permute-start(f32[2,4,8,512]{3,2,1,0:T(8,128)S(1)} %get-tuple-element.20), channel_id=1, source_target_pairs={{0,1},{1,0},{2,3},{3,2},{4,5},{5,4},{6,7},{7,6},{8,9},{9,8},{10,11... | collective-permute-start | bytes 393224 | tf_op jit(solution)/shard_map/ppermute | solution.py:571
  46.8 0.8 %shard_map.56 = f32[2,4,8,512]{3,2,1,0:T(8,128)S(1)} custom-call(s32[3]{0:T(128)S(1)} %pad_add_fusion.2.order, f32[7,80,512]{2,1,0:T(8,128)S(1)} %get-tuple-element.19.ends, f32[4,64,512]{2,1,0:T(8,128)S(1)} %first_edge.1.behind), custom_call_target="tpu_custom_call" | custom-call | flops 200000000 | bytes 4000000 | tf_op jit(solution)/shard_map/pallas_call | solution.py:556
  47.7 0.8 %shard_map.57 = f32[2,4,8,512]{3,2,1,0:T(8,128)S(1)} custom-call(s32[3]{0:T(128)S(1)} %pad_add_fusion.2.order, f32[7,80,512]{2,1,0:T(8,128)S(1)} %get-tuple-element.19.ends, f32[4,64,512]{2,1,0:T(8,128)S(1)} %first_edge.1.behind), custom_call_target="tpu_custom_call" | custom-call | flops 200000000 | bytes 4000000 | tf_op jit(solution)/shard_map/pallas_call | solution.py:556
  48.5 0.8 %shard_map.55 = f32[2,4,8,512]{3,2,1,0:T(8,128)S(1)} custom-call(s32[3]{0:T(128)S(1)} %pad_add_fusion.2.order, f32[7,80,512]{2,1,0:T(8,128)S(1)} %get-tuple-element.19.ends, f32[4,64,512]{2,1,0:T(8,128)S(1)} %first_edge.1.behind), custom_call_target="tpu_custom_call" | custom-call | flops 200000000 | bytes 4000000 | tf_op jit(solution)/shard_map/pallas_call | solution.py:556
  49.3 1.8 %collective-permute-done.9 = f32[2,4,8,512]{3,2,1,0:T(8,128)S(1)} collective-permute-done((f32[2,4,8,512]{3,2,1,0:T(8,128)S(1)}, f32[2,4,8,512]{3,2,1,0:T(8,128)S(1)}, u32[]{:S(2)}, u32[]{:S(2)}) %collective-permute-start.9) | collective-permute-done | bytes 131104 | tf_op jit(solution)/shard_map/ppermute | solution.py:571
  51.2 3.2 %collective-permute-start.10 = (f32[4,8,512]{2,1,0:T(8,128)S(1)}, f32[4,8,512]{2,1,0:T(8,128)S(1)}, u32[]{:S(2)}, u32[]{:S(2)}) collective-permute-start(f32[4,8,512]{2,1,0:T(8,128)S(1)} %get-tuple-element.38), channel_id=1, source_target_pairs={{0,4},{1,5},{2,6},{3,7},{4,0},{5,1},{6,2},{7,3},{8,12},{9,13},{10,... | collective-permute-start | bytes 196616 | tf_op jit(solution)/shard_map/ppermute | solution.py:610
  54.4 1.3 %collective-permute-start.11 = (f32[4,8,512]{2,1,0:T(8,128)S(1)}, f32[4,8,512]{2,1,0:T(8,128)S(1)}, u32[]{:S(2)}, u32[]{:S(2)}) collective-permute-start(f32[4,8,512]{2,1,0:T(8,128)S(1)} %get-tuple-element.39), channel_id=1, source_target_pairs={{0,6},{1,7},{2,4},{3,5},{4,2},{5,3},{6,0},{7,1},{8,14},{9,15},{10,... | collective-permute-start | bytes 196616 | tf_op jit(solution)/shard_map/ppermute | solution.py:610
  56.6 3.9 %collective-permute-done.11 = f32[4,8,512]{2,1,0:T(8,128)S(1)} collective-permute-done((f32[4,8,512]{2,1,0:T(8,128)S(1)}, f32[4,8,512]{2,1,0:T(8,128)S(1)}, u32[]{:S(2)}, u32[]{:S(2)}) %collective-permute-start.11) | collective-permute-done | bytes 65568 | tf_op jit(solution)/shard_map/ppermute | solution.py:610
  60.9 0.6 %pad_maximum_fusion.4 = f32[4,8,512]{2,1,0:T(8,128)} fusion(f32[1,8,512]{2,1,0:T(8,128)S(1)} %get-tuple-element.24, f32[1,8,512]{2,1,0:T(8,128)S(1)} %get-tuple-element.48, f32[1,8,512]{2,1,0:T(8,128)S(1)} %get-tuple-element.47, f32[1,8,512]{2,1,0:T(8,128)S(1)} %get-tuple-element.46), kind=kLoop, calls=%fused_computation.15 | loop fusion | flops 49152 | bytes 131072 | tf_op jit(solution)/shard_map/concatenate | solution.py:623
  (40 shorter events, 1.8 us)
Async XLA Ops:
  0.1 12.9 %copy-start = (bf16[1024,512]{1,0:T(8,128)(2,1)S(1)}, bf16[1024,512]{1,0:T(8,128)(2,1)}, u32[]{:S(2)}) copy-start(bf16[1024,512]{1,0:T(8,128)(2,1)} %constant.71.clone.by) | copy-start | bytes 3145732
  0.1 12.9 %copy-start.3 = (bf16[80,192]{1,0:T(8,128)(2,1)S(1)}, bf16[80,192]{1,0:T(8,128)(2,1)}, u32[]{:S(2)}) copy-start(bf16[80,192]{1,0:T(8,128)(2,1)} %constant.73.clone.lx) | copy-start | bytes 92164
  1.7 27.5 %collective-permute-start.4 = (s32[5,64,512]{2,1,0:T(8,128)S(1)}, s32[5,64,512]{2,1,0:T(8,128)S(1)}, u32[]{:S(2)}, u32[]{:S(2)}) collective-permute-start(s32[5,64,512]{2,1,0:T(8,128)S(1)} %pack_block.1), channel_id=1, source_target_pairs={{1,2},{2,1},{3,4},{4,3},{5,6},{6,5},{9,10},{10,9},{11,12},{12,11},... | collective-permute-start | bytes 1966088 | tf_op jit(solution)/shard_map/ppermute | solution.py:571
  5.6 19.3 %collective-permute-start = (s32[32,8,512]{2,1,0:T(8,128)}, s32[32,8,512]{2,1,0:T(8,128)S(1)}, u32[]{:S(2)}, u32[]{:S(2)}) collective-permute-start(s32[32,8,512]{2,1,0:T(8,128)} %get-tuple-element.13), channel_id=1, source_target_pairs={{0,8},{8,0},{16,24},{24,16},{1,9},{9,1},{17,25},{25,17},{2,10},{10... | collective-permute-start | bytes 1572872 | tf_op jit(solution)/shard_map/ppermute | solution.py:571
  6.1 18.8 %collective-permute-start.1 = (s32[32,8,512]{2,1,0:T(8,128)}, s32[32,8,512]{2,1,0:T(8,128)}, u32[]{:S(2)}, u32[]{:S(2)}) collective-permute-start(s32[32,8,512]{2,1,0:T(8,128)} %get-tuple-element.14), channel_id=1, source_target_pairs={{8,16},{16,8},{9,17},{17,9},{10,18},{18,10},{11,19},{19,11},{12,20... | collective-permute-start | bytes 1572872 | tf_op jit(solution)/shard_map/ppermute | solution.py:571
  7.6 17.3 %collective-permute-start.3 = (s32[5,16,512]{2,1,0:T(8,128)S(1)}, s32[5,16,512]{2,1,0:T(8,128)S(1)}, u32[]{:S(2)}, u32[]{:S(2)}) collective-permute-start(s32[5,16,512]{2,1,0:T(8,128)S(1)} %get-tuple-element.18), channel_id=1, source_target_pairs={{0,1},{1,0},{2,3},{3,2},{4,5},{5,4},{6,7},{7,6},{8,9},{9,8},{10,11... | collective-permute-start | bytes 491528 | tf_op jit(solution)/shard_map/ppermute | solution.py:571
  12.9 28.4 %collective-permute-start.2 = (s32[5,48,512]{2,1,0:T(8,128)}, s32[5,48,512]{2,1,0:T(8,128)}, u32[]{:S(2)}, u32[]{:S(2)}) collective-permute-start(s32[5,48,512]{2,1,0:T(8,128)} %get-tuple-element.17), channel_id=1, source_target_pairs={{0,1},{1,0},{2,3},{3,2},{4,5},{5,4},{6,7},{7,6},{8,9},{9,8},{10,11... | collective-permute-start | bytes 1474568 | tf_op jit(solution)/shard_map/ppermute | solution.py:571
  13.0 12.0 %copy-start.2 = (bf16[2,128,192]{2,1,0:T(8,128)(2,1)S(1)}, bf16[2,128,192]{2,1,0:T(8,128)(2,1)}, u32[]{:S(2)}) copy-start(bf16[2,128,192]{2,1,0:T(8,128)(2,1)} %constant.74.clone.lx) | copy-start | bytes 294916
  29.2 9.1 %copy-start.1 = (bf16[2,80,240]{2,1,0:T(8,128)(2,1)S(1)}, bf16[2,80,240]{2,1,0:T(8,128)(2,1)}, u32[]{:S(2)}) copy-start(bf16[2,80,240]{2,1,0:T(8,128)(2,1)} %constant.72.clone.lx) | copy-start | bytes 230404
  29.3 8.0 %collective-permute-start.6 = (s32[10,8,512]{2,1,0:T(8,128)S(1)}, s32[10,8,512]{2,1,0:T(8,128)S(1)}, u32[]{:S(2)}, u32[]{:S(2)}) collective-permute-start(s32[10,8,512]{2,1,0:T(8,128)S(1)} %pad_add_fusion.1), channel_id=1, source_target_pairs={{8,16},{16,8},{9,17},{17,9},{10,18},{18,10},{11,19},{19,11},{12,20... | collective-permute-start | bytes 491528 | tf_op jit(solution)/shard_map/ppermute | solution.py:571
  34.2 4.2 %collective-permute-start.5 = (s32[10,8,512]{2,1,0:T(8,128)S(1)}, s32[10,8,512]{2,1,0:T(8,128)S(1)}, u32[]{:S(2)}, u32[]{:S(2)}) collective-permute-start(s32[10,8,512]{2,1,0:T(8,128)S(1)} %pad_add_fusion), channel_id=1, source_target_pairs={{0,8},{8,0},{16,24},{24,16},{1,9},{9,1},{17,25},{25,17},{2,10},{10... | collective-permute-start | bytes 491528 | tf_op jit(solution)/shard_map/ppermute | solution.py:571
  44.2 6.9 %collective-permute-start.9 = (f32[2,4,8,512]{3,2,1,0:T(8,128)S(1)}, f32[2,4,8,512]{3,2,1,0:T(8,128)S(1)}, u32[]{:S(2)}, u32[]{:S(2)}) collective-permute-start(f32[2,4,8,512]{3,2,1,0:T(8,128)S(1)} %get-tuple-element.20), channel_id=1, source_target_pairs={{0,1},{1,0},{2,3},{3,2},{4,5},{5,4},{6,7},{7,6},{8,9},{9,8},{10,11... | collective-permute-start | bytes 393224 | tf_op jit(solution)/shard_map/ppermute | solution.py:571
  47.6 8.2 %collective-permute-start.7 = (f32[2,4,8,512]{3,2,1,0:T(8,128)S(1)}, f32[2,4,8,512]{3,2,1,0:T(8,128)S(1)}, u32[]{:S(2)}, u32[]{:S(2)}) collective-permute-start(f32[2,4,8,512]{3,2,1,0:T(8,128)S(1)} %shard_map.56), channel_id=1, source_target_pairs={{0,1},{1,0},{2,3},{3,2},{4,5},{5,4},{6,7},{7,6},{8,9},{9,8},{10,11... | collective-permute-start | bytes 393224 | tf_op jit(solution)/shard_map/ppermute | solution.py:571
  51.2 5.4 %collective-permute-start.10 = (f32[4,8,512]{2,1,0:T(8,128)S(1)}, f32[4,8,512]{2,1,0:T(8,128)S(1)}, u32[]{:S(2)}, u32[]{:S(2)}) collective-permute-start(f32[4,8,512]{2,1,0:T(8,128)S(1)} %get-tuple-element.38), channel_id=1, source_target_pairs={{0,4},{1,5},{2,6},{3,7},{4,0},{5,1},{6,2},{7,3},{8,12},{9,13},{10,... | collective-permute-start | bytes 196616 | tf_op jit(solution)/shard_map/ppermute | solution.py:610
  54.4 6.2 %collective-permute-start.11 = (f32[4,8,512]{2,1,0:T(8,128)S(1)}, f32[4,8,512]{2,1,0:T(8,128)S(1)}, u32[]{:S(2)}, u32[]{:S(2)}) collective-permute-start(f32[4,8,512]{2,1,0:T(8,128)S(1)} %get-tuple-element.39), channel_id=1, source_target_pairs={{0,6},{1,7},{2,4},{3,5},{4,2},{5,3},{6,0},{7,1},{8,14},{9,15},{10,... | collective-permute-start | bytes 196616 | tf_op jit(solution)/shard_map/ppermute | solution.py:610
  55.8 5.0 %collective-permute-start.8 = (f32[4,8,512]{2,1,0:T(8,128)S(1)}, f32[4,8,512]{2,1,0:T(8,128)S(1)}, u32[]{:S(2)}, u32[]{:S(2)}) collective-permute-start(f32[4,8,512]{2,1,0:T(8,128)S(1)} %slice_bitcast_fusion.2), channel_id=1, source_target_pairs={{0,2},{1,3},{2,0},{3,1},{4,6},{5,7},{6,4},{7,5},{8,10},{9,11},{10,... | collective-permute-start | bytes 196616 | tf_op jit(solution)/shard_map/ppermute | solution.py:610

commit v14 on v13

--- a/solution.py
+++ b/solution.py
@@ -21,6 +21,7 @@
 
 
 REACH = 5
+FIRST_PART = 1
 SIDE_GROUP = 4
 PAD = 8
 
@@ -195,13 +196,6 @@
         copy.wait()
 
 
-def pack_block_kernel(where, c, block, sems):
-    half = block.shape[1] // 2
-    layers = pl.ds(where[1], REACH)
-    parts = [pl.ds(n * half, half) for n in range(2)]
-    run_copies([(c.at[layers, part], block.at[:, part]) for part in parts], sems)
-
-
 def pack_rest_kernel(where, c, side_b, edge, middle, side_a, sems):
     rows = c.shape[1]
     layers = pl.ds(where[0], REACH)
@@ -363,8 +357,9 @@
 
 def render_half(scale, is_front, ends, behind, image, tile_of, half):
     places, _, owned, _ = image.shape
-    tiles = places * (owned // 8)
-    edge_render(scale, is_front, ends, behind, image, tiles, tile_of, half * tiles)
+    owner_tiles = owned // 8
+    first = half * FIRST_PART * owner_tiles
+    edge_render(scale, is_front, ends, behind, image, places * owner_tiles, tile_of, first)
 
 
 def last_edge_kernel(scale, split, flags, order, plane, smoothed, middle_any, edge, ca, cb,
@@ -428,19 +423,6 @@
     return pl.CostEstimate(flops=flops, transcendentals=0, bytes_accessed=4_000_000)
 
 
-def call_pack_block(where, c):
-    _, rows, columns = c.shape
-    return pl.pallas_call(
-        pack_block_kernel,
-        out_shape=jax.ShapeDtypeStruct((REACH, rows, columns), c.dtype),
-        in_specs=[smem(), in_hbm()],
-        out_specs=whole(1)[0],
-        scratch_shapes=[pltpu.SemaphoreType.DMA((2,))],
-        compiler_params=params(8),
-        name="pack_block",
-    )(where, c)
-
-
 def call_pack_rest(where, c):
     layers, rows, columns = c.shape
     edge = jax.ShapeDtypeStruct((REACH, 2 * PAD, columns), c.dtype)
@@ -524,16 +506,16 @@
     )(flags, order, plane, *operands)
 
 
-def half_shape(split, columns):
+def half_shape(split, half, columns):
     pairs, owner_tiles = split
-    return pairs // 2, 4, owner_tiles * 8, columns
+    return pairs - FIRST_PART if half else FIRST_PART, 4, owner_tiles * 8, columns
 
 
 def call_last_edge(scale, split, flags, order, plane, *operands):
     _, ext, columns = plane.shape
     f32 = jnp.float32
     rows = ext - 2 * PAD
-    images = [half_shape(split, columns) if split else (4, rows, columns)]
+    images = [half_shape(split, 0, columns) if split else (4, rows, columns)]
     shapes = [*images, (REACH + 2, ext, columns)]
     return pl.pallas_call(
         functools.partial(last_edge_kernel, scale, split),
@@ -552,7 +534,7 @@
 
 
 def call_part_edge(scale, split, half, kept, order, ends, behind):
-    image = jax.ShapeDtypeStruct(half_shape(split, ends.shape[2]), jnp.float32)
+    image = jax.ShapeDtypeStruct(half_shape(split, half, ends.shape[2]), jnp.float32)
     return pl.pallas_call(
         functools.partial(part_edge_kernel, scale, split, half, kept),
         out_shape=image,
@@ -589,7 +571,7 @@
     for wanted in (1 - parity, parity):
         chosen = lax.dynamic_index_in_dim(ordered, wanted, 2, keepdims=False)
         chosen = jnp.moveaxis(chosen, 1, 0)
-        both.append((chosen[: pairs // 2], chosen[pairs // 2 :]))
+        both.append((chosen[:FIRST_PART], chosen[FIRST_PART:]))
     return both
 
 
@@ -603,8 +585,8 @@
         owned, columns = send.shape[2:]
         got = swap(send, "depth", 0)
         joined = jnp.where(parity == 0, over(keep, got), over(got, keep))
-        for place in range(pairs // 2):
-            step = pairs - 1 - half * (pairs // 2) - place
+        for place in range(send.shape[0]):
+            step = pairs - 1 - half * FIRST_PART - place
             piece = joined[place]
             if step:
                 piece = lax.ppermute(piece, "depth", [(i, i ^ (2 * step)) for i in range(count)])
@@ -640,7 +622,7 @@
     by = jnp.asarray(column_matrices(columns))
     lx = jnp.asarray(row_matrices(rows))
     held = pltpu.with_memory_space_constraint(counts, pltpu.HBM)
-    block_b = call_pack_block(where, held)
+    block_b = lax.dynamic_slice_in_dim(counts, first_b, REACH, 0)
     side_b, edge_a, mid_a, side_a = call_pack_rest(where, held)
     block_b = swap(block_b, "depth", 1)
     xb = swap(side_b, "img", 1)

time: 61.9 us -> 63.2 us (1.021)
  local copies, waits for them, and re-layouts: 0.09 us -> 2.17 us
  Pallas kernels: 26.7 us -> 24.7 us
  starting transfers between devices: 19.3 us -> 21.3 us
  waiting for transfers between devices: 14.2 us -> 13.4 us
    ppermute x3, starting transfers between devices: 4.82 us -> 7.54 us  [exchange(): lax.ppermute(piece, 'depth', [(i, i ^ 2 * step) for i in range(count)])]
    dynamic_slice x0 -> x1, local copies, waits for them, and re-layouts: none -> 2.08 us  [local(): block_b = lax.dynamic_slice_in_dim(counts, first_b, REACH, 0)]
    pallas_call x1 -> x0, Pallas kernels: 1.63 us -> none  [call_pack_block(): pl.pallas_call(pack_block_kernel, out_shape=jax.ShapeDtypeStruct((REACH,...]
    ppermute x9, starting transfers between devices: 14.5 us -> 13.8 us  [swap(): return lax.ppermute(value, axis, pairs)]
  transfers between devices with their start and end apart: 12 -> 12, of which waited for: 6 -> 5; matrix products, arithmetic and copies ran while one was open for 1% -> 1% of each run, Pallas kernels for 36% -> 35%
where the time goes in v14:
time: 63.2 us; the launch traced here: 63 us
  Pallas kernels  24.7 us (39%)
  starting transfers between devices  21.3 us (34%)
  waiting for transfers between devices  13.4 us (21%)
  local copies, waits for them, and re-layouts  2.17 us (3%)
  other arithmetic  1.06 us (2%)
    ppermute x9, starting transfers between devices, swap(): return lax.ppermute(value, axis, pairs)  13.8 us
    ppermute x9, waiting for transfers between devices, swap(): return lax.ppermute(value, axis, pairs)  9.29 us
    ppermute x3, starting transfers between devices, exchange(): lax.ppermute(piece, 'depth', [(i, i ^ 2 * step) for i in range(count)])  7.54 us
    pallas_call x1, Pallas kernels, call_smooth(): pl.pallas_call(functools.partial(smooth_kernel, group), out_shape=jax.Sha...  5.23 us
    pallas_call x1, Pallas kernels, call_interior(): pl.pallas_call(functools.partial(interior_kernel, scale), out_shape=jax.S...  4.19 us
    ppermute x3, waiting for transfers between devices, exchange(): lax.ppermute(piece, 'depth', [(i, i ^ 2 * step) for i in range(count)])  4.14 us
    pallas_call x1, Pallas kernels, call_depth(): pl.pallas_call(depth_kernel, out_shape=(jax.ShapeDtypeStruct(partial.shap...  3.77 us
    pallas_call x1, Pallas kernels, call_pack_rest(): pl.pallas_call(pack_rest_kernel, out_shape=(side, edge, middle, side), in...  3.19 us
  transfers between devices with their start and end apart: 12, of which 5 were waited for; matrix products, arithmetic and copies ran while one was open for 1% of the time, Pallas kernels for 35%

profile of v14, /device:TPU:0, one launch (start us, length us, event | category | flops | bytes accessed | tf_op | source)
XLA Modules:
  0.0 63.0 jit_solution(10855203248581851419)
XLA Ops:
  0.0 2.1 %constant_dynamic-slice_fusion.3 = s32[5,64,512]{2,1,0:T(8,128)} fusion(s32[32,64,512]{2,1,0:T(8,128)} %c.1, s32[]{:T(128)S(6)} %select_n.156), kind=kLoop, calls=%fused_computation.44 | loop fusion | bytes 1310724 | tf_op jit(solution)/shard_map/dynamic_slice | solution.py:625
  2.1 0.7 %collective-permute-start.4 = (s32[5,64,512]{2,1,0:T(8,128)}, s32[5,64,512]{2,1,0:T(8,128)S(1)}, u32[]{:S(2)}, u32[]{:S(2)}) collective-permute-start(s32[5,64,512]{2,1,0:T(8,128)} %constant_dynamic-slice_fusion.3), channel_id=1, source_target_pairs={{1,2},{2,1},{3,4},{4,3},{5,6},{6,5},{9,10},{10,9},{11,12},{12,11},... | collective-permute-start | bytes 1966088 | tf_op jit(solution)/shard_map/ppermute | solution.py:553
  2.9 3.2 %pack_rest.1 = (s32[32,8,512]{2,1,0:T(8,128)}, s32[5,16,512]{2,1,0:T(8,128)S(1)}, s32[5,48,512]{2,1,0:T(8,128)}, s32[32,8,512]{2,1,0:T(8,128)}) custom-call(s32[4]{0:T(128)S(1)} %pad_add_fusion.3.where, s32[32,64,512]{2,1,0:T(8,128)} %c.1), custom_call_target="tpu_custom_call" | custom-call | tf_op jit(solution)/shard_map/pack_rest/pallas_call | solution.py:431
  6.6 0.7 %collective-permute-start.1 = (s32[32,8,512]{2,1,0:T(8,128)}, s32[32,8,512]{2,1,0:T(8,128)S(1)}, u32[]{:S(2)}, u32[]{:S(2)}) collective-permute-start(s32[32,8,512]{2,1,0:T(8,128)} %get-tuple-element.14), channel_id=1, source_target_pairs={{8,16},{16,8},{9,17},{17,9},{10,18},{18,10},{11,19},{19,11},{12,20... | collective-permute-start | bytes 1572872 | tf_op jit(solution)/shard_map/ppermute | solution.py:553
  7.3 5.3 %collective-permute-start.3 = (s32[5,16,512]{2,1,0:T(8,128)S(1)}, s32[5,16,512]{2,1,0:T(8,128)S(1)}, u32[]{:S(2)}, u32[]{:S(2)}) collective-permute-start(s32[5,16,512]{2,1,0:T(8,128)S(1)} %get-tuple-element.18), channel_id=1, source_target_pairs={{0,1},{1,0},{2,3},{3,2},{4,5},{5,4},{6,7},{7,6},{8,9},{9,8},{10,11... | collective-permute-start | bytes 491528 | tf_op jit(solution)/shard_map/ppermute | solution.py:553
  12.8 5.2 %smooth.1.partial = f32[32,80,512]{2,1,0:T(8,128)S(1)} custom-call(s32[32,64,512]{2,1,0:T(8,128)} %c.1, bf16[1024,512]{1,0:T(8,128)(2,1)S(1)} %copy-done, bf16[80,192]{1,0:T(8,128)(2,1)S(1)} %copy-done.3), custom_call_target="tpu_custom_call" | custom-call | flops 1000000000 | bytes 4000000 | tf_op jit(solution)/shard_map/smooth/pallas_call | solution.py:446
  18.1 7.3 %collective-permute-done.3.edge = s32[5,16,512]{2,1,0:T(8,128)S(1)} collective-permute-done((s32[5,16,512]{2,1,0:T(8,128)S(1)}, s32[5,16,512]{2,1,0:T(8,128)S(1)}, u32[]{:S(2)}, u32[]{:S(2)}) %collective-permute-start.3) | collective-permute-done | bytes 163872 | tf_op jit(solution)/shard_map/ppermute | solution.py:553
  25.5 3.8 %depth.1 = (f32[32,80,512]{2,1,0:T(8,128)S(1)}, f32[24,80,512]{2,1,0:T(8,128)S(1)}) custom-call(f32[4]{0:T(128)S(1)} %add_convert_fusion.flags, s32[3]{0:T(128)S(1)} %pad_add_fusion.2.order, f32[32,80,512]{2,1,0:T(8,128)S(1)} %smooth.1.partial, s32[32,8,512]{2,1,0:T(8,128)S(1)} %collective-permute-done.xa, ...), custom_call_target="tpu_custom_call", output_to_operand_aliasing={{0}: (2, {})} | custom-call | flops 500000000 | bytes 4000000 | tf_op jit(solution)/shard_map/depth/pallas_call | solution.py:463
  29.3 0.7 %collective-permute-start.6 = (s32[10,8,512]{2,1,0:T(8,128)S(1)}, s32[10,8,512]{2,1,0:T(8,128)S(1)}, u32[]{:S(2)}, u32[]{:S(2)}) collective-permute-start(s32[10,8,512]{2,1,0:T(8,128)S(1)} %pad_add_fusion.1), channel_id=1, source_target_pairs={{8,16},{16,8},{9,17},{17,9},{10,18},{18,10},{11,19},{19,11},{12,20... | collective-permute-start | bytes 491528 | tf_op jit(solution)/shard_map/ppermute | solution.py:553
  30.0 4.2 %interior.1.behind = f32[4,64,512]{2,1,0:T(8,128)S(1)} custom-call(f32[24,80,512]{2,1,0:T(8,128)S(1)} %get-tuple-element.16.smoothed), custom_call_target="tpu_custom_call" | custom-call | flops 1000000000 | bytes 4000000 | tf_op jit(solution)/shard_map/interior/pallas_call | solution.py:480
  34.2 3.1 %collective-permute-start.5 = (s32[10,8,512]{2,1,0:T(8,128)S(1)}, s32[10,8,512]{2,1,0:T(8,128)S(1)}, u32[]{:S(2)}, u32[]{:S(2)}) collective-permute-start(s32[10,8,512]{2,1,0:T(8,128)S(1)} %pad_add_fusion), channel_id=1, source_target_pairs={{0,8},{8,0},{16,24},{24,16},{1,9},{9,1},{17,25},{25,17},{2,10},{10... | collective-permute-start | bytes 491528 | tf_op jit(solution)/shard_map/ppermute | solution.py:553
  37.4 1.0 %collective-permute-done.5 = s32[10,8,512]{2,1,0:T(8,128)S(1)} collective-permute-done((s32[10,8,512]{2,1,0:T(8,128)S(1)}, s32[10,8,512]{2,1,0:T(8,128)S(1)}, u32[]{:S(2)}, u32[]{:S(2)}) %collective-permute-start.5) | collective-permute-done | bytes 163872 | tf_op jit(solution)/shard_map/ppermute | solution.py:553
  38.4 2.8 %first_edge.1.behind = f32[4,64,512]{2,1,0:T(8,128)S(1)} custom-call(f32[4]{0:T(128)S(1)} %add_convert_fusion.flags, s32[3]{0:T(128)S(1)} %pad_add_fusion.2.order, f32[32,80,512]{2,1,0:T(8,128)S(1)} %get-tuple-element.15.plane, f32[24,80,512]{2,1,0:T(8,128)S(1)} %get-tuple-element.16.smoothed, s32[5,64,512]{2,1,0:T(8,128)S(1)} %collective-permute-done.4.block, ...), custom_call_target="tpu_custom_call" | custom-call | flops 300000000 | bytes 4000000 | tf_op jit(solution)/shard_map/first_edge/pallas_call | solution.py:494
  41.3 2.9 %last_edge.1 = (f32[1,4,8,512]{3,2,1,0:T(8,128)S(1)}, f32[7,80,512]{2,1,0:T(8,128)S(1)}) custom-call(f32[4]{0:T(128)S(1)} %add_convert_fusion.flags, s32[3]{0:T(128)S(1)} %pad_add_fusion.2.order, f32[32,80,512]{2,1,0:T(8,128)S(1)} %get-tuple-element.15.plane, f32[24,80,512]{2,1,0:T(8,128)S(1)} %get-tuple-element.16.smoothed, ...), custom_call_target="tpu_custom_call" | custom-call | flops 300000000 | bytes 4000000 | tf_op jit(solution)/shard_map/last_edge/pallas_call | solution.py:520
  44.1 2.5 %collective-permute-start.10 = (f32[1,4,8,512]{3,2,1,0:T(8,128)S(1)}, f32[1,4,8,512]{3,2,1,0:T(8,128)S(1)}, u32[]{:S(2)}, u32[]{:S(2)}) collective-permute-start(f32[1,4,8,512]{3,2,1,0:T(8,128)S(1)} %get-tuple-element.20), channel_id=1, source_target_pairs={{0,1},{1,0},{2,3},{3,2},{4,5},{5,4},{6,7},{7,6},{8,9},{9,8},{10,11... | collective-permute-start | bytes 196616 | tf_op jit(solution)/shard_map/ppermute | solution.py:553
  46.7 1.0 %shard_map.56 = f32[3,4,8,512]{3,2,1,0:T(8,128)S(1)} custom-call(s32[3]{0:T(128)S(1)} %pad_add_fusion.2.order, f32[7,80,512]{2,1,0:T(8,128)S(1)} %get-tuple-element.19.ends, f32[4,64,512]{2,1,0:T(8,128)S(1)} %first_edge.1.behind), custom_call_target="tpu_custom_call" | custom-call | flops 200000000 | bytes 4000000 | tf_op jit(solution)/shard_map/pallas_call | solution.py:538
  47.8 0.7 %shard_map.57 = f32[1,4,8,512]{3,2,1,0:T(8,128)S(1)} custom-call(s32[3]{0:T(128)S(1)} %pad_add_fusion.2.order, f32[7,80,512]{2,1,0:T(8,128)S(1)} %get-tuple-element.19.ends, f32[4,64,512]{2,1,0:T(8,128)S(1)} %first_edge.1.behind), custom_call_target="tpu_custom_call" | custom-call | flops 200000000 | bytes 4000000 | tf_op jit(solution)/shard_map/pallas_call | solution.py:538
  48.5 1.0 %shard_map.55 = f32[3,4,8,512]{3,2,1,0:T(8,128)S(1)} custom-call(s32[3]{0:T(128)S(1)} %pad_add_fusion.2.order, f32[7,80,512]{2,1,0:T(8,128)S(1)} %get-tuple-element.19.ends, f32[4,64,512]{2,1,0:T(8,128)S(1)} %first_edge.1.behind), custom_call_target="tpu_custom_call" | custom-call | flops 200000000 | bytes 4000000 | tf_op jit(solution)/shard_map/pallas_call | solution.py:538
  49.5 4.2 %collective-permute-start.11 = (f32[4,8,512]{2,1,0:T(8,128)S(1)}, f32[4,8,512]{2,1,0:T(8,128)S(1)}, u32[]{:S(2)}, u32[]{:S(2)}) collective-permute-start(f32[4,8,512]{2,1,0:T(8,128)S(1)} %fusion.1), channel_id=1, source_target_pairs={{0,6},{1,7},{2,4},{3,5},{4,2},{5,3},{6,0},{7,1},{8,14},{9,15},{10,... | collective-permute-start | bytes 196616 | tf_op jit(solution)/shard_map/ppermute | solution.py:592
  53.7 1.0 %collective-permute-done.7 = f32[3,4,8,512]{3,2,1,0:T(8,128)S(1)} collective-permute-done((f32[3,4,8,512]{3,2,1,0:T(8,128)S(1)}, f32[3,4,8,512]{3,2,1,0:T(8,128)S(1)}, u32[]{:S(2)}, u32[]{:S(2)}) %collective-permute-start.7) | collective-permute-done | bytes 196640 | tf_op jit(solution)/shard_map/ppermute | solution.py:553
  54.8 1.6 %collective-permute-start.8 = (f32[4,8,512]{2,1,0:T(8,128)S(1)}, f32[4,8,512]{2,1,0:T(8,128)S(1)}, u32[]{:S(2)}, u32[]{:S(2)}) collective-permute-start(f32[4,8,512]{2,1,0:T(8,128)S(1)} %get-tuple-element.28), channel_id=1, source_target_pairs={{0,2},{1,3},{2,0},{3,1},{4,6},{5,7},{6,4},{7,5},{8,10},{9,11},{10,... | collective-permute-start | bytes 196616 | tf_op jit(solution)/shard_map/ppermute | solution.py:592
  56.4 1.7 %collective-permute-start.9 = (f32[4,8,512]{2,1,0:T(8,128)S(1)}, f32[4,8,512]{2,1,0:T(8,128)S(1)}, u32[]{:S(2)}, u32[]{:S(2)}) collective-permute-start(f32[4,8,512]{2,1,0:T(8,128)S(1)} %get-tuple-element.29), channel_id=1, source_target_pairs={{0,4},{1,5},{2,6},{3,7},{4,0},{5,1},{6,2},{7,3},{8,12},{9,13},{10,... | collective-permute-start | bytes 196616 | tf_op jit(solution)/shard_map/ppermute | solution.py:592
  58.1 1.6 %collective-permute-done.8 = f32[4,8,512]{2,1,0:T(8,128)S(1)} collective-permute-done((f32[4,8,512]{2,1,0:T(8,128)S(1)}, f32[4,8,512]{2,1,0:T(8,128)S(1)}, u32[]{:S(2)}, u32[]{:S(2)}) %collective-permute-start.8) | collective-permute-done | bytes 65568 | tf_op jit(solution)/shard_map/ppermute | solution.py:592
  59.7 2.5 %collective-permute-done.9 = f32[4,8,512]{2,1,0:T(8,128)S(1)} collective-permute-done((f32[4,8,512]{2,1,0:T(8,128)S(1)}, f32[4,8,512]{2,1,0:T(8,128)S(1)}, u32[]{:S(2)}, u32[]{:S(2)}) %collective-permute-start.9) | collective-permute-done | bytes 65568 | tf_op jit(solution)/shard_map/ppermute | solution.py:592
  (39 shorter events, 1.9 us)
Async XLA Ops:
  0.0 12.8 %copy-start = (bf16[1024,512]{1,0:T(8,128)(2,1)S(1)}, bf16[1024,512]{1,0:T(8,128)(2,1)}, u32[]{:S(2)}) copy-start(bf16[1024,512]{1,0:T(8,128)(2,1)} %constant.73.clone.by) | copy-start | bytes 3145732
  0.0 12.8 %copy-start.3 = (bf16[80,192]{1,0:T(8,128)(2,1)S(1)}, bf16[80,192]{1,0:T(8,128)(2,1)}, u32[]{:S(2)}) copy-start(bf16[80,192]{1,0:T(8,128)(2,1)} %constant.75.clone.lx) | copy-start | bytes 92164
  2.1 27.2 %collective-permute-start.4 = (s32[5,64,512]{2,1,0:T(8,128)}, s32[5,64,512]{2,1,0:T(8,128)S(1)}, u32[]{:S(2)}, u32[]{:S(2)}) collective-permute-start(s32[5,64,512]{2,1,0:T(8,128)} %constant_dynamic-slice_fusion.3), channel_id=1, source_target_pairs={{1,2},{2,1},{3,4},{4,3},{5,6},{6,5},{9,10},{10,9},{11,12},{12,11},... | collective-permute-start | bytes 1966088 | tf_op jit(solution)/shard_map/ppermute | solution.py:553
  6.1 19.4 %collective-permute-start = (s32[32,8,512]{2,1,0:T(8,128)}, s32[32,8,512]{2,1,0:T(8,128)S(1)}, u32[]{:S(2)}, u32[]{:S(2)}) collective-permute-start(s32[32,8,512]{2,1,0:T(8,128)} %get-tuple-element.13), channel_id=1, source_target_pairs={{0,8},{8,0},{16,24},{24,16},{1,9},{9,1},{17,25},{25,17},{2,10},{10... | collective-permute-start | bytes 1572872 | tf_op jit(solution)/shard_map/ppermute | solution.py:553
  6.6 18.8 %collective-permute-start.1 = (s32[32,8,512]{2,1,0:T(8,128)}, s32[32,8,512]{2,1,0:T(8,128)S(1)}, u32[]{:S(2)}, u32[]{:S(2)}) collective-permute-start(s32[32,8,512]{2,1,0:T(8,128)} %get-tuple-element.14), channel_id=1, source_target_pairs={{8,16},{16,8},{9,17},{17,9},{10,18},{18,10},{11,19},{19,11},{12,20... | collective-permute-start | bytes 1572872 | tf_op jit(solution)/shard_map/ppermute | solution.py:553
  7.3 18.1 %collective-permute-start.3 = (s32[5,16,512]{2,1,0:T(8,128)S(1)}, s32[5,16,512]{2,1,0:T(8,128)S(1)}, u32[]{:S(2)}, u32[]{:S(2)}) collective-permute-start(s32[5,16,512]{2,1,0:T(8,128)S(1)} %get-tuple-element.18), channel_id=1, source_target_pairs={{0,1},{1,0},{2,3},{3,2},{4,5},{5,4},{6,7},{7,6},{8,9},{9,8},{10,11... | collective-permute-start | bytes 491528 | tf_op jit(solution)/shard_map/ppermute | solution.py:553
  12.7 28.6 %collective-permute-start.2 = (s32[5,48,512]{2,1,0:T(8,128)}, s32[5,48,512]{2,1,0:T(8,128)}, u32[]{:S(2)}, u32[]{:S(2)}) collective-permute-start(s32[5,48,512]{2,1,0:T(8,128)} %get-tuple-element.17), channel_id=1, source_target_pairs={{0,1},{1,0},{2,3},{3,2},{4,5},{5,4},{6,7},{7,6},{8,9},{9,8},{10,11... | collective-permute-start | bytes 1474568 | tf_op jit(solution)/shard_map/ppermute | solution.py:553
  12.8 12.7 %copy-start.2 = (bf16[2,128,192]{2,1,0:T(8,128)(2,1)S(1)}, bf16[2,128,192]{2,1,0:T(8,128)(2,1)}, u32[]{:S(2)}) copy-start(bf16[2,128,192]{2,1,0:T(8,128)(2,1)} %constant.76.clone.lx) | copy-start | bytes 294916
  29.3 9.1 %copy-start.1 = (bf16[2,80,240]{2,1,0:T(8,128)(2,1)S(1)}, bf16[2,80,240]{2,1,0:T(8,128)(2,1)}, u32[]{:S(2)}) copy-start(bf16[2,80,240]{2,1,0:T(8,128)(2,1)} %constant.74.clone.lx) | copy-start | bytes 230404
  29.3 8.0 %collective-permute-start.6 = (s32[10,8,512]{2,1,0:T(8,128)S(1)}, s32[10,8,512]{2,1,0:T(8,128)S(1)}, u32[]{:S(2)}, u32[]{:S(2)}) collective-permute-start(s32[10,8,512]{2,1,0:T(8,128)S(1)} %pad_add_fusion.1), channel_id=1, source_target_pairs={{8,16},{16,8},{9,17},{17,9},{10,18},{18,10},{11,19},{19,11},{12,20... | collective-permute-start | bytes 491528 | tf_op jit(solution)/shard_map/ppermute | solution.py:553
  34.2 4.2 %collective-permute-start.5 = (s32[10,8,512]{2,1,0:T(8,128)S(1)}, s32[10,8,512]{2,1,0:T(8,128)S(1)}, u32[]{:S(2)}, u32[]{:S(2)}) collective-permute-start(s32[10,8,512]{2,1,0:T(8,128)S(1)} %pad_add_fusion), channel_id=1, source_target_pairs={{0,8},{8,0},{16,24},{24,16},{1,9},{9,1},{17,25},{25,17},{2,10},{10... | collective-permute-start | bytes 491528 | tf_op jit(solution)/shard_map/ppermute | solution.py:553
  44.1 5.3 %collective-permute-start.10 = (f32[1,4,8,512]{3,2,1,0:T(8,128)S(1)}, f32[1,4,8,512]{3,2,1,0:T(8,128)S(1)}, u32[]{:S(2)}, u32[]{:S(2)}) collective-permute-start(f32[1,4,8,512]{3,2,1,0:T(8,128)S(1)} %get-tuple-element.20), channel_id=1, source_target_pairs={{0,1},{1,0},{2,3},{3,2},{4,5},{5,4},{6,7},{7,6},{8,9},{9,8},{10,11... | collective-permute-start | bytes 196616 | tf_op jit(solution)/shard_map/ppermute | solution.py:553
  47.7 7.0 %collective-permute-start.7 = (f32[3,4,8,512]{3,2,1,0:T(8,128)S(1)}, f32[3,4,8,512]{3,2,1,0:T(8,128)S(1)}, u32[]{:S(2)}, u32[]{:S(2)}) collective-permute-start(f32[3,4,8,512]{3,2,1,0:T(8,128)S(1)} %shard_map.56), channel_id=1, source_target_pairs={{0,1},{1,0},{2,3},{3,2},{4,5},{5,4},{6,7},{7,6},{8,9},{9,8},{10,11... | collective-permute-start | bytes 589832 | tf_op jit(solution)/shard_map/ppermute | solution.py:553
  49.5 8.6 %collective-permute-start.11 = (f32[4,8,512]{2,1,0:T(8,128)S(1)}, f32[4,8,512]{2,1,0:T(8,128)S(1)}, u32[]{:S(2)}, u32[]{:S(2)}) collective-permute-start(f32[4,8,512]{2,1,0:T(8,128)S(1)} %fusion.1), channel_id=1, source_target_pairs={{0,6},{1,7},{2,4},{3,5},{4,2},{5,3},{6,0},{7,1},{8,14},{9,15},{10,... | collective-permute-start | bytes 196616 | tf_op jit(solution)/shard_map/ppermute | solution.py:592
  54.8 5.0 %collective-permute-start.8 = (f32[4,8,512]{2,1,0:T(8,128)S(1)}, f32[4,8,512]{2,1,0:T(8,128)S(1)}, u32[]{:S(2)}, u32[]{:S(2)}) collective-permute-start(f32[4,8,512]{2,1,0:T(8,128)S(1)} %get-tuple-element.28), channel_id=1, source_target_pairs={{0,2},{1,3},{2,0},{3,1},{4,6},{5,7},{6,4},{7,5},{8,10},{9,11},{10,... | collective-permute-start | bytes 196616 | tf_op jit(solution)/shard_map/ppermute | solution.py:592
  56.4 5.9 %collective-permute-start.9 = (f32[4,8,512]{2,1,0:T(8,128)S(1)}, f32[4,8,512]{2,1,0:T(8,128)S(1)}, u32[]{:S(2)}, u32[]{:S(2)}) collective-permute-start(f32[4,8,512]{2,1,0:T(8,128)S(1)} %get-tuple-element.29), channel_id=1, source_target_pairs={{0,4},{1,5},{2,6},{3,7},{4,0},{5,1},{6,2},{7,3},{8,12},{9,13},{10,... | collective-permute-start | bytes 196616 | tf_op jit(solution)/shard_map/ppermute | solution.py:592

commit v15 on v13

--- a/solution.py
+++ b/solution.py
@@ -196,10 +196,7 @@
 
 
 def pack_block_kernel(where, c, block, sems):
-    half = block.shape[1] // 2
-    layers = pl.ds(where[1], REACH)
-    parts = [pl.ds(n * half, half) for n in range(2)]
-    run_copies([(c.at[layers, part], block.at[:, part]) for part in parts], sems)
+    run_copies([(c.at[where[1] + n], block.at[n]) for n in range(REACH)], sems)
 
 
 def pack_rest_kernel(where, c, side_b, edge, middle, side_a, sems):
@@ -363,8 +360,9 @@
 
 def render_half(scale, is_front, ends, behind, image, tile_of, half):
     places, _, owned, _ = image.shape
-    tiles = places * (owned // 8)
-    edge_render(scale, is_front, ends, behind, image, tiles, tile_of, half * tiles)
+    owner_tiles = owned // 8
+    first = half * owner_tiles
+    edge_render(scale, is_front, ends, behind, image, places * owner_tiles, tile_of, first)
 
 
 def last_edge_kernel(scale, split, flags, order, plane, smoothed, middle_any, edge, ca, cb,
@@ -435,7 +433,7 @@
         out_shape=jax.ShapeDtypeStruct((REACH, rows, columns), c.dtype),
         in_specs=[smem(), in_hbm()],
         out_specs=whole(1)[0],
-        scratch_shapes=[pltpu.SemaphoreType.DMA((2,))],
+        scratch_shapes=[pltpu.SemaphoreType.DMA((REACH,))],
         compiler_params=params(8),
         name="pack_block",
     )(where, c)
@@ -524,16 +522,20 @@
     )(flags, order, plane, *operands)
 
 
-def half_shape(split, columns):
+def part_sizes(pairs):
+    return 1, 1, pairs - 2
+
+
+def part_shape(split, part, columns):
     pairs, owner_tiles = split
-    return pairs // 2, 4, owner_tiles * 8, columns
+    return part_sizes(pairs)[part], 4, owner_tiles * 8, columns
 
 
 def call_last_edge(scale, split, flags, order, plane, *operands):
     _, ext, columns = plane.shape
     f32 = jnp.float32
     rows = ext - 2 * PAD
-    images = [half_shape(split, columns) if split else (4, rows, columns)]
+    images = [part_shape(split, 0, columns) if split else (4, rows, columns)]
     shapes = [*images, (REACH + 2, ext, columns)]
     return pl.pallas_call(
         functools.partial(last_edge_kernel, scale, split),
@@ -552,7 +554,7 @@
 
 
 def call_part_edge(scale, split, half, kept, order, ends, behind):
-    image = jax.ShapeDtypeStruct(half_shape(split, ends.shape[2]), jnp.float32)
+    image = jax.ShapeDtypeStruct(part_shape(split, half, ends.shape[2]), jnp.float32)
     return pl.pallas_call(
         functools.partial(part_edge_kernel, scale, split, half, kept),
         out_shape=image,
@@ -589,7 +591,7 @@
     for wanted in (1 - parity, parity):
         chosen = lax.dynamic_index_in_dim(ordered, wanted, 2, keepdims=False)
         chosen = jnp.moveaxis(chosen, 1, 0)
-        both.append((chosen[: pairs // 2], chosen[pairs // 2 :]))
+        both.append((chosen[:1], chosen[1:2], chosen[2:]))
     return both
 
 
@@ -603,8 +605,8 @@
         owned, columns = send.shape[2:]
         got = swap(send, "depth", 0)
         joined = jnp.where(parity == 0, over(keep, got), over(got, keep))
-        for place in range(pairs // 2):
-            step = pairs - 1 - half * (pairs // 2) - place
+        for place in range(send.shape[0]):
+            step = pairs - 1 - half - place
             piece = joined[place]
             if step:
                 piece = lax.ppermute(piece, "depth", [(i, i ^ (2 * step)) for i in range(count)])
@@ -672,8 +674,8 @@
     )
     if split:
         last = (order, ends, layers)
-        sends.append(call_part_edge(scale, split, 1, False, *last))
-        keeps = [call_part_edge(scale, split, half, True, *last) for half in range(2)]
+        sends += [call_part_edge(scale, split, part, False, *last) for part in (1, 2)]
+        keeps = [call_part_edge(scale, split, part, True, *last) for part in range(3)]
     else:
         sends, keeps = halves_of(sends[0])
     return exchange(sends, keeps)

time: 61.9 us -> 62.9 us (1.016)
  waiting for transfers between devices: 14.2 us -> 12.5 us
  Pallas kernels: 26.7 us -> 28 us
  starting transfers between devices: 19.3 us -> 20.6 us
    ppermute x9 -> x10, starting transfers between devices: 14.5 us -> 16.4 us  [swap(): return lax.ppermute(value, axis, pairs)]
    ppermute x9 -> x10, waiting for transfers between devices: 9.46 us -> 7.62 us  [swap(): return lax.ppermute(value, axis, pairs)]
    pallas_call x3 -> x5, Pallas kernels: 2.41 us -> 3.68 us  [call_part_edge(): pl.pallas_call(functools.partial(part_edge_kernel, scale, split, half, ke...]
  transfers between devices with their start and end apart: 12 -> 13, of which waited for: 6 -> 5; matrix products, arithmetic and copies ran while one was open for 1% -> 1% of each run, Pallas kernels for 36% -> 36%
where the time goes in v15:
time: 62.9 us; the launch traced here: 62.6 us
  Pallas kernels  28 us (45%)
  starting transfers between devices  20.6 us (33%)
  waiting for transfers between devices  12.5 us (20%)
  other arithmetic  1.06 us (2%)
    ppermute x10, starting transfers between devices, swap(): return lax.ppermute(value, axis, pairs)  16.4 us
    ppermute x10, waiting for transfers between devices, swap(): return lax.ppermute(value, axis, pairs)  7.62 us
    pallas_call x1, Pallas kernels, call_smooth(): pl.pallas_call(functools.partial(smooth_kernel, group), out_shape=jax.Sha...  5.23 us
    ppermute x3, waiting for transfers between devices, exchange(): lax.ppermute(piece, 'depth', [(i, i ^ 2 * step) for i in range(count)])  4.9 us
    pallas_call x1, Pallas kernels, call_depth(): pl.pallas_call(depth_kernel, out_shape=(jax.ShapeDtypeStruct(partial.shap...  4.29 us
    ppermute x3, starting transfers between devices, exchange(): lax.ppermute(piece, 'depth', [(i, i ^ 2 * step) for i in range(count)])  4.21 us
    pallas_call x1, Pallas kernels, call_interior(): pl.pallas_call(functools.partial(interior_kernel, scale), out_shape=jax.S...  4.19 us
    pallas_call x5, Pallas kernels, call_part_edge(): pl.pallas_call(functools.partial(part_edge_kernel, scale, split, half, ke...  3.68 us
  transfers between devices with their start and end apart: 13, of which 5 were waited for; matrix products, arithmetic and copies ran while one was open for 1% of the time, Pallas kernels for 36%

profile of v15, /device:TPU:0, one launch (start us, length us, event | category | flops | bytes accessed | tf_op | source)
XLA Modules:
  0.0 62.6 jit_solution(14894157043232917779)
XLA Ops:
  0.1 1.7 %pack_block.1 = s32[5,64,512]{2,1,0:T(8,128)S(1)} custom-call(s32[4]{0:T(128)S(1)} %pad_add_fusion.3.where, s32[32,64,512]{2,1,0:T(8,128)} %c.3), custom_call_target="tpu_custom_call" | custom-call | tf_op jit(solution)/shard_map/pack_block/pallas_call | solution.py:431
  1.8 0.7 %collective-permute-start.4 = (s32[5,64,512]{2,1,0:T(8,128)S(1)}, s32[5,64,512]{2,1,0:T(8,128)S(1)}, u32[]{:S(2)}, u32[]{:S(2)}) collective-permute-start(s32[5,64,512]{2,1,0:T(8,128)S(1)} %pack_block.1), channel_id=1, source_target_pairs={{1,2},{2,1},{3,4},{4,3},{5,6},{6,5},{9,10},{10,9},{11,12},{12,11},... | collective-permute-start | bytes 1966088 | tf_op jit(solution)/shard_map/ppermute | solution.py:573
  2.5 3.1 %pack_rest.1 = (s32[32,8,512]{2,1,0:T(8,128)}, s32[5,16,512]{2,1,0:T(8,128)S(1)}, s32[5,48,512]{2,1,0:T(8,128)}, s32[32,8,512]{2,1,0:T(8,128)}) custom-call(s32[4]{0:T(128)S(1)} %pad_add_fusion.3.where, s32[32,64,512]{2,1,0:T(8,128)} %c.3), custom_call_target="tpu_custom_call" | custom-call | tf_op jit(solution)/shard_map/pack_rest/pallas_call | solution.py:447
  6.3 1.5 %collective-permute-start.1 = (s32[32,8,512]{2,1,0:T(8,128)}, s32[32,8,512]{2,1,0:T(8,128)}, u32[]{:S(2)}, u32[]{:S(2)}) collective-permute-start(s32[32,8,512]{2,1,0:T(8,128)} %get-tuple-element.14), channel_id=1, source_target_pairs={{8,16},{16,8},{9,17},{17,9},{10,18},{18,10},{11,19},{19,11},{12,20... | collective-permute-start | bytes 1572872 | tf_op jit(solution)/shard_map/ppermute | solution.py:573
  7.7 5.3 %collective-permute-start.3 = (s32[5,16,512]{2,1,0:T(8,128)S(1)}, s32[5,16,512]{2,1,0:T(8,128)S(1)}, u32[]{:S(2)}, u32[]{:S(2)}) collective-permute-start(s32[5,16,512]{2,1,0:T(8,128)S(1)} %get-tuple-element.18), channel_id=1, source_target_pairs={{0,1},{1,0},{2,3},{3,2},{4,5},{5,4},{6,7},{7,6},{8,9},{9,8},{10,11... | collective-permute-start | bytes 491528 | tf_op jit(solution)/shard_map/ppermute | solution.py:573
  13.1 5.2 %smooth.1.partial = f32[32,80,512]{2,1,0:T(8,128)S(1)} custom-call(s32[32,64,512]{2,1,0:T(8,128)} %c.3, bf16[1024,512]{1,0:T(8,128)(2,1)S(1)} %copy-done, bf16[80,192]{1,0:T(8,128)(2,1)S(1)} %copy-done.3), custom_call_target="tpu_custom_call" | custom-call | flops 1000000000 | bytes 4000000 | tf_op jit(solution)/shard_map/smooth/pallas_call | solution.py:462
  18.4 6.6 %collective-permute-done.3.edge = s32[5,16,512]{2,1,0:T(8,128)S(1)} collective-permute-done((s32[5,16,512]{2,1,0:T(8,128)S(1)}, s32[5,16,512]{2,1,0:T(8,128)S(1)}, u32[]{:S(2)}, u32[]{:S(2)}) %collective-permute-start.3) | collective-permute-done | bytes 163872 | tf_op jit(solution)/shard_map/ppermute | solution.py:573
  25.0 4.3 %depth.1 = (f32[32,80,512]{2,1,0:T(8,128)S(1)}, f32[24,80,512]{2,1,0:T(8,128)S(1)}) custom-call(f32[4]{0:T(128)S(1)} %add_convert_fusion.flags, s32[3]{0:T(128)S(1)} %pad_add_fusion.2.order, f32[32,80,512]{2,1,0:T(8,128)S(1)} %smooth.1.partial, s32[32,8,512]{2,1,0:T(8,128)S(1)} %collective-permute-done.xa, ...), custom_call_target="tpu_custom_call", output_to_operand_aliasing={{0}: (2, {})} | custom-call | flops 500000000 | bytes 4000000 | tf_op jit(solution)/shard_map/depth/pallas_call | solution.py:479
  30.1 4.2 %interior.1.behind = f32[4,64,512]{2,1,0:T(8,128)S(1)} custom-call(f32[24,80,512]{2,1,0:T(8,128)S(1)} %get-tuple-element.16.smoothed), custom_call_target="tpu_custom_call" | custom-call | flops 1000000000 | bytes 4000000 | tf_op jit(solution)/shard_map/interior/pallas_call | solution.py:496
  34.3 3.1 %collective-permute-start.5 = (s32[10,8,512]{2,1,0:T(8,128)S(1)}, s32[10,8,512]{2,1,0:T(8,128)S(1)}, u32[]{:S(2)}, u32[]{:S(2)}) collective-permute-start(s32[10,8,512]{2,1,0:T(8,128)S(1)} %pad_add_fusion), channel_id=1, source_target_pairs={{0,8},{8,0},{16,24},{24,16},{1,9},{9,1},{17,25},{25,17},{2,10},{10... | collective-permute-start | bytes 491528 | tf_op jit(solution)/shard_map/ppermute | solution.py:573
  37.5 1.0 %collective-permute-done.5 = s32[10,8,512]{2,1,0:T(8,128)S(1)} collective-permute-done((s32[10,8,512]{2,1,0:T(8,128)S(1)}, s32[10,8,512]{2,1,0:T(8,128)S(1)}, u32[]{:S(2)}, u32[]{:S(2)}) %collective-permute-start.5) | collective-permute-done | bytes 163872 | tf_op jit(solution)/shard_map/ppermute | solution.py:573
  38.5 2.8 %first_edge.1.behind = f32[4,64,512]{2,1,0:T(8,128)S(1)} custom-call(f32[4]{0:T(128)S(1)} %add_convert_fusion.flags, s32[3]{0:T(128)S(1)} %pad_add_fusion.2.order, f32[32,80,512]{2,1,0:T(8,128)S(1)} %get-tuple-element.15.plane, f32[24,80,512]{2,1,0:T(8,128)S(1)} %get-tuple-element.16.smoothed, s32[5,64,512]{2,1,0:T(8,128)S(1)} %collective-permute-done.4.block, ...), custom_call_target="tpu_custom_call" | custom-call | flops 300000000 | bytes 4000000 | tf_op jit(solution)/shard_map/first_edge/pallas_call | solution.py:510
  41.3 2.9 %last_edge.1 = (f32[1,4,8,512]{3,2,1,0:T(8,128)S(1)}, f32[7,80,512]{2,1,0:T(8,128)S(1)}) custom-call(f32[4]{0:T(128)S(1)} %add_convert_fusion.flags, s32[3]{0:T(128)S(1)} %pad_add_fusion.2.order, f32[32,80,512]{2,1,0:T(8,128)S(1)} %get-tuple-element.15.plane, f32[24,80,512]{2,1,0:T(8,128)S(1)} %get-tuple-element.16.smoothed, ...), custom_call_target="tpu_custom_call" | custom-call | flops 300000000 | bytes 4000000 | tf_op jit(solution)/shard_map/last_edge/pallas_call | solution.py:540
  44.2 0.7 %shard_map.58 = f32[1,4,8,512]{3,2,1,0:T(8,128)S(1)} custom-call(s32[3]{0:T(128)S(1)} %pad_add_fusion.2.order, f32[7,80,512]{2,1,0:T(8,128)S(1)} %get-tuple-element.19.ends, f32[4,64,512]{2,1,0:T(8,128)S(1)} %first_edge.1.behind), custom_call_target="tpu_custom_call" | custom-call | flops 200000000 | bytes 4000000 | tf_op jit(solution)/shard_map/pallas_call | solution.py:558
  44.9 2.5 %collective-permute-start.9 = (f32[1,4,8,512]{3,2,1,0:T(8,128)S(1)}, f32[1,4,8,512]{3,2,1,0:T(8,128)S(1)}, u32[]{:S(2)}, u32[]{:S(2)}) collective-permute-start(f32[1,4,8,512]{3,2,1,0:T(8,128)S(1)} %shard_map.58), channel_id=1, source_target_pairs={{0,1},{1,0},{2,3},{3,2},{4,5},{5,4},{6,7},{7,6},{8,9},{9,8},{10,11... | collective-permute-start | bytes 196616 | tf_op jit(solution)/shard_map/ppermute | solution.py:573
  47.4 0.8 %shard_map.56 = f32[2,4,8,512]{3,2,1,0:T(8,128)S(1)} custom-call(s32[3]{0:T(128)S(1)} %pad_add_fusion.2.order, f32[7,80,512]{2,1,0:T(8,128)S(1)} %get-tuple-element.19.ends, f32[4,64,512]{2,1,0:T(8,128)S(1)} %first_edge.1.behind), custom_call_target="tpu_custom_call" | custom-call | flops 200000000 | bytes 4000000 | tf_op jit(solution)/shard_map/pallas_call | solution.py:558
  48.3 2.0 %collective-permute-start.7 = (f32[2,4,8,512]{3,2,1,0:T(8,128)S(1)}, f32[2,4,8,512]{3,2,1,0:T(8,128)S(1)}, u32[]{:S(2)}, u32[]{:S(2)}) collective-permute-start(f32[2,4,8,512]{3,2,1,0:T(8,128)S(1)} %shard_map.56), channel_id=1, source_target_pairs={{0,1},{1,0},{2,3},{3,2},{4,5},{5,4},{6,7},{7,6},{8,9},{9,8},{10,11... | collective-permute-start | bytes 393224 | tf_op jit(solution)/shard_map/ppermute | solution.py:573
  50.3 0.7 %shard_map.57 = f32[1,4,8,512]{3,2,1,0:T(8,128)S(1)} custom-call(s32[3]{0:T(128)S(1)} %pad_add_fusion.2.order, f32[7,80,512]{2,1,0:T(8,128)S(1)} %get-tuple-element.19.ends, f32[4,64,512]{2,1,0:T(8,128)S(1)} %first_edge.1.behind), custom_call_target="tpu_custom_call" | custom-call | flops 200000000 | bytes 4000000 | tf_op jit(solution)/shard_map/pallas_call | solution.py:558
  51.0 0.7 %shard_map.59 = f32[1,4,8,512]{3,2,1,0:T(8,128)S(1)} custom-call(s32[3]{0:T(128)S(1)} %pad_add_fusion.2.order, f32[7,80,512]{2,1,0:T(8,128)S(1)} %get-tuple-element.19.ends, f32[4,64,512]{2,1,0:T(8,128)S(1)} %first_edge.1.behind), custom_call_target="tpu_custom_call" | custom-call | flops 200000000 | bytes 4000000 | tf_op jit(solution)/shard_map/pallas_call | solution.py:558
  51.7 0.8 %shard_map.55 = f32[2,4,8,512]{3,2,1,0:T(8,128)S(1)} custom-call(s32[3]{0:T(128)S(1)} %pad_add_fusion.2.order, f32[7,80,512]{2,1,0:T(8,128)S(1)} %get-tuple-element.19.ends, f32[4,64,512]{2,1,0:T(8,128)S(1)} %first_edge.1.behind), custom_call_target="tpu_custom_call" | custom-call | flops 200000000 | bytes 4000000 | tf_op jit(solution)/shard_map/pallas_call | solution.py:558
  52.6 2.7 %collective-permute-start.10 = (f32[4,8,512]{2,1,0:T(8,128)S(1)}, f32[4,8,512]{2,1,0:T(8,128)S(1)}, u32[]{:S(2)}, u32[]{:S(2)}) collective-permute-start(f32[4,8,512]{2,1,0:T(8,128)S(1)} %fusion.2), channel_id=1, source_target_pairs={{0,4},{1,5},{2,6},{3,7},{4,0},{5,1},{6,2},{7,3},{8,12},{9,13},{10,... | collective-permute-start | bytes 196616 | tf_op jit(solution)/shard_map/ppermute | solution.py:612
  55.3 1.4 %collective-permute-start.12 = (f32[4,8,512]{2,1,0:T(8,128)S(1)}, f32[4,8,512]{2,1,0:T(8,128)S(1)}, u32[]{:S(2)}, u32[]{:S(2)}) collective-permute-start(f32[4,8,512]{2,1,0:T(8,128)S(1)} %fusion.1), channel_id=1, source_target_pairs={{0,6},{1,7},{2,4},{3,5},{4,2},{5,3},{6,0},{7,1},{8,14},{9,15},{10,... | collective-permute-start | bytes 196616 | tf_op jit(solution)/shard_map/ppermute | solution.py:612
  56.9 3.3 %collective-permute-done.10 = f32[4,8,512]{2,1,0:T(8,128)S(1)} collective-permute-done((f32[4,8,512]{2,1,0:T(8,128)S(1)}, f32[4,8,512]{2,1,0:T(8,128)S(1)}, u32[]{:S(2)}, u32[]{:S(2)}) %collective-permute-start.10) | collective-permute-done | bytes 65568 | tf_op jit(solution)/shard_map/ppermute | solution.py:612
  60.2 1.3 %collective-permute-done.12 = f32[4,8,512]{2,1,0:T(8,128)S(1)} collective-permute-done((f32[4,8,512]{2,1,0:T(8,128)S(1)}, f32[4,8,512]{2,1,0:T(8,128)S(1)}, u32[]{:S(2)}, u32[]{:S(2)}) %collective-permute-start.12) | collective-permute-done | bytes 65568 | tf_op jit(solution)/shard_map/ppermute | solution.py:612
  (46 shorter events, 2.9 us)
Async XLA Ops:
  0.1 13.0 %copy-start = (bf16[1024,512]{1,0:T(8,128)(2,1)S(1)}, bf16[1024,512]{1,0:T(8,128)(2,1)}, u32[]{:S(2)}) copy-start(bf16[1024,512]{1,0:T(8,128)(2,1)} %constant.71.clone.by) | copy-start | bytes 3145732
  0.1 13.0 %copy-start.3 = (bf16[80,192]{1,0:T(8,128)(2,1)S(1)}, bf16[80,192]{1,0:T(8,128)(2,1)}, u32[]{:S(2)}) copy-start(bf16[80,192]{1,0:T(8,128)(2,1)} %constant.73.clone.lx) | copy-start | bytes 92164
  1.8 27.5 %collective-permute-start.4 = (s32[5,64,512]{2,1,0:T(8,128)S(1)}, s32[5,64,512]{2,1,0:T(8,128)S(1)}, u32[]{:S(2)}, u32[]{:S(2)}) collective-permute-start(s32[5,64,512]{2,1,0:T(8,128)S(1)} %pack_block.1), channel_id=1, source_target_pairs={{1,2},{2,1},{3,4},{4,3},{5,6},{6,5},{9,10},{10,9},{11,12},{12,11},... | collective-permute-start | bytes 1966088 | tf_op jit(solution)/shard_map/ppermute | solution.py:573
  5.7 19.3 %collective-permute-start = (s32[32,8,512]{2,1,0:T(8,128)}, s32[32,8,512]{2,1,0:T(8,128)S(1)}, u32[]{:S(2)}, u32[]{:S(2)}) collective-permute-start(s32[32,8,512]{2,1,0:T(8,128)} %get-tuple-element.13), channel_id=1, source_target_pairs={{0,8},{8,0},{16,24},{24,16},{1,9},{9,1},{17,25},{25,17},{2,10},{10... | collective-permute-start | bytes 1572872 | tf_op jit(solution)/shard_map/ppermute | solution.py:573
  6.3 18.8 %collective-permute-start.1 = (s32[32,8,512]{2,1,0:T(8,128)}, s32[32,8,512]{2,1,0:T(8,128)}, u32[]{:S(2)}, u32[]{:S(2)}) collective-permute-start(s32[32,8,512]{2,1,0:T(8,128)} %get-tuple-element.14), channel_id=1, source_target_pairs={{8,16},{16,8},{9,17},{17,9},{10,18},{18,10},{11,19},{19,11},{12,20... | collective-permute-start | bytes 1572872 | tf_op jit(solution)/shard_map/ppermute | solution.py:573
  7.7 17.3 %collective-permute-start.3 = (s32[5,16,512]{2,1,0:T(8,128)S(1)}, s32[5,16,512]{2,1,0:T(8,128)S(1)}, u32[]{:S(2)}, u32[]{:S(2)}) collective-permute-start(s32[5,16,512]{2,1,0:T(8,128)S(1)} %get-tuple-element.18), channel_id=1, source_target_pairs={{0,1},{1,0},{2,3},{3,2},{4,5},{5,4},{6,7},{7,6},{8,9},{9,8},{10,11... | collective-permute-start | bytes 491528 | tf_op jit(solution)/shard_map/ppermute | solution.py:573
  13.0 28.3 %collective-permute-start.2 = (s32[5,48,512]{2,1,0:T(8,128)}, s32[5,48,512]{2,1,0:T(8,128)}, u32[]{:S(2)}, u32[]{:S(2)}) collective-permute-start(s32[5,48,512]{2,1,0:T(8,128)} %get-tuple-element.17), channel_id=1, source_target_pairs={{0,1},{1,0},{2,3},{3,2},{4,5},{5,4},{6,7},{7,6},{8,9},{9,8},{10,11... | collective-permute-start | bytes 1474568 | tf_op jit(solution)/shard_map/ppermute | solution.py:573
  13.1 12.0 %copy-start.2 = (bf16[2,128,192]{2,1,0:T(8,128)(2,1)S(1)}, bf16[2,128,192]{2,1,0:T(8,128)(2,1)}, u32[]{:S(2)}) copy-start(bf16[2,128,192]{2,1,0:T(8,128)(2,1)} %constant.74.clone.lx) | copy-start | bytes 294916
  29.3 9.1 %copy-start.1 = (bf16[2,80,240]{2,1,0:T(8,128)(2,1)S(1)}, bf16[2,80,240]{2,1,0:T(8,128)(2,1)}, u32[]{:S(2)}) copy-start(bf16[2,80,240]{2,1,0:T(8,128)(2,1)} %constant.72.clone.lx) | copy-start | bytes 230404
  29.4 8.0 %collective-permute-start.6 = (s32[10,8,512]{2,1,0:T(8,128)S(1)}, s32[10,8,512]{2,1,0:T(8,128)S(1)}, u32[]{:S(2)}, u32[]{:S(2)}) collective-permute-start(s32[10,8,512]{2,1,0:T(8,128)S(1)} %pad_add_fusion.1), channel_id=1, source_target_pairs={{8,16},{16,8},{9,17},{17,9},{10,18},{18,10},{11,19},{19,11},{12,20... | collective-permute-start | bytes 491528 | tf_op jit(solution)/shard_map/ppermute | solution.py:573
  34.3 4.2 %collective-permute-start.5 = (s32[10,8,512]{2,1,0:T(8,128)S(1)}, s32[10,8,512]{2,1,0:T(8,128)S(1)}, u32[]{:S(2)}, u32[]{:S(2)}) collective-permute-start(s32[10,8,512]{2,1,0:T(8,128)S(1)} %pad_add_fusion), channel_id=1, source_target_pairs={{0,8},{8,0},{16,24},{24,16},{1,9},{9,1},{17,25},{25,17},{2,10},{10... | collective-permute-start | bytes 491528 | tf_op jit(solution)/shard_map/ppermute | solution.py:573
  44.9 7.6 %collective-permute-start.9 = (f32[1,4,8,512]{3,2,1,0:T(8,128)S(1)}, f32[1,4,8,512]{3,2,1,0:T(8,128)S(1)}, u32[]{:S(2)}, u32[]{:S(2)}) collective-permute-start(f32[1,4,8,512]{3,2,1,0:T(8,128)S(1)} %shard_map.58), channel_id=1, source_target_pairs={{0,1},{1,0},{2,3},{3,2},{4,5},{5,4},{6,7},{7,6},{8,9},{9,8},{10,11... | collective-permute-start | bytes 196616 | tf_op jit(solution)/shard_map/ppermute | solution.py:573
  48.2 7.0 %collective-permute-start.11 = (f32[1,4,8,512]{3,2,1,0:T(8,128)S(1)}, f32[1,4,8,512]{3,2,1,0:T(8,128)S(1)}, u32[]{:S(2)}, u32[]{:S(2)}) collective-permute-start(f32[1,4,8,512]{3,2,1,0:T(8,128)S(1)} %get-tuple-element.20), channel_id=1, source_target_pairs={{0,1},{1,0},{2,3},{3,2},{4,5},{5,4},{6,7},{7,6},{8,9},{9,8},{10,11... | collective-permute-start | bytes 196616 | tf_op jit(solution)/shard_map/ppermute | solution.py:573
  48.3 8.4 %collective-permute-start.7 = (f32[2,4,8,512]{3,2,1,0:T(8,128)S(1)}, f32[2,4,8,512]{3,2,1,0:T(8,128)S(1)}, u32[]{:S(2)}, u32[]{:S(2)}) collective-permute-start(f32[2,4,8,512]{3,2,1,0:T(8,128)S(1)} %shard_map.56), channel_id=1, source_target_pairs={{0,1},{1,0},{2,3},{3,2},{4,5},{5,4},{6,7},{7,6},{8,9},{9,8},{10,11... | collective-permute-start | bytes 393224 | tf_op jit(solution)/shard_map/ppermute | solution.py:573
  52.6 7.6 %collective-permute-start.10 = (f32[4,8,512]{2,1,0:T(8,128)S(1)}, f32[4,8,512]{2,1,0:T(8,128)S(1)}, u32[]{:S(2)}, u32[]{:S(2)}) collective-permute-start(f32[4,8,512]{2,1,0:T(8,128)S(1)} %fusion.2), channel_id=1, source_target_pairs={{0,4},{1,5},{2,6},{3,7},{4,0},{5,1},{6,2},{7,3},{8,12},{9,13},{10,... | collective-permute-start | bytes 196616 | tf_op jit(solution)/shard_map/ppermute | solution.py:612
  55.3 6.2 %collective-permute-start.12 = (f32[4,8,512]{2,1,0:T(8,128)S(1)}, f32[4,8,512]{2,1,0:T(8,128)S(1)}, u32[]{:S(2)}, u32[]{:S(2)}) collective-permute-start(f32[4,8,512]{2,1,0:T(8,128)S(1)} %fusion.1), channel_id=1, source_target_pairs={{0,6},{1,7},{2,4},{3,5},{4,2},{5,3},{6,0},{7,1},{8,14},{9,15},{10,... | collective-permute-start | bytes 196616 | tf_op jit(solution)/shard_map/ppermute | solution.py:612
  56.8 5.0 %collective-permute-start.8 = (f32[4,8,512]{2,1,0:T(8,128)S(1)}, f32[4,8,512]{2,1,0:T(8,128)S(1)}, u32[]{:S(2)}, u32[]{:S(2)}) collective-permute-start(f32[4,8,512]{2,1,0:T(8,128)S(1)} %slice_bitcast_fusion), channel_id=1, source_target_pairs={{0,2},{1,3},{2,0},{3,1},{4,6},{5,7},{6,4},{7,5},{8,10},{9,11},{10,... | collective-permute-start | bytes 196616 | tf_op jit(solution)/shard_map/ppermute | solution.py:612

commit v16 on v15

--- a/solution.py
+++ b/solution.py
@@ -395,15 +395,17 @@
     edge_smooth(0, flags, order, plane, smoothed, planes, ends, halo)
     if split:
         tile_of = half_tiles(order, *split, 1 - order[1])
-        render_half(scale, order[1] == 1, ends, behind, images[0], tile_of, 0)
+        for part, image in enumerate(images):
+            render_half(scale, order[1] == 1, ends, behind, image, tile_of, part)
     else:
         tiles = plane.shape[1] // 8 - 2
         edge_render(scale, order[1] == 1, ends, behind, images[0], tiles, lambda place: place)
 
 
-def part_edge_kernel(scale, split, half, kept, order, ends, behind, image):
-    tile_of = half_tiles(order, *split, order[1] if kept else 1 - order[1])
-    render_half(scale, order[1] == 1, ends, behind, image, tile_of, half)
+def part_edge_kernel(scale, split, parts, order, ends, behind, *images):
+    for (kept, part), image in zip(parts, images):
+        tile_of = half_tiles(order, *split, order[1] if kept else 1 - order[1])
+        render_half(scale, order[1] == 1, ends, behind, image, tile_of, part)
 
 
 def whole(count):
@@ -535,7 +537,9 @@
     _, ext, columns = plane.shape
     f32 = jnp.float32
     rows = ext - 2 * PAD
-    images = [part_shape(split, 0, columns) if split else (4, rows, columns)]
+    images = [(4, rows, columns)]
+    if split:
+        images = [part_shape(split, part, columns) for part in range(2)]
     shapes = [*images, (REACH + 2, ext, columns)]
     return pl.pallas_call(
         functools.partial(last_edge_kernel, scale, split),
@@ -553,13 +557,13 @@
     )(flags, order, plane, *operands)
 
 
-def call_part_edge(scale, split, half, kept, order, ends, behind):
-    image = jax.ShapeDtypeStruct(part_shape(split, half, ends.shape[2]), jnp.float32)
-    return pl.pallas_call(
-        functools.partial(part_edge_kernel, scale, split, half, kept),
-        out_shape=image,
+def call_part_edge(scale, split, parts, order, ends, behind):
+    shapes = [part_shape(split, part, ends.shape[2]) for _, part in parts]
+    return pl.pallas_call(
+        functools.partial(part_edge_kernel, scale, split, parts),
+        out_shape=tuple(jax.ShapeDtypeStruct(shape, jnp.float32) for shape in shapes),
         in_specs=[smem()] + whole(2),
-        out_specs=whole(1)[0],
+        out_specs=tuple(whole(len(shapes))),
         compiler_params=params(12),
         cost_estimate=cost(200_000_000),
     )(order, ends, behind)
@@ -674,8 +678,11 @@
     )
     if split:
         last = (order, ends, layers)
-        sends += [call_part_edge(scale, split, part, False, *last) for part in (1, 2)]
-        keeps = [call_part_edge(scale, split, part, True, *last) for part in range(3)]
+        sent_2, kept_0 = call_part_edge(scale, split, ((False, 2), (True, 0)), *last)
+        (kept_1,) = call_part_edge(scale, split, ((True, 1),), *last)
+        (kept_2,) = call_part_edge(scale, split, ((True, 2),), *last)
+        sends.append(sent_2)
+        keeps = [kept_0, kept_1, kept_2]
     else:
         sends, keeps = halves_of(sends[0])
     return exchange(sends, keeps)

time: 62.9 us -> 61.7 us (0.981)
  Pallas kernels: 28 us -> 26.8 us
    pallas_call x5 -> x3, Pallas kernels: 3.68 us -> 2.41 us  [call_part_edge(): pl.pallas_call(functools.partial(part_edge_kernel, scale, split, parts),...]
where the time goes in v16:
time: 61.7 us; the launch traced here: 61.4 us
  Pallas kernels  26.8 us (43%)
  starting transfers between devices  20.6 us (33%)
  waiting for transfers between devices  12.6 us (20%)
  other arithmetic  1.06 us (2%)
    ppermute x10, starting transfers between devices, swap(): return lax.ppermute(value, axis, pairs)  16.4 us
    ppermute x10, waiting for transfers between devices, swap(): return lax.ppermute(value, axis, pairs)  7.63 us
    pallas_call x1, Pallas kernels, call_smooth(): pl.pallas_call(functools.partial(smooth_kernel, group), out_shape=jax.Sha...  5.23 us
    ppermute x3, waiting for transfers between devices, exchange(): lax.ppermute(piece, 'depth', [(i, i ^ 2 * step) for i in range(count)])  4.93 us
    pallas_call x1, Pallas kernels, call_depth(): pl.pallas_call(depth_kernel, out_shape=(jax.ShapeDtypeStruct(partial.shap...  4.29 us
    pallas_call x1, Pallas kernels, call_interior(): pl.pallas_call(functools.partial(interior_kernel, scale), out_shape=jax.S...  4.19 us
    ppermute x3, starting transfers between devices, exchange(): lax.ppermute(piece, 'depth', [(i, i ^ 2 * step) for i in range(count)])  4.15 us
    pallas_call x1, Pallas kernels, call_pack_rest(): pl.pallas_call(pack_rest_kernel, out_shape=(side, edge, middle, side), in...  3.14 us
  transfers between devices with their start and end apart: 13, of which 5 were waited for; matrix products, arithmetic and copies ran while one was open for 1% of the time, Pallas kernels for 36%

profile of v16, /device:TPU:0, one launch (start us, length us, event | category | flops | bytes accessed | tf_op | source)
XLA Modules:
  0.0 61.4 jit_solution(3791502077530403649)
XLA Ops:
  0.1 1.7 %pack_block.1 = s32[5,64,512]{2,1,0:T(8,128)S(1)} custom-call(s32[4]{0:T(128)S(1)} %pad_add_fusion.3.where, s32[32,64,512]{2,1,0:T(8,128)} %c.3), custom_call_target="tpu_custom_call" | custom-call | tf_op jit(solution)/shard_map/pack_block/pallas_call | solution.py:433
  1.8 0.7 %collective-permute-start.4 = (s32[5,64,512]{2,1,0:T(8,128)S(1)}, s32[5,64,512]{2,1,0:T(8,128)S(1)}, u32[]{:S(2)}, u32[]{:S(2)}) collective-permute-start(s32[5,64,512]{2,1,0:T(8,128)S(1)} %pack_block.1), channel_id=1, source_target_pairs={{1,2},{2,1},{3,4},{4,3},{5,6},{6,5},{9,10},{10,9},{11,12},{12,11},... | collective-permute-start | bytes 1966088 | tf_op jit(solution)/shard_map/ppermute | solution.py:577
  2.5 3.1 %pack_rest.1 = (s32[32,8,512]{2,1,0:T(8,128)}, s32[5,16,512]{2,1,0:T(8,128)S(1)}, s32[5,48,512]{2,1,0:T(8,128)}, s32[32,8,512]{2,1,0:T(8,128)}) custom-call(s32[4]{0:T(128)S(1)} %pad_add_fusion.3.where, s32[32,64,512]{2,1,0:T(8,128)} %c.3), custom_call_target="tpu_custom_call" | custom-call | tf_op jit(solution)/shard_map/pack_rest/pallas_call | solution.py:449
  6.3 1.5 %collective-permute-start.1 = (s32[32,8,512]{2,1,0:T(8,128)}, s32[32,8,512]{2,1,0:T(8,128)}, u32[]{:S(2)}, u32[]{:S(2)}) collective-permute-start(s32[32,8,512]{2,1,0:T(8,128)} %get-tuple-element.17), channel_id=1, source_target_pairs={{8,16},{16,8},{9,17},{17,9},{10,18},{18,10},{11,19},{19,11},{12,20... | collective-permute-start | bytes 1572872 | tf_op jit(solution)/shard_map/ppermute | solution.py:577
  7.7 5.3 %collective-permute-start.3 = (s32[5,16,512]{2,1,0:T(8,128)S(1)}, s32[5,16,512]{2,1,0:T(8,128)S(1)}, u32[]{:S(2)}, u32[]{:S(2)}) collective-permute-start(s32[5,16,512]{2,1,0:T(8,128)S(1)} %get-tuple-element.21), channel_id=1, source_target_pairs={{0,1},{1,0},{2,3},{3,2},{4,5},{5,4},{6,7},{7,6},{8,9},{9,8},{10,11... | collective-permute-start | bytes 491528 | tf_op jit(solution)/shard_map/ppermute | solution.py:577
  13.1 5.2 %smooth.1.partial = f32[32,80,512]{2,1,0:T(8,128)S(1)} custom-call(s32[32,64,512]{2,1,0:T(8,128)} %c.3, bf16[1024,512]{1,0:T(8,128)(2,1)S(1)} %copy-done, bf16[80,192]{1,0:T(8,128)(2,1)S(1)} %copy-done.3), custom_call_target="tpu_custom_call" | custom-call | flops 1000000000 | bytes 4000000 | tf_op jit(solution)/shard_map/smooth/pallas_call | solution.py:464
  18.4 6.6 %collective-permute-done.3.edge = s32[5,16,512]{2,1,0:T(8,128)S(1)} collective-permute-done((s32[5,16,512]{2,1,0:T(8,128)S(1)}, s32[5,16,512]{2,1,0:T(8,128)S(1)}, u32[]{:S(2)}, u32[]{:S(2)}) %collective-permute-start.3) | collective-permute-done | bytes 163872 | tf_op jit(solution)/shard_map/ppermute | solution.py:577
  25.0 4.3 %depth.1 = (f32[32,80,512]{2,1,0:T(8,128)S(1)}, f32[24,80,512]{2,1,0:T(8,128)S(1)}) custom-call(f32[4]{0:T(128)S(1)} %add_convert_fusion.flags, s32[3]{0:T(128)S(1)} %pad_add_fusion.2.order, f32[32,80,512]{2,1,0:T(8,128)S(1)} %smooth.1.partial, s32[32,8,512]{2,1,0:T(8,128)S(1)} %collective-permute-done.xa, ...), custom_call_target="tpu_custom_call", output_to_operand_aliasing={{0}: (2, {})} | custom-call | flops 500000000 | bytes 4000000 | tf_op jit(solution)/shard_map/depth/pallas_call | solution.py:481
  29.4 0.7 %collective-permute-start.6 = (s32[10,8,512]{2,1,0:T(8,128)S(1)}, s32[10,8,512]{2,1,0:T(8,128)S(1)}, u32[]{:S(2)}, u32[]{:S(2)}) collective-permute-start(s32[10,8,512]{2,1,0:T(8,128)S(1)} %pad_add_fusion.1), channel_id=1, source_target_pairs={{8,16},{16,8},{9,17},{17,9},{10,18},{18,10},{11,19},{19,11},{12,20... | collective-permute-start | bytes 491528 | tf_op jit(solution)/shard_map/ppermute | solution.py:577
  30.1 4.2 %interior.1.behind = f32[4,64,512]{2,1,0:T(8,128)S(1)} custom-call(f32[24,80,512]{2,1,0:T(8,128)S(1)} %get-tuple-element.19.smoothed), custom_call_target="tpu_custom_call" | custom-call | flops 1000000000 | bytes 4000000 | tf_op jit(solution)/shard_map/interior/pallas_call | solution.py:498
  34.3 3.1 %collective-permute-start.5 = (s32[10,8,512]{2,1,0:T(8,128)S(1)}, s32[10,8,512]{2,1,0:T(8,128)S(1)}, u32[]{:S(2)}, u32[]{:S(2)}) collective-permute-start(s32[10,8,512]{2,1,0:T(8,128)S(1)} %pad_add_fusion), channel_id=1, source_target_pairs={{0,8},{8,0},{16,24},{24,16},{1,9},{9,1},{17,25},{25,17},{2,10},{10... | collective-permute-start | bytes 491528 | tf_op jit(solution)/shard_map/ppermute | solution.py:577
  37.5 1.0 %collective-permute-done.5 = s32[10,8,512]{2,1,0:T(8,128)S(1)} collective-permute-done((s32[10,8,512]{2,1,0:T(8,128)S(1)}, s32[10,8,512]{2,1,0:T(8,128)S(1)}, u32[]{:S(2)}, u32[]{:S(2)}) %collective-permute-start.5) | collective-permute-done | bytes 163872 | tf_op jit(solution)/shard_map/ppermute | solution.py:577
  38.5 2.8 %first_edge.1.behind = f32[4,64,512]{2,1,0:T(8,128)S(1)} custom-call(f32[4]{0:T(128)S(1)} %add_convert_fusion.flags, s32[3]{0:T(128)S(1)} %pad_add_fusion.2.order, f32[32,80,512]{2,1,0:T(8,128)S(1)} %get-tuple-element.18.plane, f32[24,80,512]{2,1,0:T(8,128)S(1)} %get-tuple-element.19.smoothed, s32[5,64,512]{2,1,0:T(8,128)S(1)} %collective-permute-done.4.block, ...), custom_call_target="tpu_custom_call" | custom-call | flops 300000000 | bytes 4000000 | tf_op jit(solution)/shard_map/first_edge/pallas_call | solution.py:512
  41.3 3.0 %last_edge.1 = (f32[1,4,8,512]{3,2,1,0:T(8,128)S(1)}, f32[1,4,8,512]{3,2,1,0:T(8,128)S(1)}, f32[7,80,512]{2,1,0:T(8,128)S(1)}) custom-call(f32[4]{0:T(128)S(1)} %add_convert_fusion.flags, s32[3]{0:T(128)S(1)} %pad_add_fusion.2.order, f32[32,80,512]{2,1,0:T(8,128)S(1)} %get-tuple-element.18.plane, f32[24,80,512]{2,1,0:T(8,128)S(1)} %get-tuple-element.19.smoothed, ...), custom_call_target="tpu_custom_call" | custom-call | flops 300000000 | bytes 4000000 | tf_op jit(solution)/shard_map/last_edge/pallas_call | solution.py:544
  44.3 2.5 %collective-permute-start.9 = (f32[1,4,8,512]{3,2,1,0:T(8,128)S(1)}, f32[1,4,8,512]{3,2,1,0:T(8,128)S(1)}, u32[]{:S(2)}, u32[]{:S(2)}) collective-permute-start(f32[1,4,8,512]{3,2,1,0:T(8,128)S(1)} %get-tuple-element.24), channel_id=1, source_target_pairs={{0,1},{1,0},{2,3},{3,2},{4,5},{5,4},{6,7},{7,6},{8,9},{9,8},{10,11... | collective-permute-start | bytes 196616 | tf_op jit(solution)/shard_map/ppermute | solution.py:577
  46.9 0.9 %shard_map.56 = (f32[2,4,8,512]{3,2,1,0:T(8,128)S(1)}, f32[1,4,8,512]{3,2,1,0:T(8,128)S(1)}) custom-call(s32[3]{0:T(128)S(1)} %pad_add_fusion.2.order, f32[7,80,512]{2,1,0:T(8,128)S(1)} %get-tuple-element.22.ends, f32[4,64,512]{2,1,0:T(8,128)S(1)} %first_edge.1.behind), custom_call_target="tpu_custom_call" | custom-call | flops 200000000 | bytes 4000000 | tf_op jit(solution)/shard_map/pallas_call | solution.py:562
  47.9 2.0 %collective-permute-start.7 = (f32[2,4,8,512]{3,2,1,0:T(8,128)S(1)}, f32[2,4,8,512]{3,2,1,0:T(8,128)S(1)}, u32[]{:S(2)}, u32[]{:S(2)}) collective-permute-start(f32[2,4,8,512]{3,2,1,0:T(8,128)S(1)} %get-tuple-element.23), channel_id=1, source_target_pairs={{0,1},{1,0},{2,3},{3,2},{4,5},{5,4},{6,7},{7,6},{8,9},{9,8},{10,11... | collective-permute-start | bytes 393224 | tf_op jit(solution)/shard_map/ppermute | solution.py:577
  49.9 0.7 %shard_map.57 = f32[1,4,8,512]{3,2,1,0:T(8,128)S(1)} custom-call(s32[3]{0:T(128)S(1)} %pad_add_fusion.2.order, f32[7,80,512]{2,1,0:T(8,128)S(1)} %get-tuple-element.22.ends, f32[4,64,512]{2,1,0:T(8,128)S(1)} %first_edge.1.behind), custom_call_target="tpu_custom_call" | custom-call | flops 200000000 | bytes 4000000 | tf_op jit(solution)/shard_map/pallas_call | solution.py:562
  50.6 0.8 %shard_map.55 = f32[2,4,8,512]{3,2,1,0:T(8,128)S(1)} custom-call(s32[3]{0:T(128)S(1)} %pad_add_fusion.2.order, f32[7,80,512]{2,1,0:T(8,128)S(1)} %get-tuple-element.22.ends, f32[4,64,512]{2,1,0:T(8,128)S(1)} %first_edge.1.behind), custom_call_target="tpu_custom_call" | custom-call | flops 200000000 | bytes 4000000 | tf_op jit(solution)/shard_map/pallas_call | solution.py:562
  51.4 2.7 %collective-permute-start.10 = (f32[4,8,512]{2,1,0:T(8,128)S(1)}, f32[4,8,512]{2,1,0:T(8,128)S(1)}, u32[]{:S(2)}, u32[]{:S(2)}) collective-permute-start(f32[4,8,512]{2,1,0:T(8,128)S(1)} %fusion.2), channel_id=1, source_target_pairs={{0,4},{1,5},{2,6},{3,7},{4,0},{5,1},{6,2},{7,3},{8,12},{9,13},{10,... | collective-permute-start | bytes 196616 | tf_op jit(solution)/shard_map/ppermute | solution.py:616
  54.2 1.4 %collective-permute-start.12 = (f32[4,8,512]{2,1,0:T(8,128)S(1)}, f32[4,8,512]{2,1,0:T(8,128)S(1)}, u32[]{:S(2)}, u32[]{:S(2)}) collective-permute-start(f32[4,8,512]{2,1,0:T(8,128)S(1)} %fusion.1), channel_id=1, source_target_pairs={{0,6},{1,7},{2,4},{3,5},{4,2},{5,3},{6,0},{7,1},{8,14},{9,15},{10,... | collective-permute-start | bytes 196616 | tf_op jit(solution)/shard_map/ppermute | solution.py:616
  55.8 3.3 %collective-permute-done.10 = f32[4,8,512]{2,1,0:T(8,128)S(1)} collective-permute-done((f32[4,8,512]{2,1,0:T(8,128)S(1)}, f32[4,8,512]{2,1,0:T(8,128)S(1)}, u32[]{:S(2)}, u32[]{:S(2)}) %collective-permute-start.10) | collective-permute-done | bytes 65568 | tf_op jit(solution)/shard_map/ppermute | solution.py:616
  59.1 1.3 %collective-permute-done.12 = f32[4,8,512]{2,1,0:T(8,128)S(1)} collective-permute-done((f32[4,8,512]{2,1,0:T(8,128)S(1)}, f32[4,8,512]{2,1,0:T(8,128)S(1)}, u32[]{:S(2)}, u32[]{:S(2)}) %collective-permute-start.12) | collective-permute-done | bytes 65568 | tf_op jit(solution)/shard_map/ppermute | solution.py:616
  60.8 0.6 %pad_maximum_fusion.6 = f32[4,8,512]{2,1,0:T(8,128)} fusion(f32[1,8,512]{2,1,0:T(8,128)S(1)} %get-tuple-element.30, f32[1,8,512]{2,1,0:T(8,128)S(1)} %get-tuple-element.57, f32[1,8,512]{2,1,0:T(8,128)S(1)} %get-tuple-element.56, f32[1,8,512]{2,1,0:T(8,128)S(1)} %get-tuple-element.55), kind=kLoop, calls=%fused_computation.14 | loop fusion | flops 49152 | bytes 131072 | tf_op jit(solution)/shard_map/concatenate | solution.py:629
  (44 shorter events, 1.6 us)
Async XLA Ops:
  0.1 13.0 %copy-start = (bf16[1024,512]{1,0:T(8,128)(2,1)S(1)}, bf16[1024,512]{1,0:T(8,128)(2,1)}, u32[]{:S(2)}) copy-start(bf16[1024,512]{1,0:T(8,128)(2,1)} %constant.71.clone.by) | copy-start | bytes 3145732
  0.1 13.0 %copy-start.3 = (bf16[80,192]{1,0:T(8,128)(2,1)S(1)}, bf16[80,192]{1,0:T(8,128)(2,1)}, u32[]{:S(2)}) copy-start(bf16[80,192]{1,0:T(8,128)(2,1)} %constant.73.clone.lx) | copy-start | bytes 92164
  1.8 27.5 %collective-permute-start.4 = (s32[5,64,512]{2,1,0:T(8,128)S(1)}, s32[5,64,512]{2,1,0:T(8,128)S(1)}, u32[]{:S(2)}, u32[]{:S(2)}) collective-permute-start(s32[5,64,512]{2,1,0:T(8,128)S(1)} %pack_block.1), channel_id=1, source_target_pairs={{1,2},{2,1},{3,4},{4,3},{5,6},{6,5},{9,10},{10,9},{11,12},{12,11},... | collective-permute-start | bytes 1966088 | tf_op jit(solution)/shard_map/ppermute | solution.py:577
  5.7 19.3 %collective-permute-start = (s32[32,8,512]{2,1,0:T(8,128)}, s32[32,8,512]{2,1,0:T(8,128)S(1)}, u32[]{:S(2)}, u32[]{:S(2)}) collective-permute-start(s32[32,8,512]{2,1,0:T(8,128)} %get-tuple-element.16), channel_id=1, source_target_pairs={{0,8},{8,0},{16,24},{24,16},{1,9},{9,1},{17,25},{25,17},{2,10},{10... | collective-permute-start | bytes 1572872 | tf_op jit(solution)/shard_map/ppermute | solution.py:577
  6.3 18.8 %collective-permute-start.1 = (s32[32,8,512]{2,1,0:T(8,128)}, s32[32,8,512]{2,1,0:T(8,128)}, u32[]{:S(2)}, u32[]{:S(2)}) collective-permute-start(s32[32,8,512]{2,1,0:T(8,128)} %get-tuple-element.17), channel_id=1, source_target_pairs={{8,16},{16,8},{9,17},{17,9},{10,18},{18,10},{11,19},{19,11},{12,20... | collective-permute-start | bytes 1572872 | tf_op jit(solution)/shard_map/ppermute | solution.py:577
  7.7 17.3 %collective-permute-start.3 = (s32[5,16,512]{2,1,0:T(8,128)S(1)}, s32[5,16,512]{2,1,0:T(8,128)S(1)}, u32[]{:S(2)}, u32[]{:S(2)}) collective-permute-start(s32[5,16,512]{2,1,0:T(8,128)S(1)} %get-tuple-element.21), channel_id=1, source_target_pairs={{0,1},{1,0},{2,3},{3,2},{4,5},{5,4},{6,7},{7,6},{8,9},{9,8},{10,11... | collective-permute-start | bytes 491528 | tf_op jit(solution)/shard_map/ppermute | solution.py:577
  13.0 28.4 %collective-permute-start.2 = (s32[5,48,512]{2,1,0:T(8,128)}, s32[5,48,512]{2,1,0:T(8,128)}, u32[]{:S(2)}, u32[]{:S(2)}) collective-permute-start(s32[5,48,512]{2,1,0:T(8,128)} %get-tuple-element.20), channel_id=1, source_target_pairs={{0,1},{1,0},{2,3},{3,2},{4,5},{5,4},{6,7},{7,6},{8,9},{9,8},{10,11... | collective-permute-start | bytes 1474568 | tf_op jit(solution)/shard_map/ppermute | solution.py:577
  13.1 12.0 %copy-start.2 = (bf16[2,128,192]{2,1,0:T(8,128)(2,1)S(1)}, bf16[2,128,192]{2,1,0:T(8,128)(2,1)}, u32[]{:S(2)}) copy-start(bf16[2,128,192]{2,1,0:T(8,128)(2,1)} %constant.74.clone.lx) | copy-start | bytes 294916
  29.3 9.1 %copy-start.1 = (bf16[2,80,240]{2,1,0:T(8,128)(2,1)S(1)}, bf16[2,80,240]{2,1,0:T(8,128)(2,1)}, u32[]{:S(2)}) copy-start(bf16[2,80,240]{2,1,0:T(8,128)(2,1)} %constant.72.clone.lx) | copy-start | bytes 230404
  29.4 8.0 %collective-permute-start.6 = (s32[10,8,512]{2,1,0:T(8,128)S(1)}, s32[10,8,512]{2,1,0:T(8,128)S(1)}, u32[]{:S(2)}, u32[]{:S(2)}) collective-permute-start(s32[10,8,512]{2,1,0:T(8,128)S(1)} %pad_add_fusion.1), channel_id=1, source_target_pairs={{8,16},{16,8},{9,17},{17,9},{10,18},{18,10},{11,19},{19,11},{12,20... | collective-permute-start | bytes 491528 | tf_op jit(solution)/shard_map/ppermute | solution.py:577
  34.3 4.2 %collective-permute-start.5 = (s32[10,8,512]{2,1,0:T(8,128)S(1)}, s32[10,8,512]{2,1,0:T(8,128)S(1)}, u32[]{:S(2)}, u32[]{:S(2)}) collective-permute-start(s32[10,8,512]{2,1,0:T(8,128)S(1)} %pad_add_fusion), channel_id=1, source_target_pairs={{0,8},{8,0},{16,24},{24,16},{1,9},{9,1},{17,25},{25,17},{2,10},{10... | collective-permute-start | bytes 491528 | tf_op jit(solution)/shard_map/ppermute | solution.py:577
  44.3 7.1 %collective-permute-start.9 = (f32[1,4,8,512]{3,2,1,0:T(8,128)S(1)}, f32[1,4,8,512]{3,2,1,0:T(8,128)S(1)}, u32[]{:S(2)}, u32[]{:S(2)}) collective-permute-start(f32[1,4,8,512]{3,2,1,0:T(8,128)S(1)} %get-tuple-element.24), channel_id=1, source_target_pairs={{0,1},{1,0},{2,3},{3,2},{4,5},{5,4},{6,7},{7,6},{8,9},{9,8},{10,11... | collective-permute-start | bytes 196616 | tf_op jit(solution)/shard_map/ppermute | solution.py:577
  46.9 7.3 %collective-permute-start.11 = (f32[1,4,8,512]{3,2,1,0:T(8,128)S(1)}, f32[1,4,8,512]{3,2,1,0:T(8,128)S(1)}, u32[]{:S(2)}, u32[]{:S(2)}) collective-permute-start(f32[1,4,8,512]{3,2,1,0:T(8,128)S(1)} %get-tuple-element.26), channel_id=1, source_target_pairs={{0,1},{1,0},{2,3},{3,2},{4,5},{5,4},{6,7},{7,6},{8,9},{9,8},{10,11... | collective-permute-start | bytes 196616 | tf_op jit(solution)/shard_map/ppermute | solution.py:577
  47.9 7.7 %collective-permute-start.7 = (f32[2,4,8,512]{3,2,1,0:T(8,128)S(1)}, f32[2,4,8,512]{3,2,1,0:T(8,128)S(1)}, u32[]{:S(2)}, u32[]{:S(2)}) collective-permute-start(f32[2,4,8,512]{3,2,1,0:T(8,128)S(1)} %get-tuple-element.23), channel_id=1, source_target_pairs={{0,1},{1,0},{2,3},{3,2},{4,5},{5,4},{6,7},{7,6},{8,9},{9,8},{10,11... | collective-permute-start | bytes 393224 | tf_op jit(solution)/shard_map/ppermute | solution.py:577
  51.4 7.6 %collective-permute-start.10 = (f32[4,8,512]{2,1,0:T(8,128)S(1)}, f32[4,8,512]{2,1,0:T(8,128)S(1)}, u32[]{:S(2)}, u32[]{:S(2)}) collective-permute-start(f32[4,8,512]{2,1,0:T(8,128)S(1)} %fusion.2), channel_id=1, source_target_pairs={{0,4},{1,5},{2,6},{3,7},{4,0},{5,1},{6,2},{7,3},{8,12},{9,13},{10,... | collective-permute-start | bytes 196616 | tf_op jit(solution)/shard_map/ppermute | solution.py:616
  54.2 6.2 %collective-permute-start.12 = (f32[4,8,512]{2,1,0:T(8,128)S(1)}, f32[4,8,512]{2,1,0:T(8,128)S(1)}, u32[]{:S(2)}, u32[]{:S(2)}) collective-permute-start(f32[4,8,512]{2,1,0:T(8,128)S(1)} %fusion.1), channel_id=1, source_target_pairs={{0,6},{1,7},{2,4},{3,5},{4,2},{5,3},{6,0},{7,1},{8,14},{9,15},{10,... | collective-permute-start | bytes 196616 | tf_op jit(solution)/shard_map/ppermute | solution.py:616
  55.7 5.0 %collective-permute-start.8 = (f32[4,8,512]{2,1,0:T(8,128)S(1)}, f32[4,8,512]{2,1,0:T(8,128)S(1)}, u32[]{:S(2)}, u32[]{:S(2)}) collective-permute-start(f32[4,8,512]{2,1,0:T(8,128)S(1)} %slice_bitcast_fusion), channel_id=1, source_target_pairs={{0,2},{1,3},{2,0},{3,1},{4,6},{5,7},{6,4},{7,5},{8,10},{9,11},{10,... | collective-permute-start | bytes 196616 | tf_op jit(solution)/shard_map/ppermute | solution.py:616

commit v17 on v16

--- a/solution.py
+++ b/solution.py
@@ -341,9 +341,13 @@
     lax.fori_loop(0, tiles // together, some_tiles, 0)
 
 
+def step_at(pairs, index):
+    return jnp.where(index < 2, pairs - 2 + index, pairs - 1 - index)
+
+
 def half_tiles(order, pairs, owner_tiles, wanted):
     def tile_of(place):
-        pair = order[2] ^ (pairs - 1 - place // owner_tiles)
+        pair = order[2] ^ step_at(pairs, place // owner_tiles)
         return (2 * pair + wanted) * owner_tiles + place % owner_tiles
 
     return tile_of
@@ -582,6 +586,10 @@
     return jnp.concatenate([front[:, :3] + through * back[:, :3], through * back[:, 3:]], 1)
 
 
+def served(pairs):
+    return [pairs - 2, pairs - 1, *reversed(range(pairs - 2))]
+
+
 def halves_of(layers):
     count = lax.axis_size("depth")
     me = lax.axis_index("depth")
@@ -589,7 +597,7 @@
     _, rows, columns = layers.shape
     pieces = layers.reshape(4, pairs, 2, rows // count, columns)
     ordered = jnp.concatenate(
-        [lax.dynamic_slice_in_dim(pieces, pair ^ step, 1, 1) for step in reversed(range(pairs))], 1
+        [lax.dynamic_slice_in_dim(pieces, pair ^ step, 1, 1) for step in served(pairs)], 1
     )
     both = []
     for wanted in (1 - parity, parity):
@@ -610,7 +618,7 @@
         got = swap(send, "depth", 0)
         joined = jnp.where(parity == 0, over(keep, got), over(got, keep))
         for place in range(send.shape[0]):
-            step = pairs - 1 - half - place
+            step = served(pairs)[half + place]
             piece = joined[place]
             if step:
                 piece = lax.ppermute(piece, "depth", [(i, i ^ (2 * step)) for i in range(count)])

time: 61.7 us -> 61.7 us (level)
  no operation moved by 1% of the time
where the time goes in v17:
time: 61.7 us; the launch traced here: 61.4 us
  Pallas kernels  26.8 us (43%)
  starting transfers between devices  20.6 us (33%)
  waiting for transfers between devices  12.6 us (20%)
  other arithmetic  1.06 us (2%)
    ppermute x10, starting transfers between devices, swap(): return lax.ppermute(value, axis, pairs)  16.4 us
    ppermute x10, waiting for transfers between devices, swap(): return lax.ppermute(value, axis, pairs)  7.63 us
    pallas_call x1, Pallas kernels, call_smooth(): pl.pallas_call(functools.partial(smooth_kernel, group), out_shape=jax.Sha...  5.23 us
    ppermute x3, waiting for transfers between devices, exchange(): lax.ppermute(piece, 'depth', [(i, i ^ 2 * step) for i in range(count)])  4.93 us
    pallas_call x1, Pallas kernels, call_depth(): pl.pallas_call(depth_kernel, out_shape=(jax.ShapeDtypeStruct(partial.shap...  4.29 us
    pallas_call x1, Pallas kernels, call_interior(): pl.pallas_call(functools.partial(interior_kernel, scale), out_shape=jax.S...  4.19 us
    ppermute x3, starting transfers between devices, exchange(): lax.ppermute(piece, 'depth', [(i, i ^ 2 * step) for i in range(count)])  4.15 us
    pallas_call x1, Pallas kernels, call_pack_rest(): pl.pallas_call(pack_rest_kernel, out_shape=(side, edge, middle, side), in...  3.14 us
  transfers between devices with their start and end apart: 13, of which 5 were waited for; matrix products, arithmetic and copies ran while one was open for 1% of the time, Pallas kernels for 36%

profile of v17, /device:TPU:0, one launch (start us, length us, event | category | flops | bytes accessed | tf_op | source)
XLA Modules:
  0.0 61.4 jit_solution(6611432353254211661)
XLA Ops:
  0.1 1.7 %pack_block.1 = s32[5,64,512]{2,1,0:T(8,128)S(1)} custom-call(s32[4]{0:T(128)S(1)} %pad_add_fusion.3.where, s32[32,64,512]{2,1,0:T(8,128)} %c.3), custom_call_target="tpu_custom_call" | custom-call | tf_op jit(solution)/shard_map/pack_block/pallas_call | solution.py:437
  1.8 0.7 %collective-permute-start.4 = (s32[5,64,512]{2,1,0:T(8,128)S(1)}, s32[5,64,512]{2,1,0:T(8,128)S(1)}, u32[]{:S(2)}, u32[]{:S(2)}) collective-permute-start(s32[5,64,512]{2,1,0:T(8,128)S(1)} %pack_block.1), channel_id=1, source_target_pairs={{1,2},{2,1},{3,4},{4,3},{5,6},{6,5},{9,10},{10,9},{11,12},{12,11},... | collective-permute-start | bytes 1966088 | tf_op jit(solution)/shard_map/ppermute | solution.py:581
  2.5 3.1 %pack_rest.1 = (s32[32,8,512]{2,1,0:T(8,128)}, s32[5,16,512]{2,1,0:T(8,128)S(1)}, s32[5,48,512]{2,1,0:T(8,128)}, s32[32,8,512]{2,1,0:T(8,128)}) custom-call(s32[4]{0:T(128)S(1)} %pad_add_fusion.3.where, s32[32,64,512]{2,1,0:T(8,128)} %c.3), custom_call_target="tpu_custom_call" | custom-call | tf_op jit(solution)/shard_map/pack_rest/pallas_call | solution.py:453
  6.3 1.5 %collective-permute-start.1 = (s32[32,8,512]{2,1,0:T(8,128)}, s32[32,8,512]{2,1,0:T(8,128)}, u32[]{:S(2)}, u32[]{:S(2)}) collective-permute-start(s32[32,8,512]{2,1,0:T(8,128)} %get-tuple-element.17), channel_id=1, source_target_pairs={{8,16},{16,8},{9,17},{17,9},{10,18},{18,10},{11,19},{19,11},{12,20... | collective-permute-start | bytes 1572872 | tf_op jit(solution)/shard_map/ppermute | solution.py:581
  7.7 5.3 %collective-permute-start.3 = (s32[5,16,512]{2,1,0:T(8,128)S(1)}, s32[5,16,512]{2,1,0:T(8,128)S(1)}, u32[]{:S(2)}, u32[]{:S(2)}) collective-permute-start(s32[5,16,512]{2,1,0:T(8,128)S(1)} %get-tuple-element.21), channel_id=1, source_target_pairs={{0,1},{1,0},{2,3},{3,2},{4,5},{5,4},{6,7},{7,6},{8,9},{9,8},{10,11... | collective-permute-start | bytes 491528 | tf_op jit(solution)/shard_map/ppermute | solution.py:581
  13.1 5.2 %smooth.1.partial = f32[32,80,512]{2,1,0:T(8,128)S(1)} custom-call(s32[32,64,512]{2,1,0:T(8,128)} %c.3, bf16[1024,512]{1,0:T(8,128)(2,1)S(1)} %copy-done, bf16[80,192]{1,0:T(8,128)(2,1)S(1)} %copy-done.3), custom_call_target="tpu_custom_call" | custom-call | flops 1000000000 | bytes 4000000 | tf_op jit(solution)/shard_map/smooth/pallas_call | solution.py:468
  18.4 6.6 %collective-permute-done.3.edge = s32[5,16,512]{2,1,0:T(8,128)S(1)} collective-permute-done((s32[5,16,512]{2,1,0:T(8,128)S(1)}, s32[5,16,512]{2,1,0:T(8,128)S(1)}, u32[]{:S(2)}, u32[]{:S(2)}) %collective-permute-start.3) | collective-permute-done | bytes 163872 | tf_op jit(solution)/shard_map/ppermute | solution.py:581
  25.0 4.3 %depth.1 = (f32[32,80,512]{2,1,0:T(8,128)S(1)}, f32[24,80,512]{2,1,0:T(8,128)S(1)}) custom-call(f32[4]{0:T(128)S(1)} %add_convert_fusion.flags, s32[3]{0:T(128)S(1)} %pad_add_fusion.2.order, f32[32,80,512]{2,1,0:T(8,128)S(1)} %smooth.1.partial, s32[32,8,512]{2,1,0:T(8,128)S(1)} %collective-permute-done.xa, ...), custom_call_target="tpu_custom_call", output_to_operand_aliasing={{0}: (2, {})} | custom-call | flops 500000000 | bytes 4000000 | tf_op jit(solution)/shard_map/depth/pallas_call | solution.py:485
  29.4 0.7 %collective-permute-start.6 = (s32[10,8,512]{2,1,0:T(8,128)S(1)}, s32[10,8,512]{2,1,0:T(8,128)S(1)}, u32[]{:S(2)}, u32[]{:S(2)}) collective-permute-start(s32[10,8,512]{2,1,0:T(8,128)S(1)} %pad_add_fusion.1), channel_id=1, source_target_pairs={{8,16},{16,8},{9,17},{17,9},{10,18},{18,10},{11,19},{19,11},{12,20... | collective-permute-start | bytes 491528 | tf_op jit(solution)/shard_map/ppermute | solution.py:581
  30.1 4.2 %interior.1.behind = f32[4,64,512]{2,1,0:T(8,128)S(1)} custom-call(f32[24,80,512]{2,1,0:T(8,128)S(1)} %get-tuple-element.19.smoothed), custom_call_target="tpu_custom_call" | custom-call | flops 1000000000 | bytes 4000000 | tf_op jit(solution)/shard_map/interior/pallas_call | solution.py:502
  34.3 3.1 %collective-permute-start.5 = (s32[10,8,512]{2,1,0:T(8,128)S(1)}, s32[10,8,512]{2,1,0:T(8,128)S(1)}, u32[]{:S(2)}, u32[]{:S(2)}) collective-permute-start(s32[10,8,512]{2,1,0:T(8,128)S(1)} %pad_add_fusion), channel_id=1, source_target_pairs={{0,8},{8,0},{16,24},{24,16},{1,9},{9,1},{17,25},{25,17},{2,10},{10... | collective-permute-start | bytes 491528 | tf_op jit(solution)/shard_map/ppermute | solution.py:581
  37.5 1.0 %collective-permute-done.5 = s32[10,8,512]{2,1,0:T(8,128)S(1)} collective-permute-done((s32[10,8,512]{2,1,0:T(8,128)S(1)}, s32[10,8,512]{2,1,0:T(8,128)S(1)}, u32[]{:S(2)}, u32[]{:S(2)}) %collective-permute-start.5) | collective-permute-done | bytes 163872 | tf_op jit(solution)/shard_map/ppermute | solution.py:581
  38.5 2.8 %first_edge.1.behind = f32[4,64,512]{2,1,0:T(8,128)S(1)} custom-call(f32[4]{0:T(128)S(1)} %add_convert_fusion.flags, s32[3]{0:T(128)S(1)} %pad_add_fusion.2.order, f32[32,80,512]{2,1,0:T(8,128)S(1)} %get-tuple-element.18.plane, f32[24,80,512]{2,1,0:T(8,128)S(1)} %get-tuple-element.19.smoothed, s32[5,64,512]{2,1,0:T(8,128)S(1)} %collective-permute-done.4.block, ...), custom_call_target="tpu_custom_call" | custom-call | flops 300000000 | bytes 4000000 | tf_op jit(solution)/shard_map/first_edge/pallas_call | solution.py:516
  41.3 3.0 %last_edge.1 = (f32[1,4,8,512]{3,2,1,0:T(8,128)S(1)}, f32[1,4,8,512]{3,2,1,0:T(8,128)S(1)}, f32[7,80,512]{2,1,0:T(8,128)S(1)}) custom-call(f32[4]{0:T(128)S(1)} %add_convert_fusion.flags, s32[3]{0:T(128)S(1)} %pad_add_fusion.2.order, f32[32,80,512]{2,1,0:T(8,128)S(1)} %get-tuple-element.18.plane, f32[24,80,512]{2,1,0:T(8,128)S(1)} %get-tuple-element.19.smoothed, ...), custom_call_target="tpu_custom_call" | custom-call | flops 300000000 | bytes 4000000 | tf_op jit(solution)/shard_map/last_edge/pallas_call | solution.py:548
  44.3 2.5 %collective-permute-start.9 = (f32[1,4,8,512]{3,2,1,0:T(8,128)S(1)}, f32[1,4,8,512]{3,2,1,0:T(8,128)S(1)}, u32[]{:S(2)}, u32[]{:S(2)}) collective-permute-start(f32[1,4,8,512]{3,2,1,0:T(8,128)S(1)} %get-tuple-element.25), channel_id=1, source_target_pairs={{0,1},{1,0},{2,3},{3,2},{4,5},{5,4},{6,7},{7,6},{8,9},{9,8},{10,11... | collective-permute-start | bytes 196616 | tf_op jit(solution)/shard_map/ppermute | solution.py:581
  46.9 0.9 %shard_map.56 = (f32[2,4,8,512]{3,2,1,0:T(8,128)S(1)}, f32[1,4,8,512]{3,2,1,0:T(8,128)S(1)}) custom-call(s32[3]{0:T(128)S(1)} %pad_add_fusion.2.order, f32[7,80,512]{2,1,0:T(8,128)S(1)} %get-tuple-element.22.ends, f32[4,64,512]{2,1,0:T(8,128)S(1)} %first_edge.1.behind), custom_call_target="tpu_custom_call" | custom-call | flops 200000000 | bytes 4000000 | tf_op jit(solution)/shard_map/pallas_call | solution.py:566
  47.9 2.0 %collective-permute-start.7 = (f32[2,4,8,512]{3,2,1,0:T(8,128)S(1)}, f32[2,4,8,512]{3,2,1,0:T(8,128)S(1)}, u32[]{:S(2)}, u32[]{:S(2)}) collective-permute-start(f32[2,4,8,512]{3,2,1,0:T(8,128)S(1)} %get-tuple-element.23), channel_id=1, source_target_pairs={{0,1},{1,0},{2,3},{3,2},{4,5},{5,4},{6,7},{7,6},{8,9},{9,8},{10,11... | collective-permute-start | bytes 393224 | tf_op jit(solution)/shard_map/ppermute | solution.py:581
  49.9 0.7 %shard_map.57 = f32[1,4,8,512]{3,2,1,0:T(8,128)S(1)} custom-call(s32[3]{0:T(128)S(1)} %pad_add_fusion.2.order, f32[7,80,512]{2,1,0:T(8,128)S(1)} %get-tuple-element.22.ends, f32[4,64,512]{2,1,0:T(8,128)S(1)} %first_edge.1.behind), custom_call_target="tpu_custom_call" | custom-call | flops 200000000 | bytes 4000000 | tf_op jit(solution)/shard_map/pallas_call | solution.py:566
  50.6 0.8 %shard_map.55 = f32[2,4,8,512]{3,2,1,0:T(8,128)S(1)} custom-call(s32[3]{0:T(128)S(1)} %pad_add_fusion.2.order, f32[7,80,512]{2,1,0:T(8,128)S(1)} %get-tuple-element.22.ends, f32[4,64,512]{2,1,0:T(8,128)S(1)} %first_edge.1.behind), custom_call_target="tpu_custom_call" | custom-call | flops 200000000 | bytes 4000000 | tf_op jit(solution)/shard_map/pallas_call | solution.py:566
  51.4 2.7 %collective-permute-start.10 = (f32[4,8,512]{2,1,0:T(8,128)S(1)}, f32[4,8,512]{2,1,0:T(8,128)S(1)}, u32[]{:S(2)}, u32[]{:S(2)}) collective-permute-start(f32[4,8,512]{2,1,0:T(8,128)S(1)} %fusion.2), channel_id=1, source_target_pairs={{0,4},{1,5},{2,6},{3,7},{4,0},{5,1},{6,2},{7,3},{8,12},{9,13},{10,... | collective-permute-start | bytes 196616 | tf_op jit(solution)/shard_map/ppermute | solution.py:624
  54.2 1.4 %collective-permute-start.12 = (f32[4,8,512]{2,1,0:T(8,128)S(1)}, f32[4,8,512]{2,1,0:T(8,128)S(1)}, u32[]{:S(2)}, u32[]{:S(2)}) collective-permute-start(f32[4,8,512]{2,1,0:T(8,128)S(1)} %fusion.1), channel_id=1, source_target_pairs={{0,6},{1,7},{2,4},{3,5},{4,2},{5,3},{6,0},{7,1},{8,14},{9,15},{10,... | collective-permute-start | bytes 196616 | tf_op jit(solution)/shard_map/ppermute | solution.py:624
  55.8 3.3 %collective-permute-done.10 = f32[4,8,512]{2,1,0:T(8,128)S(1)} collective-permute-done((f32[4,8,512]{2,1,0:T(8,128)S(1)}, f32[4,8,512]{2,1,0:T(8,128)S(1)}, u32[]{:S(2)}, u32[]{:S(2)}) %collective-permute-start.10) | collective-permute-done | bytes 65568 | tf_op jit(solution)/shard_map/ppermute | solution.py:624
  59.1 1.3 %collective-permute-done.12 = f32[4,8,512]{2,1,0:T(8,128)S(1)} collective-permute-done((f32[4,8,512]{2,1,0:T(8,128)S(1)}, f32[4,8,512]{2,1,0:T(8,128)S(1)}, u32[]{:S(2)}, u32[]{:S(2)}) %collective-permute-start.12) | collective-permute-done | bytes 65568 | tf_op jit(solution)/shard_map/ppermute | solution.py:624
  60.8 0.6 %pad_maximum_fusion.6 = f32[4,8,512]{2,1,0:T(8,128)} fusion(f32[1,8,512]{2,1,0:T(8,128)S(1)} %get-tuple-element.30, f32[1,8,512]{2,1,0:T(8,128)S(1)} %get-tuple-element.57, f32[1,8,512]{2,1,0:T(8,128)S(1)} %get-tuple-element.56, f32[1,8,512]{2,1,0:T(8,128)S(1)} %get-tuple-element.55), kind=kLoop, calls=%fused_computation.14 | loop fusion | flops 49152 | bytes 131072 | tf_op jit(solution)/shard_map/concatenate | solution.py:637
  (44 shorter events, 1.6 us)
Async XLA Ops:
  0.1 13.0 %copy-start = (bf16[1024,512]{1,0:T(8,128)(2,1)S(1)}, bf16[1024,512]{1,0:T(8,128)(2,1)}, u32[]{:S(2)}) copy-start(bf16[1024,512]{1,0:T(8,128)(2,1)} %constant.71.clone.by) | copy-start | bytes 3145732
  0.1 13.0 %copy-start.3 = (bf16[80,192]{1,0:T(8,128)(2,1)S(1)}, bf16[80,192]{1,0:T(8,128)(2,1)}, u32[]{:S(2)}) copy-start(bf16[80,192]{1,0:T(8,128)(2,1)} %constant.73.clone.lx) | copy-start | bytes 92164
  1.8 27.5 %collective-permute-start.4 = (s32[5,64,512]{2,1,0:T(8,128)S(1)}, s32[5,64,512]{2,1,0:T(8,128)S(1)}, u32[]{:S(2)}, u32[]{:S(2)}) collective-permute-start(s32[5,64,512]{2,1,0:T(8,128)S(1)} %pack_block.1), channel_id=1, source_target_pairs={{1,2},{2,1},{3,4},{4,3},{5,6},{6,5},{9,10},{10,9},{11,12},{12,11},... | collective-permute-start | bytes 1966088 | tf_op jit(solution)/shard_map/ppermute | solution.py:581
  5.7 19.3 %collective-permute-start = (s32[32,8,512]{2,1,0:T(8,128)}, s32[32,8,512]{2,1,0:T(8,128)S(1)}, u32[]{:S(2)}, u32[]{:S(2)}) collective-permute-start(s32[32,8,512]{2,1,0:T(8,128)} %get-tuple-element.16), channel_id=1, source_target_pairs={{0,8},{8,0},{16,24},{24,16},{1,9},{9,1},{17,25},{25,17},{2,10},{10... | collective-permute-start | bytes 1572872 | tf_op jit(solution)/shard_map/ppermute | solution.py:581
  6.3 18.8 %collective-permute-start.1 = (s32[32,8,512]{2,1,0:T(8,128)}, s32[32,8,512]{2,1,0:T(8,128)}, u32[]{:S(2)}, u32[]{:S(2)}) collective-permute-start(s32[32,8,512]{2,1,0:T(8,128)} %get-tuple-element.17), channel_id=1, source_target_pairs={{8,16},{16,8},{9,17},{17,9},{10,18},{18,10},{11,19},{19,11},{12,20... | collective-permute-start | bytes 1572872 | tf_op jit(solution)/shard_map/ppermute | solution.py:581
  7.7 17.3 %collective-permute-start.3 = (s32[5,16,512]{2,1,0:T(8,128)S(1)}, s32[5,16,512]{2,1,0:T(8,128)S(1)}, u32[]{:S(2)}, u32[]{:S(2)}) collective-permute-start(s32[5,16,512]{2,1,0:T(8,128)S(1)} %get-tuple-element.21), channel_id=1, source_target_pairs={{0,1},{1,0},{2,3},{3,2},{4,5},{5,4},{6,7},{7,6},{8,9},{9,8},{10,11... | collective-permute-start | bytes 491528 | tf_op jit(solution)/shard_map/ppermute | solution.py:581
  13.0 28.4 %collective-permute-start.2 = (s32[5,48,512]{2,1,0:T(8,128)}, s32[5,48,512]{2,1,0:T(8,128)}, u32[]{:S(2)}, u32[]{:S(2)}) collective-permute-start(s32[5,48,512]{2,1,0:T(8,128)} %get-tuple-element.20), channel_id=1, source_target_pairs={{0,1},{1,0},{2,3},{3,2},{4,5},{5,4},{6,7},{7,6},{8,9},{9,8},{10,11... | collective-permute-start | bytes 1474568 | tf_op jit(solution)/shard_map/ppermute | solution.py:581
  13.1 12.0 %copy-start.2 = (bf16[2,128,192]{2,1,0:T(8,128)(2,1)S(1)}, bf16[2,128,192]{2,1,0:T(8,128)(2,1)}, u32[]{:S(2)}) copy-start(bf16[2,128,192]{2,1,0:T(8,128)(2,1)} %constant.74.clone.lx) | copy-start | bytes 294916
  29.3 9.1 %copy-start.1 = (bf16[2,80,240]{2,1,0:T(8,128)(2,1)S(1)}, bf16[2,80,240]{2,1,0:T(8,128)(2,1)}, u32[]{:S(2)}) copy-start(bf16[2,80,240]{2,1,0:T(8,128)(2,1)} %constant.72.clone.lx) | copy-start | bytes 230404
  29.4 8.0 %collective-permute-start.6 = (s32[10,8,512]{2,1,0:T(8,128)S(1)}, s32[10,8,512]{2,1,0:T(8,128)S(1)}, u32[]{:S(2)}, u32[]{:S(2)}) collective-permute-start(s32[10,8,512]{2,1,0:T(8,128)S(1)} %pad_add_fusion.1), channel_id=1, source_target_pairs={{8,16},{16,8},{9,17},{17,9},{10,18},{18,10},{11,19},{19,11},{12,20... | collective-permute-start | bytes 491528 | tf_op jit(solution)/shard_map/ppermute | solution.py:581
  34.3 4.2 %collective-permute-start.5 = (s32[10,8,512]{2,1,0:T(8,128)S(1)}, s32[10,8,512]{2,1,0:T(8,128)S(1)}, u32[]{:S(2)}, u32[]{:S(2)}) collective-permute-start(s32[10,8,512]{2,1,0:T(8,128)S(1)} %pad_add_fusion), channel_id=1, source_target_pairs={{0,8},{8,0},{16,24},{24,16},{1,9},{9,1},{17,25},{25,17},{2,10},{10... | collective-permute-start | bytes 491528 | tf_op jit(solution)/shard_map/ppermute | solution.py:581
  44.3 7.1 %collective-permute-start.9 = (f32[1,4,8,512]{3,2,1,0:T(8,128)S(1)}, f32[1,4,8,512]{3,2,1,0:T(8,128)S(1)}, u32[]{:S(2)}, u32[]{:S(2)}) collective-permute-start(f32[1,4,8,512]{3,2,1,0:T(8,128)S(1)} %get-tuple-element.25), channel_id=1, source_target_pairs={{0,1},{1,0},{2,3},{3,2},{4,5},{5,4},{6,7},{7,6},{8,9},{9,8},{10,11... | collective-permute-start | bytes 196616 | tf_op jit(solution)/shard_map/ppermute | solution.py:581
  46.9 7.3 %collective-permute-start.11 = (f32[1,4,8,512]{3,2,1,0:T(8,128)S(1)}, f32[1,4,8,512]{3,2,1,0:T(8,128)S(1)}, u32[]{:S(2)}, u32[]{:S(2)}) collective-permute-start(f32[1,4,8,512]{3,2,1,0:T(8,128)S(1)} %get-tuple-element.26), channel_id=1, source_target_pairs={{0,1},{1,0},{2,3},{3,2},{4,5},{5,4},{6,7},{7,6},{8,9},{9,8},{10,11... | collective-permute-start | bytes 196616 | tf_op jit(solution)/shard_map/ppermute | solution.py:581
  47.9 7.7 %collective-permute-start.7 = (f32[2,4,8,512]{3,2,1,0:T(8,128)S(1)}, f32[2,4,8,512]{3,2,1,0:T(8,128)S(1)}, u32[]{:S(2)}, u32[]{:S(2)}) collective-permute-start(f32[2,4,8,512]{3,2,1,0:T(8,128)S(1)} %get-tuple-element.23), channel_id=1, source_target_pairs={{0,1},{1,0},{2,3},{3,2},{4,5},{5,4},{6,7},{7,6},{8,9},{9,8},{10,11... | collective-permute-start | bytes 393224 | tf_op jit(solution)/shard_map/ppermute | solution.py:581
  51.4 7.6 %collective-permute-start.10 = (f32[4,8,512]{2,1,0:T(8,128)S(1)}, f32[4,8,512]{2,1,0:T(8,128)S(1)}, u32[]{:S(2)}, u32[]{:S(2)}) collective-permute-start(f32[4,8,512]{2,1,0:T(8,128)S(1)} %fusion.2), channel_id=1, source_target_pairs={{0,4},{1,5},{2,6},{3,7},{4,0},{5,1},{6,2},{7,3},{8,12},{9,13},{10,... | collective-permute-start | bytes 196616 | tf_op jit(solution)/shard_map/ppermute | solution.py:624
  54.2 6.2 %collective-permute-start.12 = (f32[4,8,512]{2,1,0:T(8,128)S(1)}, f32[4,8,512]{2,1,0:T(8,128)S(1)}, u32[]{:S(2)}, u32[]{:S(2)}) collective-permute-start(f32[4,8,512]{2,1,0:T(8,128)S(1)} %fusion.1), channel_id=1, source_target_pairs={{0,6},{1,7},{2,4},{3,5},{4,2},{5,3},{6,0},{7,1},{8,14},{9,15},{10,... | collective-permute-start | bytes 196616 | tf_op jit(solution)/shard_map/ppermute | solution.py:624
  55.7 5.0 %collective-permute-start.8 = (f32[4,8,512]{2,1,0:T(8,128)S(1)}, f32[4,8,512]{2,1,0:T(8,128)S(1)}, u32[]{:S(2)}, u32[]{:S(2)}) collective-permute-start(f32[4,8,512]{2,1,0:T(8,128)S(1)} %slice_bitcast_fusion), channel_id=1, source_target_pairs={{0,2},{1,3},{2,0},{3,1},{4,6},{5,7},{6,4},{7,5},{8,10},{9,11},{10,... | collective-permute-start | bytes 196616 | tf_op jit(solution)/shard_map/ppermute | solution.py:624
